TPU v7x, 8 devices: a whole 2x2x1 slice. The times are simulated.
8 devices in a mesh: dp: 2 (over z, y), vp: 4 (over x, core).
Axes of the slice: x: 2, y: 2, z: 1, core: 2. Of those that a mesh axis runs over, the one named last changes fastest.
Arguments:
- hidden: bfloat16 [512, 4096], P('dp'), parts along dimension 0
- w_head: bfloat16 [4096, 64000], P(None, 'vp')
- inv_temp: float32 [512], P('dp'), parts along dimension 0
- target_ids: int32 [512], P('dp'), parts along dimension 0
Outputs:
- output 1: float32 [512, 64000], P(('dp', 'vp')), parts along dimension 0
- output 2: float32 [512], P('dp'), parts along dimension 0
There are 2 independent parts. A program takes and returns all parts, laid end to end along the dimension named above; an argument that names none is the same for every part.
All inputs are finite; a program needn't handle non-finite values.
Results may differ from a plain program's by a relative error of at most 0.001.
Values are sent between devices in bfloat16 or wider.
A program may use at most 1 GiB of HBM per device.

v0:
```python
import jax
import jax.numpy as jnp
from jax import lax
from jax.sharding import PartitionSpec as P, NamedSharding


def solution(mesh):
    group_size = mesh.shape["vp"]

    def local_step(hidden, w_local, inv_temp, target_ids):
        group_index = lax.axis_index("vp")
        local_vocab = w_local.shape[1]
        logits = jnp.dot(hidden, w_local, preferred_element_type=jnp.float32)
        scaled = logits * inv_temp[:, None]
        local_max = jnp.max(scaled, axis=1)
        exp_vals = jnp.exp(scaled - local_max[:, None])
        local_sum = jnp.sum(exp_vals, axis=1)
        shard_stats = lax.all_gather(jnp.stack([local_max, local_sum]), "vp")
        global_max = jnp.max(shard_stats[:, 0], axis=0)
        global_sum = jnp.sum(shard_stats[:, 1] * jnp.exp(shard_stats[:, 0] - global_max[None, :]), axis=0)
        row_scale = jnp.exp(local_max - global_max) / global_sum
        local_cdf = jnp.cumsum(exp_vals * row_scale[:, None], axis=1)
        totals = lax.all_gather(local_cdf[:, -1], "vp")
        earlier = (jnp.arange(group_size) < group_index)[:, None]
        offset = jnp.sum(jnp.where(earlier, totals, 0.0), axis=0)
        cdf_cols = local_cdf + offset[:, None]
        local_ids = target_ids - group_index * local_vocab
        in_shard = (local_ids >= 0) & (local_ids < local_vocab)
        picked = jnp.take_along_axis(cdf_cols, jnp.clip(local_ids, 0, local_vocab - 1)[:, None], axis=1)[:, 0]
        cdf_at_target = lax.psum(jnp.where(in_shard, picked, 0.0), "vp")
        cdf_rows = lax.all_to_all(cdf_cols, "vp", 0, 1, tiled=True)
        return cdf_rows, cdf_at_target

    return jax.shard_map(
        local_step,
        mesh=mesh,
        in_specs=(P("dp", None), P(None, "vp"), P("dp"), P("dp")),
        out_specs=(P(("dp", "vp"), None), P("dp")),
        check_vma=False,
    )
```

profile of v0, /device:TPU:0, one launch (start us, length us, event | category | flops | bytes accessed | tf_op | source)
XLA Modules:
  0.0 516.5 jit_solution(16779865213221294828)
XLA Ops:
  0.6 0.0 copy-start
  0.7 1.6 copy-done
  2.2 54.0 %fusion.10 = (f32[256]{0:T(256)S(1)}, f32[256,16000]{1,0:T(8,128)}) fusion(f32[256]{0:T(256)} %param.6, bf16[256,4096]{1,0:T(8,128)(2,1)S(1)} %copy-done, bf16[4096,16000]{1,0:T(8,128)(2,1)} %param.5), kind=kOutput, calls=%fused_computation.30 | convolution fusion | flops 33562624000 | bytes 149555200 | tf_op jit(solution)/shard_map/dot_general | solution.py:13
  56.2 8.0 %fusion.3 = f32[256]{0:T(256)S(1)} fusion(f32[256,16000]{1,0:T(8,128)} %get-tuple-element.6, f32[256]{0:T(256)S(1)} %get-tuple-element.5), kind=kLoop, calls=%fused_computation.6 | loop fusion | flops 8191744 | bytes 16386048 | tf_op jit(solution)/shard_map/reduce_sum | solution.py:17
  64.2 9.8 %all-gather.2 = f32[4,2,256]{2,1,0:T(2,128)S(1)} all-gather(f32[1,2,256]{2,1,0:T(2,128)S(1)} %maximum_bitcast_fusion), channel_id=2, replica_groups=mesh['dp'=2,'vp'=4] {'vp'}, dimensions={0}, use_global_device_ids=true | all-gather | bytes 10240 | tf_op jit(solution)/shard_map/all_gather | solution.py:18
  74.1 12.0 %fusion.2 = f32[256,16000]{1,0:T(8,128)} fusion(f32[256,16000]{1,0:T(8,128)} %get-tuple-element.6, f32[256]{0:T(256)S(1)} %exponential_divide_fusion, f32[256]{0:T(256)S(1)} %get-tuple-element.5), kind=kLoop, calls=%fused_computation.5 | loop fusion | flops 8192000 | bytes 32770048 | tf_op jit(solution)/shard_map/mul | solution.py:22
  86.1 16.9 %copy.20 = f32[256,16000]{0,1:T(8,128)} copy(f32[256,16000]{1,0:T(8,128)} %fusion.2) | data formatting | bytes 32768000 | tf_op jit(solution)/shard_map/mul | solution.py:22
  102.9 134.4 %fusion = f32[256,125,128]{0,1,2:T(8,128)} fusion(f32[256,125,128]{0,2,1:T(8,128)} %bitcast.33), kind=kOutput, calls=%fused_computation.2 | output fusion | flops 520192000 | bytes 32768000 | tf_op jit(solution)/shard_map/reduce-window
  237.3 0.9 slice_bitcast_fusion
  238.2 0.2 reduce-window.9
  238.4 6.9 %broadcast_add_fusion = f32[256,125,128]{0,1,2:T(8,128)S(1)} fusion(f32[256,125,128]{0,1,2:T(8,128)} %fusion, f32[256,125]{0,1:T(8,128)S(1)} %bitcast.36), kind=kLoop, calls=%fused_computation.7 | loop fusion | flops 4096000 | bytes 32896000 | tf_op jit(solution)/shard_map/reduce_window_sum
  245.3 0.0 copy-start.2
  245.3 5.7 %copy-done.2 = f32[256,125,128]{0,1,2:T(8,128)} copy-done((f32[256,125,128]{0,1,2:T(8,128)}, f32[256,125,128]{0,1,2:T(8,128)S(1)}, u32[]{:S(2)}) %copy-start.2) | copy-done | bytes 16384024
  251.0 11.4 %copy.23 = f32[256,125,128]{0,2,1:T(8,128)} copy(f32[256,125,128]{0,1,2:T(8,128)S(1)} %broadcast_add_fusion) | data formatting | bytes 32768000 | tf_op jit(solution)/shard_map/reduce_window_sum
  262.4 18.3 %copy.22 = f32[256,125,128]{2,1,0:T(8,128)} copy(f32[256,125,128]{0,1,2:T(8,128)} %copy-done.2) | data formatting | bytes 32768000 | tf_op jit(solution)/shard_map/reduce_window_sum
  280.7 0.7 slice.27
  281.4 6.4 %all-gather.1 = f32[1024,1]{0,1:T(1,128)S(1)} all-gather(f32[256,1]{0,1:T(1,128)S(1)} %slice.27), channel_id=3, replica_groups=mesh['dp'=2,'vp'=4] {'vp'}, dimensions={0}, use_global_device_ids=true | all-gather | bytes 5120 | tf_op jit(solution)/shard_map/all_gather | solution.py:23
  287.9 0.5 broadcast.50
  288.4 0.7 reduce.4
  289.1 16.3 %reduce_window_sum.20 = f32[4,64,16000]{2,1,0:T(8,128)} reshape(f32[256,125,128]{2,1,0:T(8,128)} %copy.22) | data formatting | bytes 32768000 | tf_op jit(solution)/shard_map/reduce_window_sum
  305.3 0.1 select_reduce_fusion
  305.4 0.1 add.24
  305.5 11.4 %broadcast_add_fusion.2 = f32[4,64,16000]{2,1,0:T(8,128)} fusion(f32[4,64,16000]{2,1,0:T(8,128)} %reduce_window_sum.20, f32[4,64]{1,0:T(4,128)S(1)} %add.24), kind=kLoop, calls=%fused_computation.9 | loop fusion | flops 4096000 | bytes 32769024 | tf_op jit(solution)/shard_map/add | solution.py:26
  316.9 0.0 copy-start.3
  316.9 7.0 %all-to-all-start = ((f32[4,64,16000]{2,1,0:T(8,128)}), f32[4,64,16000]{2,1,0:T(8,128)}, u32[]{:S(2)}, u32[]{:S(2)}) async-start(f32[4,64,16000]{2,1,0:T(8,128)} %broadcast_add_fusion.2), calls=%async_computation | async-start | bytes 32768000 | tf_op jit(solution)/shard_map/all_to_all | solution.py:31
  324.0 0.0 copy-done.3
  324.1 11.3 %broadcast_add_fusion.1 = f32[256,16000]{0,1:T(8,128)} fusion(f32[256]{0:T(256)S(1)} %select_reduce_fusion, f32[256,125,128]{0,2,1:T(8,128)} %copy.23), kind=kLoop, calls=%fused_computation.8 | loop fusion | flops 4096000 | bytes 32769024 | tf_op jit(solution)/shard_map/add | solution.py:26
  335.3 7.4 %gather_fusion = f32[256]{0:T(256)S(1)} fusion(f32[256,16000]{0,1:T(8,128)} %broadcast_add_fusion.1, s32[256]{0:T(256)S(1)} %bitcast.34), kind=kCustom, calls=%fused_computation | custom fusion | bytes 4096 | tf_op jit(solution)/shard_map/jit(take_along_axis)/gather | solution.py:29
  342.8 161.8 %psum.7 = f32[256]{0:T(256)} all-reduce(f32[256]{0:T(256)S(1)} %and_select_fusion.1), channel_id=1, replica_groups=mesh['dp'=2,'vp'=4] {'vp'}, use_global_device_ids=true, to_apply=%region_7.8 | all-reduce | flops 256 | bytes 2048 | tf_op jit(solution)/shard_map/psum | solution.py:30
  504.6 0.0 all-to-all-done
  504.6 11.5 %copy.27 = f32[4,8,8,16000]{3,2,0,1:T(8,128)} copy(f32[4,8,8,16000]{3,2,1,0:T(8,128)} %bitcast.12) | data formatting | bytes 32768000 | tf_op jit(solution)/shard_map/all_to_all | solution.py:31
  516.1 0.0 copy-done.1
  (12 shorter events, 0.1 us)
Async XLA Ops:
  0.6 1.6 copy-start
  245.3 5.7 %copy-start.2 = (f32[256,125,128]{0,1,2:T(8,128)}, f32[256,125,128]{0,1,2:T(8,128)S(1)}, u32[]{:S(2)}) copy-start(f32[256,125,128]{0,1,2:T(8,128)S(1)} %broadcast_add_fusion) | copy-start | bytes 49152004
  316.9 7.1 %copy-start.3 = (s32[256]{0:T(256)S(1)}, s32[256]{0:T(256)}, u32[]{:S(2)}) copy-start(s32[256]{0:T(256)} %param.7) | copy-start | bytes 3076
  316.9 187.7 %all-to-all-start = ((f32[4,64,16000]{2,1,0:T(8,128)}), f32[4,64,16000]{2,1,0:T(8,128)}, u32[]{:S(2)}, u32[]{:S(2)}) async-start(f32[4,64,16000]{2,1,0:T(8,128)} %broadcast_add_fusion.2), calls=%async_computation | async-start | bytes 32768000 | tf_op jit(solution)/shard_map/all_to_all | solution.py:31
  504.6 11.5 %copy-start.1 = (bf16[256,4096]{1,0:T(8,128)(2,1)S(1)}, bf16[256,4096]{1,0:T(8,128)(2,1)}, u32[]{:S(2)}) copy-start(bf16[256,4096]{1,0:T(8,128)(2,1)} %param.4) | copy-start | bytes 6291460
where the time goes:
time: 524 us; the launch traced here: 516 us
  other arithmetic  185 us (35%)
  blocking collectives  178 us (34%)
  local copies, waits for them, and re-layouts  91.2 us (17%)
  matrix products  54 us (10%)
  starting transfers between devices  7.04 us (1%)
    psum x1, blocking collectives, local_step(): cdf_at_target = lax.psum(jnp.where(in_shard, picked, 0.0), 'vp')  162 us
    another operation x3, other arithmetic  141 us
    dot_general x1, matrix products, local_step(): logits = jnp.dot(hidden, w_local, preferred_element_type=jnp.float32)  54 us
    another operation x4, local copies, waits for them, and re-layouts  46.9 us
    add x2, other arithmetic, local_step(): cdf_cols = local_cdf + offset[:, None]  22.7 us
    mul x1, local copies, waits for them, and re-layouts, local_step(): local_cdf = jnp.cumsum(exp_vals * row_scale[:, None], axis=1)  16.9 us
    mul x1, other arithmetic, local_step(): local_cdf = jnp.cumsum(exp_vals * row_scale[:, None], axis=1)  12 us
    all_to_all x1, local copies, waits for them, and re-layouts, local_step(): cdf_rows = lax.all_to_all(cdf_cols, 'vp', 0, 1, tiled=True)  11.5 us
  transfers between devices with their start and end apart: 1, of which 0 were waited for; matrix products, arithmetic and copies ran while one was open for 4% of the time, Pallas kernels for 0%

commit v1 on v0

v1 whole, which is shorter than its diff:
```python
import functools

import jax
import jax.numpy as jnp
from jax import lax
from jax.experimental import pallas as pl
from jax.experimental.pallas import tpu as pltpu
from jax.sharding import PartitionSpec as P


LANES = 128
UNIT = 640
CHUNKS = (1, 3, 6, 7, 5, 2, 1)


def _to_rows(vec_1xn):
    n = vec_1xn.shape[1]
    return jnp.transpose(jnp.broadcast_to(vec_1xn, (LANES, n)))


def _logits_kernel(cfg, x_ref, w_ref, invt_ref, tgt_ref, *refs):
    n_dev, shard, base, first, last = cfg
    refs = list(refs)
    if first:
        m_in = s_in = t_in = None
    else:
        m_in, s_in, t_in = refs[:3]
        refs = refs[3:]
    outs, refs = refs[:n_dev], refs[n_dev:]
    m_ref, s_ref, t_ref = refs[:3]
    refs = refs[3:]
    if last:
        pack_ref = refs.pop(0)
    z_ref, invt_rows, tgt_rows = refs
    step = pl.program_id(0)
    me = lax.axis_index("vp")
    rows = x_ref.shape[0] // n_dev

    @pl.when(step == 0)
    def _():
        invt_rows[...] = _to_rows(invt_ref[...])
        tgt_rows[...] = _to_rows(tgt_ref[...].astype(jnp.float32))
        if first:
            m_ref[...] = jnp.full(m_ref.shape, -jnp.inf, jnp.float32)
            s_ref[...] = jnp.zeros_like(s_ref)
            t_ref[...] = jnp.zeros_like(t_ref)
        else:
            m_ref[...] = m_in[...]
            s_ref[...] = s_in[...]
            t_ref[...] = t_in[...]

    z_ref[...] = jnp.dot(x_ref[...], w_ref[...], preferred_element_type=jnp.float32)
    col0 = me * shard + base + step * UNIT
    lane = lax.broadcasted_iota(jnp.int32, (rows, LANES), 1)
    for p in range(n_dev):
        block = pl.ds(pl.multiple_of((me ^ p) * rows, rows), rows)
        scale = invt_rows[block, :]
        tiles = [z_ref[block, t * LANES:(t + 1) * LANES] * scale for t in range(UNIT // LANES)]
        for t, tile in enumerate(tiles):
            outs[p][:, t * LANES:(t + 1) * LANES] = tile
        m_old = m_ref[block, :]
        m_new = functools.reduce(jnp.maximum, tiles, m_old)
        keep = jnp.exp(m_old - m_new)
        total = s_ref[block, :] * keep
        upto = t_ref[block, :] * keep
        target = tgt_rows[block, :]
        for t, tile in enumerate(tiles):
            e = jnp.exp(tile - m_new)
            cols = (lane + (col0 + t * LANES)).astype(jnp.float32)
            total += e
            upto += jnp.where(cols <= target, e, 0.0)
        m_ref[block, :] = m_new
        s_ref[block, :] = total
        t_ref[block, :] = upto

    if last:
        @pl.when(step == pl.num_programs(0) - 1)
        def _():
            m = m_ref[...]
            m_row = jnp.max(m, axis=1, keepdims=True)
            keep = jnp.exp(m - m_row)
            s_row = jnp.sum(s_ref[...] * keep, axis=1, keepdims=True)
            t_row = jnp.sum(t_ref[...] * keep, axis=1, keepdims=True)
            which = lax.broadcasted_iota(jnp.int32, m.shape, 1)
            packed = jnp.where(which == 0, m_row, jnp.where(which == 1, s_row, t_row))
            pack_ref[...] = jnp.transpose(packed)[:8, :]


def _logits(x, w, invt, tgt, stats, n_dev, unit0, units, last):
    batch, depth = x.shape
    shard = w.shape[1]
    rows = batch // n_dev
    first = stats is None
    whole = lambda a: pl.BlockSpec(a, lambda i: (0, 0))
    stat = jax.ShapeDtypeStruct((batch, LANES), jnp.float32)
    out_shape = [jax.ShapeDtypeStruct((rows, units * UNIT), jnp.float32)] * n_dev + [stat] * 3
    out_specs = [pl.BlockSpec((rows, UNIT), lambda i: (0, i))] * n_dev + [whole((batch, LANES))] * 3
    if last:
        out_shape.append(jax.ShapeDtypeStruct((8, batch), jnp.float32))
        out_specs.append(whole((8, batch)))
    in_specs = [
        whole((batch, depth)),
        pl.BlockSpec((depth, UNIT), lambda i: (0, unit0 + i)),
        whole((1, batch)),
        whole((1, batch)),
    ] + ([] if first else [whole((batch, LANES))] * 3)
    cfg = (n_dev, shard, unit0 * UNIT, first, last)
    res = pl.pallas_call(
        functools.partial(_logits_kernel, cfg),
        grid=(units,),
        in_specs=in_specs,
        out_specs=out_specs,
        out_shape=out_shape,
        scratch_shapes=[
            pltpu.VMEM((batch, UNIT), jnp.float32),
            pltpu.VMEM((batch, LANES), jnp.float32),
            pltpu.VMEM((batch, LANES), jnp.float32),
        ],
        compiler_params=pltpu.CompilerParams(
            dimension_semantics=("arbitrary",), vmem_limit_bytes=40 * 2**20
        ),
        cost_estimate=pl.CostEstimate(
            flops=2 * batch * depth * units * UNIT,
            bytes_accessed=2 * depth * (units * UNIT + batch),
            transcendentals=batch * units * UNIT,
        ),
        name="logits",
    )(x, w, invt, tgt, *(() if first else stats))
    return res[:n_dev], res[n_dev:n_dev + 3], (res[n_dev + 3] if last else None)


def _merge_kernel(n_dev, *refs):
    stats, (params_ref, at_ref) = refs[:n_dev], refs[n_dev:]
    me = lax.axis_index("vp")
    batch = stats[0].shape[1]
    rows = batch // n_dev
    ms = [s[0:1, :] for s in stats]
    top = functools.reduce(jnp.maximum, ms)
    keep = [jnp.exp(m - top) for m in ms]
    mass = [s[1:2, :] * k for s, k in zip(stats, keep)]
    upto = sum(s[2:3, :] * k for s, k in zip(stats, keep))
    total = sum(mass)
    at_ref[...] = upto / total
    values = [top, 1.0 / total]
    for p in range(n_dev):
        start = jnp.zeros_like(total)
        for q in range(n_dev):
            start += jnp.where((me ^ q) < (me ^ p), mass[q], 0.0)
        values.append(start)
    which = lax.broadcasted_iota(jnp.int32, (LANES, batch), 0)
    table = jnp.zeros((LANES, batch), jnp.float32)
    for i, v in enumerate(values):
        table = jnp.where(which == i, v, table)
    per_row = jnp.transpose(table)
    out = jnp.zeros((rows, LANES), jnp.float32)
    for d in range(n_dev):
        out = jnp.where(me == d, per_row[d * rows:(d + 1) * rows, :], out)
    params_ref[...] = out


def _merge(stats):
    n_dev = len(stats)
    batch = stats[0].shape[1]
    vmem = pl.BlockSpec(memory_space=pltpu.VMEM)
    return pl.pallas_call(
        functools.partial(_merge_kernel, n_dev),
        in_specs=[vmem] * n_dev,
        out_specs=[vmem] * 2,
        out_shape=[
            jax.ShapeDtypeStruct((batch // n_dev, LANES), jnp.float32),
            jax.ShapeDtypeStruct((1, batch), jnp.float32),
        ],
        cost_estimate=pl.CostEstimate(flops=100_000, bytes_accessed=100_000, transcendentals=1000),
        name="merge",
    )(*stats)


def _cdf_kernel(cfg, *refs):
    peers, shard, base, units, first = cfg
    n = len(peers)
    params_ref = refs[n]
    out_ref, params_out, y_ref, sems = refs[n + (1 if first else 2):]
    me = lax.axis_index("vp")
    rows = params_ref.shape[0]
    tiles = UNIT // LANES
    params = params_ref[...]
    top = jnp.broadcast_to(params[:, 0:1], (rows, LANES))
    inv = jnp.broadcast_to(params[:, 1:2], (rows, LANES))
    k_id = lax.broadcasted_iota(jnp.int32, (3 * LANES, LANES), 0) % LANES
    n_id = lax.broadcasted_iota(jnp.int32, (3 * LANES, LANES), 1)
    tri = jnp.where(k_id <= n_id, 1.0, 0.0).astype(jnp.bfloat16)
    lane = lax.broadcasted_iota(jnp.int32, (rows, LANES), 1)
    updated = params
    copies = []
    for j, p in enumerate(peers):
        z_ref = refs[j]

        def unit(u, carry):
            def cols(t):
                return pl.ds(pl.multiple_of(u * UNIT, UNIT) + t * LANES, LANES)

            e = jnp.concatenate([jnp.exp(z_ref[:, cols(t)] - top) for t in range(tiles)], axis=0)
            hi = e.astype(jnp.bfloat16)
            r1 = e - hi.astype(jnp.float32)
            mid = r1.astype(jnp.bfloat16)
            lo = (r1 - mid.astype(jnp.float32)).astype(jnp.bfloat16)
            prefix = jnp.dot(
                jnp.concatenate([hi, mid, lo], axis=1), tri, preferred_element_type=jnp.float32
            )
            for t in range(tiles):
                part = prefix[t * rows:(t + 1) * rows, :] + carry
                y_ref[j, :, cols(t)] = part * inv
                carry = jnp.broadcast_to(part[:, LANES - 1:LANES], (rows, LANES))
            return carry

        start = jnp.broadcast_to(params[:, 2 + p:3 + p], (rows, LANES))
        end = lax.fori_loop(0, units, unit, start)
        updated = jnp.where(lane == 2 + p, end, updated)
        where = pl.multiple_of((me ^ p) * shard + base, LANES)
        copy = pltpu.make_async_copy(
            y_ref.at[j], out_ref.at[:, pl.ds(where, units * UNIT)], sems.at[j]
        )
        copy.start()
        copies.append(copy)
    params_out[...] = updated
    for copy in copies:
        copy.wait()


def _cdf(blocks, peers, params, out, n_dev, shard, unit0):
    rows, width = blocks[0].shape
    n = len(peers)
    first = out is None
    vmem = pl.BlockSpec(memory_space=pltpu.VMEM)
    hbm = pl.BlockSpec(memory_space=pl.ANY)
    cfg = (peers, shard, unit0 * UNIT, width // UNIT, first)
    return pl.pallas_call(
        functools.partial(_cdf_kernel, cfg),
        in_specs=[vmem] * (n + 1) + ([] if first else [hbm]),
        out_specs=[hbm, vmem],
        out_shape=[
            jax.ShapeDtypeStruct((rows, n_dev * shard), jnp.float32),
            jax.ShapeDtypeStruct(params.shape, jnp.float32),
        ],
        scratch_shapes=[
            pltpu.VMEM((n, rows, width), jnp.float32),
            pltpu.SemaphoreType.DMA((n,)),
        ],
        input_output_aliases={} if first else {n + 1: 0},
        compiler_params=pltpu.CompilerParams(vmem_limit_bytes=32 * 2**20),
        cost_estimate=pl.CostEstimate(
            flops=n * 2 * rows * width * 384,
            bytes_accessed=n * rows * width * 8,
            transcendentals=n * rows * width,
        ),
        name="cdf",
    )(*blocks, params, *(() if first else (out,)))


def solution(mesh):
    n_dev = mesh.shape["vp"]

    def swap(a, p):
        return lax.ppermute(a, "vp", [(i, i ^ p) for i in range(n_dev)])

    def local_step(hidden, w_local, inv_temp, target_ids):
        shard = w_local.shape[1]
        invt = inv_temp.reshape(1, -1)
        tgt = target_ids.reshape(1, -1)
        starts = [sum(CHUNKS[:k]) for k in range(len(CHUNKS))]
        stats, chunks = None, []
        for k, units in enumerate(CHUNKS):
            blocks, stats, packed = _logits(
                hidden, w_local, invt, tgt, stats, n_dev, starts[k], units, k == len(CHUNKS) - 1
            )
            got = [blocks[0]]
            for p in range(1, n_dev):
                got.append(swap(blocks[p], p))
            chunks.append(got)
        packs = [packed]
        for p in range(1, n_dev):
            packs.append(swap(packed, p))
        params, at_target = _merge(packs)
        out = None
        for k in range(len(CHUNKS)):
            out, params = _cdf(chunks[k][:2], (0, 1), params, out, n_dev, shard, starts[k])
        for k in range(len(CHUNKS)):
            out, params = _cdf(chunks[k][2:], (2, 3), params, out, n_dev, shard, starts[k])
        return out, at_target.reshape(-1)

    return jax.shard_map(
        local_step,
        mesh=mesh,
        in_specs=(P("dp", None), P(None, "vp"), P("dp"), P("dp")),
        out_specs=(P(("dp", "vp"), None), P("dp")),
        check_vma=False,
    )
```

time: 524 us -> 280 us (0.53); the launches traced: 516 us -> 279 us
  other arithmetic: 185 us -> 0 us
  blocking collectives: 178 us -> 0 us
  Pallas kernels: 0 us -> 148 us
  waiting for transfers between devices: 0.01 us -> 86.8 us
  local copies, waits for them, and re-layouts: 91.2 us -> 23.8 us
  matrix products: 54 us -> 0 us
  starting transfers between devices: 7.04 us -> 18.8 us
    psum x1 -> x0, blocking collectives: 162 us -> none  [local_step(): cdf_at_target = lax.psum(jnp.where(in_shard, picked, 0.0), 'vp')]
    pallas_call x0 -> x22, Pallas kernels: none -> 148 us  [the longest x7 78.3 us: _logits(): pl.pallas_call(functools.partial(_logits_kernel, cfg), grid=(units,), in_...]
    another operation x3 -> x0, other arithmetic: 141 us -> none
    ppermute x0 -> x24, waiting for transfers between devices: none -> 86.8 us  [swap(): return lax.ppermute(a, 'vp', [(i, i ^ p) for i in range(n_dev)])]
    dot_general x1 -> x0, matrix products: 54 us -> none  [local_step(): logits = jnp.dot(hidden, w_local, preferred_element_type=jnp.float32)]
    another operation x4 -> x0, local copies, waits for them, and re-layouts: 46.9 us -> none
    add x2 -> x0, other arithmetic: 22.7 us -> none  [local_step(): cdf_cols = local_cdf + offset[:, None]]
    ppermute x0 -> x24, starting transfers between devices: none -> 18.8 us  [swap(): return lax.ppermute(a, 'vp', [(i, i ^ p) for i in range(n_dev)])]
  transfers between devices with their start and end apart: 1 -> 24, of which waited for: 0 -> 7; matrix products, arithmetic and copies ran while one was open for 4% -> 0% of each run, Pallas kernels for 0% -> 51%
where the time goes in v1:
time: 280 us; the launch traced here: 279 us
  Pallas kernels  148 us (53%)
  waiting for transfers between devices  86.8 us (31%)
  local copies, waits for them, and re-layouts  23.8 us (8%)
  starting transfers between devices  18.8 us (7%)
    ppermute x24, waiting for transfers between devices, swap(): return lax.ppermute(a, 'vp', [(i, i ^ p) for i in range(n_dev)])  86.8 us
    pallas_call x7, Pallas kernels, _logits(): pl.pallas_call(functools.partial(_logits_kernel, cfg), grid=(units,), in_...  78.3 us
    pallas_call x14, Pallas kernels, _cdf(): pl.pallas_call(functools.partial(_cdf_kernel, cfg), in_specs=[vmem] * (n...  68.2 us
    unnamed x100, local copies, waits for them, and re-layouts  23.8 us
    ppermute x24, starting transfers between devices, swap(): return lax.ppermute(a, 'vp', [(i, i ^ p) for i in range(n_dev)])  18.8 us
  transfers between devices with their start and end apart: 24, of which 7 were waited for; matrix products, arithmetic and copies ran while one was open for 0% of the time, Pallas kernels for 51%

profile of v1, /device:TPU:0, one launch (start us, length us, event | category | flops | bytes accessed | tf_op | source)
XLA Modules:
  0.0 278.7 jit_solution(9441716411230113278)
XLA Ops:
  0.6 1.6 copy-done
  3.6 5.1 %logits.7 = (f32[64,640]{1,0:T(8,128)S(1)}, f32[64,640]{1,0:T(8,128)S(1)}, f32[64,640]{1,0:T(8,128)}, f32[64,640]{1,0:T(8,128)S(1)}, f32[256,128]{1,0:T(8,128)S(...) custom-call(bf16[256,4096]{1,0:T(8,128)(2,1)S(1)} %copy-done, bf16[4096,16000]{1,0:T(8,128)(2,1)} %w_ref.13, ...), custom_call_target="tpu_custom_call" | custom-call | flops 1342177280 | bytes 7340032 | tf_op jit(solution)/shard_map/logits/pallas_call | solution.py:108
  9.3 3.3 %collective-permute-start.12 = (f32[64,640]{1,0:T(8,128)}, f32[64,640]{1,0:T(8,128)}, u32[]{:S(2)}, u32[]{:S(2)}) collective-permute-start(f32[64,640]{1,0:T(8,128)} %get-tuple-element.108), channel_id=1, source_target_pairs={{0,2},{1,3},{2,0},{3,1},{4,6},{5,7},{6,4},{7,5}} | collective-permute-start | bytes 491528 | tf_op jit(solution)/shard_map/ppermute | solution.py:264
  12.6 9.4 %logits.8 = (f32[64,1920]{1,0:T(8,128)S(1)}, f32[64,1920]{1,0:T(8,128)S(1)}, f32[64,1920]{1,0:T(8,128)S(1)}, f32[64,1920]{1,0:T(8,128)S(1)}, f32[256,128]{1,0:T(...) custom-call(bf16[256,4096]{1,0:T(8,128)(2,1)S(1)} %copy-done, bf16[4096,16000]{1,0:T(8,128)(2,1)} %w_ref.13, ...), custom_call_target="tpu_custom_call" | custom-call | flops 4026531840 | bytes 17825792 | tf_op jit(solution)/shard_map/logits/pallas_call | solution.py:108
  22.9 16.4 %logits.9 = (f32[64,3840]{1,0:T(8,128)S(1)}, f32[64,3840]{1,0:T(8,128)S(1)}, f32[64,3840]{1,0:T(8,128)S(1)}, f32[64,3840]{1,0:T(8,128)S(1)}, f32[256,128]{1,0:T(...) custom-call(bf16[256,4096]{1,0:T(8,128)(2,1)S(1)} %copy-done, bf16[4096,16000]{1,0:T(8,128)(2,1)} %w_ref.13, ...), custom_call_target="tpu_custom_call" | custom-call | flops 8053063680 | bytes 33554432 | tf_op jit(solution)/shard_map/logits/pallas_call | solution.py:108
  39.3 19.9 %logits.10 = (f32[64,4480]{1,0:T(8,128)S(1)}, f32[64,4480]{1,0:T(8,128)S(1)}, f32[64,4480]{1,0:T(8,128)}, f32[64,4480]{1,0:T(8,128)}, f32[256,128]{1,0:T(8,128)S...) custom-call(bf16[256,4096]{1,0:T(8,128)(2,1)S(1)} %copy-done, bf16[4096,16000]{1,0:T(8,128)(2,1)} %w_ref.13, ...), custom_call_target="tpu_custom_call" | custom-call | flops 9395240960 | bytes 38797312 | tf_op jit(solution)/shard_map/logits/pallas_call | solution.py:108
  59.2 14.7 %logits.11 = (f32[64,3200]{1,0:T(8,128)S(1)}, f32[64,3200]{1,0:T(8,128)S(1)}, f32[64,3200]{1,0:T(8,128)S(1)}, f32[64,3200]{1,0:T(8,128)}, f32[256,128]{1,0:T(8,1...) custom-call(bf16[256,4096]{1,0:T(8,128)(2,1)S(1)} %copy-done, bf16[4096,16000]{1,0:T(8,128)(2,1)} %w_ref.13, ...), custom_call_target="tpu_custom_call" | custom-call | flops 6710886400 | bytes 28311552 | tf_op jit(solution)/shard_map/logits/pallas_call | solution.py:108
  74.8 7.5 %logits.12 = (f32[64,1280]{1,0:T(8,128)S(1)}, f32[64,1280]{1,0:T(8,128)S(1)}, f32[64,1280]{1,0:T(8,128)}, f32[64,1280]{1,0:T(8,128)}, f32[256,128]{1,0:T(8,128)S...) custom-call(bf16[256,4096]{1,0:T(8,128)(2,1)S(1)} %copy-done, bf16[4096,16000]{1,0:T(8,128)(2,1)} %w_ref.13, ...), custom_call_target="tpu_custom_call" | custom-call | flops 2684354560 | bytes 12582912 | tf_op jit(solution)/shard_map/logits/pallas_call | solution.py:108
  83.0 5.3 %logits.13 = (f32[64,640]{1,0:T(8,128)S(1)}, f32[64,640]{1,0:T(8,128)S(1)}, f32[64,640]{1,0:T(8,128)S(1)}, f32[64,640]{1,0:T(8,128)S(1)}, f32[256,128]{1,0:T(8,1...) custom-call(bf16[256,4096]{1,0:T(8,128)(2,1)S(1)} %copy-done, bf16[4096,16000]{1,0:T(8,128)(2,1)} %w_ref.13, ...), custom_call_target="tpu_custom_call" | custom-call | flops 1342177280 | bytes 7340032 | tf_op jit(solution)/shard_map/logits/pallas_call | solution.py:108
  90.3 1.7 collective-permute-start.13
  93.4 3.7 %collective-permute-done.22.refs_2_ = f32[8,256]{1,0:T(8,128)S(1)} collective-permute-done((f32[8,256]{1,0:T(8,128)S(1)}, f32[8,256]{1,0:T(8,128)S(1)}, u32[]{:S(2)}, u32[]{:S(2)}) %collective-permute-start.22) | collective-permute-done | bytes 8224 | tf_op jit(solution)/shard_map/ppermute | solution.py:264
  104.0 7.2 %collective-permute-done.10.refs_0_ = f32[64,1920]{1,0:T(8,128)S(1)} collective-permute-done((f32[64,1920]{1,0:T(8,128)S(1)}, f32[64,1920]{1,0:T(8,128)S(1)}, u32[]{:S(2)}, u32[]{:S(2)}) %collective-permute-start.10) | collective-permute-done | bytes 491552 | tf_op jit(solution)/shard_map/ppermute | solution.py:264
  112.0 8.8 %collective-permute-done.11.refs_1_ = f32[64,1920]{1,0:T(8,128)S(1)} collective-permute-done((f32[64,1920]{1,0:T(8,128)S(1)}, f32[64,1920]{1,0:T(8,128)S(1)}, u32[]{:S(2)}, u32[]{:S(2)}) %collective-permute-start.11) | collective-permute-done | bytes 491552 | tf_op jit(solution)/shard_map/ppermute | solution.py:264
  121.6 1.5 collective-permute-start.9
  123.9 36.5 %collective-permute-done.4.refs_0_ = f32[64,3200]{1,0:T(8,128)S(1)} collective-permute-done((f32[64,3200]{1,0:T(8,128)S(1)}, f32[64,3200]{1,0:T(8,128)S(1)}, u32[]{:S(2)}, u32[]{:S(2)}) %collective-permute-start.4) | collective-permute-done | bytes 819232 | tf_op jit(solution)/shard_map/ppermute | solution.py:264
  165.3 15.2 %collective-permute-done.9.refs_1_ = f32[64,3840]{1,0:T(8,128)S(1)} collective-permute-done((f32[64,3840]{1,0:T(8,128)S(1)}, f32[64,3840]{1,0:T(8,128)S(1)}, u32[]{:S(2)}, u32[]{:S(2)}) %collective-permute-start.9) | collective-permute-done | bytes 983072 | tf_op jit(solution)/shard_map/ppermute | solution.py:264
  181.4 1.5 collective-permute-start.5
  186.1 1.5 merge.1
  193.7 4.1 %cdf.15 = (f32[64,64000]{1,0:T(8,128)}, f32[64,128]{1,0:T(8,128)S(1)}) custom-call(f32[64,1920]{1,0:T(8,128)S(1)} %copy-done.18, f32[64,1920]{1,0:T(8,128)S(1)} %copy-done.24, f32[64,128]{1,0:T(8,128)S(1)} %get-tuple-element.126.refs_2_, f32[64,64000]{1,0:T(8,128)} %get-tuple-element.127.refs_3_), custom_call_target="tpu_custom_call", output_to_operand_aliasing={{0}: (3, {})} | custom-call | flops 188743680 | bytes 1966080 | tf_op jit(solution)/shard_map/cdf/pallas_call | solution.py:237
  197.9 7.5 %cdf.16 = (f32[64,64000]{1,0:T(8,128)}, f32[64,128]{1,0:T(8,128)S(1)}) custom-call(f32[64,3840]{1,0:T(8,128)S(1)} %copy-done.4, f32[64,3840]{1,0:T(8,128)S(1)} %copy-done.10, f32[64,128]{1,0:T(8,128)S(1)} %get-tuple-element.128.refs_2_, f32[64,64000]{1,0:T(8,128)} %get-tuple-element.129.refs_3_), custom_call_target="tpu_custom_call", output_to_operand_aliasing={{0}: (3, {})} | custom-call | flops 377487360 | bytes 3932160 | tf_op jit(solution)/shard_map/cdf/pallas_call | solution.py:237
  205.4 8.6 %cdf.17 = (f32[64,64000]{1,0:T(8,128)}, f32[64,128]{1,0:T(8,128)S(1)}) custom-call(f32[64,4480]{1,0:T(8,128)S(1)} %get-tuple-element.116.refs_0_, f32[64,4480]{1,0:T(8,128)S(1)} %copy-done.2, f32[64,128]{1,0:T(8,128)S(1)} %get-tuple-element.130.refs_2_, f32[64,64000]{1,0:T(8,128)} %get-tuple-element.131.refs_3_), custom_call_target="tpu_custom_call", output_to_operand_aliasing={{0}: (3, {})} | custom-call | flops 440401920 | bytes 4587520 | tf_op jit(solution)/shard_map/cdf/pallas_call | solution.py:237
  215.0 14.6 %collective-permute-done.7.refs_1_ = f32[64,4480]{1,0:T(8,128)S(1)} collective-permute-done((f32[64,4480]{1,0:T(8,128)}, f32[64,4480]{1,0:T(8,128)S(1)}, u32[]{:S(2)}, u32[]{:S(2)}) %collective-permute-start.7) | collective-permute-done | bytes 1146912 | tf_op jit(solution)/shard_map/ppermute | solution.py:264
  229.6 1.9 collective-permute-start.1
  231.5 6.4 %cdf.18 = (f32[64,64000]{1,0:T(8,128)}, f32[64,128]{1,0:T(8,128)S(1)}) custom-call(f32[64,3200]{1,0:T(8,128)S(1)} %copy-done.12, f32[64,3200]{1,0:T(8,128)S(1)} %copy-done.16, f32[64,128]{1,0:T(8,128)S(1)} %get-tuple-element.132.refs_2_, f32[64,64000]{1,0:T(8,128)} %get-tuple-element.133.refs_3_), custom_call_target="tpu_custom_call", output_to_operand_aliasing={{0}: (3, {})} | custom-call | flops 314572800 | bytes 3276800 | tf_op jit(solution)/shard_map/cdf/pallas_call | solution.py:237
  237.9 3.0 %cdf.19 = (f32[64,64000]{1,0:T(8,128)}, f32[64,128]{1,0:T(8,128)S(1)}) custom-call(f32[64,1280]{1,0:T(8,128)S(1)} %copy-done.26, f32[64,1280]{1,0:T(8,128)S(1)} %copy-done.28, f32[64,128]{1,0:T(8,128)S(1)} %get-tuple-element.134.refs_2_, f32[64,64000]{1,0:T(8,128)} %get-tuple-element.135.refs_3_), custom_call_target="tpu_custom_call", output_to_operand_aliasing={{0}: (3, {})} | custom-call | flops 125829120 | bytes 1310720 | tf_op jit(solution)/shard_map/cdf/pallas_call | solution.py:237
  242.3 2.4 cdf.21
  244.7 4.1 %cdf.22 = (f32[64,64000]{1,0:T(8,128)}, f32[64,128]{1,0:T(8,128)S(1)}) custom-call(f32[64,1920]{1,0:T(8,128)S(1)} %copy-done.20, f32[64,1920]{1,0:T(8,128)S(1)} %copy-done.22, f32[64,128]{1,0:T(8,128)S(1)} %get-tuple-element.140.refs_2_, f32[64,64000]{1,0:T(8,128)} %get-tuple-element.141.refs_3_), custom_call_target="tpu_custom_call", output_to_operand_aliasing={{0}: (3, {})} | custom-call | flops 188743680 | bytes 1966080 | tf_op jit(solution)/shard_map/cdf/pallas_call | solution.py:237
  248.9 7.5 %cdf.23 = (f32[64,64000]{1,0:T(8,128)}, f32[64,128]{1,0:T(8,128)S(1)}) custom-call(f32[64,3840]{1,0:T(8,128)S(1)} %copy-done.6, f32[64,3840]{1,0:T(8,128)S(1)} %copy-done.8, f32[64,128]{1,0:T(8,128)S(1)} %get-tuple-element.142.refs_2_, f32[64,64000]{1,0:T(8,128)} %get-tuple-element.143.refs_3_), custom_call_target="tpu_custom_call", output_to_operand_aliasing={{0}: (3, {})} | custom-call | flops 377487360 | bytes 3932160 | tf_op jit(solution)/shard_map/cdf/pallas_call | solution.py:237
  256.4 8.6 %cdf.24 = (f32[64,64000]{1,0:T(8,128)}, f32[64,128]{1,0:T(8,128)S(1)}) custom-call(f32[64,4480]{1,0:T(8,128)S(1)} %collective-permute-done.6.refs_0_, f32[64,4480]{1,0:T(8,128)S(1)} %collective-permute-done.7.refs_1_, f32[64,128]{1,0:T(8,128)S(1)} %get-tuple-element.144.refs_2_, f32[64,64000]{1,0:T(8,128)} %get-tuple-element.145.refs_3_), custom_call_target="tpu_custom_call", output_to_operand_aliasing={{0}: (3, {})} | custom-call | flops 440401920 | bytes 4587520 | tf_op jit(solution)/shard_map/cdf/pallas_call | solution.py:237
  265.0 7.5 %cdf.25 = (f32[64,64000]{1,0:T(8,128)}, f32[64,128]{1,0:T(8,128)S(1)}) custom-call(f32[64,3200]{1,0:T(8,128)S(1)} %copy-done.14, f32[64,3200]{1,0:T(8,128)} %collective-permute-done.5.refs_1_, f32[64,128]{1,0:T(8,128)S(1)} %get-tuple-element.146.refs_2_, f32[64,64000]{1,0:T(8,128)} %get-tuple-element.147.refs_3_), custom_call_target="tpu_custom_call", output_to_operand_aliasing={{0}: (3, {})} | custom-call | flops 314572800 | bytes 3276800 | tf_op jit(solution)/shard_map/cdf/pallas_call | solution.py:237
  272.5 4.0 %cdf.26 = (f32[64,64000]{1,0:T(8,128)}, f32[64,128]{1,0:T(8,128)S(1)}) custom-call(f32[64,1280]{1,0:T(8,128)} %collective-permute-done.2.refs_0_, f32[64,1280]{1,0:T(8,128)} %collective-permute-done.3.refs_1_, f32[64,128]{1,0:T(8,128)S(1)} %get-tuple-element.148.refs_2_, f32[64,64000]{1,0:T(8,128)} %get-tuple-element.149.refs_3_), custom_call_target="tpu_custom_call", output_to_operand_aliasing={{0}: (3, {})} | custom-call | flops 125829120 | bytes 1310720 | tf_op jit(solution)/shard_map/cdf/pallas_call | solution.py:237
  276.6 1.9 cdf.27
  (138 shorter events, 34.7 us)
Async XLA Ops:
  9.3 88.9 %collective-permute-start.12 = (f32[64,640]{1,0:T(8,128)}, f32[64,640]{1,0:T(8,128)}, u32[]{:S(2)}, u32[]{:S(2)}) collective-permute-start(f32[64,640]{1,0:T(8,128)} %get-tuple-element.108), channel_id=1, source_target_pairs={{0,2},{1,3},{2,0},{3,1},{4,6},{5,7},{6,4},{7,5}} | collective-permute-start | bytes 491528 | tf_op jit(solution)/shard_map/ppermute | solution.py:264
  90.3 95.7 %copy-start.42 = (f32[8,256]{1,0:T(8,128)}, f32[8,256]{1,0:T(8,128)S(1)}, u32[]{:S(2)}) copy-start(f32[8,256]{1,0:T(8,128)S(1)} %get-tuple-element.124.refs_0_) | copy-start | bytes 24580
  90.3 3.1 %collective-permute-start.23 = (f32[8,256]{1,0:T(8,128)S(1)}, f32[8,256]{1,0:T(8,128)S(1)}, u32[]{:S(2)}, u32[]{:S(2)}) collective-permute-start(f32[8,256]{1,0:T(8,128)S(1)} %get-tuple-element.124.refs_0_), channel_id=1, source_target_pairs={{0,3},{1,2},{2,1},{3,0},{4,7},{5,6},{6,5},{7,4}} | collective-permute-start | bytes 24584 | tf_op jit(solution)/shard_map/ppermute | solution.py:264
  90.3 8.6 %collective-permute-start.13 = (f32[64,640]{1,0:T(8,128)S(1)}, f32[64,640]{1,0:T(8,128)S(1)}, u32[]{:S(2)}, u32[]{:S(2)}) collective-permute-start(f32[64,640]{1,0:T(8,128)S(1)} %get-tuple-element.109), channel_id=1, source_target_pairs={{0,3},{1,2},{2,1},{3,0},{4,7},{5,6},{6,5},{7,4}} | collective-permute-start | bytes 491528 | tf_op jit(solution)/shard_map/ppermute | solution.py:264
  92.1 11.2 %collective-permute-start.15 = (f32[64,1280]{1,0:T(8,128)S(1)}, f32[64,1280]{1,0:T(8,128)S(1)}, u32[]{:S(2)}, u32[]{:S(2)}) collective-permute-start(f32[64,1280]{1,0:T(8,128)S(1)} %get-tuple-element.113), channel_id=1, source_target_pairs={{0,1},{1,0},{2,3},{3,2},{4,5},{5,4},{6,7},{7,6}} | collective-permute-start | bytes 983048 | tf_op jit(solution)/shard_map/ppermute | solution.py:264
  92.1 5.0 %collective-permute-start.22 = (f32[8,256]{1,0:T(8,128)S(1)}, f32[8,256]{1,0:T(8,128)S(1)}, u32[]{:S(2)}, u32[]{:S(2)}) collective-permute-start(f32[8,256]{1,0:T(8,128)S(1)} %get-tuple-element.124.refs_0_), channel_id=1, source_target_pairs={{0,2},{1,3},{2,0},{3,1},{4,6},{5,7},{6,4},{7,5}} | collective-permute-start | bytes 24584 | tf_op jit(solution)/shard_map/ppermute | solution.py:264
  93.4 92.6 %copy-start.47 = (f32[8,256]{1,0:T(8,128)}, f32[8,256]{1,0:T(8,128)S(1)}, u32[]{:S(2)}) copy-start(f32[8,256]{1,0:T(8,128)S(1)} %collective-permute-done.23.refs_3_) | copy-start | bytes 24580
  93.4 3.7 %collective-permute-start.21 = (f32[8,256]{1,0:T(8,128)S(1)}, f32[8,256]{1,0:T(8,128)S(1)}, u32[]{:S(2)}, u32[]{:S(2)}) collective-permute-start(f32[8,256]{1,0:T(8,128)S(1)} %get-tuple-element.124.refs_0_), channel_id=1, source_target_pairs={{0,1},{1,0},{2,3},{3,2},{4,5},{5,4},{6,7},{7,6}} | collective-permute-start | bytes 24584 | tf_op jit(solution)/shard_map/ppermute | solution.py:264
  97.1 89.0 %copy-start.48 = (f32[8,256]{1,0:T(8,128)}, f32[8,256]{1,0:T(8,128)S(1)}, u32[]{:S(2)}) copy-start(f32[8,256]{1,0:T(8,128)S(1)} %collective-permute-done.22.refs_2_) | copy-start | bytes 24580
  97.1 2.9 %collective-permute-start.20 = (f32[64,640]{1,0:T(8,128)S(1)}, f32[64,640]{1,0:T(8,128)S(1)}, u32[]{:S(2)}, u32[]{:S(2)}) collective-permute-start(f32[64,640]{1,0:T(8,128)S(1)} %get-tuple-element.123), channel_id=1, source_target_pairs={{0,1},{1,0},{2,3},{3,2},{4,5},{5,4},{6,7},{7,6}} | collective-permute-start | bytes 491528 | tf_op jit(solution)/shard_map/ppermute | solution.py:264
  97.1 89.0 %copy-start.49 = (f32[8,256]{1,0:T(8,128)}, f32[8,256]{1,0:T(8,128)S(1)}, u32[]{:S(2)}) copy-start(f32[8,256]{1,0:T(8,128)S(1)} %collective-permute-done.21.refs_1_) | copy-start | bytes 24580
  97.1 14.1 %collective-permute-start.10 = (f32[64,1920]{1,0:T(8,128)S(1)}, f32[64,1920]{1,0:T(8,128)S(1)}, u32[]{:S(2)}, u32[]{:S(2)}) collective-permute-start(f32[64,1920]{1,0:T(8,128)S(1)} %get-tuple-element.106), channel_id=1, source_target_pairs={{0,2},{1,3},{2,0},{3,1},{4,6},{5,7},{6,4},{7,5}} | collective-permute-start | bytes 1474568 | tf_op jit(solution)/shard_map/ppermute | solution.py:264
  98.2 22.5 %collective-permute-start.11 = (f32[64,1920]{1,0:T(8,128)S(1)}, f32[64,1920]{1,0:T(8,128)S(1)}, u32[]{:S(2)}, u32[]{:S(2)}) collective-permute-start(f32[64,1920]{1,0:T(8,128)S(1)} %get-tuple-element.107), channel_id=1, source_target_pairs={{0,3},{1,2},{2,1},{3,0},{4,7},{5,6},{6,5},{7,4}} | collective-permute-start | bytes 1474568 | tf_op jit(solution)/shard_map/ppermute | solution.py:264
  99.6 2.1 collective-permute-start.14
  100.6 62.7 %collective-permute-start.8 = (f32[64,3840]{1,0:T(8,128)S(1)}, f32[64,3840]{1,0:T(8,128)S(1)}, u32[]{:S(2)}, u32[]{:S(2)}) collective-permute-start(f32[64,3840]{1,0:T(8,128)S(1)} %get-tuple-element.104), channel_id=1, source_target_pairs={{0,2},{1,3},{2,0},{3,1},{4,6},{5,7},{6,4},{7,5}} | collective-permute-start | bytes 2949128 | tf_op jit(solution)/shard_map/ppermute | solution.py:264
  102.4 58.0 %collective-permute-start.4 = (f32[64,3200]{1,0:T(8,128)S(1)}, f32[64,3200]{1,0:T(8,128)S(1)}, u32[]{:S(2)}, u32[]{:S(2)}) collective-permute-start(f32[64,3200]{1,0:T(8,128)S(1)} %get-tuple-element.100), channel_id=1, source_target_pairs={{0,2},{1,3},{2,0},{3,1},{4,6},{5,7},{6,4},{7,5}} | collective-permute-start | bytes 2457608 | tf_op jit(solution)/shard_map/ppermute | solution.py:264
  104.0 58.3 %collective-permute-start.16 = (f32[64,3200]{1,0:T(8,128)S(1)}, f32[64,3200]{1,0:T(8,128)S(1)}, u32[]{:S(2)}, u32[]{:S(2)}) collective-permute-start(f32[64,3200]{1,0:T(8,128)S(1)} %get-tuple-element.115), channel_id=1, source_target_pairs={{0,1},{1,0},{2,3},{3,2},{4,5},{5,4},{6,7},{7,6}} | collective-permute-start | bytes 2457608 | tf_op jit(solution)/shard_map/ppermute | solution.py:264
  112.0 11.1 %collective-permute-start.19 = (f32[64,1920]{1,0:T(8,128)S(1)}, f32[64,1920]{1,0:T(8,128)S(1)}, u32[]{:S(2)}, u32[]{:S(2)}) collective-permute-start(f32[64,1920]{1,0:T(8,128)S(1)} %get-tuple-element.121), channel_id=1, source_target_pairs={{0,1},{1,0},{2,3},{3,2},{4,5},{5,4},{6,7},{7,6}} | collective-permute-start | bytes 1474568 | tf_op jit(solution)/shard_map/ppermute | solution.py:264
  121.6 58.9 %collective-permute-start.9 = (f32[64,3840]{1,0:T(8,128)S(1)}, f32[64,3840]{1,0:T(8,128)S(1)}, u32[]{:S(2)}, u32[]{:S(2)}) collective-permute-start(f32[64,3840]{1,0:T(8,128)S(1)} %get-tuple-element.105), channel_id=1, source_target_pairs={{0,3},{1,2},{2,1},{3,0},{4,7},{5,6},{6,5},{7,4}} | collective-permute-start | bytes 2949128 | tf_op jit(solution)/shard_map/ppermute | solution.py:264
  123.9 61.0 %collective-permute-start.17 = (f32[64,4480]{1,0:T(8,128)S(1)}, f32[64,4480]{1,0:T(8,128)S(1)}, u32[]{:S(2)}, u32[]{:S(2)}) collective-permute-start(f32[64,4480]{1,0:T(8,128)S(1)} %get-tuple-element.117), channel_id=1, source_target_pairs={{0,1},{1,0},{2,3},{3,2},{4,5},{5,4},{6,7},{7,6}} | collective-permute-start | bytes 3440648 | tf_op jit(solution)/shard_map/ppermute | solution.py:264
  161.3 52.7 %collective-permute-start.6 = (f32[64,4480]{1,0:T(8,128)}, f32[64,4480]{1,0:T(8,128)S(1)}, u32[]{:S(2)}, u32[]{:S(2)}) collective-permute-start(f32[64,4480]{1,0:T(8,128)} %get-tuple-element.102), channel_id=1, source_target_pairs={{0,2},{1,3},{2,0},{3,1},{4,6},{5,7},{6,4},{7,5}} | collective-permute-start | bytes 3440648 | tf_op jit(solution)/shard_map/ppermute | solution.py:264
  163.3 66.3 %collective-permute-start.7 = (f32[64,4480]{1,0:T(8,128)}, f32[64,4480]{1,0:T(8,128)S(1)}, u32[]{:S(2)}, u32[]{:S(2)}) collective-permute-start(f32[64,4480]{1,0:T(8,128)} %get-tuple-element.103), channel_id=1, source_target_pairs={{0,3},{1,2},{2,1},{3,0},{4,7},{5,6},{6,5},{7,4}} | collective-permute-start | bytes 3440648 | tf_op jit(solution)/shard_map/ppermute | solution.py:264
  164.3 18.6 %collective-permute-start.18 = (f32[64,3840]{1,0:T(8,128)S(1)}, f32[64,3840]{1,0:T(8,128)S(1)}, u32[]{:S(2)}, u32[]{:S(2)}) collective-permute-start(f32[64,3840]{1,0:T(8,128)S(1)} %get-tuple-element.119), channel_id=1, source_target_pairs={{0,1},{1,0},{2,3},{3,2},{4,5},{5,4},{6,7},{7,6}} | collective-permute-start | bytes 2949128 | tf_op jit(solution)/shard_map/ppermute | solution.py:264
  181.4 83.6 %collective-permute-start.5 = (f32[64,3200]{1,0:T(8,128)}, f32[64,3200]{1,0:T(8,128)}, u32[]{:S(2)}, u32[]{:S(2)}) collective-permute-start(f32[64,3200]{1,0:T(8,128)} %get-tuple-element.101), channel_id=1, source_target_pairs={{0,3},{1,2},{2,1},{3,0},{4,7},{5,6},{6,5},{7,4}} | collective-permute-start | bytes 2457608 | tf_op jit(solution)/shard_map/ppermute | solution.py:264
  184.0 88.6 %collective-permute-start.2 = (f32[64,1280]{1,0:T(8,128)}, f32[64,1280]{1,0:T(8,128)}, u32[]{:S(2)}, u32[]{:S(2)}) collective-permute-start(f32[64,1280]{1,0:T(8,128)} %get-tuple-element.98), channel_id=1, source_target_pairs={{0,2},{1,3},{2,0},{3,1},{4,6},{5,7},{6,4},{7,5}} | collective-permute-start | bytes 983048 | tf_op jit(solution)/shard_map/ppermute | solution.py:264
  185.9 86.6 %collective-permute-start.3 = (f32[64,1280]{1,0:T(8,128)}, f32[64,1280]{1,0:T(8,128)}, u32[]{:S(2)}, u32[]{:S(2)}) collective-permute-start(f32[64,1280]{1,0:T(8,128)} %get-tuple-element.99), channel_id=1, source_target_pairs={{0,3},{1,2},{2,1},{3,0},{4,7},{5,6},{6,5},{7,4}} | collective-permute-start | bytes 983048 | tf_op jit(solution)/shard_map/ppermute | solution.py:264
  197.8 33.7 %copy-start.12 = (f32[64,3200]{1,0:T(8,128)S(1)}, f32[64,3200]{1,0:T(8,128)}, u32[]{:S(2)}) copy-start(f32[64,3200]{1,0:T(8,128)} %copy-done.11) | copy-start | bytes 2457604
  197.9 33.7 %copy-start.16 = (f32[64,3200]{1,0:T(8,128)S(1)}, f32[64,3200]{1,0:T(8,128)}, u32[]{:S(2)}) copy-start(f32[64,3200]{1,0:T(8,128)} %copy-done.15) | copy-start | bytes 2457604
  205.4 32.5 %copy-start.26 = (f32[64,1280]{1,0:T(8,128)S(1)}, f32[64,1280]{1,0:T(8,128)}, u32[]{:S(2)}) copy-start(f32[64,1280]{1,0:T(8,128)} %copy-done.25) | copy-start | bytes 983044
  205.4 32.5 %copy-start.28 = (f32[64,1280]{1,0:T(8,128)S(1)}, f32[64,1280]{1,0:T(8,128)}, u32[]{:S(2)}) copy-start(f32[64,1280]{1,0:T(8,128)} %copy-done.27) | copy-start | bytes 983044
  214.0 62.6 %collective-permute-start = (f32[64,640]{1,0:T(8,128)S(1)}, f32[64,640]{1,0:T(8,128)S(1)}, u32[]{:S(2)}, u32[]{:S(2)}) collective-permute-start(f32[64,640]{1,0:T(8,128)S(1)} %copy-done.46), channel_id=1, source_target_pairs={{0,2},{1,3},{2,0},{3,1},{4,6},{5,7},{6,4},{7,5}} | collective-permute-start | bytes 491528 | tf_op jit(solution)/shard_map/ppermute | solution.py:264
  229.6 47.0 %collective-permute-start.1 = (f32[64,640]{1,0:T(8,128)S(1)}, f32[64,640]{1,0:T(8,128)S(1)}, u32[]{:S(2)}, u32[]{:S(2)}) collective-permute-start(f32[64,640]{1,0:T(8,128)S(1)} %copy-done.44), channel_id=1, source_target_pairs={{0,3},{1,2},{2,1},{3,0},{4,7},{5,6},{6,5},{7,4}} | collective-permute-start | bytes 491528 | tf_op jit(solution)/shard_map/ppermute | solution.py:264
  (42 other events, 183.8 us)

commit v2 on v1

v2 whole, which is shorter than its diff:
```python
import functools

import jax
import jax.numpy as jnp
from jax import lax
from jax.experimental import pallas as pl
from jax.experimental.pallas import tpu as pltpu
from jax.sharding import PartitionSpec as P


LANES = 128
UNIT = 512
HALF = 256
SLOTS = 3
CHUNKS = (1024, 2048, 4096, 4608, 2560, 1024, 640)
EARLY = 3


def _to_rows(vec_1xn):
    n = vec_1xn.shape[1]
    return jnp.transpose(jnp.broadcast_to(vec_1xn, (LANES, n)))


def _logits_kernel(cfg, x_ref, w_ref, invt_ref, tgt_ref, *refs):
    n_dev, shard, base, widths, first, last = cfg
    refs = list(refs)
    if not first:
        m_in, s_in, t_in = refs[:3]
        refs = refs[3:]
    outs = [refs[c * n_dev:(c + 1) * n_dev] for c in range(len(widths))]
    refs = refs[len(widths) * n_dev:]
    m_ref, s_ref, t_ref = refs[:3]
    refs = refs[3:]
    if last:
        pack_ref = refs.pop(0)
    xs, wbuf, zbuf, invt_v, tgt_v, scale_rows, left_rows, tmp, x_sem, w_sem, z_sem, v_sem = refs
    me = lax.axis_index("vp")
    batch = xs.shape[0]
    rows = batch // n_dev
    total_cols = sum(widths)
    n_full, tail = total_cols // UNIT, total_cols % UNIT

    def rows_of(p):
        return pl.ds(pl.multiple_of((me ^ p) * rows, rows), rows)

    def fetch_x(p):
        return pltpu.make_async_copy(x_ref.at[rows_of(p), :], xs.at[pl.ds(p * rows, rows), :], x_sem.at[p])

    def fetch_w(step, width):
        slot = lax.rem(step, SLOTS)
        col = base + step * UNIT
        return [
            pltpu.make_async_copy(
                w_ref.at[:, pl.ds(pl.multiple_of(col + off, LANES), min(HALF, width - off))],
                wbuf.at[slot, :, pl.ds(off, min(HALF, width - off))],
                w_sem.at[slot, off // HALF],
            )
            for off in range(0, width, HALF)
        ]

    def put_z(step, c, off, width):
        slot = lax.rem(step, 2)
        return [
            pltpu.make_async_copy(
                zbuf.at[slot, pl.ds(p * rows, rows), pl.ds(0, width)],
                outs[c][p].at[:, pl.ds(off, width)],
                z_sem.at[slot, p],
            )
            for p in range(n_dev)
        ]

    small = [
        pltpu.make_async_copy(invt_ref, invt_v, v_sem.at[0]),
        pltpu.make_async_copy(tgt_ref, tgt_v, v_sem.at[1]),
    ]
    for copy in small:
        copy.start()
    for p in range(n_dev):
        fetch_x(p).start()
    for i in range(min(SLOTS - 1, n_full)):
        for copy in fetch_w(jnp.int32(i), UNIT):
            copy.start()
    if first:
        m_ref[...] = jnp.full(m_ref.shape, -jnp.inf, jnp.float32)
        s_ref[...] = jnp.zeros_like(s_ref)
        t_ref[...] = jnp.zeros_like(t_ref)
    else:
        m_ref[...] = m_in[...]
        s_ref[...] = s_in[...]
        t_ref[...] = t_in[...]
    for copy in small:
        copy.wait()
    tmp[...] = _to_rows(invt_v[...])
    for p in range(n_dev):
        scale_rows[pl.ds(p * rows, rows), :] = tmp[rows_of(p), :]
    tmp[...] = _to_rows(tgt_v[...].astype(jnp.float32))
    lane = lax.broadcasted_iota(jnp.int32, (rows, LANES), 1)
    for p in range(n_dev):
        left_rows[pl.ds(p * rows, rows), :] = tmp[rows_of(p), :].astype(jnp.int32) - me * shard - lane
    for p in range(n_dev):
        fetch_x(p).wait()

    def compute(step, width):
        slot, zslot = lax.rem(step, SLOTS), lax.rem(step, 2)
        for off, copy in zip(range(0, width, HALF), fetch_w(step, width)):
            wide = min(HALF, width - off)
            copy.wait()
            z = jnp.dot(xs[...], wbuf[slot, :, off:off + wide], preferred_element_type=jnp.float32)
            for t in range(0, wide, LANES):
                zbuf[zslot, :, off + t:off + t + LANES] = z[:, t:t + LANES] * scale_rows[...]
        col = base + step * UNIT
        group = 32
        for r in range(0, batch, group):
            block = slice(r, r + group)
            tiles = [zbuf[zslot, block, t:t + LANES] for t in range(0, width, LANES)]
            m_old = m_ref[block, :]
            m_new = functools.reduce(jnp.maximum, tiles, m_old)
            keep = jnp.exp(m_old - m_new)
            total = s_ref[block, :] * keep
            upto = t_ref[block, :] * keep
            left = left_rows[block, :]
            for t, tile in enumerate(tiles):
                e = jnp.exp(tile - m_new)
                total += e
                upto += jnp.where(left >= col + t * LANES, e, 0.0)
            m_ref[block, :] = m_new
            s_ref[block, :] = total
            t_ref[block, :] = upto

    def body(step, _):
        ahead = step + SLOTS - 1

        @pl.when(ahead < n_full)
        def _():
            for copy in fetch_w(ahead, UNIT):
                copy.start()

        if tail:
            @pl.when(ahead == n_full)
            def _():
                for copy in fetch_w(ahead, tail):
                    copy.start()

        @pl.when(step >= 2)
        def _():
            for copy in put_z(step, 0, 0, UNIT):
                copy.wait()

        compute(step, UNIT)
        begin = 0
        for c, width in enumerate(widths):
            lo = begin // UNIT
            hi = lo + width // UNIT

            @pl.when((step >= lo) & (step < hi))
            def _(c=c, lo=lo):
                for copy in put_z(step, c, pl.multiple_of((step - lo) * UNIT, UNIT), UNIT):
                    copy.start()

            begin += width
        return 0

    lax.fori_loop(0, n_full, body, 0)
    left_over = [(i, UNIT) for i in range(max(0, n_full - 2), n_full)]
    if tail:
        if n_full >= 2:
            for copy in put_z(jnp.int32(n_full), 0, 0, UNIT):
                copy.wait()
            left_over = left_over[1:]
        compute(jnp.int32(n_full), tail)
        for copy in put_z(jnp.int32(n_full), len(widths) - 1, widths[-1] - tail, tail):
            copy.start()
        left_over.append((n_full, tail))
    if last:
        m = m_ref[...]
        m_row = jnp.max(m, axis=1, keepdims=True)
        keep = jnp.exp(m - m_row)
        s_row = jnp.sum(s_ref[...] * keep, axis=1, keepdims=True)
        t_row = jnp.sum(t_ref[...] * keep, axis=1, keepdims=True)
        which = lax.broadcasted_iota(jnp.int32, m.shape, 1)
        packed = jnp.where(which == 0, m_row, jnp.where(which == 1, s_row, t_row))
        for p in range(n_dev):
            tmp[rows_of(p), :] = packed[p * rows:(p + 1) * rows, :]
        pack_ref[...] = jnp.transpose(tmp[...])[:8, :]
    for step, width in left_over:
        for copy in put_z(jnp.int32(step), 0, 0, width):
            copy.wait()


def _logits(x, w, invt, tgt, stats, n_dev, base, widths, last):
    batch, depth = x.shape
    shard = w.shape[1]
    rows = batch // n_dev
    first = stats is None
    cols = sum(widths)
    hbm = pl.BlockSpec(memory_space=pltpu.HBM)
    vmem = pl.BlockSpec(memory_space=pltpu.VMEM)
    stat = jax.ShapeDtypeStruct((batch, LANES), jnp.float32)
    out_shape = [pltpu.HBM((rows, width), jnp.float32) for width in widths for _ in range(n_dev)] + [stat] * 3
    out_specs = [hbm] * (n_dev * len(widths)) + [vmem] * 3
    if last:
        out_shape.append(jax.ShapeDtypeStruct((8, batch), jnp.float32))
        out_specs.append(vmem)
    cfg = (n_dev, shard, base, widths, first, last)
    res = pl.pallas_call(
        functools.partial(_logits_kernel, cfg),
        in_specs=[hbm] * 4 + ([] if first else [vmem] * 3),
        out_specs=out_specs,
        out_shape=out_shape,
        scratch_shapes=[
            pltpu.VMEM((batch, depth), jnp.bfloat16),
            pltpu.VMEM((SLOTS, depth, UNIT), jnp.bfloat16),
            pltpu.VMEM((2, batch, UNIT), jnp.float32),
            pltpu.VMEM((1, batch), jnp.float32),
            pltpu.VMEM((1, batch), jnp.int32),
            pltpu.VMEM((batch, LANES), jnp.float32),
            pltpu.VMEM((batch, LANES), jnp.int32),
            pltpu.VMEM((batch, LANES), jnp.float32),
            pltpu.SemaphoreType.DMA((n_dev,)),
            pltpu.SemaphoreType.DMA((SLOTS, UNIT // HALF)),
            pltpu.SemaphoreType.DMA((2, n_dev)),
            pltpu.SemaphoreType.DMA((2,)),
        ],
        compiler_params=pltpu.CompilerParams(vmem_limit_bytes=32 * 2**20),
        cost_estimate=pl.CostEstimate(
            flops=2 * batch * depth * cols,
            bytes_accessed=2 * depth * (cols + batch),
            transcendentals=batch * cols,
        ),
        name="logits",
    )(*(pltpu.with_memory_space_constraint(a, pltpu.HBM) for a in (x, w, invt, tgt)), *(() if first else stats))
    k = n_dev * len(widths)
    blocks = [res[c * n_dev:(c + 1) * n_dev] for c in range(len(widths))]
    return blocks, res[k:k + 3], (res[k + 3] if last else None)


def _merge_kernel(n_dev, *refs):
    stats, (params_ref, at_ref) = refs[:n_dev], refs[n_dev:]
    me = lax.axis_index("vp")
    batch = stats[0].shape[1]
    rows = batch // n_dev
    ms = [s[0:1, :] for s in stats]
    top = functools.reduce(jnp.maximum, ms)
    keep = [jnp.exp(m - top) for m in ms]
    mass = [s[1:2, :] * k for s, k in zip(stats, keep)]
    upto = sum(s[2:3, :] * k for s, k in zip(stats, keep))
    total = sum(mass)
    at_ref[...] = upto / total
    values = [top, 1.0 / total]
    for p in range(n_dev):
        start = jnp.zeros_like(total)
        for q in range(n_dev):
            start += jnp.where((me ^ q) < (me ^ p), mass[q], 0.0)
        values.append(start)
    which = lax.broadcasted_iota(jnp.int32, (LANES, batch), 0)
    table = jnp.zeros((LANES, batch), jnp.float32)
    for i, v in enumerate(values):
        table = jnp.where(which == i, v, table)
    per_row = jnp.transpose(table)
    out = jnp.zeros((rows, LANES), jnp.float32)
    for d in range(n_dev):
        out = jnp.where(me == d, per_row[d * rows:(d + 1) * rows, :], out)
    params_ref[...] = out


def _merge(stats):
    n_dev = len(stats)
    batch = stats[0].shape[1]
    vmem = pl.BlockSpec(memory_space=pltpu.VMEM)
    return pl.pallas_call(
        functools.partial(_merge_kernel, n_dev),
        in_specs=[vmem] * n_dev,
        out_specs=[vmem] * 2,
        out_shape=[
            jax.ShapeDtypeStruct((batch // n_dev, LANES), jnp.float32),
            jax.ShapeDtypeStruct((1, batch), jnp.float32),
        ],
        cost_estimate=pl.CostEstimate(flops=100_000, bytes_accessed=100_000, transcendentals=1000),
        name="merge",
    )(*stats)


def _cdf_kernel(cfg, *refs):
    peers, shard, base, width, first = cfg
    n = len(peers)
    params_ref = refs[n]
    out_ref, params_out, y_ref, sems = refs[n + (1 if first else 2):]
    me = lax.axis_index("vp")
    rows = params_ref.shape[0]
    params = params_ref[...]
    top = jnp.broadcast_to(params[:, 0:1], (rows, LANES))
    inv = jnp.broadcast_to(params[:, 1:2], (rows, LANES))
    k_id = lax.broadcasted_iota(jnp.int32, (3 * LANES, 2 * LANES), 0) % LANES
    n_id = lax.broadcasted_iota(jnp.int32, (3 * LANES, 2 * LANES), 1)
    tri = jnp.where(k_id <= n_id, 1.0, 0.0).astype(jnp.bfloat16)
    lane = lax.broadcasted_iota(jnp.int32, (rows, LANES), 1)

    def unit(col, wide, carries):
        ends = []
        for j in range(n):
            cols = [pl.ds(col + t, LANES) for t in range(0, wide, LANES)]
            e = jnp.concatenate([jnp.exp(refs[j][:, c] - top) for c in cols], axis=0)
            hi = e.astype(jnp.bfloat16)
            r1 = e - hi.astype(jnp.float32)
            mid = r1.astype(jnp.bfloat16)
            lo = (r1 - mid.astype(jnp.float32)).astype(jnp.bfloat16)
            sums = jnp.dot(jnp.concatenate([hi, mid, lo], axis=1), tri, preferred_element_type=jnp.float32)
            carry = carries[j]
            for t, c in enumerate(cols):
                block = slice(t * rows, (t + 1) * rows)
                y_ref[j, :, c] = (sums[block, :LANES] + carry) * inv
                carry = carry + sums[block, LANES:]
            ends.append(carry)
        return tuple(ends)

    carries = tuple(jnp.broadcast_to(params[:, 2 + p:3 + p], (rows, LANES)) for p in peers)
    n_full = width // UNIT
    if n_full:
        carries = lax.fori_loop(
            0, n_full, lambda u, c: unit(pl.multiple_of(u * UNIT, UNIT), UNIT, c), carries
        )
    if width % UNIT:
        carries = unit(n_full * UNIT, width % UNIT, carries)
    copies = []
    updated = params
    for j, p in enumerate(peers):
        where = pl.multiple_of((me ^ p) * shard + base, LANES)
        copy = pltpu.make_async_copy(y_ref.at[j], out_ref.at[:, pl.ds(where, width)], sems.at[j])
        copy.start()
        copies.append(copy)
        updated = jnp.where(lane == 2 + p, carries[j], updated)
    params_out[...] = updated
    for copy in copies:
        copy.wait()


def _cdf(blocks, peers, params, out, n_dev, shard, base):
    rows, width = blocks[0].shape
    n = len(peers)
    first = out is None
    vmem = pl.BlockSpec(memory_space=pltpu.VMEM)
    hbm = pl.BlockSpec(memory_space=pl.ANY)
    return pl.pallas_call(
        functools.partial(_cdf_kernel, (peers, shard, base, width, first)),
        in_specs=[vmem] * (n + 1) + ([] if first else [hbm]),
        out_specs=[hbm, vmem],
        out_shape=[
            jax.ShapeDtypeStruct((rows, n_dev * shard), jnp.float32),
            jax.ShapeDtypeStruct(params.shape, jnp.float32),
        ],
        scratch_shapes=[
            pltpu.VMEM((n, rows, width), jnp.float32),
            pltpu.SemaphoreType.DMA((n,)),
        ],
        input_output_aliases={} if first else {n + 1: 0},
        compiler_params=pltpu.CompilerParams(vmem_limit_bytes=24 * 2**20),
        cost_estimate=pl.CostEstimate(
            flops=n * 2 * rows * width * 384,
            bytes_accessed=n * rows * width * 8,
            transcendentals=n * rows * width,
        ),
        name="cdf",
    )(*blocks, params, *(() if first else (out,)))


def solution(mesh):
    n_dev = mesh.shape["vp"]

    def swap(a, p):
        return lax.ppermute(a, "vp", [(i, i ^ p) for i in range(n_dev)])

    def local_step(hidden, w_local, inv_temp, target_ids):
        shard = w_local.shape[1]
        invt = inv_temp.reshape(1, -1)
        tgt = target_ids.reshape(1, -1)
        starts = [sum(CHUNKS[:k]) for k in range(len(CHUNKS))]
        stats, chunks = None, []
        groups = [[k] for k in range(EARLY)] + [list(range(EARLY, len(CHUNKS)))]
        for g, group in enumerate(groups):
            blocks, stats, packed = _logits(
                hidden, w_local, invt, tgt, stats, n_dev, starts[group[0]],
                tuple(CHUNKS[k] for k in group), g == len(groups) - 1,
            )
            for k, sent in zip(group, blocks):
                got = [sent[0]]
                for p in range(1, n_dev):
                    got.append(swap(sent[p], p))
                chunks.append(got)
        packs = [packed]
        for p in range(1, n_dev):
            packs.append(swap(packed, p))
        params, at_target = _merge(packs)
        out = None
        for peers in ((0, 1), (2, 3)):
            for k, got in enumerate(chunks):
                out, params = _cdf([got[p] for p in peers], peers, params, out, n_dev, shard, starts[k])
        return out, at_target.reshape(-1)

    return jax.shard_map(
        local_step,
        mesh=mesh,
        in_specs=(P("dp", None), P(None, "vp"), P("dp"), P("dp")),
        out_specs=(P(("dp", "vp"), None), P("dp")),
        check_vma=False,
    )
```

time: 280 us -> 272 us (0.971)
  waiting for transfers between devices: 86.8 us -> 97.5 us
  local copies, waits for them, and re-layouts: 23.8 us -> 15.1 us
  Pallas kernels: 148 us -> 140 us
    ppermute x24, waiting for transfers between devices: 86.8 us -> 97.5 us  [swap(): return lax.ppermute(a, 'vp', [(i, i ^ p) for i in range(n_dev)])]
    unnamed x100 -> x86, local copies, waits for them, and re-layouts: 23.8 us -> 15.1 us
    pallas_call x21 -> x18, Pallas kernels: 147 us -> 139 us  [the longest x4 100 us: _logits(): pl.pallas_call(functools.partial(_logits_kernel, cfg), in_specs=[hbm] * 4...]
  transfers between devices with their start and end apart: 24 -> 24, of which waited for: 7 -> 11; matrix products, arithmetic and copies ran while one was open for 0% -> 0% of each run, Pallas kernels for 51% -> 47%
where the time goes in v2:
time: 272 us; the launch traced here: 271 us
  Pallas kernels  140 us (51%)
  waiting for transfers between devices  97.5 us (36%)
  starting transfers between devices  17.6 us (6%)
  local copies, waits for them, and re-layouts  15.1 us (6%)
    pallas_call x4, Pallas kernels, _logits(): pl.pallas_call(functools.partial(_logits_kernel, cfg), in_specs=[hbm] * 4...  100 us
    ppermute x24, waiting for transfers between devices, swap(): return lax.ppermute(a, 'vp', [(i, i ^ p) for i in range(n_dev)])  97.5 us
    pallas_call x14, Pallas kernels, _cdf(): pl.pallas_call(functools.partial(_cdf_kernel, (peers, shard, base, width,...  38.5 us
    ppermute x24, starting transfers between devices, swap(): return lax.ppermute(a, 'vp', [(i, i ^ p) for i in range(n_dev)])  17.6 us
    unnamed x86, local copies, waits for them, and re-layouts  15.1 us
  transfers between devices with their start and end apart: 24, of which 11 were waited for; matrix products, arithmetic and copies ran while one was open for 0% of the time, Pallas kernels for 47%

profile of v2, /device:TPU:0, one launch (start us, length us, event | category | flops | bytes accessed | tf_op | source)
XLA Modules:
  0.0 271.3 jit_solution(15001580762521930824)
XLA Ops:
  0.6 9.6 %logits.4 = (f32[64,1024]{1,0:T(8,128)}, f32[64,1024]{1,0:T(8,128)}, f32[64,1024]{1,0:T(8,128)}, f32[64,1024]{1,0:T(8,128)}, f32[256,128]{1,0:T(8,128)S(1)}, /*i...) custom-call(bf16[256,4096]{1,0:T(8,128)(2,1)} %x_ref.7, bf16[4096,16000]{1,0:T(8,128)(2,1)} %w_ref.7, f32[1,256]{1,0:T(1,128)} %bitcast.3, ...), custom_call_target="tpu_custom_call" | custom-call | flops 2147483648 | bytes 10485760 | tf_op jit(solution)/shard_map/logits/pallas_call | solution.py:205
  10.3 3.3 %collective-permute-start.12 = (f32[64,1024]{1,0:T(8,128)}, f32[64,1024]{1,0:T(8,128)S(1)}, u32[]{:S(2)}, u32[]{:S(2)}) collective-permute-start(f32[64,1024]{1,0:T(8,128)} %get-tuple-element.90), channel_id=1, source_target_pairs={{0,2},{1,3},{2,0},{3,1},{4,6},{5,7},{6,4},{7,5}} | collective-permute-start | bytes 786440 | tf_op jit(solution)/shard_map/ppermute | solution.py:370
  13.6 14.8 %logits.5 = (f32[64,2048]{1,0:T(8,128)}, f32[64,2048]{1,0:T(8,128)}, f32[64,2048]{1,0:T(8,128)}, f32[64,2048]{1,0:T(8,128)}, f32[256,128]{1,0:T(8,128)S(1)}, /*i...) custom-call(bf16[256,4096]{1,0:T(8,128)(2,1)} %x_ref.7, bf16[4096,16000]{1,0:T(8,128)(2,1)} %w_ref.7, f32[1,256]{1,0:T(1,128)} %bitcast.4, ...), custom_call_target="tpu_custom_call" | custom-call | flops 4294967296 | bytes 18874368 | tf_op jit(solution)/shard_map/logits/pallas_call | solution.py:205
  29.6 25.1 %logits.6 = (f32[64,4096]{1,0:T(8,128)}, f32[64,4096]{1,0:T(8,128)}, f32[64,4096]{1,0:T(8,128)}, f32[64,4096]{1,0:T(8,128)}, f32[256,128]{1,0:T(8,128)S(1)}, /*i...) custom-call(bf16[256,4096]{1,0:T(8,128)(2,1)} %x_ref.7, bf16[4096,16000]{1,0:T(8,128)(2,1)} %w_ref.7, f32[1,256]{1,0:T(1,128)} %bitcast.5, ...), custom_call_target="tpu_custom_call" | custom-call | flops 8589934592 | bytes 35651584 | tf_op jit(solution)/shard_map/logits/pallas_call | solution.py:205
  54.8 50.6 %logits.7 = (f32[64,4608]{1,0:T(8,128)}, f32[64,4608]{1,0:T(8,128)}, f32[64,4608]{1,0:T(8,128)}, f32[64,4608]{1,0:T(8,128)}, f32[64,2560]{1,0:T(8,128)}, /*index...) custom-call(bf16[256,4096]{1,0:T(8,128)(2,1)} %x_ref.7, ...), custom_call_target="tpu_custom_call" | custom-call | flops 18522046464 | bytes 74448896 | tf_op jit(solution)/shard_map/logits/pallas_call | solution.py:205
  106.4 2.8 %collective-permute-done.23.refs_3_ = f32[8,256]{1,0:T(8,128)S(1)} collective-permute-done((f32[8,256]{1,0:T(8,128)S(1)}, f32[8,256]{1,0:T(8,128)S(1)}, u32[]{:S(2)}, u32[]{:S(2)}) %collective-permute-start.23) | collective-permute-done | bytes 8224 | tf_op jit(solution)/shard_map/ppermute | solution.py:370
  109.5 3.3 %collective-permute-done.22.refs_2_ = f32[8,256]{1,0:T(8,128)S(1)} collective-permute-done((f32[8,256]{1,0:T(8,128)S(1)}, f32[8,256]{1,0:T(8,128)S(1)}, u32[]{:S(2)}, u32[]{:S(2)}) %collective-permute-start.22) | collective-permute-done | bytes 8224 | tf_op jit(solution)/shard_map/ppermute | solution.py:370
  121.9 28.3 %collective-permute-done.11.refs_1_ = f32[64,2048]{1,0:T(8,128)S(1)} collective-permute-done((f32[64,2048]{1,0:T(8,128)S(1)}, f32[64,2048]{1,0:T(8,128)S(1)}, u32[]{:S(2)}, u32[]{:S(2)}) %collective-permute-start.11) | collective-permute-done | bytes 524320 | tf_op jit(solution)/shard_map/ppermute | solution.py:370
  153.3 12.6 %collective-permute-done.4.refs_0_ = f32[64,2560]{1,0:T(8,128)S(1)} collective-permute-done((f32[64,2560]{1,0:T(8,128)}, f32[64,2560]{1,0:T(8,128)S(1)}, u32[]{:S(2)}, u32[]{:S(2)}) %collective-permute-start.4) | collective-permute-done | bytes 655392 | tf_op jit(solution)/shard_map/ppermute | solution.py:370
  168.9 1.8 collective-permute-start.18
  170.8 16.0 %collective-permute-done.9.refs_1_ = f32[64,4096]{1,0:T(8,128)S(1)} collective-permute-done((f32[64,4096]{1,0:T(8,128)S(1)}, f32[64,4096]{1,0:T(8,128)S(1)}, u32[]{:S(2)}, u32[]{:S(2)}) %collective-permute-start.9) | collective-permute-done | bytes 1048608 | tf_op jit(solution)/shard_map/ppermute | solution.py:370
  189.1 1.5 merge.1
  193.3 1.5 cdf.14
  194.9 1.7 collective-permute-start.2
  198.7 2.4 cdf.15
  201.1 5.3 %cdf.16 = (f32[64,64000]{1,0:T(8,128)}, f32[64,128]{1,0:T(8,128)S(1)}) custom-call(f32[64,4096]{1,0:T(8,128)S(1)} %copy-done.3, f32[64,4096]{1,0:T(8,128)} %collective-permute-done.18.refs_1_, f32[64,128]{1,0:T(8,128)S(1)} %get-tuple-element.110.refs_2_, f32[64,64000]{1,0:T(8,128)} %get-tuple-element.111.refs_3_), custom_call_target="tpu_custom_call", output_to_operand_aliasing={{0}: (3, {})} | custom-call | flops 402653184 | bytes 4194304 | tf_op jit(solution)/shard_map/cdf/pallas_call | solution.py:343
  206.5 4.4 %cdf.17 = (f32[64,64000]{1,0:T(8,128)}, f32[64,128]{1,0:T(8,128)S(1)}) custom-call(f32[64,4608]{1,0:T(8,128)S(1)} %copy-done, f32[64,4608]{1,0:T(8,128)S(1)} %collective-permute-done.17.refs_1_, f32[64,128]{1,0:T(8,128)S(1)} %get-tuple-element.112.refs_2_, f32[64,64000]{1,0:T(8,128)} %get-tuple-element.113.refs_3_), custom_call_target="tpu_custom_call", output_to_operand_aliasing={{0}: (3, {})} | custom-call | flops 452984832 | bytes 4718592 | tf_op jit(solution)/shard_map/cdf/pallas_call | solution.py:343
  210.9 2.8 %collective-permute-done.6.refs_0_ = f32[64,4608]{1,0:T(8,128)S(1)} collective-permute-done((f32[64,4608]{1,0:T(8,128)}, f32[64,4608]{1,0:T(8,128)S(1)}, u32[]{:S(2)}, u32[]{:S(2)}) %collective-permute-start.6) | collective-permute-done | bytes 1179680 | tf_op jit(solution)/shard_map/ppermute | solution.py:370
  213.9 23.4 %collective-permute-done.7.refs_1_ = f32[64,4608]{1,0:T(8,128)S(1)} collective-permute-done((f32[64,4608]{1,0:T(8,128)}, f32[64,4608]{1,0:T(8,128)S(1)}, u32[]{:S(2)}, u32[]{:S(2)}) %collective-permute-start.7) | collective-permute-done | bytes 1179680 | tf_op jit(solution)/shard_map/ppermute | solution.py:370
  237.3 1.7 collective-permute-start.1
  239.1 2.8 %cdf.18 = (f32[64,64000]{1,0:T(8,128)}, f32[64,128]{1,0:T(8,128)S(1)}) custom-call(f32[64,2560]{1,0:T(8,128)S(1)} %copy-done.6, f32[64,2560]{1,0:T(8,128)S(1)} %copy-done.10, f32[64,128]{1,0:T(8,128)S(1)} %get-tuple-element.114.refs_2_, f32[64,64000]{1,0:T(8,128)} %get-tuple-element.115.refs_3_), custom_call_target="tpu_custom_call", output_to_operand_aliasing={{0}: (3, {})} | custom-call | flops 251658240 | bytes 2621440 | tf_op jit(solution)/shard_map/cdf/pallas_call | solution.py:343
  241.9 1.5 cdf.19
  244.7 1.5 cdf.21
  246.2 2.4 cdf.22
  248.6 4.0 %cdf.23 = (f32[64,64000]{1,0:T(8,128)}, f32[64,128]{1,0:T(8,128)S(1)}) custom-call(f32[64,4096]{1,0:T(8,128)S(1)} %copy-done.2, f32[64,4096]{1,0:T(8,128)S(1)} %copy-done.5, f32[64,128]{1,0:T(8,128)S(1)} %get-tuple-element.124.refs_2_, f32[64,64000]{1,0:T(8,128)} %get-tuple-element.125.refs_3_), custom_call_target="tpu_custom_call", output_to_operand_aliasing={{0}: (3, {})} | custom-call | flops 402653184 | bytes 4194304 | tf_op jit(solution)/shard_map/cdf/pallas_call | solution.py:343
  252.6 4.4 %cdf.24 = (f32[64,64000]{1,0:T(8,128)}, f32[64,128]{1,0:T(8,128)S(1)}) custom-call(f32[64,4608]{1,0:T(8,128)S(1)} %collective-permute-done.6.refs_0_, f32[64,4608]{1,0:T(8,128)S(1)} %collective-permute-done.7.refs_1_, f32[64,128]{1,0:T(8,128)S(1)} %get-tuple-element.126.refs_2_, f32[64,64000]{1,0:T(8,128)} %get-tuple-element.127.refs_3_), custom_call_target="tpu_custom_call", output_to_operand_aliasing={{0}: (3, {})} | custom-call | flops 452984832 | bytes 4718592 | tf_op jit(solution)/shard_map/cdf/pallas_call | solution.py:343
  257.0 3.8 %cdf.25 = (f32[64,64000]{1,0:T(8,128)}, f32[64,128]{1,0:T(8,128)S(1)}) custom-call(f32[64,2560]{1,0:T(8,128)S(1)} %copy-done.8, f32[64,2560]{1,0:T(8,128)} %collective-permute-done.5.refs_1_, f32[64,128]{1,0:T(8,128)S(1)} %get-tuple-element.128.refs_2_, f32[64,64000]{1,0:T(8,128)} %get-tuple-element.129.refs_3_), custom_call_target="tpu_custom_call", output_to_operand_aliasing={{0}: (3, {})} | custom-call | flops 251658240 | bytes 2621440 | tf_op jit(solution)/shard_map/cdf/pallas_call | solution.py:343
  260.9 1.7 collective-permute-done.3.refs_1_
  262.6 1.5 cdf.26
  264.1 3.6 %collective-permute-done.refs_0_ = f32[64,640]{1,0:T(8,128)S(1)} collective-permute-done((f32[64,640]{1,0:T(8,128)S(1)}, f32[64,640]{1,0:T(8,128)S(1)}, u32[]{:S(2)}, u32[]{:S(2)}) %collective-permute-start) | collective-permute-done | bytes 163872 | tf_op jit(solution)/shard_map/ppermute | solution.py:370
  267.7 1.9 collective-permute-done.1.refs_1_
  269.6 1.7 cdf.27
  (121 shorter events, 26.4 us)
Async XLA Ops:
  10.3 105.3 %collective-permute-start.12 = (f32[64,1024]{1,0:T(8,128)}, f32[64,1024]{1,0:T(8,128)S(1)}, u32[]{:S(2)}, u32[]{:S(2)}) collective-permute-start(f32[64,1024]{1,0:T(8,128)} %get-tuple-element.90), channel_id=1, source_target_pairs={{0,2},{1,3},{2,0},{3,1},{4,6},{5,7},{6,4},{7,5}} | collective-permute-start | bytes 786440 | tf_op jit(solution)/shard_map/ppermute | solution.py:370
  13.6 103.2 %collective-permute-start.13 = (f32[64,1024]{1,0:T(8,128)}, f32[64,1024]{1,0:T(8,128)S(1)}, u32[]{:S(2)}, u32[]{:S(2)}) collective-permute-start(f32[64,1024]{1,0:T(8,128)} %get-tuple-element.91), channel_id=1, source_target_pairs={{0,3},{1,2},{2,1},{3,0},{4,7},{5,6},{6,5},{7,4}} | collective-permute-start | bytes 786440 | tf_op jit(solution)/shard_map/ppermute | solution.py:370
  28.4 92.3 %collective-permute-start.10 = (f32[64,2048]{1,0:T(8,128)}, f32[64,2048]{1,0:T(8,128)S(1)}, u32[]{:S(2)}, u32[]{:S(2)}) collective-permute-start(f32[64,2048]{1,0:T(8,128)} %get-tuple-element.88), channel_id=1, source_target_pairs={{0,2},{1,3},{2,0},{3,1},{4,6},{5,7},{6,4},{7,5}} | collective-permute-start | bytes 1572872 | tf_op jit(solution)/shard_map/ppermute | solution.py:370
  54.7 59.8 %copy-start.37 = (f32[64,4096]{1,0:T(8,128)S(1)}, f32[64,4096]{1,0:T(8,128)}, u32[]{:S(2)}) copy-start(f32[64,4096]{1,0:T(8,128)} %get-tuple-element.86) | copy-start | bytes 3145732
  54.8 60.8 %copy-start.40 = (f32[64,1024]{1,0:T(8,128)S(1)}, f32[64,1024]{1,0:T(8,128)}, u32[]{:S(2)}) copy-start(f32[64,1024]{1,0:T(8,128)} %get-tuple-element.105) | copy-start | bytes 786436
  54.8 62.7 %copy-start.39 = (f32[64,2048]{1,0:T(8,128)S(1)}, f32[64,2048]{1,0:T(8,128)}, u32[]{:S(2)}) copy-start(f32[64,2048]{1,0:T(8,128)} %get-tuple-element.89) | copy-start | bytes 1572868
  54.8 66.8 %copy-start.38 = (f32[64,2048]{1,0:T(8,128)S(1)}, f32[64,2048]{1,0:T(8,128)}, u32[]{:S(2)}) copy-start(f32[64,2048]{1,0:T(8,128)} %get-tuple-element.103) | copy-start | bytes 1572868
  54.8 96.2 %copy-start.36 = (f32[64,4096]{1,0:T(8,128)S(1)}, f32[64,4096]{1,0:T(8,128)}, u32[]{:S(2)}) copy-start(f32[64,4096]{1,0:T(8,128)} %get-tuple-element.87) | copy-start | bytes 3145732
  105.4 83.7 %copy-start.32 = (f32[8,256]{1,0:T(8,128)}, f32[8,256]{1,0:T(8,128)S(1)}, u32[]{:S(2)}) copy-start(f32[8,256]{1,0:T(8,128)S(1)} %get-tuple-element.106.refs_0_) | copy-start | bytes 24580
  105.4 9.5 %collective-permute-start.14 = (f32[64,640]{1,0:T(8,128)}, f32[64,640]{1,0:T(8,128)S(1)}, u32[]{:S(2)}, u32[]{:S(2)}) collective-permute-start(f32[64,640]{1,0:T(8,128)} %get-tuple-element.93), channel_id=1, source_target_pairs={{0,1},{1,0},{2,3},{3,2},{4,5},{5,4},{6,7},{7,6}} | collective-permute-start | bytes 491528 | tf_op jit(solution)/shard_map/ppermute | solution.py:370
  106.1 3.1 %collective-permute-start.23 = (f32[8,256]{1,0:T(8,128)S(1)}, f32[8,256]{1,0:T(8,128)S(1)}, u32[]{:S(2)}, u32[]{:S(2)}) collective-permute-start(f32[8,256]{1,0:T(8,128)S(1)} %get-tuple-element.106.refs_0_), channel_id=1, source_target_pairs={{0,3},{1,2},{2,1},{3,0},{4,7},{5,6},{6,5},{7,4}} | collective-permute-start | bytes 24584 | tf_op jit(solution)/shard_map/ppermute | solution.py:370
  109.1 79.9 %copy-start.33 = (f32[8,256]{1,0:T(8,128)}, f32[8,256]{1,0:T(8,128)S(1)}, u32[]{:S(2)}) copy-start(f32[8,256]{1,0:T(8,128)S(1)} %collective-permute-done.23.refs_3_) | copy-start | bytes 24580
  109.1 3.7 %collective-permute-start.22 = (f32[8,256]{1,0:T(8,128)S(1)}, f32[8,256]{1,0:T(8,128)S(1)}, u32[]{:S(2)}, u32[]{:S(2)}) collective-permute-start(f32[8,256]{1,0:T(8,128)S(1)} %get-tuple-element.106.refs_0_), channel_id=1, source_target_pairs={{0,2},{1,3},{2,0},{3,1},{4,6},{5,7},{6,4},{7,5}} | collective-permute-start | bytes 24584 | tf_op jit(solution)/shard_map/ppermute | solution.py:370
  112.8 1.2 collective-permute-start.21
  114.6 53.3 %collective-permute-start.8 = (f32[64,4096]{1,0:T(8,128)S(1)}, f32[64,4096]{1,0:T(8,128)S(1)}, u32[]{:S(2)}, u32[]{:S(2)}) collective-permute-start(f32[64,4096]{1,0:T(8,128)S(1)} %copy-done.37), channel_id=1, source_target_pairs={{0,2},{1,3},{2,0},{3,1},{4,6},{5,7},{6,4},{7,5}} | collective-permute-start | bytes 3145736 | tf_op jit(solution)/shard_map/ppermute | solution.py:370
  115.5 3.3 %collective-permute-start.20 = (f32[64,1024]{1,0:T(8,128)S(1)}, f32[64,1024]{1,0:T(8,128)S(1)}, u32[]{:S(2)}, u32[]{:S(2)}) collective-permute-start(f32[64,1024]{1,0:T(8,128)S(1)} %copy-done.40), channel_id=1, source_target_pairs={{0,1},{1,0},{2,3},{3,2},{4,5},{5,4},{6,7},{7,6}} | collective-permute-start | bytes 786440 | tf_op jit(solution)/shard_map/ppermute | solution.py:370
  116.3 3.7 %collective-permute-start.15 = (f32[64,1024]{1,0:T(8,128)}, f32[64,1024]{1,0:T(8,128)S(1)}, u32[]{:S(2)}, u32[]{:S(2)}) collective-permute-start(f32[64,1024]{1,0:T(8,128)} %get-tuple-element.95), channel_id=1, source_target_pairs={{0,1},{1,0},{2,3},{3,2},{4,5},{5,4},{6,7},{7,6}} | collective-permute-start | bytes 786440 | tf_op jit(solution)/shard_map/ppermute | solution.py:370
  117.5 32.8 %collective-permute-start.11 = (f32[64,2048]{1,0:T(8,128)S(1)}, f32[64,2048]{1,0:T(8,128)S(1)}, u32[]{:S(2)}, u32[]{:S(2)}) collective-permute-start(f32[64,2048]{1,0:T(8,128)S(1)} %copy-done.39), channel_id=1, source_target_pairs={{0,3},{1,2},{2,1},{3,0},{4,7},{5,6},{6,5},{7,4}} | collective-permute-start | bytes 1572872 | tf_op jit(solution)/shard_map/ppermute | solution.py:370
  119.5 46.4 %collective-permute-start.4 = (f32[64,2560]{1,0:T(8,128)}, f32[64,2560]{1,0:T(8,128)S(1)}, u32[]{:S(2)}, u32[]{:S(2)}) collective-permute-start(f32[64,2560]{1,0:T(8,128)} %get-tuple-element.82), channel_id=1, source_target_pairs={{0,2},{1,3},{2,0},{3,1},{4,6},{5,7},{6,4},{7,5}} | collective-permute-start | bytes 1966088 | tf_op jit(solution)/shard_map/ppermute | solution.py:370
  120.6 46.4 %collective-permute-start.16 = (f32[64,2560]{1,0:T(8,128)}, f32[64,2560]{1,0:T(8,128)S(1)}, u32[]{:S(2)}, u32[]{:S(2)}) collective-permute-start(f32[64,2560]{1,0:T(8,128)} %get-tuple-element.97), channel_id=1, source_target_pairs={{0,1},{1,0},{2,3},{3,2},{4,5},{5,4},{6,7},{7,6}} | collective-permute-start | bytes 1966088 | tf_op jit(solution)/shard_map/ppermute | solution.py:370
  121.6 30.8 %collective-permute-start.19 = (f32[64,2048]{1,0:T(8,128)S(1)}, f32[64,2048]{1,0:T(8,128)S(1)}, u32[]{:S(2)}, u32[]{:S(2)}) collective-permute-start(f32[64,2048]{1,0:T(8,128)S(1)} %copy-done.38), channel_id=1, source_target_pairs={{0,1},{1,0},{2,3},{3,2},{4,5},{5,4},{6,7},{7,6}} | collective-permute-start | bytes 1572872 | tf_op jit(solution)/shard_map/ppermute | solution.py:370
  151.0 35.7 %collective-permute-start.9 = (f32[64,4096]{1,0:T(8,128)S(1)}, f32[64,4096]{1,0:T(8,128)S(1)}, u32[]{:S(2)}, u32[]{:S(2)}) collective-permute-start(f32[64,4096]{1,0:T(8,128)S(1)} %copy-done.36), channel_id=1, source_target_pairs={{0,3},{1,2},{2,1},{3,0},{4,7},{5,6},{6,5},{7,4}} | collective-permute-start | bytes 3145736 | tf_op jit(solution)/shard_map/ppermute | solution.py:370
  153.2 43.4 %collective-permute-start.17 = (f32[64,4608]{1,0:T(8,128)}, f32[64,4608]{1,0:T(8,128)S(1)}, u32[]{:S(2)}, u32[]{:S(2)}) collective-permute-start(f32[64,4608]{1,0:T(8,128)} %get-tuple-element.99), channel_id=1, source_target_pairs={{0,1},{1,0},{2,3},{3,2},{4,5},{5,4},{6,7},{7,6}} | collective-permute-start | bytes 3538952 | tf_op jit(solution)/shard_map/ppermute | solution.py:370
  166.7 46.9 %collective-permute-start.6 = (f32[64,4608]{1,0:T(8,128)}, f32[64,4608]{1,0:T(8,128)S(1)}, u32[]{:S(2)}, u32[]{:S(2)}) collective-permute-start(f32[64,4608]{1,0:T(8,128)} %get-tuple-element.84), channel_id=1, source_target_pairs={{0,2},{1,3},{2,0},{3,1},{4,6},{5,7},{6,4},{7,5}} | collective-permute-start | bytes 3538952 | tf_op jit(solution)/shard_map/ppermute | solution.py:370
  167.9 69.4 %collective-permute-start.7 = (f32[64,4608]{1,0:T(8,128)}, f32[64,4608]{1,0:T(8,128)S(1)}, u32[]{:S(2)}, u32[]{:S(2)}) collective-permute-start(f32[64,4608]{1,0:T(8,128)} %get-tuple-element.85), channel_id=1, source_target_pairs={{0,3},{1,2},{2,1},{3,0},{4,7},{5,6},{6,5},{7,4}} | collective-permute-start | bytes 3538952 | tf_op jit(solution)/shard_map/ppermute | solution.py:370
  168.9 25.9 %collective-permute-start.18 = (f32[64,4096]{1,0:T(8,128)}, f32[64,4096]{1,0:T(8,128)}, u32[]{:S(2)}, u32[]{:S(2)}) collective-permute-start(f32[64,4096]{1,0:T(8,128)} %get-tuple-element.101), channel_id=1, source_target_pairs={{0,1},{1,0},{2,3},{3,2},{4,5},{5,4},{6,7},{7,6}} | collective-permute-start | bytes 3145736 | tf_op jit(solution)/shard_map/ppermute | solution.py:370
  187.7 69.3 %collective-permute-start.5 = (f32[64,2560]{1,0:T(8,128)}, f32[64,2560]{1,0:T(8,128)}, u32[]{:S(2)}, u32[]{:S(2)}) collective-permute-start(f32[64,2560]{1,0:T(8,128)} %get-tuple-element.83), channel_id=1, source_target_pairs={{0,3},{1,2},{2,1},{3,0},{4,7},{5,6},{6,5},{7,4}} | collective-permute-start | bytes 1966088 | tf_op jit(solution)/shard_map/ppermute | solution.py:370
  194.9 66.0 %collective-permute-start.2 = (f32[64,1024]{1,0:T(8,128)}, f32[64,1024]{1,0:T(8,128)S(1)}, u32[]{:S(2)}, u32[]{:S(2)}) collective-permute-start(f32[64,1024]{1,0:T(8,128)} %get-tuple-element.80), channel_id=1, source_target_pairs={{0,2},{1,3},{2,0},{3,1},{4,6},{5,7},{6,4},{7,5}} | collective-permute-start | bytes 786440 | tf_op jit(solution)/shard_map/ppermute | solution.py:370
  196.6 66.0 %collective-permute-start.3 = (f32[64,1024]{1,0:T(8,128)}, f32[64,1024]{1,0:T(8,128)S(1)}, u32[]{:S(2)}, u32[]{:S(2)}) collective-permute-start(f32[64,1024]{1,0:T(8,128)} %get-tuple-element.81), channel_id=1, source_target_pairs={{0,3},{1,2},{2,1},{3,0},{4,7},{5,6},{6,5},{7,4}} | collective-permute-start | bytes 786440 | tf_op jit(solution)/shard_map/ppermute | solution.py:370
  201.1 37.9 %copy-start.6 = (f32[64,2560]{1,0:T(8,128)S(1)}, f32[64,2560]{1,0:T(8,128)}, u32[]{:S(2)}) copy-start(f32[64,2560]{1,0:T(8,128)} %get-tuple-element.96.refs_0_) | copy-start | bytes 1966084
  213.6 54.1 %collective-permute-start = (f32[64,640]{1,0:T(8,128)S(1)}, f32[64,640]{1,0:T(8,128)S(1)}, u32[]{:S(2)}, u32[]{:S(2)}) collective-permute-start(f32[64,640]{1,0:T(8,128)S(1)} %copy-done.42), channel_id=1, source_target_pairs={{0,2},{1,3},{2,0},{3,1},{4,6},{5,7},{6,4},{7,5}} | collective-permute-start | bytes 491528 | tf_op jit(solution)/shard_map/ppermute | solution.py:370
  237.3 32.3 %collective-permute-start.1 = (f32[64,640]{1,0:T(8,128)S(1)}, f32[64,640]{1,0:T(8,128)S(1)}, u32[]{:S(2)}, u32[]{:S(2)}) collective-permute-start(f32[64,640]{1,0:T(8,128)S(1)} %copy-done.41), channel_id=1, source_target_pairs={{0,3},{1,2},{2,1},{3,0},{4,7},{5,6},{6,5},{7,4}} | collective-permute-start | bytes 491528 | tf_op jit(solution)/shard_map/ppermute | solution.py:370
  (35 other events, 228.0 us)

commit v3 on v2

v3 whole, which is shorter than its diff:
```python
import functools

import jax
import jax.numpy as jnp
from jax import lax
from jax.experimental import pallas as pl
from jax.experimental.pallas import tpu as pltpu
from jax.sharding import PartitionSpec as P


LANES = 128
UNIT = 512
HALF = 256
DEPTH = 512
SLOTS = 6
EARLY = ((512, 2), (1024, 1), (2048, 2))
LATE = (4096, 2048, 2048, 1024, 640)
LATE_UNITS = ((2048, 2), (2048, 1), (2048, 1), (1024, 1), (640, 1))


def _to_rows(vec_1xn):
    n = vec_1xn.shape[1]
    return jnp.transpose(jnp.broadcast_to(vec_1xn, (LANES, n)))


def _peer(me, p):
    return [me, me + 1 - 2 * lax.rem(me, 2), lax.rem(me + 2, 4), 3 - me][p]


def _logits_kernel(cfg, x_ref, w_ref, invt_ref, tgt_ref, *refs):
    n_dev, shard, segments, n_late = cfg
    refs = list(refs)

    def take(n):
        out = refs[:n]
        del refs[:n]
        return out

    early = take(n_dev)
    late = [take(n_dev) for _ in range(n_late)]
    packs = take(n_dev)
    xs, wbuf, acc, zsend, zbuf, invt_v, tgt_v, pack_v = take(8)
    scale_rows, left_rows, tmp, m_ref, s_ref, t_ref = take(6)
    w_sem, z_sem, x_sem, v_sem, own_sem, send_sem, recv_sem, pack_send, pack_recv = take(9)
    me = lax.axis_index("vp")
    batch, depth = xs.shape
    rows = batch // n_dev
    k_steps = depth // DEPTH

    def rows_of(p):
        return pl.ds(pl.multiple_of(_peer(me, p) * rows, rows), rows)

    def fetch_w(seg, step):
        width, col0, g0 = segments[seg][0], segments[seg][3], segments[seg][4]
        slot = lax.rem(g0 + step, SLOTS)
        col = col0 + lax.div(step, k_steps) * width
        row = pl.multiple_of(lax.rem(step, k_steps) * DEPTH, DEPTH)
        return pltpu.make_async_copy(
            w_ref.at[pl.ds(row, DEPTH), pl.ds(pl.multiple_of(col, LANES), width)],
            wbuf.at[slot, :, pl.ds(0, width)],
            w_sem.at[slot],
        )

    def put_late(slot, c, off, width):
        return [
            pltpu.make_async_copy(
                zbuf.at[slot, pl.ds(p * rows, rows), pl.ds(0, width)],
                late[c][p].at[:, pl.ds(off, width)],
                z_sem.at[slot, p],
            )
            for p in range(n_dev)
        ]

    def put_own(u, off, width):
        return pltpu.make_async_copy(
            zsend.at[pl.ds(0, rows), pl.ds(off, width)], early[0].at[:, pl.ds(off, width)], own_sem.at[u]
        )

    def send(u, p, off, width):
        return pltpu.make_async_remote_copy(
            src_ref=zsend.at[pl.ds(p * rows, rows), pl.ds(off, width)],
            dst_ref=early[p].at[:, pl.ds(off, width)],
            send_sem=send_sem.at[u, p],
            recv_sem=recv_sem.at[u, p],
            device_id={"vp": _peer(me, p)},
            device_id_type=pl.DeviceIdType.MESH,
        )

    x_copies = [
        pltpu.make_async_copy(x_ref.at[rows_of(p), :], xs.at[pl.ds(p * rows, rows), :], x_sem.at[p])
        for p in range(n_dev)
    ]
    small = [
        pltpu.make_async_copy(invt_ref, invt_v, v_sem.at[0]),
        pltpu.make_async_copy(tgt_ref, tgt_v, v_sem.at[1]),
    ]
    for copy in small + x_copies:
        copy.start()
    for i in range(SLOTS - 1):
        fetch_w(0, jnp.int32(i)).start()
    barrier = pltpu.get_barrier_semaphore()
    for p in range(1, n_dev):
        pl.semaphore_signal(
            barrier, inc=1, device_id={"vp": _peer(me, p)}, device_id_type=pl.DeviceIdType.MESH
        )
    m_ref[...] = jnp.full(m_ref.shape, -jnp.inf, jnp.float32)
    s_ref[...] = jnp.zeros_like(s_ref)
    t_ref[...] = jnp.zeros_like(t_ref)
    for copy in small:
        copy.wait()
    tmp[...] = _to_rows(invt_v[...])
    for p in range(n_dev):
        scale_rows[pl.ds(p * rows, rows), :] = tmp[rows_of(p), :]
    tmp[...] = _to_rows(tgt_v[...].astype(jnp.float32))
    lane = lax.broadcasted_iota(jnp.int32, (rows, LANES), 1)
    for p in range(n_dev):
        left_rows[pl.ds(p * rows, rows), :] = tmp[rows_of(p), :].astype(jnp.int32) - me * shard - lane
    for copy in x_copies:
        copy.wait()

    def multiply(seg, step):
        width = segments[seg][0]
        slot, k = lax.rem(segments[seg][4] + step, SLOTS), lax.rem(step, k_steps)
        fetch_w(seg, step).wait()
        x = xs[:, pl.ds(pl.multiple_of(k * DEPTH, DEPTH), DEPTH)]
        for off in range(0, width, HALF):
            wide = min(HALF, width - off)
            part = jnp.dot(x, wbuf[slot, :, off:off + wide], preferred_element_type=jnp.float32)
            acc[:, off:off + wide] = part + jnp.where(k == 0, 0.0, acc[:, off:off + wide])

    def finish(col, width, out_ref, out_off):
        group = 32
        span = UNIT if width % UNIT == 0 else LANES

        def some(j, _):
            at = pl.multiple_of(j * span, span)
            for r in range(0, batch, group):
                block = slice(r, r + group)
                scale = scale_rows[block, :]
                tiles = []
                for t in range(0, span, LANES):
                    tile = acc[block, pl.ds(at + t, LANES)] * scale
                    out_ref[block, pl.ds(pl.multiple_of(out_off + at + t, LANES), LANES)] = tile
                    tiles.append(tile)
                m_old = m_ref[block, :]
                m_new = functools.reduce(jnp.maximum, tiles, m_old)
                keep = jnp.exp(m_old - m_new)
                total = s_ref[block, :] * keep
                upto = t_ref[block, :] * keep
                left = left_rows[block, :]
                for t, tile in enumerate(tiles):
                    e = jnp.exp(tile - m_new)
                    total += e
                    upto += jnp.where(left >= col + at + t * LANES, e, 0.0)
                m_ref[block, :] = m_new
                s_ref[block, :] = total
                t_ref[block, :] = upto
            return 0

        lax.fori_loop(0, width // span, some, 0)

    sent, own, stored = [], [], []
    for seg, (width, n, chunk, col0, g0) in enumerate(segments):
        for i in range(n):

            def body(k, _, seg=seg, i=i, n=n):
                step = i * k_steps + k
                ahead = step + SLOTS - 1

                @pl.when(ahead < n * k_steps)
                def _():
                    fetch_w(seg, ahead).start()

                if seg + 1 < len(segments):
                    @pl.when(ahead >= n * k_steps)
                    def _():
                        fetch_w(seg + 1, ahead - n * k_steps).start()

                multiply(seg, step)
                return 0

            lax.fori_loop(0, k_steps, body, 0)
            col = col0 + i * width
            if chunk is None:
                finish(col, width, zsend, col)
                if not sent:
                    pl.semaphore_wait(barrier, n_dev - 1)
                u = len(own)
                for p in (2, 3, 1):
                    copy = send(u, p, col, width)
                    copy.start()
                    sent.append(copy)
                copy = put_own(u, col, width)
                copy.start()
                own.append(copy)
            else:
                slot = len(stored) % 2
                if len(stored) >= 2:
                    for copy in stored[-2]:
                        copy.wait()
                finish(col, width, zbuf.at[slot], 0)
                c, off = chunk
                copies = put_late(slot, c, off + i * width, width)
                for copy in copies:
                    copy.start()
                stored.append(copies)
    m = m_ref[...]
    m_row = jnp.max(m, axis=1, keepdims=True)
    keep = jnp.exp(m - m_row)
    s_row = jnp.sum(s_ref[...] * keep, axis=1, keepdims=True)
    t_row = jnp.sum(t_ref[...] * keep, axis=1, keepdims=True)
    which = lax.broadcasted_iota(jnp.int32, m.shape, 1)
    packed = jnp.where(which == 0, m_row, jnp.where(which == 1, s_row, t_row))
    for p in range(n_dev):
        tmp[rows_of(p), :] = packed[p * rows:(p + 1) * rows, :]
    pack_v[...] = jnp.transpose(tmp[...])[:8, :]
    for p in (2, 3, 1):
        copy = pltpu.make_async_remote_copy(
            src_ref=pack_v,
            dst_ref=packs[p],
            send_sem=pack_send.at[p],
            recv_sem=pack_recv.at[p],
            device_id={"vp": _peer(me, p)},
            device_id_type=pl.DeviceIdType.MESH,
        )
        copy.start()
        sent.append(copy)
    copy = pltpu.make_async_copy(pack_v, packs[0], pack_send.at[0])
    copy.start()
    own.append(copy)
    for copies in stored[-2:]:
        for copy in copies:
            copy.wait()
    for copy in own + sent:
        copy.wait()


def _logits(x, w, invt, tgt, n_dev):
    batch, depth = x.shape
    shard = w.shape[1]
    rows = batch // n_dev
    segments, col, g0 = [], 0, 0
    chunk_of = {}
    begin = sum(width * n for width, n in EARLY)
    for c, width in enumerate(LATE):
        chunk_of.update({begin + i: (c, i) for i in range(0, width, LANES)})
        begin += width
    for i, (width, n) in enumerate(EARLY + LATE_UNITS):
        segments.append((width, n, None if i < len(EARLY) else chunk_of[col], col, g0))
        col += width * n
        g0 += n * (depth // DEPTH)
    assert col == shard == begin
    n_early = sum(n for _, n in EARLY)
    sent = sum(width * n for width, n in EARLY)
    hbm = pl.BlockSpec(memory_space=pltpu.HBM)
    out_shape = [pltpu.HBM((rows, sent), jnp.float32)] * n_dev
    out_shape += [pltpu.HBM((rows, width), jnp.float32) for width in LATE for _ in range(n_dev)]
    out_shape += [pltpu.HBM((8, batch), jnp.float32)] * n_dev
    table = pltpu.VMEM((batch, LANES), jnp.float32)
    widest = max(width for width, _ in EARLY + LATE_UNITS)
    dma = pltpu.SemaphoreType.DMA
    res = pl.pallas_call(
        functools.partial(_logits_kernel, (n_dev, shard, segments, len(LATE))),
        in_specs=[hbm] * 4,
        out_specs=[hbm] * len(out_shape),
        out_shape=out_shape,
        scratch_shapes=[
            pltpu.VMEM((batch, depth), jnp.bfloat16),
            pltpu.VMEM((SLOTS, DEPTH, widest), jnp.bfloat16),
            pltpu.VMEM((batch, widest), jnp.float32),
            pltpu.VMEM((batch, sent), jnp.float32),
            pltpu.VMEM((2, batch, widest), jnp.float32),
            pltpu.VMEM((1, batch), jnp.float32),
            pltpu.VMEM((1, batch), jnp.int32),
            pltpu.VMEM((8, batch), jnp.float32),
            table,
            pltpu.VMEM((batch, LANES), jnp.int32),
            table,
            table,
            table,
            table,
            dma((SLOTS,)),
            dma((2, n_dev)),
            dma((n_dev,)),
            dma((2,)),
            dma((n_early,)),
            dma((n_early, n_dev)),
            dma((n_early, n_dev)),
            dma((n_dev,)),
            dma((n_dev,)),
        ],
        compiler_params=pltpu.CompilerParams(
            collective_id=0, has_side_effects=True, vmem_limit_bytes=40 * 2**20
        ),
        cost_estimate=pl.CostEstimate(
            flops=2 * batch * depth * shard,
            bytes_accessed=2 * depth * shard,
            transcendentals=batch * shard,
        ),
        name="logits",
    )(*(pltpu.with_memory_space_constraint(a, pltpu.HBM) for a in (x, w, invt, tgt)))
    blocks = [res[c * n_dev:(c + 1) * n_dev] for c in range(len(LATE) + 2)]
    return blocks[0], blocks[1:-1], blocks[-1]


def _merge_kernel(n_dev, *refs):
    stats, (params_ref, at_ref) = refs[:n_dev], refs[n_dev:]
    me = lax.axis_index("vp")
    batch = stats[0].shape[1]
    rows = batch // n_dev
    ms = [s[0:1, :] for s in stats]
    top = functools.reduce(jnp.maximum, ms)
    keep = [jnp.exp(m - top) for m in ms]
    mass = [s[1:2, :] * k for s, k in zip(stats, keep)]
    upto = sum(s[2:3, :] * k for s, k in zip(stats, keep))
    total = sum(mass)
    at_ref[...] = upto / total
    values = [top, 1.0 / total]
    for p in range(n_dev):
        start = jnp.zeros_like(total)
        for q in range(n_dev):
            start += jnp.where((me ^ q) < (me ^ p), mass[q], 0.0)
        values.append(start)
    which = lax.broadcasted_iota(jnp.int32, (LANES, batch), 0)
    table = jnp.zeros((LANES, batch), jnp.float32)
    for i, v in enumerate(values):
        table = jnp.where(which == i, v, table)
    per_row = jnp.transpose(table)
    out = jnp.zeros((rows, LANES), jnp.float32)
    for d in range(n_dev):
        out = jnp.where(me == d, per_row[d * rows:(d + 1) * rows, :], out)
    params_ref[...] = out


def _merge(stats):
    n_dev = len(stats)
    batch = stats[0].shape[1]
    vmem = pl.BlockSpec(memory_space=pltpu.VMEM)
    return pl.pallas_call(
        functools.partial(_merge_kernel, n_dev),
        in_specs=[vmem] * n_dev,
        out_specs=[vmem] * 2,
        out_shape=[
            jax.ShapeDtypeStruct((batch // n_dev, LANES), jnp.float32),
            jax.ShapeDtypeStruct((1, batch), jnp.float32),
        ],
        cost_estimate=pl.CostEstimate(flops=100_000, bytes_accessed=100_000, transcendentals=1000),
        name="merge",
    )(*stats)


def _cdf_kernel(cfg, *refs):
    peers, shard, base, width, first = cfg
    n = len(peers)
    params_ref = refs[n]
    out_ref, params_out, y_ref, sems = refs[n + (1 if first else 2):]
    me = lax.axis_index("vp")
    rows = params_ref.shape[0]
    params = params_ref[...]
    top = jnp.broadcast_to(params[:, 0:1], (rows, LANES))
    inv = jnp.broadcast_to(params[:, 1:2], (rows, LANES))
    k_id = lax.broadcasted_iota(jnp.int32, (3 * LANES, 2 * LANES), 0) % LANES
    n_id = lax.broadcasted_iota(jnp.int32, (3 * LANES, 2 * LANES), 1)
    tri = jnp.where(k_id <= n_id, 1.0, 0.0).astype(jnp.bfloat16)
    lane = lax.broadcasted_iota(jnp.int32, (rows, LANES), 1)

    def unit(col, wide, carries):
        ends = []
        for j in range(n):
            cols = [pl.ds(col + t, LANES) for t in range(0, wide, LANES)]
            e = jnp.concatenate([jnp.exp(refs[j][:, c] - top) for c in cols], axis=0)
            hi = e.astype(jnp.bfloat16)
            r1 = e - hi.astype(jnp.float32)
            mid = r1.astype(jnp.bfloat16)
            lo = (r1 - mid.astype(jnp.float32)).astype(jnp.bfloat16)
            sums = jnp.dot(jnp.concatenate([hi, mid, lo], axis=1), tri, preferred_element_type=jnp.float32)
            carry = carries[j]
            for t, c in enumerate(cols):
                block = slice(t * rows, (t + 1) * rows)
                y_ref[j, :, c] = (sums[block, :LANES] + carry) * inv
                carry = carry + sums[block, LANES:]
            ends.append(carry)
        return tuple(ends)

    carries = tuple(jnp.broadcast_to(params[:, 2 + p:3 + p], (rows, LANES)) for p in peers)
    n_full = width // UNIT
    if n_full:
        carries = lax.fori_loop(
            0, n_full, lambda u, c: unit(pl.multiple_of(u * UNIT, UNIT), UNIT, c), carries
        )
    if width % UNIT:
        carries = unit(n_full * UNIT, width % UNIT, carries)
    copies = []
    updated = params
    for j, p in enumerate(peers):
        where = pl.multiple_of((me ^ p) * shard + base, LANES)
        copy = pltpu.make_async_copy(y_ref.at[j], out_ref.at[:, pl.ds(where, width)], sems.at[j])
        copy.start()
        copies.append(copy)
        updated = jnp.where(lane == 2 + p, carries[j], updated)
    params_out[...] = updated
    for copy in copies:
        copy.wait()


def _cdf(blocks, peers, params, out, n_dev, shard, base):
    rows, width = blocks[0].shape
    n = len(peers)
    first = out is None
    vmem = pl.BlockSpec(memory_space=pltpu.VMEM)
    hbm = pl.BlockSpec(memory_space=pl.ANY)
    return pl.pallas_call(
        functools.partial(_cdf_kernel, (peers, shard, base, width, first)),
        in_specs=[vmem] * (n + 1) + ([] if first else [hbm]),
        out_specs=[hbm, vmem],
        out_shape=[
            jax.ShapeDtypeStruct((rows, n_dev * shard), jnp.float32),
            jax.ShapeDtypeStruct(params.shape, jnp.float32),
        ],
        scratch_shapes=[
            pltpu.VMEM((n, rows, width), jnp.float32),
            pltpu.SemaphoreType.DMA((n,)),
        ],
        input_output_aliases={} if first else {n + 1: 0},
        compiler_params=pltpu.CompilerParams(vmem_limit_bytes=24 * 2**20),
        cost_estimate=pl.CostEstimate(
            flops=n * 2 * rows * width * 384,
            bytes_accessed=n * rows * width * 8,
            transcendentals=n * rows * width,
        ),
        name="cdf",
    )(*blocks, params, *(() if first else (out,)))


def solution(mesh):
    n_dev = mesh.shape["vp"]
    assert n_dev == 4

    def swap(a, p):
        return lax.ppermute(a, "vp", [(i, i ^ p) for i in range(n_dev)])

    def local_step(hidden, w_local, inv_temp, target_ids):
        shard = w_local.shape[1]
        early, late, packs = _logits(
            hidden, w_local, inv_temp.reshape(1, -1), target_ids.reshape(1, -1), n_dev
        )
        chunks = [(0, early)]
        begin = early[0].shape[1]
        for made in late:
            got = [made[0]]
            for p in range(1, n_dev):
                got.append(swap(made[p], p))
            chunks.append((begin, got))
            begin += made[0].shape[1]
        params, at_target = _merge(packs)
        out = None
        for peers in ((0, 1), (2, 3)):
            for begin, got in chunks:
                out, params = _cdf([got[p] for p in peers], peers, params, out, n_dev, shard, begin)
        return out, at_target.reshape(-1)

    return jax.shard_map(
        local_step,
        mesh=mesh,
        in_specs=(P("dp", None), P(None, "vp"), P("dp"), P("dp")),
        out_specs=(P(("dp", "vp"), None), P("dp")),
        check_vma=False,
    )
```

time: 272 us -> 190 us (0.70)
  waiting for transfers between devices: 97.5 us -> 54.5 us
  Pallas kernels: 140 us -> 116 us
  starting transfers between devices: 17.6 us -> 10.2 us
  local copies, waits for them, and re-layouts: 15.1 us -> 8.75 us
    ppermute x24 -> x15, waiting for transfers between devices: 97.5 us -> 54.5 us  [swap(): return lax.ppermute(a, 'vp', [(i, i ^ p) for i in range(n_dev)])]
    pallas_call x4 -> x1, Pallas kernels: 100 us -> 77.4 us  [_logits(): pl.pallas_call(functools.partial(_logits_kernel, (n_dev, shard, segments,...]
    ppermute x24 -> x15, starting transfers between devices: 17.6 us -> 10.2 us  [swap(): return lax.ppermute(a, 'vp', [(i, i ^ p) for i in range(n_dev)])]
    unnamed x86 -> x44, local copies, waits for them, and re-layouts: 15.1 us -> 8.75 us
    pallas_call x14 -> x12, Pallas kernels: 38.5 us -> 36.7 us  [_cdf(): pl.pallas_call(functools.partial(_cdf_kernel, (peers, shard, base, width,...]
  transfers between devices with their start and end apart: 24 -> 15, of which waited for: 11 -> 8; matrix products, arithmetic and copies ran while one was open for 0% -> 0% of each run, Pallas kernels for 47% -> 19%
where the time goes in v3:
time: 190 us
  Pallas kernels  116 us (61%)
  waiting for transfers between devices  54.5 us (29%)
  starting transfers between devices  10.2 us (5%)
  local copies, waits for them, and re-layouts  8.75 us (5%)
    pallas_call x1, Pallas kernels, _logits(): pl.pallas_call(functools.partial(_logits_kernel, (n_dev, shard, segments,...  77.4 us
    ppermute x15, waiting for transfers between devices, swap(): return lax.ppermute(a, 'vp', [(i, i ^ p) for i in range(n_dev)])  54.5 us
    pallas_call x12, Pallas kernels, _cdf(): pl.pallas_call(functools.partial(_cdf_kernel, (peers, shard, base, width,...  36.7 us
    ppermute x15, starting transfers between devices, swap(): return lax.ppermute(a, 'vp', [(i, i ^ p) for i in range(n_dev)])  10.2 us
    unnamed x44, local copies, waits for them, and re-layouts  8.75 us
  transfers between devices with their start and end apart: 15, of which 8 were waited for; matrix products, arithmetic and copies ran while one was open for 0% of the time, Pallas kernels for 19%

profile of v3, /device:TPU:0, one launch (start us, length us, event | category | flops | bytes accessed | tf_op | source)
XLA Modules:
  0.0 190.0 jit_solution(8041027839503244963)
XLA Ops:
  0.6 77.4 %logits.1 = (f32[64,6144]{1,0:T(8,128)}, f32[64,6144]{1,0:T(8,128)}, f32[64,6144]{1,0:T(8,128)}, f32[64,6144]{1,0:T(8,128)}, f32[64,4096]{1,0:T(8,128)}, /*index...) custom-call(bf16[256,4096]{1,0:T(8,128)(2,1)} %x_ref.1, ...), custom_call_target="tpu_custom_call" | custom-call | flops 33554432000 | bytes 131072000 | tf_op jit(solution)/shard_map/logits/pallas_call | solution.py:262
  78.1 2.0 %collective-permute-start.6 = (f32[64,2048]{1,0:T(8,128)}, f32[64,2048]{1,0:T(8,128)S(1)}, u32[]{:S(2)}, u32[]{:S(2)}) collective-permute-start(f32[64,2048]{1,0:T(8,128)} %get-tuple-element.61), channel_id=1, source_target_pairs={{0,2},{1,3},{2,0},{3,1},{4,6},{5,7},{6,4},{7,5}} | collective-permute-start | bytes 1572872 | tf_op jit(solution)/shard_map/ppermute | solution.py:440
  80.6 1.1 collective-permute-done.10.refs_1_
  82.5 0.9 collective-permute-start.8
  83.4 9.7 %collective-permute-done.4.refs_0_ = f32[64,2048]{1,0:T(8,128)S(1)} collective-permute-done((f32[64,2048]{1,0:T(8,128)}, f32[64,2048]{1,0:T(8,128)S(1)}, u32[]{:S(2)}, u32[]{:S(2)}) %collective-permute-start.4) | collective-permute-done | bytes 524320 | tf_op jit(solution)/shard_map/ppermute | solution.py:440
  93.1 0.8 copy-done.5
  93.9 10.4 %collective-permute-done.6.refs_0_ = f32[64,2048]{1,0:T(8,128)S(1)} collective-permute-done((f32[64,2048]{1,0:T(8,128)}, f32[64,2048]{1,0:T(8,128)S(1)}, u32[]{:S(2)}, u32[]{:S(2)}) %collective-permute-start.6) | collective-permute-done | bytes 524320 | tf_op jit(solution)/shard_map/ppermute | solution.py:440
  105.1 8.7 %collective-permute-done.7.refs_1_ = f32[64,2048]{1,0:T(8,128)S(1)} collective-permute-done((f32[64,2048]{1,0:T(8,128)}, f32[64,2048]{1,0:T(8,128)S(1)}, u32[]{:S(2)}, u32[]{:S(2)}) %collective-permute-start.7) | collective-permute-done | bytes 524320 | tf_op jit(solution)/shard_map/ppermute | solution.py:440
  114.6 1.5 collective-permute-start.13
  116.2 0.8 copy-done.13
  117.0 1.5 merge.1
  118.5 1.6 collective-permute-start.2
  120.3 1.4 copy-done.2
  121.7 1.4 copy-done.3
  123.9 5.6 %cdf.12 = (f32[64,64000]{1,0:T(8,128)}, f32[64,128]{1,0:T(8,128)S(1)}) custom-call(f32[64,6144]{1,0:T(8,128)S(1)} %copy-done.2, f32[64,6144]{1,0:T(8,128)S(1)} %copy-done.3, f32[64,128]{1,0:T(8,128)S(1)} %copy-done.19), custom_call_target="tpu_custom_call" | custom-call | flops 603979776 | bytes 6291456 | tf_op jit(solution)/shard_map/cdf/pallas_call | solution.py:412
  129.5 1.2 copy-done.4
  130.7 4.0 %cdf.13 = (f32[64,64000]{1,0:T(8,128)}, f32[64,128]{1,0:T(8,128)S(1)}) custom-call(f32[64,4096]{1,0:T(8,128)S(1)} %copy-done.4, f32[64,4096]{1,0:T(8,128)S(1)} %collective-permute-done.14.refs_1_, f32[64,128]{1,0:T(8,128)S(1)} %get-tuple-element.84.refs_2_, f32[64,64000]{1,0:T(8,128)} %get-tuple-element.85.refs_3_), custom_call_target="tpu_custom_call", output_to_operand_aliasing={{0}: (3, {})} | custom-call | flops 402653184 | bytes 4194304 | tf_op jit(solution)/shard_map/cdf/pallas_call | solution.py:412
  134.7 3.4 %cdf.14 = (f32[64,64000]{1,0:T(8,128)}, f32[64,128]{1,0:T(8,128)S(1)}) custom-call(f32[64,2048]{1,0:T(8,128)S(1)} %copy-done.12, f32[64,2048]{1,0:T(8,128)} %collective-permute-done.13.refs_1_, f32[64,128]{1,0:T(8,128)S(1)} %get-tuple-element.86.refs_2_, f32[64,64000]{1,0:T(8,128)} %get-tuple-element.87.refs_3_), custom_call_target="tpu_custom_call", output_to_operand_aliasing={{0}: (3, {})} | custom-call | flops 201326592 | bytes 2097152 | tf_op jit(solution)/shard_map/cdf/pallas_call | solution.py:412
  138.2 1.7 collective-permute-start
  139.9 18.8 %collective-permute-done.9.refs_1_ = f32[64,4096]{1,0:T(8,128)S(1)} collective-permute-done((f32[64,4096]{1,0:T(8,128)}, f32[64,4096]{1,0:T(8,128)S(1)}, u32[]{:S(2)}, u32[]{:S(2)}) %collective-permute-start.9) | collective-permute-done | bytes 1048608 | tf_op jit(solution)/shard_map/ppermute | solution.py:440
  158.8 1.5 collective-permute-start.1
  160.3 2.4 %cdf.15 = (f32[64,64000]{1,0:T(8,128)}, f32[64,128]{1,0:T(8,128)S(1)}) custom-call(f32[64,2048]{1,0:T(8,128)S(1)} %copy-done.11, f32[64,2048]{1,0:T(8,128)S(1)} %copy-done.14, f32[64,128]{1,0:T(8,128)S(1)} %get-tuple-element.88.refs_2_, f32[64,64000]{1,0:T(8,128)} %get-tuple-element.89.refs_3_), custom_call_target="tpu_custom_call", output_to_operand_aliasing={{0}: (3, {})} | custom-call | flops 201326592 | bytes 2097152 | tf_op jit(solution)/shard_map/cdf/pallas_call | solution.py:412
  162.7 1.5 cdf.16
  164.3 1.1 cdf.17
  165.5 5.6 %cdf.18 = (f32[64,64000]{1,0:T(8,128)}, f32[64,128]{1,0:T(8,128)S(1)}) custom-call(f32[64,6144]{1,0:T(8,128)S(1)} %copy-done, f32[64,6144]{1,0:T(8,128)S(1)} %copy-done.1, f32[64,128]{1,0:T(8,128)S(1)} %get-tuple-element.94.refs_2_, f32[64,64000]{1,0:T(8,128)} %get-tuple-element.95.refs_3_), custom_call_target="tpu_custom_call", output_to_operand_aliasing={{0}: (3, {})} | custom-call | flops 603979776 | bytes 6291456 | tf_op jit(solution)/shard_map/cdf/pallas_call | solution.py:412
  171.1 4.0 %cdf.19 = (f32[64,64000]{1,0:T(8,128)}, f32[64,128]{1,0:T(8,128)S(1)}) custom-call(f32[64,4096]{1,0:T(8,128)S(1)} %collective-permute-done.8.refs_0_, f32[64,4096]{1,0:T(8,128)S(1)} %collective-permute-done.9.refs_1_, f32[64,128]{1,0:T(8,128)S(1)} %get-tuple-element.96.refs_2_, f32[64,64000]{1,0:T(8,128)} %get-tuple-element.97.refs_3_), custom_call_target="tpu_custom_call", output_to_operand_aliasing={{0}: (3, {})} | custom-call | flops 402653184 | bytes 4194304 | tf_op jit(solution)/shard_map/cdf/pallas_call | solution.py:412
  175.1 2.4 %cdf.20 = (f32[64,64000]{1,0:T(8,128)}, f32[64,128]{1,0:T(8,128)S(1)}) custom-call(f32[64,2048]{1,0:T(8,128)S(1)} %copy-done.8, f32[64,2048]{1,0:T(8,128)S(1)} %copy-done.10, f32[64,128]{1,0:T(8,128)S(1)} %get-tuple-element.98.refs_2_, f32[64,64000]{1,0:T(8,128)} %get-tuple-element.99.refs_3_), custom_call_target="tpu_custom_call", output_to_operand_aliasing={{0}: (3, {})} | custom-call | flops 201326592 | bytes 2097152 | tf_op jit(solution)/shard_map/cdf/pallas_call | solution.py:412
  177.5 3.4 %cdf.21 = (f32[64,64000]{1,0:T(8,128)}, f32[64,128]{1,0:T(8,128)S(1)}) custom-call(f32[64,2048]{1,0:T(8,128)S(1)} %copy-done.6, f32[64,2048]{1,0:T(8,128)} %collective-permute-done.5.refs_1_, f32[64,128]{1,0:T(8,128)S(1)} %get-tuple-element.100.refs_2_, f32[64,64000]{1,0:T(8,128)} %get-tuple-element.101.refs_3_), custom_call_target="tpu_custom_call", output_to_operand_aliasing={{0}: (3, {})} | custom-call | flops 201326592 | bytes 2097152 | tf_op jit(solution)/shard_map/cdf/pallas_call | solution.py:412
  181.2 1.5 cdf.22
  182.8 3.7 %collective-permute-done.refs_0_ = f32[64,640]{1,0:T(8,128)S(1)} collective-permute-done((f32[64,640]{1,0:T(8,128)S(1)}, f32[64,640]{1,0:T(8,128)S(1)}, u32[]{:S(2)}, u32[]{:S(2)}) %collective-permute-start) | collective-permute-done | bytes 163872 | tf_op jit(solution)/shard_map/ppermute | solution.py:440
  186.4 1.8 collective-permute-done.1.refs_1_
  188.2 1.7 cdf.23
  (56 shorter events, 4.3 us)
Async XLA Ops:
  78.0 15.0 %collective-permute-start.4 = (f32[64,2048]{1,0:T(8,128)}, f32[64,2048]{1,0:T(8,128)S(1)}, u32[]{:S(2)}, u32[]{:S(2)}) collective-permute-start(f32[64,2048]{1,0:T(8,128)} %get-tuple-element.59), channel_id=1, source_target_pairs={{0,2},{1,3},{2,0},{3,1},{4,6},{5,7},{6,4},{7,5}} | collective-permute-start | bytes 1572872 | tf_op jit(solution)/shard_map/ppermute | solution.py:440
  78.1 26.2 %collective-permute-start.6 = (f32[64,2048]{1,0:T(8,128)}, f32[64,2048]{1,0:T(8,128)S(1)}, u32[]{:S(2)}, u32[]{:S(2)}) collective-permute-start(f32[64,2048]{1,0:T(8,128)} %get-tuple-element.61), channel_id=1, source_target_pairs={{0,2},{1,3},{2,0},{3,1},{4,6},{5,7},{6,4},{7,5}} | collective-permute-start | bytes 1572872 | tf_op jit(solution)/shard_map/ppermute | solution.py:440
  80.1 1.6 collective-permute-start.10
  80.1 2.4 %collective-permute-start.11 = (f32[64,1024]{1,0:T(8,128)}, f32[64,1024]{1,0:T(8,128)S(1)}, u32[]{:S(2)}, u32[]{:S(2)}) collective-permute-start(f32[64,1024]{1,0:T(8,128)} %get-tuple-element.70), channel_id=1, source_target_pairs={{0,1},{1,0},{2,3},{3,2},{4,5},{5,4},{6,7},{7,6}} | collective-permute-start | bytes 786440 | tf_op jit(solution)/shard_map/ppermute | solution.py:440
  80.6 33.2 %collective-permute-start.7 = (f32[64,2048]{1,0:T(8,128)}, f32[64,2048]{1,0:T(8,128)S(1)}, u32[]{:S(2)}, u32[]{:S(2)}) collective-permute-start(f32[64,2048]{1,0:T(8,128)} %get-tuple-element.62), channel_id=1, source_target_pairs={{0,3},{1,2},{2,1},{3,0},{4,7},{5,6},{6,5},{7,4}} | collective-permute-start | bytes 1572872 | tf_op jit(solution)/shard_map/ppermute | solution.py:440
  82.3 37.8 %collective-permute-start.14 = (f32[64,4096]{1,0:T(8,128)}, f32[64,4096]{1,0:T(8,128)S(1)}, u32[]{:S(2)}, u32[]{:S(2)}) collective-permute-start(f32[64,4096]{1,0:T(8,128)} %get-tuple-element.76), channel_id=1, source_target_pairs={{0,1},{1,0},{2,3},{3,2},{4,5},{5,4},{6,7},{7,6}} | collective-permute-start | bytes 3145736 | tf_op jit(solution)/shard_map/ppermute | solution.py:440
  82.5 55.7 %collective-permute-start.8 = (f32[64,4096]{1,0:T(8,128)}, f32[64,4096]{1,0:T(8,128)S(1)}, u32[]{:S(2)}, u32[]{:S(2)}) collective-permute-start(f32[64,4096]{1,0:T(8,128)} %get-tuple-element.63), channel_id=1, source_target_pairs={{0,2},{1,3},{2,0},{3,1},{4,6},{5,7},{6,4},{7,5}} | collective-permute-start | bytes 3145736 | tf_op jit(solution)/shard_map/ppermute | solution.py:440
  93.9 64.9 %collective-permute-start.9 = (f32[64,4096]{1,0:T(8,128)}, f32[64,4096]{1,0:T(8,128)S(1)}, u32[]{:S(2)}, u32[]{:S(2)}) collective-permute-start(f32[64,4096]{1,0:T(8,128)} %get-tuple-element.64), channel_id=1, source_target_pairs={{0,3},{1,2},{2,1},{3,0},{4,7},{5,6},{6,5},{7,4}} | collective-permute-start | bytes 3145736 | tf_op jit(solution)/shard_map/ppermute | solution.py:440
  105.1 11.1 %collective-permute-start.12 = (f32[64,2048]{1,0:T(8,128)}, f32[64,2048]{1,0:T(8,128)S(1)}, u32[]{:S(2)}, u32[]{:S(2)}) collective-permute-start(f32[64,2048]{1,0:T(8,128)} %get-tuple-element.72), channel_id=1, source_target_pairs={{0,1},{1,0},{2,3},{3,2},{4,5},{5,4},{6,7},{7,6}} | collective-permute-start | bytes 1572872 | tf_op jit(solution)/shard_map/ppermute | solution.py:440
  114.6 3.9 %collective-permute-start.13 = (f32[64,2048]{1,0:T(8,128)}, f32[64,2048]{1,0:T(8,128)}, u32[]{:S(2)}, u32[]{:S(2)}) collective-permute-start(f32[64,2048]{1,0:T(8,128)} %get-tuple-element.74), channel_id=1, source_target_pairs={{0,1},{1,0},{2,3},{3,2},{4,5},{5,4},{6,7},{7,6}} | collective-permute-start | bytes 1572872 | tf_op jit(solution)/shard_map/ppermute | solution.py:440
  116.2 0.8 copy-start.13
  117.0 60.5 %collective-permute-start.5 = (f32[64,2048]{1,0:T(8,128)}, f32[64,2048]{1,0:T(8,128)}, u32[]{:S(2)}, u32[]{:S(2)}) collective-permute-start(f32[64,2048]{1,0:T(8,128)} %get-tuple-element.60), channel_id=1, source_target_pairs={{0,3},{1,2},{2,1},{3,0},{4,7},{5,6},{6,5},{7,4}} | collective-permute-start | bytes 1572872 | tf_op jit(solution)/shard_map/ppermute | solution.py:440
  118.5 62.4 %collective-permute-start.2 = (f32[64,1024]{1,0:T(8,128)}, f32[64,1024]{1,0:T(8,128)S(1)}, u32[]{:S(2)}, u32[]{:S(2)}) collective-permute-start(f32[64,1024]{1,0:T(8,128)} %get-tuple-element.57), channel_id=1, source_target_pairs={{0,2},{1,3},{2,0},{3,1},{4,6},{5,7},{6,4},{7,5}} | collective-permute-start | bytes 786440 | tf_op jit(solution)/shard_map/ppermute | solution.py:440
  120.2 61.1 %collective-permute-start.3 = (f32[64,1024]{1,0:T(8,128)}, f32[64,1024]{1,0:T(8,128)S(1)}, u32[]{:S(2)}, u32[]{:S(2)}) collective-permute-start(f32[64,1024]{1,0:T(8,128)} %get-tuple-element.58), channel_id=1, source_target_pairs={{0,3},{1,2},{2,1},{3,0},{4,7},{5,6},{6,5},{7,4}} | collective-permute-start | bytes 786440 | tf_op jit(solution)/shard_map/ppermute | solution.py:440
  120.3 1.4 copy-start.2
  121.7 1.4 copy-start.3
  123.9 10.8 %copy-start.12 = (f32[64,2048]{1,0:T(8,128)S(1)}, f32[64,2048]{1,0:T(8,128)}, u32[]{:S(2)}) copy-start(f32[64,2048]{1,0:T(8,128)} %get-tuple-element.73.refs_0_) | copy-start | bytes 1572868
  129.5 1.2 copy-start.4
  130.7 7.5 %copy-start.21 = (f32[64,640]{1,0:T(8,128)S(1)}, f32[64,640]{1,0:T(8,128)}, u32[]{:S(2)}) copy-start(f32[64,640]{1,0:T(8,128)} %get-tuple-element.55) | copy-start | bytes 491524
  130.7 28.0 %copy-start.20 = (f32[64,640]{1,0:T(8,128)S(1)}, f32[64,640]{1,0:T(8,128)}, u32[]{:S(2)}) copy-start(f32[64,640]{1,0:T(8,128)} %get-tuple-element.56) | copy-start | bytes 491524
  130.7 29.6 %copy-start.11 = (f32[64,2048]{1,0:T(8,128)S(1)}, f32[64,2048]{1,0:T(8,128)}, u32[]{:S(2)}) copy-start(f32[64,2048]{1,0:T(8,128)} %get-tuple-element.71.refs_0_) | copy-start | bytes 1572868
  130.7 29.6 %copy-start.14 = (f32[64,2048]{1,0:T(8,128)S(1)}, f32[64,2048]{1,0:T(8,128)}, u32[]{:S(2)}) copy-start(f32[64,2048]{1,0:T(8,128)} %copy-done.13) | copy-start | bytes 1572868
  134.7 28.0 %copy-start.15 = (f32[64,1024]{1,0:T(8,128)S(1)}, f32[64,1024]{1,0:T(8,128)}, u32[]{:S(2)}) copy-start(f32[64,1024]{1,0:T(8,128)} %get-tuple-element.69.refs_0_) | copy-start | bytes 786436
  138.2 48.3 %collective-permute-start = (f32[64,640]{1,0:T(8,128)S(1)}, f32[64,640]{1,0:T(8,128)S(1)}, u32[]{:S(2)}, u32[]{:S(2)}) collective-permute-start(f32[64,640]{1,0:T(8,128)S(1)} %copy-done.21), channel_id=1, source_target_pairs={{0,2},{1,3},{2,0},{3,1},{4,6},{5,7},{6,4},{7,5}} | collective-permute-start | bytes 491528 | tf_op jit(solution)/shard_map/ppermute | solution.py:440
  158.8 29.5 %collective-permute-start.1 = (f32[64,640]{1,0:T(8,128)S(1)}, f32[64,640]{1,0:T(8,128)S(1)}, u32[]{:S(2)}, u32[]{:S(2)}) collective-permute-start(f32[64,640]{1,0:T(8,128)S(1)} %copy-done.20), channel_id=1, source_target_pairs={{0,3},{1,2},{2,1},{3,0},{4,7},{5,6},{6,5},{7,4}} | collective-permute-start | bytes 491528 | tf_op jit(solution)/shard_map/ppermute | solution.py:440
  160.3 4.0 %copy-start.16 = (f32[64,640]{1,0:T(8,128)S(1)}, f32[64,640]{1,0:T(8,128)}, u32[]{:S(2)}) copy-start(f32[64,640]{1,0:T(8,128)} %get-tuple-element.67.refs_0_) | copy-start | bytes 491524
  160.3 4.0 %copy-start.18 = (f32[64,640]{1,0:T(8,128)S(1)}, f32[64,640]{1,0:T(8,128)}, u32[]{:S(2)}) copy-start(f32[64,640]{1,0:T(8,128)} %copy-done.17) | copy-start | bytes 491524
  162.7 2.7 %copy-start = (f32[64,6144]{1,0:T(8,128)S(1)}, f32[64,6144]{1,0:T(8,128)}, u32[]{:S(2)}) copy-start(f32[64,6144]{1,0:T(8,128)} %get-tuple-element.65.refs_0_) | copy-start | bytes 4718596
  162.7 2.7 %copy-start.1 = (f32[64,6144]{1,0:T(8,128)S(1)}, f32[64,6144]{1,0:T(8,128)}, u32[]{:S(2)}) copy-start(f32[64,6144]{1,0:T(8,128)} %get-tuple-element.66.refs_1_) | copy-start | bytes 4718596
  165.5 9.6 %copy-start.8 = (f32[64,2048]{1,0:T(8,128)S(1)}, f32[64,2048]{1,0:T(8,128)}, u32[]{:S(2)}) copy-start(f32[64,2048]{1,0:T(8,128)} %copy-done.7) | copy-start | bytes 1572868
  165.5 9.6 %copy-start.10 = (f32[64,2048]{1,0:T(8,128)S(1)}, f32[64,2048]{1,0:T(8,128)}, u32[]{:S(2)}) copy-start(f32[64,2048]{1,0:T(8,128)} %copy-done.9) | copy-start | bytes 1572868
  171.1 6.4 %copy-start.6 = (f32[64,2048]{1,0:T(8,128)S(1)}, f32[64,2048]{1,0:T(8,128)}, u32[]{:S(2)}) copy-start(f32[64,2048]{1,0:T(8,128)} %copy-done.5) | copy-start | bytes 1572868
  (5 other events, 3.8 us)

commit v4 on v3

--- a/solution.py
+++ b/solution.py
@@ -12,10 +12,10 @@
 UNIT = 512
 HALF = 256
 DEPTH = 512
-SLOTS = 6
-EARLY = ((512, 2), (1024, 1), (2048, 2))
-LATE = (4096, 2048, 2048, 1024, 640)
-LATE_UNITS = ((2048, 2), (2048, 1), (2048, 1), (1024, 1), (640, 1))
+SLOTS = 9
+EARLY = ((256, 2), (512, 1), (1024, 1), (2048, 3))
+LATE = (4096, 2048, 1024, 640)
+LATE_UNITS = ((2048, 2), (2048, 1), (1024, 1), (640, 1))
 
 
 def _to_rows(vec_1xn):
@@ -130,7 +130,7 @@
 
     def finish(col, width, out_ref, out_off):
         group = 32
-        span = UNIT if width % UNIT == 0 else LANES
+        span = next(n for n in (UNIT, HALF, LANES) if width % n == 0)
 
         def some(j, _):
             at = pl.multiple_of(j * span, span)
@@ -290,7 +290,7 @@
             dma((n_dev,)),
         ],
         compiler_params=pltpu.CompilerParams(
-            collective_id=0, has_side_effects=True, vmem_limit_bytes=40 * 2**20
+            collective_id=0, has_side_effects=True, vmem_limit_bytes=52 * 2**20
         ),
         cost_estimate=pl.CostEstimate(
             flops=2 * batch * depth * shard,
@@ -455,8 +455,11 @@
         params, at_target = _merge(packs)
         out = None
         for peers in ((0, 1), (2, 3)):
-            for begin, got in chunks:
-                out, params = _cdf([got[p] for p in peers], peers, params, out, n_dev, shard, begin)
+            for k, (begin, got) in enumerate(chunks):
+                blocks = [got[p] for p in peers]
+                if k < len(chunks) - 1 or peers[0] == 0:
+                    blocks = [pltpu.with_memory_space_constraint(a, pltpu.HBM) for a in blocks]
+                out, params = _cdf(blocks, peers, params, out, n_dev, shard, begin)
         return out, at_target.reshape(-1)
 
     return jax.shard_map(

time: 190 us -> 213 us (1.12)
  Pallas kernels: 116 us -> 147 us
  local copies, waits for them, and re-layouts: 8.75 us -> 1.55 us
  starting transfers between devices: 10.2 us -> 6.62 us
  waiting for transfers between devices: 54.5 us -> 56.7 us
    pallas_call x1, Pallas kernels: 77.4 us -> 99.3 us  [_logits(): pl.pallas_call(functools.partial(_logits_kernel, (n_dev, shard, segments,...]
    pallas_call x12 -> x10, Pallas kernels: 36.7 us -> 46.4 us  [_cdf(): pl.pallas_call(functools.partial(_cdf_kernel, (peers, shard, base, width,...]
    unnamed x44 -> x20, local copies, waits for them, and re-layouts: 8.75 us -> 1.55 us
    ppermute x15 -> x12, starting transfers between devices: 10.2 us -> 6.62 us  [swap(): return lax.ppermute(a, 'vp', [(i, i ^ p) for i in range(n_dev)])]
    ppermute x15 -> x12, waiting for transfers between devices: 54.5 us -> 56.7 us  [swap(): return lax.ppermute(a, 'vp', [(i, i ^ p) for i in range(n_dev)])]
  transfers between devices with their start and end apart: 15 -> 12, of which waited for: 8 -> 3; matrix products, arithmetic and copies ran while one was open for 0% -> 0% of each run, Pallas kernels for 19% -> 22%
where the time goes in v4:
time: 213 us
  Pallas kernels  147 us (69%)
  waiting for transfers between devices  56.7 us (27%)
  starting transfers between devices  6.62 us (3%)
    pallas_call x1, Pallas kernels, _logits(): pl.pallas_call(functools.partial(_logits_kernel, (n_dev, shard, segments,...  99.3 us
    ppermute x12, waiting for transfers between devices, swap(): return lax.ppermute(a, 'vp', [(i, i ^ p) for i in range(n_dev)])  56.7 us
    pallas_call x10, Pallas kernels, _cdf(): pl.pallas_call(functools.partial(_cdf_kernel, (peers, shard, base, width,...  46.4 us
    ppermute x12, starting transfers between devices, swap(): return lax.ppermute(a, 'vp', [(i, i ^ p) for i in range(n_dev)])  6.62 us
  transfers between devices with their start and end apart: 12, of which 3 were waited for; matrix products, arithmetic and copies ran while one was open for 0% of the time, Pallas kernels for 22%

profile of v4, /device:TPU:0, one launch (start us, length us, event | category | flops | bytes accessed | tf_op | source)
XLA Modules:
  0.0 212.9 jit_solution(1012880540538741591)
XLA Ops:
  0.6 99.3 %logits.1 = (f32[64,8192]{1,0:T(8,128)}, f32[64,8192]{1,0:T(8,128)}, f32[64,8192]{1,0:T(8,128)}, f32[64,8192]{1,0:T(8,128)}, f32[64,4096]{1,0:T(8,128)}, /*index...) custom-call(bf16[256,4096]{1,0:T(8,128)(2,1)} %x_ref.1, ...), custom_call_target="tpu_custom_call" | custom-call | flops 33554432000 | bytes 131072000 | tf_op jit(solution)/shard_map/logits/pallas_call | solution.py:262
  100.0 0.1 collective-permute-start.11
  100.1 0.4 collective-permute-start.8
  100.5 1.5 collective-permute-start.7
  102.0 0.7 collective-permute-start.9
  102.6 0.5 collective-permute-done.8.refs_1_
  103.1 0.0 collective-permute-start.4
  103.1 0.9 collective-permute-done.9.refs_1_
  104.0 0.4 collective-permute-start.10
  104.4 55.3 %collective-permute-done.4.refs_0_ = f32[64,2048]{1,0:T(8,128)} collective-permute-done((f32[64,2048]{1,0:T(8,128)}, f32[64,2048]{1,0:T(8,128)}, u32[]{:S(2)}, u32[]{:S(2)}) %collective-permute-start.4) | collective-permute-done | bytes 524320 | tf_op jit(solution)/shard_map/ppermute | solution.py:440
  159.7 0.0 collective-permute-start.5
  159.7 1.5 merge.1
  161.2 0.9 collective-permute-start.2
  162.1 0.9 collective-permute-start.3
  163.0 0.8 copy-done
  163.8 9.5 %cdf.10 = (f32[64,64000]{1,0:T(8,128)}, f32[64,128]{1,0:T(8,128)S(1)}) custom-call(f32[64,8192]{1,0:T(8,128)} %get-tuple-element.65.refs_0_, f32[64,8192]{1,0:T(8,128)} %get-tuple-element.66.refs_1_, f32[64,128]{1,0:T(8,128)S(1)} %copy-done), custom_call_target="tpu_custom_call" | custom-call | flops 805306368 | bytes 8388608 | tf_op jit(solution)/shard_map/cdf/pallas_call | solution.py:412
  173.3 5.5 %cdf.11 = (f32[64,64000]{1,0:T(8,128)}, f32[64,128]{1,0:T(8,128)S(1)}) custom-call(f32[64,4096]{1,0:T(8,128)} %get-tuple-element.63.refs_0_, f32[64,4096]{1,0:T(8,128)} %copy-done.3, f32[64,128]{1,0:T(8,128)S(1)} %get-tuple-element.72.refs_2_, f32[64,64000]{1,0:T(8,128)} %get-tuple-element.73.refs_3_), custom_call_target="tpu_custom_call", output_to_operand_aliasing={{0}: (3, {})} | custom-call | flops 402653184 | bytes 4194304 | tf_op jit(solution)/shard_map/cdf/pallas_call | solution.py:412
  178.8 0.0 collective-permute-done.6.refs_0_
  178.8 1.7 collective-permute-start
  180.5 0.0 collective-permute-done.7.refs_1_
  180.6 0.1 collective-permute-start.1
  180.6 3.9 %cdf.12 = (f32[64,64000]{1,0:T(8,128)}, f32[64,128]{1,0:T(8,128)S(1)}) custom-call(f32[64,2048]{1,0:T(8,128)} %get-tuple-element.61.refs_0_, f32[64,2048]{1,0:T(8,128)} %collective-permute-done.10.refs_1_, f32[64,128]{1,0:T(8,128)S(1)} %get-tuple-element.74.refs_2_, f32[64,64000]{1,0:T(8,128)} %get-tuple-element.75.refs_3_), custom_call_target="tpu_custom_call", output_to_operand_aliasing={{0}: (3, {})} | custom-call | flops 201326592 | bytes 2097152 | tf_op jit(solution)/shard_map/cdf/pallas_call | solution.py:412
  184.5 2.6 %cdf.13 = (f32[64,64000]{1,0:T(8,128)}, f32[64,128]{1,0:T(8,128)S(1)}) custom-call(f32[64,1024]{1,0:T(8,128)} %get-tuple-element.59.refs_0_, f32[64,1024]{1,0:T(8,128)} %copy-done.6, f32[64,128]{1,0:T(8,128)S(1)} %get-tuple-element.76.refs_2_, f32[64,64000]{1,0:T(8,128)} %get-tuple-element.77.refs_3_), custom_call_target="tpu_custom_call", output_to_operand_aliasing={{0}: (3, {})} | custom-call | flops 100663296 | bytes 1048576 | tf_op jit(solution)/shard_map/cdf/pallas_call | solution.py:412
  187.1 2.1 %cdf.14 = (f32[64,64000]{1,0:T(8,128)}, f32[64,128]{1,0:T(8,128)S(1)}) custom-call(f32[64,640]{1,0:T(8,128)} %get-tuple-element.57.refs_0_, f32[64,640]{1,0:T(8,128)} %copy-done.7, f32[64,128]{1,0:T(8,128)S(1)} %get-tuple-element.78.refs_2_, f32[64,64000]{1,0:T(8,128)} %get-tuple-element.79.refs_3_), custom_call_target="tpu_custom_call", output_to_operand_aliasing={{0}: (3, {})} | custom-call | flops 62914560 | bytes 655360 | tf_op jit(solution)/shard_map/cdf/pallas_call | solution.py:412
  189.3 9.4 %cdf.15 = (f32[64,64000]{1,0:T(8,128)}, f32[64,128]{1,0:T(8,128)S(1)}) custom-call(f32[64,8192]{1,0:T(8,128)} %get-tuple-element.55.refs_0_, f32[64,8192]{1,0:T(8,128)} %get-tuple-element.56.refs_1_, f32[64,128]{1,0:T(8,128)S(1)} %get-tuple-element.80.refs_2_, f32[64,64000]{1,0:T(8,128)} %get-tuple-element.81.refs_3_), custom_call_target="tpu_custom_call", output_to_operand_aliasing={{0}: (3, {})} | custom-call | flops 805306368 | bytes 8388608 | tf_op jit(solution)/shard_map/cdf/pallas_call | solution.py:412
  198.7 5.5 %cdf.16 = (f32[64,64000]{1,0:T(8,128)}, f32[64,128]{1,0:T(8,128)S(1)}) custom-call(f32[64,4096]{1,0:T(8,128)} %copy-done.1, f32[64,4096]{1,0:T(8,128)} %copy-done.2, f32[64,128]{1,0:T(8,128)S(1)} %get-tuple-element.82.refs_2_, f32[64,64000]{1,0:T(8,128)} %get-tuple-element.83.refs_3_), custom_call_target="tpu_custom_call", output_to_operand_aliasing={{0}: (3, {})} | custom-call | flops 402653184 | bytes 4194304 | tf_op jit(solution)/shard_map/cdf/pallas_call | solution.py:412
  204.2 0.0 collective-permute-done.5.refs_1_
  204.2 3.6 %cdf.17 = (f32[64,64000]{1,0:T(8,128)}, f32[64,128]{1,0:T(8,128)S(1)}) custom-call(f32[64,2048]{1,0:T(8,128)} %collective-permute-done.4.refs_0_, f32[64,2048]{1,0:T(8,128)} %collective-permute-done.5.refs_1_, f32[64,128]{1,0:T(8,128)S(1)} %get-tuple-element.84.refs_2_, f32[64,64000]{1,0:T(8,128)} %get-tuple-element.85.refs_3_), custom_call_target="tpu_custom_call", output_to_operand_aliasing={{0}: (3, {})} | custom-call | flops 201326592 | bytes 2097152 | tf_op jit(solution)/shard_map/cdf/pallas_call | solution.py:412
  207.8 0.7 copy-done.4
  208.5 0.1 copy-done.5
  208.6 2.6 %cdf.18 = (f32[64,64000]{1,0:T(8,128)}, f32[64,128]{1,0:T(8,128)S(1)}) custom-call(f32[64,1024]{1,0:T(8,128)} %copy-done.4, f32[64,1024]{1,0:T(8,128)} %copy-done.5, f32[64,128]{1,0:T(8,128)S(1)} %get-tuple-element.86.refs_2_, f32[64,64000]{1,0:T(8,128)} %get-tuple-element.87.refs_3_), custom_call_target="tpu_custom_call", output_to_operand_aliasing={{0}: (3, {})} | custom-call | flops 100663296 | bytes 1048576 | tf_op jit(solution)/shard_map/cdf/pallas_call | solution.py:412
  211.2 1.7 cdf.19
  (24 shorter events, 0.1 us)
Async XLA Ops:
  100.0 62.1 %collective-permute-start.11 = (f32[64,4096]{1,0:T(8,128)}, f32[64,4096]{1,0:T(8,128)S(1)}, u32[]{:S(2)}, u32[]{:S(2)}) collective-permute-start(f32[64,4096]{1,0:T(8,128)} %get-tuple-element.64), channel_id=1, source_target_pairs={{0,1},{1,0},{2,3},{3,2},{4,5},{5,4},{6,7},{7,6}} | collective-permute-start | bytes 3145736 | tf_op jit(solution)/shard_map/ppermute | solution.py:440
  100.1 3.0 %collective-permute-start.8 = (f32[64,640]{1,0:T(8,128)}, f32[64,640]{1,0:T(8,128)S(1)}, u32[]{:S(2)}, u32[]{:S(2)}) collective-permute-start(f32[64,640]{1,0:T(8,128)} %get-tuple-element.58), channel_id=1, source_target_pairs={{0,1},{1,0},{2,3},{3,2},{4,5},{5,4},{6,7},{7,6}} | collective-permute-start | bytes 491528 | tf_op jit(solution)/shard_map/ppermute | solution.py:440
  100.5 78.3 %collective-permute-start.6 = (f32[64,4096]{1,0:T(8,128)}, f32[64,4096]{1,0:T(8,128)S(1)}, u32[]{:S(2)}, u32[]{:S(2)}) collective-permute-start(f32[64,4096]{1,0:T(8,128)} %get-tuple-element.53), channel_id=1, source_target_pairs={{0,2},{1,3},{2,0},{3,1},{4,6},{5,7},{6,4},{7,5}} | collective-permute-start | bytes 3145736 | tf_op jit(solution)/shard_map/ppermute | solution.py:440
  100.5 80.0 %collective-permute-start.7 = (f32[64,4096]{1,0:T(8,128)}, f32[64,4096]{1,0:T(8,128)S(1)}, u32[]{:S(2)}, u32[]{:S(2)}) collective-permute-start(f32[64,4096]{1,0:T(8,128)} %get-tuple-element.54), channel_id=1, source_target_pairs={{0,3},{1,2},{2,1},{3,0},{4,7},{5,6},{6,5},{7,4}} | collective-permute-start | bytes 3145736 | tf_op jit(solution)/shard_map/ppermute | solution.py:440
  102.0 2.1 collective-permute-start.9
  103.1 0.9 copy-start.7
  103.1 56.6 %collective-permute-start.4 = (f32[64,2048]{1,0:T(8,128)}, f32[64,2048]{1,0:T(8,128)}, u32[]{:S(2)}, u32[]{:S(2)}) collective-permute-start(f32[64,2048]{1,0:T(8,128)} %get-tuple-element.51), channel_id=1, source_target_pairs={{0,2},{1,3},{2,0},{3,1},{4,6},{5,7},{6,4},{7,5}} | collective-permute-start | bytes 1572872 | tf_op jit(solution)/shard_map/ppermute | solution.py:440
  104.0 80.5 %copy-start.6 = (f32[64,1024]{1,0:T(8,128)}, f32[64,1024]{1,0:T(8,128)S(1)}, u32[]{:S(2)}) copy-start(f32[64,1024]{1,0:T(8,128)S(1)} %collective-permute-done.9.refs_1_) | copy-start | bytes 786436
  104.0 57.2 %collective-permute-start.10 = (f32[64,2048]{1,0:T(8,128)}, f32[64,2048]{1,0:T(8,128)}, u32[]{:S(2)}, u32[]{:S(2)}) collective-permute-start(f32[64,2048]{1,0:T(8,128)} %get-tuple-element.62), channel_id=1, source_target_pairs={{0,1},{1,0},{2,3},{3,2},{4,5},{5,4},{6,7},{7,6}} | collective-permute-start | bytes 1572872 | tf_op jit(solution)/shard_map/ppermute | solution.py:440
  159.7 44.5 %collective-permute-start.5 = (f32[64,2048]{1,0:T(8,128)}, f32[64,2048]{1,0:T(8,128)}, u32[]{:S(2)}, u32[]{:S(2)}) collective-permute-start(f32[64,2048]{1,0:T(8,128)} %get-tuple-element.52), channel_id=1, source_target_pairs={{0,3},{1,2},{2,1},{3,0},{4,7},{5,6},{6,5},{7,4}} | collective-permute-start | bytes 1572872 | tf_op jit(solution)/shard_map/ppermute | solution.py:440
  161.2 46.6 %collective-permute-start.2 = (f32[64,1024]{1,0:T(8,128)}, f32[64,1024]{1,0:T(8,128)S(1)}, u32[]{:S(2)}, u32[]{:S(2)}) collective-permute-start(f32[64,1024]{1,0:T(8,128)} %get-tuple-element.49), channel_id=1, source_target_pairs={{0,2},{1,3},{2,0},{3,1},{4,6},{5,7},{6,4},{7,5}} | collective-permute-start | bytes 786440 | tf_op jit(solution)/shard_map/ppermute | solution.py:440
  162.1 11.1 %copy-start.3 = (f32[64,4096]{1,0:T(8,128)}, f32[64,4096]{1,0:T(8,128)S(1)}, u32[]{:S(2)}) copy-start(f32[64,4096]{1,0:T(8,128)S(1)} %collective-permute-done.11.refs_1_) | copy-start | bytes 3145732
  162.1 45.7 %collective-permute-start.3 = (f32[64,1024]{1,0:T(8,128)}, f32[64,1024]{1,0:T(8,128)S(1)}, u32[]{:S(2)}, u32[]{:S(2)}) collective-permute-start(f32[64,1024]{1,0:T(8,128)} %get-tuple-element.50), channel_id=1, source_target_pairs={{0,3},{1,2},{2,1},{3,0},{4,7},{5,6},{6,5},{7,4}} | collective-permute-start | bytes 786440 | tf_op jit(solution)/shard_map/ppermute | solution.py:440
  163.0 0.8 copy-start
  163.8 15.0 %copy-start.9 = (f32[64,640]{1,0:T(8,128)S(1)}, f32[64,640]{1,0:T(8,128)}, u32[]{:S(2)}) copy-start(f32[64,640]{1,0:T(8,128)} %get-tuple-element.47) | copy-start | bytes 491524
  163.8 16.8 %copy-start.8 = (f32[64,640]{1,0:T(8,128)S(1)}, f32[64,640]{1,0:T(8,128)}, u32[]{:S(2)}) copy-start(f32[64,640]{1,0:T(8,128)} %get-tuple-element.48) | copy-start | bytes 491524
  178.8 8.3 %copy-start.1 = (f32[64,4096]{1,0:T(8,128)}, f32[64,4096]{1,0:T(8,128)S(1)}, u32[]{:S(2)}) copy-start(f32[64,4096]{1,0:T(8,128)S(1)} %collective-permute-done.6.refs_0_) | copy-start | bytes 3145732
  178.8 32.4 %collective-permute-start = (f32[64,640]{1,0:T(8,128)S(1)}, f32[64,640]{1,0:T(8,128)S(1)}, u32[]{:S(2)}, u32[]{:S(2)}) collective-permute-start(f32[64,640]{1,0:T(8,128)S(1)} %copy-done.9), channel_id=1, source_target_pairs={{0,2},{1,3},{2,0},{3,1},{4,6},{5,7},{6,4},{7,5}} | collective-permute-start | bytes 491528 | tf_op jit(solution)/shard_map/ppermute | solution.py:440
  180.6 6.6 %copy-start.2 = (f32[64,4096]{1,0:T(8,128)}, f32[64,4096]{1,0:T(8,128)S(1)}, u32[]{:S(2)}) copy-start(f32[64,4096]{1,0:T(8,128)S(1)} %collective-permute-done.7.refs_1_) | copy-start | bytes 3145732
  180.6 30.6 %collective-permute-start.1 = (f32[64,640]{1,0:T(8,128)S(1)}, f32[64,640]{1,0:T(8,128)S(1)}, u32[]{:S(2)}, u32[]{:S(2)}) collective-permute-start(f32[64,640]{1,0:T(8,128)S(1)} %copy-done.8), channel_id=1, source_target_pairs={{0,3},{1,2},{2,1},{3,0},{4,7},{5,6},{6,5},{7,4}} | collective-permute-start | bytes 491528 | tf_op jit(solution)/shard_map/ppermute | solution.py:440
  207.8 0.7 copy-start.4
  207.8 0.8 copy-start.5

commit v5 on v4

--- a/solution.py
+++ b/solution.py
@@ -14,8 +14,8 @@
 DEPTH = 512
 SLOTS = 9
 EARLY = ((256, 2), (512, 1), (1024, 1), (2048, 3))
-LATE = (4096, 2048, 1024, 640)
-LATE_UNITS = ((2048, 2), (2048, 1), (1024, 1), (640, 1))
+LATE = (4096, 2048, 1280, 384)
+LATE_UNITS = ((2048, 2), (2048, 1), (1280, 1), (384, 1))
 
 
 def _to_rows(vec_1xn):
@@ -350,10 +350,13 @@
 
 
 def _cdf_kernel(cfg, *refs):
-    peers, shard, base, width, first = cfg
+    peers, shard, base, width, first, last = cfg
     n = len(peers)
     params_ref = refs[n]
-    out_ref, params_out, y_ref, sems = refs[n + (1 if first else 2):]
+    if last:
+        out_ref, y_ref, sems = refs[n + 2:]
+    else:
+        out_ref, params_out, y_ref, sems = refs[n + (1 if first else 2):]
     me = lax.axis_index("vp")
     rows = params_ref.shape[0]
     params = params_ref[...]
@@ -398,25 +401,24 @@
         copy.start()
         copies.append(copy)
         updated = jnp.where(lane == 2 + p, carries[j], updated)
-    params_out[...] = updated
+    if not last:
+        params_out[...] = updated
     for copy in copies:
         copy.wait()
 
 
-def _cdf(blocks, peers, params, out, n_dev, shard, base):
+def _cdf(blocks, peers, params, out, n_dev, shard, base, last=False):
     rows, width = blocks[0].shape
     n = len(peers)
     first = out is None
     vmem = pl.BlockSpec(memory_space=pltpu.VMEM)
     hbm = pl.BlockSpec(memory_space=pl.ANY)
     return pl.pallas_call(
-        functools.partial(_cdf_kernel, (peers, shard, base, width, first)),
+        functools.partial(_cdf_kernel, (peers, shard, base, width, first, last)),
         in_specs=[vmem] * (n + 1) + ([] if first else [hbm]),
-        out_specs=[hbm, vmem],
-        out_shape=[
-            jax.ShapeDtypeStruct((rows, n_dev * shard), jnp.float32),
-            jax.ShapeDtypeStruct(params.shape, jnp.float32),
-        ],
+        out_specs=[hbm] + ([] if last else [vmem]),
+        out_shape=[jax.ShapeDtypeStruct((rows, n_dev * shard), jnp.float32)]
+        + ([] if last else [jax.ShapeDtypeStruct(params.shape, jnp.float32)]),
         scratch_shapes=[
             pltpu.VMEM((n, rows, width), jnp.float32),
             pltpu.SemaphoreType.DMA((n,)),
@@ -454,12 +456,17 @@
             begin += made[0].shape[1]
         params, at_target = _merge(packs)
         out = None
-        for peers in ((0, 1), (2, 3)):
-            for k, (begin, got) in enumerate(chunks):
-                blocks = [got[p] for p in peers]
-                if k < len(chunks) - 1 or peers[0] == 0:
-                    blocks = [pltpu.with_memory_space_constraint(a, pltpu.HBM) for a in blocks]
-                out, params = _cdf(blocks, peers, params, out, n_dev, shard, begin)
+        final = len(chunks) - 1
+        plan = [(k, (0, 1)) for k in range(final + 1)] + [(k, (2, 3)) for k in range(final)]
+        plan += [(final, (2,)), (final, (3,))]
+        for i, (k, peers) in enumerate(plan):
+            begin, got = chunks[k]
+            blocks = [got[p] for p in peers]
+            if k < final or peers[0] == 0:
+                blocks = [pltpu.with_memory_space_constraint(a, pltpu.HBM) for a in blocks]
+            res = _cdf(blocks, peers, params, out, n_dev, shard, begin, i == len(plan) - 1)
+            out = res[0]
+            params = res[1] if len(res) > 1 else None
         return out, at_target.reshape(-1)
 
     return jax.shard_map(

time: 213 us -> 214 us (level)
    pallas_call x10 -> x11, Pallas kernels: 46.4 us -> 46.6 us  [_cdf(): pl.pallas_call(functools.partial(_cdf_kernel, (peers, shard, base, width,...]
  transfers between devices with their start and end apart: 12 -> 12, of which waited for: 3 -> 2; matrix products, arithmetic and copies ran while one was open for 0% -> 0% of each run, Pallas kernels for 22% -> 22%
where the time goes in v5:
time: 214 us; the launch traced here: 213 us
  Pallas kernels  147 us (69%)
  waiting for transfers between devices  55.4 us (26%)
  starting transfers between devices  6.65 us (3%)
  local copies, waits for them, and re-layouts  2.86 us (1%)
    pallas_call x1, Pallas kernels, _logits(): pl.pallas_call(functools.partial(_logits_kernel, (n_dev, shard, segments,...  99.3 us
    ppermute x12, waiting for transfers between devices, swap(): return lax.ppermute(a, 'vp', [(i, i ^ p) for i in range(n_dev)])  55.4 us
    pallas_call x11, Pallas kernels, _cdf(): pl.pallas_call(functools.partial(_cdf_kernel, (peers, shard, base, width,...  46.6 us
    ppermute x12, starting transfers between devices, swap(): return lax.ppermute(a, 'vp', [(i, i ^ p) for i in range(n_dev)])  6.65 us
  transfers between devices with their start and end apart: 12, of which 2 were waited for; matrix products, arithmetic and copies ran while one was open for 0% of the time, Pallas kernels for 22%

profile of v5, /device:TPU:0, one launch (start us, length us, event | category | flops | bytes accessed | tf_op | source)
XLA Modules:
  0.0 213.2 jit_solution(13826271973125999441)
XLA Ops:
  0.6 99.3 %logits.1 = (f32[64,8192]{1,0:T(8,128)}, f32[64,8192]{1,0:T(8,128)}, f32[64,8192]{1,0:T(8,128)}, f32[64,8192]{1,0:T(8,128)}, f32[64,4096]{1,0:T(8,128)}, /*index...) custom-call(bf16[256,4096]{1,0:T(8,128)(2,1)} %x_ref.1, ...), custom_call_target="tpu_custom_call" | custom-call | flops 33554432000 | bytes 131072000 | tf_op jit(solution)/shard_map/logits/pallas_call | solution.py:262
  100.0 0.1 collective-permute-start.11
  100.1 0.0 collective-permute-start.6
  100.1 1.7 collective-permute-start.7
  101.9 0.4 collective-permute-start.9
  102.2 0.1 collective-permute-start.8
  102.4 1.5 collective-permute-done.8.refs_1_
  103.9 0.6 copy-done.8
  104.5 0.3 collective-permute-start.4
  104.8 0.7 copy-done.7
  105.5 0.1 collective-permute-start.10
  105.6 53.9 %collective-permute-done.4.refs_0_ = f32[64,2048]{1,0:T(8,128)S(1)} collective-permute-done((f32[64,2048]{1,0:T(8,128)}, f32[64,2048]{1,0:T(8,128)S(1)}, u32[]{:S(2)}, u32[]{:S(2)}) %collective-permute-start.4) | collective-permute-done | bytes 524320 | tf_op jit(solution)/shard_map/ppermute | solution.py:442
  159.5 1.2 collective-permute-start.2
  160.7 1.4 collective-permute-start.3
  162.1 1.5 merge.1
  163.6 0.8 copy-done
  164.3 9.4 %cdf.11 = (f32[64,64000]{1,0:T(8,128)}, f32[64,128]{1,0:T(8,128)S(1)}) custom-call(f32[64,8192]{1,0:T(8,128)} %get-tuple-element.66.refs_0_, f32[64,8192]{1,0:T(8,128)} %get-tuple-element.67.refs_1_, f32[64,128]{1,0:T(8,128)S(1)} %copy-done), custom_call_target="tpu_custom_call" | custom-call | flops 805306368 | bytes 8388608 | tf_op jit(solution)/shard_map/cdf/pallas_call | solution.py:416
  173.8 5.5 %cdf.12 = (f32[64,64000]{1,0:T(8,128)}, f32[64,128]{1,0:T(8,128)S(1)}) custom-call(f32[64,4096]{1,0:T(8,128)} %get-tuple-element.64.refs_0_, f32[64,4096]{1,0:T(8,128)} %copy-done.3, f32[64,128]{1,0:T(8,128)S(1)} %get-tuple-element.73.refs_2_, f32[64,64000]{1,0:T(8,128)} %get-tuple-element.74.refs_3_), custom_call_target="tpu_custom_call", output_to_operand_aliasing={{0}: (3, {})} | custom-call | flops 402653184 | bytes 4194304 | tf_op jit(solution)/shard_map/cdf/pallas_call | solution.py:416
  179.3 3.6 %cdf.13 = (f32[64,64000]{1,0:T(8,128)}, f32[64,128]{1,0:T(8,128)S(1)}) custom-call(f32[64,2048]{1,0:T(8,128)} %get-tuple-element.62.refs_0_, f32[64,2048]{1,0:T(8,128)} %copy-done.5, f32[64,128]{1,0:T(8,128)S(1)} %get-tuple-element.75.refs_2_, f32[64,64000]{1,0:T(8,128)} %get-tuple-element.76.refs_3_), custom_call_target="tpu_custom_call", output_to_operand_aliasing={{0}: (3, {})} | custom-call | flops 201326592 | bytes 2097152 | tf_op jit(solution)/shard_map/cdf/pallas_call | solution.py:416
  182.9 2.9 %cdf.14 = (f32[64,64000]{1,0:T(8,128)}, f32[64,128]{1,0:T(8,128)S(1)}) custom-call(f32[64,1280]{1,0:T(8,128)} %get-tuple-element.60.refs_0_, f32[64,1280]{1,0:T(8,128)} %copy-done.7, f32[64,128]{1,0:T(8,128)S(1)} %get-tuple-element.77.refs_2_, f32[64,64000]{1,0:T(8,128)} %get-tuple-element.78.refs_3_), custom_call_target="tpu_custom_call", output_to_operand_aliasing={{0}: (3, {})} | custom-call | flops 125829120 | bytes 1310720 | tf_op jit(solution)/shard_map/cdf/pallas_call | solution.py:416
  185.8 2.0 cdf.15
  187.8 0.4 collective-permute-start
  188.2 0.9 collective-permute-start.1
  189.2 9.4 %cdf.16 = (f32[64,64000]{1,0:T(8,128)}, f32[64,128]{1,0:T(8,128)S(1)}) custom-call(f32[64,8192]{1,0:T(8,128)} %get-tuple-element.56.refs_0_, f32[64,8192]{1,0:T(8,128)} %get-tuple-element.57.refs_1_, f32[64,128]{1,0:T(8,128)S(1)} %get-tuple-element.81.refs_2_, f32[64,64000]{1,0:T(8,128)} %get-tuple-element.82.refs_3_), custom_call_target="tpu_custom_call", output_to_operand_aliasing={{0}: (3, {})} | custom-call | flops 805306368 | bytes 8388608 | tf_op jit(solution)/shard_map/cdf/pallas_call | solution.py:416
  198.6 5.5 %cdf.17 = (f32[64,64000]{1,0:T(8,128)}, f32[64,128]{1,0:T(8,128)S(1)}) custom-call(f32[64,4096]{1,0:T(8,128)} %copy-done.1, f32[64,4096]{1,0:T(8,128)} %copy-done.2, f32[64,128]{1,0:T(8,128)S(1)} %get-tuple-element.83.refs_2_, f32[64,64000]{1,0:T(8,128)} %get-tuple-element.84.refs_3_), custom_call_target="tpu_custom_call", output_to_operand_aliasing={{0}: (3, {})} | custom-call | flops 402653184 | bytes 4194304 | tf_op jit(solution)/shard_map/cdf/pallas_call | solution.py:416
  204.2 3.6 %cdf.18 = (f32[64,64000]{1,0:T(8,128)}, f32[64,128]{1,0:T(8,128)S(1)}) custom-call(f32[64,2048]{1,0:T(8,128)} %copy-done.4, f32[64,2048]{1,0:T(8,128)} %collective-permute-done.5.refs_1_, f32[64,128]{1,0:T(8,128)S(1)} %get-tuple-element.85.refs_2_, f32[64,64000]{1,0:T(8,128)} %get-tuple-element.86.refs_3_), custom_call_target="tpu_custom_call", output_to_operand_aliasing={{0}: (3, {})} | custom-call | flops 201326592 | bytes 2097152 | tf_op jit(solution)/shard_map/cdf/pallas_call | solution.py:416
  207.7 0.0 collective-permute-done.3.refs_1_
  207.8 0.7 copy-done.6
  208.5 2.9 %cdf.19 = (f32[64,64000]{1,0:T(8,128)}, f32[64,128]{1,0:T(8,128)S(1)}) custom-call(f32[64,1280]{1,0:T(8,128)} %copy-done.6, f32[64,1280]{1,0:T(8,128)} %collective-permute-done.3.refs_1_, f32[64,128]{1,0:T(8,128)S(1)} %get-tuple-element.87.refs_2_, f32[64,64000]{1,0:T(8,128)} %get-tuple-element.88.refs_3_), custom_call_target="tpu_custom_call", output_to_operand_aliasing={{0}: (3, {})} | custom-call | flops 125829120 | bytes 1310720 | tf_op jit(solution)/shard_map/cdf/pallas_call | solution.py:416
  211.4 0.9 cdf.20
  212.3 0.0 collective-permute-done.refs_0_
  212.3 0.9 cdf.21
  (27 shorter events, 0.1 us)
Async XLA Ops:
  100.0 60.7 %collective-permute-start.11 = (f32[64,4096]{1,0:T(8,128)}, f32[64,4096]{1,0:T(8,128)S(1)}, u32[]{:S(2)}, u32[]{:S(2)}) collective-permute-start(f32[64,4096]{1,0:T(8,128)} %get-tuple-element.65), channel_id=1, source_target_pairs={{0,1},{1,0},{2,3},{3,2},{4,5},{5,4},{6,7},{7,6}} | collective-permute-start | bytes 3145736 | tf_op jit(solution)/shard_map/ppermute | solution.py:442
  100.1 87.7 %collective-permute-start.6 = (f32[64,4096]{1,0:T(8,128)}, f32[64,4096]{1,0:T(8,128)S(1)}, u32[]{:S(2)}, u32[]{:S(2)}) collective-permute-start(f32[64,4096]{1,0:T(8,128)} %get-tuple-element.54), channel_id=1, source_target_pairs={{0,2},{1,3},{2,0},{3,1},{4,6},{5,7},{6,4},{7,5}} | collective-permute-start | bytes 3145736 | tf_op jit(solution)/shard_map/ppermute | solution.py:442
  100.1 88.1 %collective-permute-start.7 = (f32[64,4096]{1,0:T(8,128)}, f32[64,4096]{1,0:T(8,128)S(1)}, u32[]{:S(2)}, u32[]{:S(2)}) collective-permute-start(f32[64,4096]{1,0:T(8,128)} %get-tuple-element.55), channel_id=1, source_target_pairs={{0,3},{1,2},{2,1},{3,0},{4,7},{5,6},{6,5},{7,4}} | collective-permute-start | bytes 3145736 | tf_op jit(solution)/shard_map/ppermute | solution.py:442
  101.9 2.9 %collective-permute-start.9 = (f32[64,1280]{1,0:T(8,128)}, f32[64,1280]{1,0:T(8,128)S(1)}, u32[]{:S(2)}, u32[]{:S(2)}) collective-permute-start(f32[64,1280]{1,0:T(8,128)} %get-tuple-element.61), channel_id=1, source_target_pairs={{0,1},{1,0},{2,3},{3,2},{4,5},{5,4},{6,7},{7,6}} | collective-permute-start | bytes 983048 | tf_op jit(solution)/shard_map/ppermute | solution.py:442
  102.2 1.6 collective-permute-start.8
  103.9 0.6 copy-start.8
  104.5 55.0 %collective-permute-start.4 = (f32[64,2048]{1,0:T(8,128)}, f32[64,2048]{1,0:T(8,128)S(1)}, u32[]{:S(2)}, u32[]{:S(2)}) collective-permute-start(f32[64,2048]{1,0:T(8,128)} %get-tuple-element.52), channel_id=1, source_target_pairs={{0,2},{1,3},{2,0},{3,1},{4,6},{5,7},{6,4},{7,5}} | collective-permute-start | bytes 1572872 | tf_op jit(solution)/shard_map/ppermute | solution.py:442
  104.8 0.7 copy-start.7
  105.5 54.0 %collective-permute-start.10 = (f32[64,2048]{1,0:T(8,128)}, f32[64,2048]{1,0:T(8,128)S(1)}, u32[]{:S(2)}, u32[]{:S(2)}) collective-permute-start(f32[64,2048]{1,0:T(8,128)} %get-tuple-element.63), channel_id=1, source_target_pairs={{0,1},{1,0},{2,3},{3,2},{4,5},{5,4},{6,7},{7,6}} | collective-permute-start | bytes 1572872 | tf_op jit(solution)/shard_map/ppermute | solution.py:442
  159.5 1.2 copy-start.4
  159.5 44.7 %collective-permute-start.5 = (f32[64,2048]{1,0:T(8,128)}, f32[64,2048]{1,0:T(8,128)}, u32[]{:S(2)}, u32[]{:S(2)}) collective-permute-start(f32[64,2048]{1,0:T(8,128)} %get-tuple-element.53), channel_id=1, source_target_pairs={{0,3},{1,2},{2,1},{3,0},{4,7},{5,6},{6,5},{7,4}} | collective-permute-start | bytes 1572872 | tf_op jit(solution)/shard_map/ppermute | solution.py:442
  159.5 1.2 copy-start.5
  159.5 48.2 %collective-permute-start.2 = (f32[64,1280]{1,0:T(8,128)}, f32[64,1280]{1,0:T(8,128)S(1)}, u32[]{:S(2)}, u32[]{:S(2)}) collective-permute-start(f32[64,1280]{1,0:T(8,128)} %get-tuple-element.50), channel_id=1, source_target_pairs={{0,2},{1,3},{2,0},{3,1},{4,6},{5,7},{6,4},{7,5}} | collective-permute-start | bytes 983048 | tf_op jit(solution)/shard_map/ppermute | solution.py:442
  160.7 13.1 %copy-start.3 = (f32[64,4096]{1,0:T(8,128)}, f32[64,4096]{1,0:T(8,128)S(1)}, u32[]{:S(2)}) copy-start(f32[64,4096]{1,0:T(8,128)S(1)} %collective-permute-done.11.refs_1_) | copy-start | bytes 3145732
  160.7 47.1 %collective-permute-start.3 = (f32[64,1280]{1,0:T(8,128)}, f32[64,1280]{1,0:T(8,128)}, u32[]{:S(2)}, u32[]{:S(2)}) collective-permute-start(f32[64,1280]{1,0:T(8,128)} %get-tuple-element.51), channel_id=1, source_target_pairs={{0,3},{1,2},{2,1},{3,0},{4,7},{5,6},{6,5},{7,4}} | collective-permute-start | bytes 983048 | tf_op jit(solution)/shard_map/ppermute | solution.py:442
  163.6 0.8 copy-start
  182.9 5.0 %copy-start.9 = (f32[64,384]{1,0:T(8,128)S(1)}, f32[64,384]{1,0:T(8,128)}, u32[]{:S(2)}) copy-start(f32[64,384]{1,0:T(8,128)} %get-tuple-element.48) | copy-start | bytes 294916
  182.9 5.4 %copy-start.10 = (f32[64,384]{1,0:T(8,128)S(1)}, f32[64,384]{1,0:T(8,128)}, u32[]{:S(2)}) copy-start(f32[64,384]{1,0:T(8,128)} %get-tuple-element.49) | copy-start | bytes 294916
  187.8 10.8 %copy-start.1 = (f32[64,4096]{1,0:T(8,128)}, f32[64,4096]{1,0:T(8,128)S(1)}, u32[]{:S(2)}) copy-start(f32[64,4096]{1,0:T(8,128)S(1)} %collective-permute-done.6.refs_0_) | copy-start | bytes 3145732
  187.8 24.5 %collective-permute-start = (f32[64,384]{1,0:T(8,128)S(1)}, f32[64,384]{1,0:T(8,128)S(1)}, u32[]{:S(2)}, u32[]{:S(2)}) collective-permute-start(f32[64,384]{1,0:T(8,128)S(1)} %copy-done.9), channel_id=1, source_target_pairs={{0,3},{1,2},{2,1},{3,0},{4,7},{5,6},{6,5},{7,4}} | collective-permute-start | bytes 294920 | tf_op jit(solution)/shard_map/ppermute | solution.py:442
  188.2 10.4 %copy-start.2 = (f32[64,4096]{1,0:T(8,128)}, f32[64,4096]{1,0:T(8,128)S(1)}, u32[]{:S(2)}) copy-start(f32[64,4096]{1,0:T(8,128)S(1)} %collective-permute-done.7.refs_1_) | copy-start | bytes 3145732
  188.2 23.1 %collective-permute-start.1 = (f32[64,384]{1,0:T(8,128)S(1)}, f32[64,384]{1,0:T(8,128)S(1)}, u32[]{:S(2)}, u32[]{:S(2)}) collective-permute-start(f32[64,384]{1,0:T(8,128)S(1)} %copy-done.10), channel_id=1, source_target_pairs={{0,2},{1,3},{2,0},{3,1},{4,6},{5,7},{6,4},{7,5}} | collective-permute-start | bytes 294920 | tf_op jit(solution)/shard_map/ppermute | solution.py:442
  207.7 0.7 copy-start.6

commit v6 on v5

--- a/solution.py
+++ b/solution.py
@@ -13,9 +13,10 @@
 HALF = 256
 DEPTH = 512
 SLOTS = 9
-EARLY = ((256, 2), (512, 1), (1024, 1), (2048, 3))
-LATE = (4096, 2048, 1280, 384)
-LATE_UNITS = ((2048, 2), (2048, 1), (1280, 1), (384, 1))
+EARLY = ((128, 2), (256, 1), (512, 1), (1024, 1), (2048, 3))
+LATE = (1536, 2048, 2560, 1280, 384)
+LATE_UNITS = ((1536, 1), (2048, 1), (1280, 2), (1280, 1), (384, 1))
+STATS = 4
 
 
 def _to_rows(vec_1xn):
@@ -39,9 +40,10 @@
     early = take(n_dev)
     late = [take(n_dev) for _ in range(n_late)]
     packs = take(n_dev)
-    xs, wbuf, acc, zsend, zbuf, invt_v, tgt_v, pack_v = take(8)
+    (extra,) = take(1)
+    xs, wbuf, acc, zsend, zextra, zbuf, invt_v, tgt_v, pack_v = take(9)
     scale_rows, left_rows, tmp, m_ref, s_ref, t_ref = take(6)
-    w_sem, z_sem, x_sem, v_sem, own_sem, send_sem, recv_sem, pack_send, pack_recv = take(9)
+    w_sem, z_sem, x_sem, v_sem, own_sem, send_sem, recv_sem, pack_send, pack_recv, extra_sem = take(10)
     me = lax.axis_index("vp")
     batch, depth = xs.shape
     rows = batch // n_dev
@@ -61,15 +63,25 @@
             w_sem.at[slot],
         )
 
-    def put_late(slot, c, off, width):
+    def put_late(src, slot, c, off, width):
         return [
             pltpu.make_async_copy(
-                zbuf.at[slot, pl.ds(p * rows, rows), pl.ds(0, width)],
+                src.at[pl.ds(p * rows, rows), pl.ds(0, width)],
                 late[c][p].at[:, pl.ds(off, width)],
                 z_sem.at[slot, p],
             )
             for p in range(n_dev)
         ]
+
+    def send_extra():
+        return pltpu.make_async_remote_copy(
+            src_ref=zextra.at[pl.ds(2 * rows, rows), :],
+            dst_ref=extra,
+            send_sem=extra_sem.at[0],
+            recv_sem=extra_sem.at[1],
+            device_id={"vp": _peer(me, 2)},
+            device_id_type=pl.DeviceIdType.MESH,
+        )
 
     def put_own(u, off, width):
         return pltpu.make_async_copy(
@@ -194,13 +206,14 @@
                 copy.start()
                 own.append(copy)
             else:
-                slot = len(stored) % 2
-                if len(stored) >= 2:
+                c, off = chunk
+                slot = 2 if c == 0 else len(stored) % 2
+                if c and len(stored) > 2:
                     for copy in stored[-2]:
                         copy.wait()
-                finish(col, width, zbuf.at[slot], 0)
-                c, off = chunk
-                copies = put_late(slot, c, off + i * width, width)
+                src = zbuf.at[slot] if c else zextra
+                finish(col, width, src, 0)
+                copies = put_late(src, slot, c, off + i * width, width)
                 for copy in copies:
                     copy.start()
                 stored.append(copies)
@@ -213,7 +226,7 @@
     packed = jnp.where(which == 0, m_row, jnp.where(which == 1, s_row, t_row))
     for p in range(n_dev):
         tmp[rows_of(p), :] = packed[p * rows:(p + 1) * rows, :]
-    pack_v[...] = jnp.transpose(tmp[...])[:8, :]
+    pack_v[...] = jnp.transpose(tmp[...])[:STATS, :]
     for p in (2, 3, 1):
         copy = pltpu.make_async_remote_copy(
             src_ref=pack_v,
@@ -228,11 +241,20 @@
     copy = pltpu.make_async_copy(pack_v, packs[0], pack_send.at[0])
     copy.start()
     own.append(copy)
-    for copies in stored[-2:]:
+
+    @pl.when(lax.rem(me, 2) == 1)
+    def _():
+        send_extra().start()
+
+    for copies in [stored[0]] + stored[-2:]:
         for copy in copies:
             copy.wait()
     for copy in own + sent:
         copy.wait()
+
+    @pl.when(lax.rem(me, 2) == 1)
+    def _():
+        send_extra().wait()
 
 
 def _logits(x, w, invt, tgt, n_dev):
@@ -255,7 +277,9 @@
     hbm = pl.BlockSpec(memory_space=pltpu.HBM)
     out_shape = [pltpu.HBM((rows, sent), jnp.float32)] * n_dev
     out_shape += [pltpu.HBM((rows, width), jnp.float32) for width in LATE for _ in range(n_dev)]
-    out_shape += [pltpu.HBM((8, batch), jnp.float32)] * n_dev
+    out_shape += [pltpu.HBM((STATS, batch), jnp.float32)] * n_dev
+    out_shape += [pltpu.HBM((rows, LATE[0]), jnp.float32)]
+    assert LATE_UNITS[0] == (LATE[0], 1)
     table = pltpu.VMEM((batch, LANES), jnp.float32)
     widest = max(width for width, _ in EARLY + LATE_UNITS)
     dma = pltpu.SemaphoreType.DMA
@@ -269,10 +293,11 @@
             pltpu.VMEM((SLOTS, DEPTH, widest), jnp.bfloat16),
             pltpu.VMEM((batch, widest), jnp.float32),
             pltpu.VMEM((batch, sent), jnp.float32),
+            pltpu.VMEM((batch, LATE[0]), jnp.float32),
             pltpu.VMEM((2, batch, widest), jnp.float32),
             pltpu.VMEM((1, batch), jnp.float32),
             pltpu.VMEM((1, batch), jnp.int32),
-            pltpu.VMEM((8, batch), jnp.float32),
+            pltpu.VMEM((STATS, batch), jnp.float32),
             table,
             pltpu.VMEM((batch, LANES), jnp.int32),
             table,
@@ -280,7 +305,7 @@
             table,
             table,
             dma((SLOTS,)),
-            dma((2, n_dev)),
+            dma((3, n_dev)),
             dma((n_dev,)),
             dma((2,)),
             dma((n_early,)),
@@ -288,6 +313,7 @@
             dma((n_early, n_dev)),
             dma((n_dev,)),
             dma((n_dev,)),
+            dma((2,)),
         ],
         compiler_params=pltpu.CompilerParams(
             collective_id=0, has_side_effects=True, vmem_limit_bytes=52 * 2**20
@@ -300,7 +326,7 @@
         name="logits",
     )(*(pltpu.with_memory_space_constraint(a, pltpu.HBM) for a in (x, w, invt, tgt)))
     blocks = [res[c * n_dev:(c + 1) * n_dev] for c in range(len(LATE) + 2)]
-    return blocks[0], blocks[1:-1], blocks[-1]
+    return blocks[0], blocks[1:-1], blocks[-1], res[-1]
 
 
 def _merge_kernel(n_dev, *refs):
@@ -350,8 +376,10 @@
 
 
 def _cdf_kernel(cfg, *refs):
-    peers, shard, base, width, first, last = cfg
+    peers, shard, base, width, first, last, two_sources = cfg
     n = len(peers)
+    if two_sources:
+        other_ref, refs = refs[n], refs[:n] + refs[n + 1:]
     params_ref = refs[n]
     if last:
         out_ref, y_ref, sems = refs[n + 2:]
@@ -367,11 +395,16 @@
     tri = jnp.where(k_id <= n_id, 1.0, 0.0).astype(jnp.bfloat16)
     lane = lax.broadcasted_iota(jnp.int32, (rows, LANES), 1)
 
+    odd = lax.rem(me, 2) == 1
+
     def unit(col, wide, carries):
         ends = []
         for j in range(n):
             cols = [pl.ds(col + t, LANES) for t in range(0, wide, LANES)]
-            e = jnp.concatenate([jnp.exp(refs[j][:, c] - top) for c in cols], axis=0)
+            zs = [refs[j][:, c] for c in cols]
+            if two_sources and j == 0:
+                zs = [jnp.where(odd, other_ref[:, c], z) for c, z in zip(cols, zs)]
+            e = jnp.concatenate([jnp.exp(z - top) for z in zs], axis=0)
             hi = e.astype(jnp.bfloat16)
             r1 = e - hi.astype(jnp.float32)
             mid = r1.astype(jnp.bfloat16)
@@ -407,15 +440,16 @@
         copy.wait()
 
 
-def _cdf(blocks, peers, params, out, n_dev, shard, base, last=False):
+def _cdf(blocks, peers, params, out, n_dev, shard, base, last=False, other=None):
     rows, width = blocks[0].shape
     n = len(peers)
     first = out is None
+    extra = [] if other is None else [other]
     vmem = pl.BlockSpec(memory_space=pltpu.VMEM)
     hbm = pl.BlockSpec(memory_space=pl.ANY)
     return pl.pallas_call(
-        functools.partial(_cdf_kernel, (peers, shard, base, width, first, last)),
-        in_specs=[vmem] * (n + 1) + ([] if first else [hbm]),
+        functools.partial(_cdf_kernel, (peers, shard, base, width, first, last, bool(extra))),
+        in_specs=[vmem] * (n + len(extra) + 1) + ([] if first else [hbm]),
         out_specs=[hbm] + ([] if last else [vmem]),
         out_shape=[jax.ShapeDtypeStruct((rows, n_dev * shard), jnp.float32)]
         + ([] if last else [jax.ShapeDtypeStruct(params.shape, jnp.float32)]),
@@ -423,7 +457,7 @@
             pltpu.VMEM((n, rows, width), jnp.float32),
             pltpu.SemaphoreType.DMA((n,)),
         ],
-        input_output_aliases={} if first else {n + 1: 0},
+        input_output_aliases={} if first else {n + len(extra) + 1: 0},
         compiler_params=pltpu.CompilerParams(vmem_limit_bytes=24 * 2**20),
         cost_estimate=pl.CostEstimate(
             flops=n * 2 * rows * width * 384,
@@ -431,27 +465,25 @@
             transcendentals=n * rows * width,
         ),
         name="cdf",
-    )(*blocks, params, *(() if first else (out,)))
+    )(*blocks, *extra, params, *(() if first else (out,)))
 
 
 def solution(mesh):
     n_dev = mesh.shape["vp"]
     assert n_dev == 4
 
-    def swap(a, p):
-        return lax.ppermute(a, "vp", [(i, i ^ p) for i in range(n_dev)])
+    def swap(a, p, step=1):
+        return lax.ppermute(a, "vp", [(i, i ^ p) for i in range(0, n_dev, step)])
 
     def local_step(hidden, w_local, inv_temp, target_ids):
         shard = w_local.shape[1]
-        early, late, packs = _logits(
-            hidden, w_local, inv_temp.reshape(1, -1), target_ids.reshape(1, -1), n_dev
-        )
+        early, late, packs, extra = _logits(hidden, w_local, inv_temp.reshape(1, -1), target_ids.reshape(1, -1), n_dev)
         chunks = [(0, early)]
         begin = early[0].shape[1]
-        for made in late:
+        for k, made in enumerate(late):
             got = [made[0]]
             for p in range(1, n_dev):
-                got.append(swap(made[p], p))
+                got.append(swap(made[p], p, 2 if k == 0 and p == 2 else 1))
             chunks.append((begin, got))
             begin += made[0].shape[1]
         params, at_target = _merge(packs)
@@ -464,7 +496,8 @@
             blocks = [got[p] for p in peers]
             if k < final or peers[0] == 0:
                 blocks = [pltpu.with_memory_space_constraint(a, pltpu.HBM) for a in blocks]
-            res = _cdf(blocks, peers, params, out, n_dev, shard, begin, i == len(plan) - 1)
+            other = pltpu.with_memory_space_constraint(extra, pltpu.HBM) if k == 1 and peers[0] == 2 else None
+            res = _cdf(blocks, peers, params, out, n_dev, shard, begin, i == len(plan) - 1, other)
             out = res[0]
             params = res[1] if len(res) > 1 else None
         return out, at_target.reshape(-1)

time: 214 us -> 202 us (0.944)
  waiting for transfers between devices: 55.4 us -> 30.6 us
  starting transfers between devices: 6.65 us -> 13.3 us
  Pallas kernels: 147 us -> 153 us
    ppermute x12 -> x15, waiting for transfers between devices: 55.4 us -> 30.6 us  [swap(): return lax.ppermute(a, 'vp', [(i, i ^ p) for i in range(0, n_dev, step)])]
    ppermute x12 -> x15, starting transfers between devices: 6.65 us -> 13.3 us  [swap(): return lax.ppermute(a, 'vp', [(i, i ^ p) for i in range(0, n_dev, step)])]
    pallas_call x11 -> x13, Pallas kernels: 46.6 us -> 50.2 us  [_cdf(): pl.pallas_call(functools.partial(_cdf_kernel, (peers, shard, base, width,...]
  transfers between devices with their start and end apart: 12 -> 15, of which waited for: 2 -> 4; matrix products, arithmetic and copies ran while one was open for 0% -> 0% of each run, Pallas kernels for 22% -> 25%
where the time goes in v6:
time: 202 us; the launch traced here: 201 us
  Pallas kernels  153 us (76%)
  waiting for transfers between devices  30.6 us (15%)
  starting transfers between devices  13.3 us (7%)
  local copies, waits for them, and re-layouts  3.59 us (2%)
    pallas_call x1, Pallas kernels, _logits(): pl.pallas_call(functools.partial(_logits_kernel, (n_dev, shard, segments,...  101 us
    pallas_call x13, Pallas kernels, _cdf(): pl.pallas_call(functools.partial(_cdf_kernel, (peers, shard, base, width,...  50.2 us
    ppermute x15, waiting for transfers between devices, swap(): return lax.ppermute(a, 'vp', [(i, i ^ p) for i in range(0, n_dev, step)])  30.6 us
    ppermute x15, starting transfers between devices, swap(): return lax.ppermute(a, 'vp', [(i, i ^ p) for i in range(0, n_dev, step)])  13.3 us
  transfers between devices with their start and end apart: 15, of which 4 were waited for; matrix products, arithmetic and copies ran while one was open for 0% of the time, Pallas kernels for 25%

profile of v6, /device:TPU:0, one launch (start us, length us, event | category | flops | bytes accessed | tf_op | source)
XLA Modules:
  0.0 201.4 jit_solution(16531969184120997199)
XLA Ops:
  0.6 101.3 %logits.1 = (f32[64,8192]{1,0:T(8,128)}, f32[64,8192]{1,0:T(8,128)}, f32[64,8192]{1,0:T(8,128)}, f32[64,8192]{1,0:T(8,128)}, f32[64,1536]{1,0:T(8,128)}, /*index...) custom-call(bf16[256,4096]{1,0:T(8,128)(2,1)} %x_ref.1, ...), custom_call_target="tpu_custom_call" | custom-call | flops 33554432000 | bytes 131072000 | tf_op jit(solution)/shard_map/logits/pallas_call | solution.py:286
  101.9 3.4 %collective-permute-start.11 = (f32[64,1280]{1,0:T(8,128)}, f32[64,1280]{1,0:T(8,128)S(1)}, u32[]{:S(2)}, u32[]{:S(2)}) collective-permute-start(f32[64,1280]{1,0:T(8,128)} %get-tuple-element.73), channel_id=1, source_target_pairs={{0,1},{1,0},{2,3},{3,2},{4,5},{5,4},{6,7},{7,6}} | collective-permute-start | bytes 983048 | tf_op jit(solution)/shard_map/ppermute | solution.py:476
  105.3 2.1 %collective-permute-start.8 = (f32[64,1536]{1,0:T(8,128)}, f32[64,1536]{1,0:T(8,128)S(1)}, u32[]{:S(2)}, u32[]{:S(2)}) collective-permute-start(f32[64,1536]{1,0:T(8,128)} %get-tuple-element.65), channel_id=1, source_target_pairs={{0,2},{2,0},{4,6},{6,4}} | collective-permute-start | bytes 1179656 | tf_op jit(solution)/shard_map/ppermute | solution.py:476
  107.4 2.0 %collective-permute-start.6 = (f32[64,2048]{1,0:T(8,128)}, f32[64,2048]{1,0:T(8,128)S(1)}, u32[]{:S(2)}, u32[]{:S(2)}) collective-permute-start(f32[64,2048]{1,0:T(8,128)} %get-tuple-element.63), channel_id=1, source_target_pairs={{0,2},{1,3},{2,0},{3,1},{4,6},{5,7},{6,4},{7,5}} | collective-permute-start | bytes 1572872 | tf_op jit(solution)/shard_map/ppermute | solution.py:476
  109.6 1.4 collective-permute-done.10.refs_1_
  111.1 0.5 copy-done.11
  111.6 0.7 copy-done.10
  112.4 6.9 %collective-permute-done.8.refs_0_ = f32[64,1536]{1,0:T(8,128)S(1)} collective-permute-done((f32[64,1536]{1,0:T(8,128)}, f32[64,1536]{1,0:T(8,128)S(1)}, u32[]{:S(2)}, u32[]{:S(2)}) %collective-permute-start.8) | collective-permute-done | bytes 393248 | tf_op jit(solution)/shard_map/ppermute | solution.py:476
  119.4 11.4 %collective-permute-done.9.refs_1_ = f32[64,1536]{1,0:T(8,128)S(1)} collective-permute-done((f32[64,1536]{1,0:T(8,128)}, f32[64,1536]{1,0:T(8,128)S(1)}, u32[]{:S(2)}, u32[]{:S(2)}) %collective-permute-start.9) | collective-permute-done | bytes 393248 | tf_op jit(solution)/shard_map/ppermute | solution.py:476
  130.8 1.7 collective-permute-start.4
  132.5 0.8 copy-done.9
  133.3 1.5 collective-permute-start.5
  134.8 0.2 collective-permute-start.7
  135.1 0.3 collective-permute-start.2
  135.4 1.3 collective-permute-start.3
  136.7 1.5 merge.1
  138.1 0.8 copy-done
  138.9 9.4 %cdf.13 = (f32[64,64000]{1,0:T(8,128)}, f32[64,128]{1,0:T(8,128)S(1)}) custom-call(f32[64,8192]{1,0:T(8,128)} %get-tuple-element.80.refs_0_, f32[64,8192]{1,0:T(8,128)} %get-tuple-element.81.refs_1_, f32[64,128]{1,0:T(8,128)S(1)} %copy-done), custom_call_target="tpu_custom_call" | custom-call | flops 805306368 | bytes 8388608 | tf_op jit(solution)/shard_map/cdf/pallas_call | solution.py:450
  148.3 3.1 %cdf.14 = (f32[64,64000]{1,0:T(8,128)}, f32[64,128]{1,0:T(8,128)S(1)}) custom-call(f32[64,1536]{1,0:T(8,128)} %get-tuple-element.78.refs_0_, f32[64,1536]{1,0:T(8,128)} %copy-done.9, f32[64,128]{1,0:T(8,128)S(1)} %get-tuple-element.87.refs_2_, f32[64,64000]{1,0:T(8,128)} %get-tuple-element.88.refs_3_), custom_call_target="tpu_custom_call", output_to_operand_aliasing={{0}: (3, {})} | custom-call | flops 150994944 | bytes 1572864 | tf_op jit(solution)/shard_map/cdf/pallas_call | solution.py:450
  151.4 3.6 %cdf.15 = (f32[64,64000]{1,0:T(8,128)}, f32[64,128]{1,0:T(8,128)S(1)}) custom-call(f32[64,2048]{1,0:T(8,128)} %get-tuple-element.76.refs_0_, f32[64,2048]{1,0:T(8,128)} %copy-done.6, f32[64,128]{1,0:T(8,128)S(1)} %get-tuple-element.89.refs_2_, f32[64,64000]{1,0:T(8,128)} %get-tuple-element.90.refs_3_), custom_call_target="tpu_custom_call", output_to_operand_aliasing={{0}: (3, {})} | custom-call | flops 201326592 | bytes 2097152 | tf_op jit(solution)/shard_map/cdf/pallas_call | solution.py:450
  155.0 4.0 %cdf.16 = (f32[64,64000]{1,0:T(8,128)}, f32[64,128]{1,0:T(8,128)S(1)}) custom-call(f32[64,2560]{1,0:T(8,128)} %get-tuple-element.74.refs_0_, f32[64,2560]{1,0:T(8,128)} %copy-done.3, f32[64,128]{1,0:T(8,128)S(1)} %get-tuple-element.91.refs_2_, f32[64,64000]{1,0:T(8,128)} %get-tuple-element.92.refs_3_), custom_call_target="tpu_custom_call", output_to_operand_aliasing={{0}: (3, {})} | custom-call | flops 251658240 | bytes 2621440 | tf_op jit(solution)/shard_map/cdf/pallas_call | solution.py:450
  159.1 2.9 %cdf.17 = (f32[64,64000]{1,0:T(8,128)}, f32[64,128]{1,0:T(8,128)S(1)}) custom-call(f32[64,1280]{1,0:T(8,128)} %get-tuple-element.72.refs_0_, f32[64,1280]{1,0:T(8,128)} %copy-done.10, f32[64,128]{1,0:T(8,128)S(1)} %get-tuple-element.93.refs_2_, f32[64,64000]{1,0:T(8,128)} %get-tuple-element.94.refs_3_), custom_call_target="tpu_custom_call", output_to_operand_aliasing={{0}: (3, {})} | custom-call | flops 125829120 | bytes 1310720 | tf_op jit(solution)/shard_map/cdf/pallas_call | solution.py:450
  162.0 2.0 cdf.18
  164.0 10.8 %collective-permute-done.7.refs_1_ = f32[64,2048]{1,0:T(8,128)S(1)} collective-permute-done((f32[64,2048]{1,0:T(8,128)}, f32[64,2048]{1,0:T(8,128)S(1)}, u32[]{:S(2)}, u32[]{:S(2)}) %collective-permute-start.7) | collective-permute-done | bytes 524320 | tf_op jit(solution)/shard_map/ppermute | solution.py:476
  175.1 9.6 %cdf.19 = (f32[64,64000]{1,0:T(8,128)}, f32[64,128]{1,0:T(8,128)S(1)}) custom-call(f32[64,8192]{1,0:T(8,128)} %get-tuple-element.68.refs_0_, f32[64,8192]{1,0:T(8,128)} %get-tuple-element.69.refs_1_, f32[64,128]{1,0:T(8,128)S(1)} %get-tuple-element.97.refs_2_, f32[64,64000]{1,0:T(8,128)} %get-tuple-element.98.refs_3_), custom_call_target="tpu_custom_call", output_to_operand_aliasing={{0}: (3, {})} | custom-call | flops 805306368 | bytes 8388608 | tf_op jit(solution)/shard_map/cdf/pallas_call | solution.py:450
  184.7 3.2 %cdf.20 = (f32[64,64000]{1,0:T(8,128)}, f32[64,128]{1,0:T(8,128)S(1)}) custom-call(f32[64,1536]{1,0:T(8,128)} %copy-done.7, f32[64,1536]{1,0:T(8,128)} %copy-done.8, f32[64,1536]{1,0:T(8,128)} %get-tuple-element.67.refs_2_, f32[64,128]{1,0:T(8,128)S(1)} %get-tuple-element.99.refs_3_, ...), custom_call_target="tpu_custom_call", output_to_operand_aliasing={{0}: (4, {})} | custom-call | flops 150994944 | bytes 1572864 | tf_op jit(solution)/shard_map/cdf/pallas_call | solution.py:450
  188.0 3.6 %cdf.21 = (f32[64,64000]{1,0:T(8,128)}, f32[64,128]{1,0:T(8,128)S(1)}) custom-call(f32[64,2048]{1,0:T(8,128)} %copy-done.4, f32[64,2048]{1,0:T(8,128)} %copy-done.5, f32[64,128]{1,0:T(8,128)S(1)} %get-tuple-element.101.refs_2_, f32[64,64000]{1,0:T(8,128)} %get-tuple-element.102.refs_3_), custom_call_target="tpu_custom_call", output_to_operand_aliasing={{0}: (3, {})} | custom-call | flops 201326592 | bytes 2097152 | tf_op jit(solution)/shard_map/cdf/pallas_call | solution.py:450
  191.6 0.8 copy-done.2
  192.4 4.0 %cdf.22 = (f32[64,64000]{1,0:T(8,128)}, f32[64,128]{1,0:T(8,128)S(1)}) custom-call(f32[64,2560]{1,0:T(8,128)} %copy-done.1, f32[64,2560]{1,0:T(8,128)} %copy-done.2, f32[64,128]{1,0:T(8,128)S(1)} %get-tuple-element.103.refs_2_, f32[64,64000]{1,0:T(8,128)} %get-tuple-element.104.refs_3_), custom_call_target="tpu_custom_call", output_to_operand_aliasing={{0}: (3, {})} | custom-call | flops 251658240 | bytes 2621440 | tf_op jit(solution)/shard_map/cdf/pallas_call | solution.py:450
  196.5 2.9 %cdf.23 = (f32[64,64000]{1,0:T(8,128)}, f32[64,128]{1,0:T(8,128)S(1)}) custom-call(f32[64,1280]{1,0:T(8,128)} %collective-permute-done.2.refs_0_, f32[64,1280]{1,0:T(8,128)} %collective-permute-done.3.refs_1_, f32[64,128]{1,0:T(8,128)S(1)} %get-tuple-element.105.refs_2_, f32[64,64000]{1,0:T(8,128)} %get-tuple-element.106.refs_3_), custom_call_target="tpu_custom_call", output_to_operand_aliasing={{0}: (3, {})} | custom-call | flops 125829120 | bytes 1310720 | tf_op jit(solution)/shard_map/cdf/pallas_call | solution.py:450
  199.4 0.9 cdf.24
  200.3 0.9 cdf.25
  (41 shorter events, 0.8 us)
Async XLA Ops:
  101.9 9.2 %collective-permute-start.11 = (f32[64,1280]{1,0:T(8,128)}, f32[64,1280]{1,0:T(8,128)S(1)}, u32[]{:S(2)}, u32[]{:S(2)}) collective-permute-start(f32[64,1280]{1,0:T(8,128)} %get-tuple-element.73), channel_id=1, source_target_pairs={{0,1},{1,0},{2,3},{3,2},{4,5},{5,4},{6,7},{7,6}} | collective-permute-start | bytes 983048 | tf_op jit(solution)/shard_map/ppermute | solution.py:476
  105.3 14.1 %collective-permute-start.8 = (f32[64,1536]{1,0:T(8,128)}, f32[64,1536]{1,0:T(8,128)S(1)}, u32[]{:S(2)}, u32[]{:S(2)}) collective-permute-start(f32[64,1536]{1,0:T(8,128)} %get-tuple-element.65), channel_id=1, source_target_pairs={{0,2},{2,0},{4,6},{6,4}} | collective-permute-start | bytes 1179656 | tf_op jit(solution)/shard_map/ppermute | solution.py:476
  107.4 27.4 %collective-permute-start.6 = (f32[64,2048]{1,0:T(8,128)}, f32[64,2048]{1,0:T(8,128)S(1)}, u32[]{:S(2)}, u32[]{:S(2)}) collective-permute-start(f32[64,2048]{1,0:T(8,128)} %get-tuple-element.63), channel_id=1, source_target_pairs={{0,2},{1,3},{2,0},{3,1},{4,6},{5,7},{6,4},{7,5}} | collective-permute-start | bytes 1572872 | tf_op jit(solution)/shard_map/ppermute | solution.py:476
  109.4 21.4 %collective-permute-start.9 = (f32[64,1536]{1,0:T(8,128)}, f32[64,1536]{1,0:T(8,128)S(1)}, u32[]{:S(2)}, u32[]{:S(2)}) collective-permute-start(f32[64,1536]{1,0:T(8,128)} %get-tuple-element.66), channel_id=1, source_target_pairs={{0,3},{1,2},{2,1},{3,0},{4,7},{5,6},{6,5},{7,4}} | collective-permute-start | bytes 1179656 | tf_op jit(solution)/shard_map/ppermute | solution.py:476
  109.4 1.5 collective-permute-start.10
  110.9 0.6 copy-start.11
  110.9 21.6 %collective-permute-start.14 = (f32[64,1536]{1,0:T(8,128)}, f32[64,1536]{1,0:T(8,128)S(1)}, u32[]{:S(2)}, u32[]{:S(2)}) collective-permute-start(f32[64,1536]{1,0:T(8,128)} %get-tuple-element.79), channel_id=1, source_target_pairs={{0,1},{1,0},{2,3},{3,2},{4,5},{5,4},{6,7},{7,6}} | collective-permute-start | bytes 1179656 | tf_op jit(solution)/shard_map/ppermute | solution.py:476
  111.6 0.7 copy-start.10
  112.3 23.1 %collective-permute-start.12 = (f32[64,2560]{1,0:T(8,128)}, f32[64,2560]{1,0:T(8,128)S(1)}, u32[]{:S(2)}, u32[]{:S(2)}) collective-permute-start(f32[64,2560]{1,0:T(8,128)} %get-tuple-element.75), channel_id=1, source_target_pairs={{0,1},{1,0},{2,3},{3,2},{4,5},{5,4},{6,7},{7,6}} | collective-permute-start | bytes 1966088 | tf_op jit(solution)/shard_map/ppermute | solution.py:476
  119.4 16.0 %copy-start.7 = (f32[64,1536]{1,0:T(8,128)}, f32[64,1536]{1,0:T(8,128)S(1)}, u32[]{:S(2)}) copy-start(f32[64,1536]{1,0:T(8,128)S(1)} %collective-permute-done.8.refs_0_) | copy-start | bytes 1179652
  119.4 15.7 %collective-permute-start.13 = (f32[64,2048]{1,0:T(8,128)}, f32[64,2048]{1,0:T(8,128)S(1)}, u32[]{:S(2)}, u32[]{:S(2)}) collective-permute-start(f32[64,2048]{1,0:T(8,128)} %get-tuple-element.77), channel_id=1, source_target_pairs={{0,1},{1,0},{2,3},{3,2},{4,5},{5,4},{6,7},{7,6}} | collective-permute-start | bytes 1572872 | tf_op jit(solution)/shard_map/ppermute | solution.py:476
  130.8 4.0 %copy-start.8 = (f32[64,1536]{1,0:T(8,128)}, f32[64,1536]{1,0:T(8,128)S(1)}, u32[]{:S(2)}) copy-start(f32[64,1536]{1,0:T(8,128)S(1)} %collective-permute-done.9.refs_1_) | copy-start | bytes 1179652
  130.8 44.3 %collective-permute-start.4 = (f32[64,2560]{1,0:T(8,128)}, f32[64,2560]{1,0:T(8,128)S(1)}, u32[]{:S(2)}, u32[]{:S(2)}) collective-permute-start(f32[64,2560]{1,0:T(8,128)} %get-tuple-element.61), channel_id=1, source_target_pairs={{0,2},{1,3},{2,0},{3,1},{4,6},{5,7},{6,4},{7,5}} | collective-permute-start | bytes 1966088 | tf_op jit(solution)/shard_map/ppermute | solution.py:476
  132.5 0.8 copy-start.9
  133.3 58.2 %collective-permute-start.5 = (f32[64,2560]{1,0:T(8,128)}, f32[64,2560]{1,0:T(8,128)S(1)}, u32[]{:S(2)}, u32[]{:S(2)}) collective-permute-start(f32[64,2560]{1,0:T(8,128)} %get-tuple-element.62), channel_id=1, source_target_pairs={{0,3},{1,2},{2,1},{3,0},{4,7},{5,6},{6,5},{7,4}} | collective-permute-start | bytes 1966088 | tf_op jit(solution)/shard_map/ppermute | solution.py:476
  134.8 20.1 %copy-start.4 = (f32[64,2048]{1,0:T(8,128)}, f32[64,2048]{1,0:T(8,128)S(1)}, u32[]{:S(2)}) copy-start(f32[64,2048]{1,0:T(8,128)S(1)} %collective-permute-done.6.refs_0_) | copy-start | bytes 1572868
  134.8 40.0 %collective-permute-start.7 = (f32[64,2048]{1,0:T(8,128)}, f32[64,2048]{1,0:T(8,128)S(1)}, u32[]{:S(2)}, u32[]{:S(2)}) collective-permute-start(f32[64,2048]{1,0:T(8,128)} %get-tuple-element.64), channel_id=1, source_target_pairs={{0,3},{1,2},{2,1},{3,0},{4,7},{5,6},{6,5},{7,4}} | collective-permute-start | bytes 1572872 | tf_op jit(solution)/shard_map/ppermute | solution.py:476
  135.1 16.3 %copy-start.6 = (f32[64,2048]{1,0:T(8,128)}, f32[64,2048]{1,0:T(8,128)S(1)}, u32[]{:S(2)}) copy-start(f32[64,2048]{1,0:T(8,128)S(1)} %collective-permute-done.13.refs_1_) | copy-start | bytes 1572868
  135.1 61.4 %collective-permute-start.2 = (f32[64,1280]{1,0:T(8,128)}, f32[64,1280]{1,0:T(8,128)}, u32[]{:S(2)}, u32[]{:S(2)}) collective-permute-start(f32[64,1280]{1,0:T(8,128)} %get-tuple-element.59), channel_id=1, source_target_pairs={{0,2},{1,3},{2,0},{3,1},{4,6},{5,7},{6,4},{7,5}} | collective-permute-start | bytes 983048 | tf_op jit(solution)/shard_map/ppermute | solution.py:476
  135.4 19.6 %copy-start.3 = (f32[64,2560]{1,0:T(8,128)}, f32[64,2560]{1,0:T(8,128)S(1)}, u32[]{:S(2)}) copy-start(f32[64,2560]{1,0:T(8,128)S(1)} %collective-permute-done.12.refs_1_) | copy-start | bytes 1966084
  135.4 61.1 %collective-permute-start.3 = (f32[64,1280]{1,0:T(8,128)}, f32[64,1280]{1,0:T(8,128)}, u32[]{:S(2)}, u32[]{:S(2)}) collective-permute-start(f32[64,1280]{1,0:T(8,128)} %get-tuple-element.60), channel_id=1, source_target_pairs={{0,3},{1,2},{2,1},{3,0},{4,7},{5,6},{6,5},{7,4}} | collective-permute-start | bytes 983048 | tf_op jit(solution)/shard_map/ppermute | solution.py:476
  138.1 0.8 copy-start
  159.1 15.8 %copy-start.12 = (f32[64,384]{1,0:T(8,128)S(1)}, f32[64,384]{1,0:T(8,128)}, u32[]{:S(2)}) copy-start(f32[64,384]{1,0:T(8,128)} %get-tuple-element.57) | copy-start | bytes 294916
  159.1 16.0 %copy-start.13 = (f32[64,384]{1,0:T(8,128)S(1)}, f32[64,384]{1,0:T(8,128)}, u32[]{:S(2)}) copy-start(f32[64,384]{1,0:T(8,128)} %get-tuple-element.58) | copy-start | bytes 294916
  174.8 13.1 %copy-start.5 = (f32[64,2048]{1,0:T(8,128)}, f32[64,2048]{1,0:T(8,128)S(1)}, u32[]{:S(2)}) copy-start(f32[64,2048]{1,0:T(8,128)S(1)} %collective-permute-done.7.refs_1_) | copy-start | bytes 1572868
  174.8 25.5 %collective-permute-start = (f32[64,384]{1,0:T(8,128)S(1)}, f32[64,384]{1,0:T(8,128)S(1)}, u32[]{:S(2)}, u32[]{:S(2)}) collective-permute-start(f32[64,384]{1,0:T(8,128)S(1)} %copy-done.12), channel_id=1, source_target_pairs={{0,3},{1,2},{2,1},{3,0},{4,7},{5,6},{6,5},{7,4}} | collective-permute-start | bytes 294920 | tf_op jit(solution)/shard_map/ppermute | solution.py:476
  175.1 12.9 %copy-start.1 = (f32[64,2560]{1,0:T(8,128)}, f32[64,2560]{1,0:T(8,128)S(1)}, u32[]{:S(2)}) copy-start(f32[64,2560]{1,0:T(8,128)S(1)} %collective-permute-done.4.refs_0_) | copy-start | bytes 1966084
  175.1 24.3 %collective-permute-start.1 = (f32[64,384]{1,0:T(8,128)S(1)}, f32[64,384]{1,0:T(8,128)S(1)}, u32[]{:S(2)}, u32[]{:S(2)}) collective-permute-start(f32[64,384]{1,0:T(8,128)S(1)} %copy-done.13), channel_id=1, source_target_pairs={{0,2},{1,3},{2,0},{3,1},{4,6},{5,7},{6,4},{7,5}} | collective-permute-start | bytes 294920 | tf_op jit(solution)/shard_map/ppermute | solution.py:476
  191.6 0.8 copy-start.2

commit v7 on v5

--- a/solution.py
+++ b/solution.py
@@ -16,6 +16,7 @@
 EARLY = ((256, 2), (512, 1), (1024, 1), (2048, 3))
 LATE = (4096, 2048, 1280, 384)
 LATE_UNITS = ((2048, 2), (2048, 1), (1280, 1), (384, 1))
+STATS = 4
 
 
 def _to_rows(vec_1xn):
@@ -46,6 +47,7 @@
     batch, depth = xs.shape
     rows = batch // n_dev
     k_steps = depth // DEPTH
+    assert SLOTS == k_steps + 1
 
     def rows_of(p):
         return pl.ds(pl.multiple_of(_peer(me, p) * rows, rows), rows)
@@ -94,10 +96,12 @@
         pltpu.make_async_copy(invt_ref, invt_v, v_sem.at[0]),
         pltpu.make_async_copy(tgt_ref, tgt_v, v_sem.at[1]),
     ]
-    for copy in small + x_copies:
+    for copy in small + x_copies[2:]:
         copy.start()
-    for i in range(SLOTS - 1):
+    for i in range(k_steps):
         fetch_w(0, jnp.int32(i)).start()
+    for copy in x_copies[:2]:
+        copy.start()
     barrier = pltpu.get_barrier_semaphore()
     for p in range(1, n_dev):
         pl.semaphore_signal(
@@ -115,26 +119,25 @@
     lane = lax.broadcasted_iota(jnp.int32, (rows, LANES), 1)
     for p in range(n_dev):
         left_rows[pl.ds(p * rows, rows), :] = tmp[rows_of(p), :].astype(jnp.int32) - me * shard - lane
-    for copy in x_copies:
+    for copy in x_copies[2:]:
         copy.wait()
 
-    def multiply(seg, step):
+    def multiply(seg, step, lo=0, hi=batch):
         width = segments[seg][0]
         slot, k = lax.rem(segments[seg][4] + step, SLOTS), lax.rem(step, k_steps)
-        fetch_w(seg, step).wait()
-        x = xs[:, pl.ds(pl.multiple_of(k * DEPTH, DEPTH), DEPTH)]
+        x = xs[lo:hi, pl.ds(pl.multiple_of(k * DEPTH, DEPTH), DEPTH)]
         for off in range(0, width, HALF):
             wide = min(HALF, width - off)
             part = jnp.dot(x, wbuf[slot, :, off:off + wide], preferred_element_type=jnp.float32)
-            acc[:, off:off + wide] = part + jnp.where(k == 0, 0.0, acc[:, off:off + wide])
-
-    def finish(col, width, out_ref, out_off):
+            acc[lo:hi, off:off + wide] = part + jnp.where(k == 0, 0.0, acc[lo:hi, off:off + wide])
+
+    def finish(col, width, out_ref, out_off, lo=0, hi=batch):
         group = 32
         span = next(n for n in (UNIT, HALF, LANES) if width % n == 0)
 
         def some(j, _):
             at = pl.multiple_of(j * span, span)
-            for r in range(0, batch, group):
+            for r in range(lo, hi, group):
                 block = slice(r, r + group)
                 scale = scale_rows[block, :]
                 tiles = []
@@ -160,10 +163,33 @@
         lax.fori_loop(0, width // span, some, 0)
 
     sent, own, stored = [], [], []
+
+    def send_early(u, peers, col, width):
+        for p in peers:
+            copy = send(u, p, col, width)
+            copy.start()
+            sent.append(copy)
+
+    far, first_width = 2 * rows, segments[0][0]
+
+    def far_body(k, _):
+        fetch_w(0, k).wait()
+        multiply(0, k, far, batch)
+        return 0
+
+    lax.fori_loop(0, k_steps, far_body, 0)
+    finish(0, first_width, zsend, 0, far, batch)
+    pl.semaphore_wait(barrier, n_dev - 1)
+    send_early(0, (2, 3), 0, first_width)
+    for copy in x_copies[:2]:
+        copy.wait()
+
     for seg, (width, n, chunk, col0, g0) in enumerate(segments):
         for i in range(n):
 
-            def body(k, _, seg=seg, i=i, n=n):
+            again = seg == 0 and i == 0
+
+            def body(k, _, seg=seg, i=i, n=n, again=again):
                 step = i * k_steps + k
                 ahead = step + SLOTS - 1
 
@@ -176,20 +202,19 @@
                     def _():
                         fetch_w(seg + 1, ahead - n * k_steps).start()
 
-                multiply(seg, step)
+                if again:
+                    multiply(seg, step, 0, far)
+                else:
+                    fetch_w(seg, step).wait()
+                    multiply(seg, step)
                 return 0
 
             lax.fori_loop(0, k_steps, body, 0)
             col = col0 + i * width
             if chunk is None:
-                finish(col, width, zsend, col)
-                if not sent:
-                    pl.semaphore_wait(barrier, n_dev - 1)
+                finish(col, width, zsend, col, 0, far if again else batch)
                 u = len(own)
-                for p in (2, 3, 1):
-                    copy = send(u, p, col, width)
-                    copy.start()
-                    sent.append(copy)
+                send_early(u, (1,) if again else (2, 3, 1), col, width)
                 copy = put_own(u, col, width)
                 copy.start()
                 own.append(copy)
@@ -213,7 +238,7 @@
     packed = jnp.where(which == 0, m_row, jnp.where(which == 1, s_row, t_row))
     for p in range(n_dev):
         tmp[rows_of(p), :] = packed[p * rows:(p + 1) * rows, :]
-    pack_v[...] = jnp.transpose(tmp[...])[:8, :]
+    pack_v[...] = jnp.transpose(tmp[...])[:STATS, :]
     for p in (2, 3, 1):
         copy = pltpu.make_async_remote_copy(
             src_ref=pack_v,
@@ -255,7 +280,7 @@
     hbm = pl.BlockSpec(memory_space=pltpu.HBM)
     out_shape = [pltpu.HBM((rows, sent), jnp.float32)] * n_dev
     out_shape += [pltpu.HBM((rows, width), jnp.float32) for width in LATE for _ in range(n_dev)]
-    out_shape += [pltpu.HBM((8, batch), jnp.float32)] * n_dev
+    out_shape += [pltpu.HBM((STATS, batch), jnp.float32)] * n_dev
     table = pltpu.VMEM((batch, LANES), jnp.float32)
     widest = max(width for width, _ in EARLY + LATE_UNITS)
     dma = pltpu.SemaphoreType.DMA
@@ -272,7 +297,7 @@
             pltpu.VMEM((2, batch, widest), jnp.float32),
             pltpu.VMEM((1, batch), jnp.float32),
             pltpu.VMEM((1, batch), jnp.int32),
-            pltpu.VMEM((8, batch), jnp.float32),
+            pltpu.VMEM((STATS, batch), jnp.float32),
             table,
             pltpu.VMEM((batch, LANES), jnp.int32),
             table,
@@ -457,8 +482,7 @@
         params, at_target = _merge(packs)
         out = None
         final = len(chunks) - 1
-        plan = [(k, (0, 1)) for k in range(final + 1)] + [(k, (2, 3)) for k in range(final)]
-        plan += [(final, (2,)), (final, (3,))]
+        plan = [(k, peers) for peers in ((0, 1), (2, 3)) for k in range(final + 1)]
         for i, (k, peers) in enumerate(plan):
             begin, got = chunks[k]
             blocks = [got[p] for p in peers]

time: 214 us -> 213 us (level)
    pallas_call x11 -> x10, Pallas kernels: 46.6 us -> 46.1 us  [_cdf(): pl.pallas_call(functools.partial(_cdf_kernel, (peers, shard, base, width,...]
where the time goes in v7:
time: 213 us
  Pallas kernels  147 us (69%)
  waiting for transfers between devices  55.4 us (26%)
  starting transfers between devices  6.37 us (3%)
  local copies, waits for them, and re-layouts  2.85 us (1%)
    pallas_call x1, Pallas kernels, _logits(): pl.pallas_call(functools.partial(_logits_kernel, (n_dev, shard, segments,...  99.7 us
    ppermute x12, waiting for transfers between devices, swap(): return lax.ppermute(a, 'vp', [(i, i ^ p) for i in range(n_dev)])  55.4 us
    pallas_call x10, Pallas kernels, _cdf(): pl.pallas_call(functools.partial(_cdf_kernel, (peers, shard, base, width,...  46.1 us
    ppermute x12, starting transfers between devices, swap(): return lax.ppermute(a, 'vp', [(i, i ^ p) for i in range(n_dev)])  6.37 us
  transfers between devices with their start and end apart: 12, of which 2 were waited for; matrix products, arithmetic and copies ran while one was open for 0% of the time, Pallas kernels for 22%

profile of v7, /device:TPU:0, one launch (start us, length us, event | category | flops | bytes accessed | tf_op | source)
XLA Modules:
  0.0 212.7 jit_solution(7009833155236223544)
XLA Ops:
  0.6 99.7 %logits.1 = (f32[64,8192]{1,0:T(8,128)}, f32[64,8192]{1,0:T(8,128)}, f32[64,8192]{1,0:T(8,128)}, f32[64,8192]{1,0:T(8,128)}, f32[64,4096]{1,0:T(8,128)}, /*index...) custom-call(bf16[256,4096]{1,0:T(8,128)(2,1)} %x_ref.1, ...), custom_call_target="tpu_custom_call" | custom-call | flops 33554432000 | bytes 131072000 | tf_op jit(solution)/shard_map/logits/pallas_call | solution.py:287
  100.3 0.1 collective-permute-start.11
  100.5 1.7 collective-permute-start.7
  102.2 0.4 collective-permute-start.9
  102.6 0.1 collective-permute-start.8
  102.7 1.5 collective-permute-done.8.refs_1_
  104.2 0.6 copy-done.8
  104.9 0.3 collective-permute-start.4
  105.1 0.7 copy-done.7
  105.8 0.1 collective-permute-start.10
  106.0 53.9 %collective-permute-done.4.refs_0_ = f32[64,2048]{1,0:T(8,128)S(1)} collective-permute-done((f32[64,2048]{1,0:T(8,128)}, f32[64,2048]{1,0:T(8,128)S(1)}, u32[]{:S(2)}, u32[]{:S(2)}) %collective-permute-start.4) | collective-permute-done | bytes 524320 | tf_op jit(solution)/shard_map/ppermute | solution.py:467
  159.9 1.2 collective-permute-start.2
  161.0 0.0 collective-permute-done.11.refs_1_
  161.0 1.4 collective-permute-start.3
  162.4 1.5 merge.1
  163.9 0.8 copy-done
  164.6 9.4 %cdf.10 = (f32[64,64000]{1,0:T(8,128)}, f32[64,128]{1,0:T(8,128)S(1)}) custom-call(f32[64,8192]{1,0:T(8,128)} %get-tuple-element.64.refs_0_, f32[64,8192]{1,0:T(8,128)} %get-tuple-element.65.refs_1_, f32[64,128]{1,0:T(8,128)S(1)} %copy-done), custom_call_target="tpu_custom_call" | custom-call | flops 805306368 | bytes 8388608 | tf_op jit(solution)/shard_map/cdf/pallas_call | solution.py:441
  174.1 5.5 %cdf.11 = (f32[64,64000]{1,0:T(8,128)}, f32[64,128]{1,0:T(8,128)S(1)}) custom-call(f32[64,4096]{1,0:T(8,128)} %get-tuple-element.62.refs_0_, f32[64,4096]{1,0:T(8,128)} %copy-done.3, f32[64,128]{1,0:T(8,128)S(1)} %get-tuple-element.71.refs_2_, f32[64,64000]{1,0:T(8,128)} %get-tuple-element.72.refs_3_), custom_call_target="tpu_custom_call", output_to_operand_aliasing={{0}: (3, {})} | custom-call | flops 402653184 | bytes 4194304 | tf_op jit(solution)/shard_map/cdf/pallas_call | solution.py:441
  179.6 3.6 %cdf.12 = (f32[64,64000]{1,0:T(8,128)}, f32[64,128]{1,0:T(8,128)S(1)}) custom-call(f32[64,2048]{1,0:T(8,128)} %get-tuple-element.60.refs_0_, f32[64,2048]{1,0:T(8,128)} %copy-done.5, f32[64,128]{1,0:T(8,128)S(1)} %get-tuple-element.73.refs_2_, f32[64,64000]{1,0:T(8,128)} %get-tuple-element.74.refs_3_), custom_call_target="tpu_custom_call", output_to_operand_aliasing={{0}: (3, {})} | custom-call | flops 201326592 | bytes 2097152 | tf_op jit(solution)/shard_map/cdf/pallas_call | solution.py:441
  183.2 2.9 %cdf.13 = (f32[64,64000]{1,0:T(8,128)}, f32[64,128]{1,0:T(8,128)S(1)}) custom-call(f32[64,1280]{1,0:T(8,128)} %get-tuple-element.58.refs_0_, f32[64,1280]{1,0:T(8,128)} %copy-done.7, f32[64,128]{1,0:T(8,128)S(1)} %get-tuple-element.75.refs_2_, f32[64,64000]{1,0:T(8,128)} %get-tuple-element.76.refs_3_), custom_call_target="tpu_custom_call", output_to_operand_aliasing={{0}: (3, {})} | custom-call | flops 125829120 | bytes 1310720 | tf_op jit(solution)/shard_map/cdf/pallas_call | solution.py:441
  186.1 2.0 cdf.14
  188.1 0.0 collective-permute-done.6.refs_0_
  188.1 1.0 collective-permute-start
  189.1 0.0 collective-permute-done.7.refs_1_
  189.1 0.1 collective-permute-start.1
  189.2 9.7 %cdf.15 = (f32[64,64000]{1,0:T(8,128)}, f32[64,128]{1,0:T(8,128)S(1)}) custom-call(f32[64,8192]{1,0:T(8,128)} %get-tuple-element.54.refs_0_, f32[64,8192]{1,0:T(8,128)} %get-tuple-element.55.refs_1_, f32[64,128]{1,0:T(8,128)S(1)} %get-tuple-element.79.refs_2_, f32[64,64000]{1,0:T(8,128)} %get-tuple-element.80.refs_3_), custom_call_target="tpu_custom_call", output_to_operand_aliasing={{0}: (3, {})} | custom-call | flops 805306368 | bytes 8388608 | tf_op jit(solution)/shard_map/cdf/pallas_call | solution.py:441
  199.0 5.5 %cdf.16 = (f32[64,64000]{1,0:T(8,128)}, f32[64,128]{1,0:T(8,128)S(1)}) custom-call(f32[64,4096]{1,0:T(8,128)} %copy-done.1, f32[64,4096]{1,0:T(8,128)} %copy-done.2, f32[64,128]{1,0:T(8,128)S(1)} %get-tuple-element.81.refs_2_, f32[64,64000]{1,0:T(8,128)} %get-tuple-element.82.refs_3_), custom_call_target="tpu_custom_call", output_to_operand_aliasing={{0}: (3, {})} | custom-call | flops 402653184 | bytes 4194304 | tf_op jit(solution)/shard_map/cdf/pallas_call | solution.py:441
  204.5 3.6 %cdf.17 = (f32[64,64000]{1,0:T(8,128)}, f32[64,128]{1,0:T(8,128)S(1)}) custom-call(f32[64,2048]{1,0:T(8,128)} %copy-done.4, f32[64,2048]{1,0:T(8,128)} %collective-permute-done.5.refs_1_, f32[64,128]{1,0:T(8,128)S(1)} %get-tuple-element.83.refs_2_, f32[64,64000]{1,0:T(8,128)} %get-tuple-element.84.refs_3_), custom_call_target="tpu_custom_call", output_to_operand_aliasing={{0}: (3, {})} | custom-call | flops 201326592 | bytes 2097152 | tf_op jit(solution)/shard_map/cdf/pallas_call | solution.py:441
  208.1 0.0 collective-permute-done.2.refs_0_
  208.1 0.7 copy-done.6
  208.8 2.9 %cdf.18 = (f32[64,64000]{1,0:T(8,128)}, f32[64,128]{1,0:T(8,128)S(1)}) custom-call(f32[64,1280]{1,0:T(8,128)} %copy-done.6, f32[64,1280]{1,0:T(8,128)} %collective-permute-done.3.refs_1_, f32[64,128]{1,0:T(8,128)S(1)} %get-tuple-element.85.refs_2_, f32[64,64000]{1,0:T(8,128)} %get-tuple-element.86.refs_3_), custom_call_target="tpu_custom_call", output_to_operand_aliasing={{0}: (3, {})} | custom-call | flops 125829120 | bytes 1310720 | tf_op jit(solution)/shard_map/cdf/pallas_call | solution.py:441
  211.7 1.0 cdf.19
  (26 shorter events, 0.1 us)
Async XLA Ops:
  100.3 60.7 %collective-permute-start.11 = (f32[64,4096]{1,0:T(8,128)}, f32[64,4096]{1,0:T(8,128)S(1)}, u32[]{:S(2)}, u32[]{:S(2)}) collective-permute-start(f32[64,4096]{1,0:T(8,128)} %get-tuple-element.63), channel_id=1, source_target_pairs={{0,1},{1,0},{2,3},{3,2},{4,5},{5,4},{6,7},{7,6}} | collective-permute-start | bytes 3145736 | tf_op jit(solution)/shard_map/ppermute | solution.py:467
  100.5 87.6 %collective-permute-start.6 = (f32[64,4096]{1,0:T(8,128)}, f32[64,4096]{1,0:T(8,128)S(1)}, u32[]{:S(2)}, u32[]{:S(2)}) collective-permute-start(f32[64,4096]{1,0:T(8,128)} %get-tuple-element.52), channel_id=1, source_target_pairs={{0,2},{1,3},{2,0},{3,1},{4,6},{5,7},{6,4},{7,5}} | collective-permute-start | bytes 3145736 | tf_op jit(solution)/shard_map/ppermute | solution.py:467
  100.5 88.7 %collective-permute-start.7 = (f32[64,4096]{1,0:T(8,128)}, f32[64,4096]{1,0:T(8,128)S(1)}, u32[]{:S(2)}, u32[]{:S(2)}) collective-permute-start(f32[64,4096]{1,0:T(8,128)} %get-tuple-element.53), channel_id=1, source_target_pairs={{0,3},{1,2},{2,1},{3,0},{4,7},{5,6},{6,5},{7,4}} | collective-permute-start | bytes 3145736 | tf_op jit(solution)/shard_map/ppermute | solution.py:467
  102.2 2.9 %collective-permute-start.9 = (f32[64,1280]{1,0:T(8,128)}, f32[64,1280]{1,0:T(8,128)S(1)}, u32[]{:S(2)}, u32[]{:S(2)}) collective-permute-start(f32[64,1280]{1,0:T(8,128)} %get-tuple-element.59), channel_id=1, source_target_pairs={{0,1},{1,0},{2,3},{3,2},{4,5},{5,4},{6,7},{7,6}} | collective-permute-start | bytes 983048 | tf_op jit(solution)/shard_map/ppermute | solution.py:467
  102.6 1.6 collective-permute-start.8
  104.2 0.6 copy-start.8
  104.9 55.0 %collective-permute-start.4 = (f32[64,2048]{1,0:T(8,128)}, f32[64,2048]{1,0:T(8,128)S(1)}, u32[]{:S(2)}, u32[]{:S(2)}) collective-permute-start(f32[64,2048]{1,0:T(8,128)} %get-tuple-element.50), channel_id=1, source_target_pairs={{0,2},{1,3},{2,0},{3,1},{4,6},{5,7},{6,4},{7,5}} | collective-permute-start | bytes 1572872 | tf_op jit(solution)/shard_map/ppermute | solution.py:467
  105.1 0.7 copy-start.7
  105.8 54.0 %collective-permute-start.10 = (f32[64,2048]{1,0:T(8,128)}, f32[64,2048]{1,0:T(8,128)S(1)}, u32[]{:S(2)}, u32[]{:S(2)}) collective-permute-start(f32[64,2048]{1,0:T(8,128)} %get-tuple-element.61), channel_id=1, source_target_pairs={{0,1},{1,0},{2,3},{3,2},{4,5},{5,4},{6,7},{7,6}} | collective-permute-start | bytes 1572872 | tf_op jit(solution)/shard_map/ppermute | solution.py:467
  159.8 1.2 copy-start.4
  159.8 44.6 %collective-permute-start.5 = (f32[64,2048]{1,0:T(8,128)}, f32[64,2048]{1,0:T(8,128)}, u32[]{:S(2)}, u32[]{:S(2)}) collective-permute-start(f32[64,2048]{1,0:T(8,128)} %get-tuple-element.51), channel_id=1, source_target_pairs={{0,3},{1,2},{2,1},{3,0},{4,7},{5,6},{6,5},{7,4}} | collective-permute-start | bytes 1572872 | tf_op jit(solution)/shard_map/ppermute | solution.py:467
  159.9 1.2 copy-start.5
  159.9 48.2 %collective-permute-start.2 = (f32[64,1280]{1,0:T(8,128)}, f32[64,1280]{1,0:T(8,128)S(1)}, u32[]{:S(2)}, u32[]{:S(2)}) collective-permute-start(f32[64,1280]{1,0:T(8,128)} %get-tuple-element.48), channel_id=1, source_target_pairs={{0,2},{1,3},{2,0},{3,1},{4,6},{5,7},{6,4},{7,5}} | collective-permute-start | bytes 983048 | tf_op jit(solution)/shard_map/ppermute | solution.py:467
  161.0 13.0 %copy-start.3 = (f32[64,4096]{1,0:T(8,128)}, f32[64,4096]{1,0:T(8,128)S(1)}, u32[]{:S(2)}) copy-start(f32[64,4096]{1,0:T(8,128)S(1)} %collective-permute-done.11.refs_1_) | copy-start | bytes 3145732
  161.0 47.1 %collective-permute-start.3 = (f32[64,1280]{1,0:T(8,128)}, f32[64,1280]{1,0:T(8,128)}, u32[]{:S(2)}, u32[]{:S(2)}) collective-permute-start(f32[64,1280]{1,0:T(8,128)} %get-tuple-element.49), channel_id=1, source_target_pairs={{0,3},{1,2},{2,1},{3,0},{4,7},{5,6},{6,5},{7,4}} | collective-permute-start | bytes 983048 | tf_op jit(solution)/shard_map/ppermute | solution.py:467
  163.9 0.8 copy-start
  183.2 5.0 %copy-start.10 = (f32[64,384]{1,0:T(8,128)S(1)}, f32[64,384]{1,0:T(8,128)}, u32[]{:S(2)}) copy-start(f32[64,384]{1,0:T(8,128)} %get-tuple-element.46) | copy-start | bytes 294916
  183.2 6.0 %copy-start.9 = (f32[64,384]{1,0:T(8,128)S(1)}, f32[64,384]{1,0:T(8,128)}, u32[]{:S(2)}) copy-start(f32[64,384]{1,0:T(8,128)} %get-tuple-element.47) | copy-start | bytes 294916
  188.1 10.8 %copy-start.1 = (f32[64,4096]{1,0:T(8,128)}, f32[64,4096]{1,0:T(8,128)S(1)}, u32[]{:S(2)}) copy-start(f32[64,4096]{1,0:T(8,128)S(1)} %collective-permute-done.6.refs_0_) | copy-start | bytes 3145732
  188.1 23.6 %collective-permute-start = (f32[64,384]{1,0:T(8,128)S(1)}, f32[64,384]{1,0:T(8,128)S(1)}, u32[]{:S(2)}, u32[]{:S(2)}) collective-permute-start(f32[64,384]{1,0:T(8,128)S(1)} %copy-done.10), channel_id=1, source_target_pairs={{0,2},{1,3},{2,0},{3,1},{4,6},{5,7},{6,4},{7,5}} | collective-permute-start | bytes 294920 | tf_op jit(solution)/shard_map/ppermute | solution.py:467
  189.1 9.8 %copy-start.2 = (f32[64,4096]{1,0:T(8,128)}, f32[64,4096]{1,0:T(8,128)S(1)}, u32[]{:S(2)}) copy-start(f32[64,4096]{1,0:T(8,128)S(1)} %collective-permute-done.7.refs_1_) | copy-start | bytes 3145732
  189.1 22.6 %collective-permute-start.1 = (f32[64,384]{1,0:T(8,128)S(1)}, f32[64,384]{1,0:T(8,128)S(1)}, u32[]{:S(2)}, u32[]{:S(2)}) collective-permute-start(f32[64,384]{1,0:T(8,128)S(1)} %copy-done.9), channel_id=1, source_target_pairs={{0,3},{1,2},{2,1},{3,0},{4,7},{5,6},{6,5},{7,4}} | collective-permute-start | bytes 294920 | tf_op jit(solution)/shard_map/ppermute | solution.py:467
  208.1 0.7 copy-start.6

commit v8 on v7

--- a/solution.py
+++ b/solution.py
@@ -13,7 +13,8 @@
 HALF = 256
 DEPTH = 512
 SLOTS = 9
-EARLY = ((256, 2), (512, 1), (1024, 1), (2048, 3))
+FIRST = 256
+EARLY = ((256, 1), (512, 1), (1024, 1), (2048, 3))
 LATE = (4096, 2048, 1280, 384)
 LATE_UNITS = ((2048, 2), (2048, 1), (1280, 1), (384, 1))
 STATS = 4
@@ -40,9 +41,9 @@
     early = take(n_dev)
     late = [take(n_dev) for _ in range(n_late)]
     packs = take(n_dev)
-    xs, wbuf, acc, zsend, zbuf, invt_v, tgt_v, pack_v = take(8)
+    xs, wfirst, wbuf, acc, zsend, zbuf, invt_v, tgt_v, pack_v = take(9)
     scale_rows, left_rows, tmp, m_ref, s_ref, t_ref = take(6)
-    w_sem, z_sem, x_sem, v_sem, own_sem, send_sem, recv_sem, pack_send, pack_recv = take(9)
+    first_sem, w_sem, z_sem, x_sem, v_sem, own_sem, send_sem, recv_sem, pack_send, pack_recv = take(10)
     me = lax.axis_index("vp")
     batch, depth = xs.shape
     rows = batch // n_dev
@@ -62,6 +63,10 @@
             wbuf.at[slot, :, pl.ds(0, width)],
             w_sem.at[slot],
         )
+
+    def fetch_first(k):
+        row = pl.ds(pl.multiple_of(k * DEPTH, DEPTH), DEPTH)
+        return pltpu.make_async_copy(w_ref.at[row, pl.ds(0, FIRST)], wfirst.at[row, :], first_sem.at[k])
 
     def put_late(slot, c, off, width):
         return [
@@ -98,10 +103,12 @@
     ]
     for copy in small + x_copies[2:]:
         copy.start()
-    for i in range(k_steps):
-        fetch_w(0, jnp.int32(i)).start()
+    for k in range(k_steps):
+        fetch_first(k).start()
     for copy in x_copies[:2]:
         copy.start()
+    for i in range(SLOTS - 1):
+        fetch_w(0, jnp.int32(i)).start()
     barrier = pltpu.get_barrier_semaphore()
     for p in range(1, n_dev):
         pl.semaphore_signal(
@@ -122,14 +129,14 @@
     for copy in x_copies[2:]:
         copy.wait()
 
-    def multiply(seg, step, lo=0, hi=batch):
+    def multiply(seg, step):
         width = segments[seg][0]
         slot, k = lax.rem(segments[seg][4] + step, SLOTS), lax.rem(step, k_steps)
-        x = xs[lo:hi, pl.ds(pl.multiple_of(k * DEPTH, DEPTH), DEPTH)]
+        x = xs[:, pl.ds(pl.multiple_of(k * DEPTH, DEPTH), DEPTH)]
         for off in range(0, width, HALF):
             wide = min(HALF, width - off)
             part = jnp.dot(x, wbuf[slot, :, off:off + wide], preferred_element_type=jnp.float32)
-            acc[lo:hi, off:off + wide] = part + jnp.where(k == 0, 0.0, acc[lo:hi, off:off + wide])
+            acc[:, off:off + wide] = part + jnp.where(k == 0, 0.0, acc[:, off:off + wide])
 
     def finish(col, width, out_ref, out_off, lo=0, hi=batch):
         group = 32
@@ -170,26 +177,38 @@
             copy.start()
             sent.append(copy)
 
-    far, first_width = 2 * rows, segments[0][0]
-
-    def far_body(k, _):
-        fetch_w(0, k).wait()
-        multiply(0, k, far, batch)
+    far = 2 * rows
+
+    def multiply_first(k, lo, hi):
+        at = pl.ds(pl.multiple_of(k * DEPTH, DEPTH), DEPTH)
+        part = jnp.dot(xs[lo:hi, at], wfirst[at, :], preferred_element_type=jnp.float32)
+        acc[lo:hi, :FIRST] = part + jnp.where(k == 0, 0.0, acc[lo:hi, :FIRST])
+
+    def far_step(k, _):
+        fetch_first(k).wait()
+        multiply_first(k, far, batch)
         return 0
 
-    lax.fori_loop(0, k_steps, far_body, 0)
-    finish(0, first_width, zsend, 0, far, batch)
+    def near_step(k, _):
+        multiply_first(k, 0, far)
+        return 0
+
+    lax.fori_loop(0, k_steps, far_step, 0)
+    finish(0, FIRST, zsend, 0, far, batch)
     pl.semaphore_wait(barrier, n_dev - 1)
-    send_early(0, (2, 3), 0, first_width)
+    send_early(0, (2, 3), 0, FIRST)
     for copy in x_copies[:2]:
         copy.wait()
+    lax.fori_loop(0, k_steps, near_step, 0)
+    finish(0, FIRST, zsend, 0, 0, far)
+    send_early(0, (1,), 0, FIRST)
+    own.append(put_own(0, 0, FIRST))
+    own[0].start()
 
     for seg, (width, n, chunk, col0, g0) in enumerate(segments):
         for i in range(n):
 
-            again = seg == 0 and i == 0
-
-            def body(k, _, seg=seg, i=i, n=n, again=again):
+            def body(k, _, seg=seg, i=i, n=n):
                 step = i * k_steps + k
                 ahead = step + SLOTS - 1
 
@@ -202,19 +221,16 @@
                     def _():
                         fetch_w(seg + 1, ahead - n * k_steps).start()
 
-                if again:
-                    multiply(seg, step, 0, far)
-                else:
-                    fetch_w(seg, step).wait()
-                    multiply(seg, step)
+                fetch_w(seg, step).wait()
+                multiply(seg, step)
                 return 0
 
             lax.fori_loop(0, k_steps, body, 0)
             col = col0 + i * width
             if chunk is None:
-                finish(col, width, zsend, col, 0, far if again else batch)
+                finish(col, width, zsend, col)
                 u = len(own)
-                send_early(u, (1,) if again else (2, 3, 1), col, width)
+                send_early(u, (2, 3, 1), col, width)
                 copy = put_own(u, col, width)
                 copy.start()
                 own.append(copy)
@@ -264,9 +280,9 @@
     batch, depth = x.shape
     shard = w.shape[1]
     rows = batch // n_dev
-    segments, col, g0 = [], 0, 0
+    segments, col, g0 = [], FIRST, 0
     chunk_of = {}
-    begin = sum(width * n for width, n in EARLY)
+    sent = begin = FIRST + sum(width * n for width, n in EARLY)
     for c, width in enumerate(LATE):
         chunk_of.update({begin + i: (c, i) for i in range(0, width, LANES)})
         begin += width
@@ -275,8 +291,7 @@
         col += width * n
         g0 += n * (depth // DEPTH)
     assert col == shard == begin
-    n_early = sum(n for _, n in EARLY)
-    sent = sum(width * n for width, n in EARLY)
+    n_early = 1 + sum(n for _, n in EARLY)
     hbm = pl.BlockSpec(memory_space=pltpu.HBM)
     out_shape = [pltpu.HBM((rows, sent), jnp.float32)] * n_dev
     out_shape += [pltpu.HBM((rows, width), jnp.float32) for width in LATE for _ in range(n_dev)]
@@ -291,6 +306,7 @@
         out_shape=out_shape,
         scratch_shapes=[
             pltpu.VMEM((batch, depth), jnp.bfloat16),
+            pltpu.VMEM((depth, FIRST), jnp.bfloat16),
             pltpu.VMEM((SLOTS, DEPTH, widest), jnp.bfloat16),
             pltpu.VMEM((batch, widest), jnp.float32),
             pltpu.VMEM((batch, sent), jnp.float32),
@@ -304,6 +320,7 @@
             table,
             table,
             table,
+            dma((depth // DEPTH,)),
             dma((SLOTS,)),
             dma((2, n_dev)),
             dma((n_dev,)),

time: 213 us -> 214 us (level)
  no operation moved by 1% of the time
where the time goes in v8:
time: 214 us; the launch traced here: 213 us
  Pallas kernels  148 us (69%)
  waiting for transfers between devices  55.4 us (26%)
  starting transfers between devices  6.36 us (3%)
  local copies, waits for them, and re-layouts  2.85 us (1%)
    pallas_call x1, Pallas kernels, _logits(): pl.pallas_call(functools.partial(_logits_kernel, (n_dev, shard, segments,...  100 us
    ppermute x12, waiting for transfers between devices, swap(): return lax.ppermute(a, 'vp', [(i, i ^ p) for i in range(n_dev)])  55.4 us
    pallas_call x10, Pallas kernels, _cdf(): pl.pallas_call(functools.partial(_cdf_kernel, (peers, shard, base, width,...  46.1 us
    ppermute x12, starting transfers between devices, swap(): return lax.ppermute(a, 'vp', [(i, i ^ p) for i in range(n_dev)])  6.36 us
  transfers between devices with their start and end apart: 12, of which 2 were waited for; matrix products, arithmetic and copies ran while one was open for 0% of the time, Pallas kernels for 22%

profile of v8, /device:TPU:0, one launch (start us, length us, event | category | flops | bytes accessed | tf_op | source)
XLA Modules:
  0.0 213.2 jit_solution(15256997421218641980)
XLA Ops:
  0.6 100.2 %logits.1 = (f32[64,8192]{1,0:T(8,128)}, f32[64,8192]{1,0:T(8,128)}, f32[64,8192]{1,0:T(8,128)}, f32[64,8192]{1,0:T(8,128)}, f32[64,4096]{1,0:T(8,128)}, /*index...) custom-call(bf16[256,4096]{1,0:T(8,128)(2,1)} %x_ref.1, ...), custom_call_target="tpu_custom_call" | custom-call | flops 33554432000 | bytes 131072000 | tf_op jit(solution)/shard_map/logits/pallas_call | solution.py:302
  100.8 0.1 collective-permute-start.11
  100.9 0.0 collective-permute-start.6
  100.9 1.7 collective-permute-start.7
  102.7 0.4 collective-permute-start.9
  103.1 0.1 collective-permute-start.8
  103.2 1.5 collective-permute-done.8.refs_1_
  104.7 0.6 copy-done.8
  105.3 0.3 collective-permute-start.4
  105.6 0.0 collective-permute-done.9.refs_1_
  105.6 0.7 copy-done.7
  106.3 0.1 collective-permute-start.10
  106.4 53.9 %collective-permute-done.4.refs_0_ = f32[64,2048]{1,0:T(8,128)S(1)} collective-permute-done((f32[64,2048]{1,0:T(8,128)}, f32[64,2048]{1,0:T(8,128)S(1)}, u32[]{:S(2)}, u32[]{:S(2)}) %collective-permute-start.4) | collective-permute-done | bytes 524320 | tf_op jit(solution)/shard_map/ppermute | solution.py:484
  160.3 0.0 collective-permute-start.5
  160.3 0.0 collective-permute-done.10.refs_1_
  160.3 1.2 collective-permute-start.2
  161.5 1.4 collective-permute-start.3
  162.9 1.5 merge.1
  164.3 0.8 copy-done
  165.1 9.4 %cdf.10 = (f32[64,64000]{1,0:T(8,128)}, f32[64,128]{1,0:T(8,128)S(1)}) custom-call(f32[64,8192]{1,0:T(8,128)} %get-tuple-element.64.refs_0_, f32[64,8192]{1,0:T(8,128)} %get-tuple-element.65.refs_1_, f32[64,128]{1,0:T(8,128)S(1)} %copy-done), custom_call_target="tpu_custom_call" | custom-call | flops 805306368 | bytes 8388608 | tf_op jit(solution)/shard_map/cdf/pallas_call | solution.py:458
  174.5 5.5 %cdf.11 = (f32[64,64000]{1,0:T(8,128)}, f32[64,128]{1,0:T(8,128)S(1)}) custom-call(f32[64,4096]{1,0:T(8,128)} %get-tuple-element.62.refs_0_, f32[64,4096]{1,0:T(8,128)} %copy-done.3, f32[64,128]{1,0:T(8,128)S(1)} %get-tuple-element.71.refs_2_, f32[64,64000]{1,0:T(8,128)} %get-tuple-element.72.refs_3_), custom_call_target="tpu_custom_call", output_to_operand_aliasing={{0}: (3, {})} | custom-call | flops 402653184 | bytes 4194304 | tf_op jit(solution)/shard_map/cdf/pallas_call | solution.py:458
  180.1 3.6 %cdf.12 = (f32[64,64000]{1,0:T(8,128)}, f32[64,128]{1,0:T(8,128)S(1)}) custom-call(f32[64,2048]{1,0:T(8,128)} %get-tuple-element.60.refs_0_, f32[64,2048]{1,0:T(8,128)} %copy-done.5, f32[64,128]{1,0:T(8,128)S(1)} %get-tuple-element.73.refs_2_, f32[64,64000]{1,0:T(8,128)} %get-tuple-element.74.refs_3_), custom_call_target="tpu_custom_call", output_to_operand_aliasing={{0}: (3, {})} | custom-call | flops 201326592 | bytes 2097152 | tf_op jit(solution)/shard_map/cdf/pallas_call | solution.py:458
  183.7 2.9 %cdf.13 = (f32[64,64000]{1,0:T(8,128)}, f32[64,128]{1,0:T(8,128)S(1)}) custom-call(f32[64,1280]{1,0:T(8,128)} %get-tuple-element.58.refs_0_, f32[64,1280]{1,0:T(8,128)} %copy-done.7, f32[64,128]{1,0:T(8,128)S(1)} %get-tuple-element.75.refs_2_, f32[64,64000]{1,0:T(8,128)} %get-tuple-element.76.refs_3_), custom_call_target="tpu_custom_call", output_to_operand_aliasing={{0}: (3, {})} | custom-call | flops 125829120 | bytes 1310720 | tf_op jit(solution)/shard_map/cdf/pallas_call | solution.py:458
  186.6 2.0 cdf.14
  188.6 1.0 collective-permute-start
  189.6 0.1 collective-permute-start.1
  189.7 9.7 %cdf.15 = (f32[64,64000]{1,0:T(8,128)}, f32[64,128]{1,0:T(8,128)S(1)}) custom-call(f32[64,8192]{1,0:T(8,128)} %get-tuple-element.54.refs_0_, f32[64,8192]{1,0:T(8,128)} %get-tuple-element.55.refs_1_, f32[64,128]{1,0:T(8,128)S(1)} %get-tuple-element.79.refs_2_, f32[64,64000]{1,0:T(8,128)} %get-tuple-element.80.refs_3_), custom_call_target="tpu_custom_call", output_to_operand_aliasing={{0}: (3, {})} | custom-call | flops 805306368 | bytes 8388608 | tf_op jit(solution)/shard_map/cdf/pallas_call | solution.py:458
  199.4 5.5 %cdf.16 = (f32[64,64000]{1,0:T(8,128)}, f32[64,128]{1,0:T(8,128)S(1)}) custom-call(f32[64,4096]{1,0:T(8,128)} %copy-done.1, f32[64,4096]{1,0:T(8,128)} %copy-done.2, f32[64,128]{1,0:T(8,128)S(1)} %get-tuple-element.81.refs_2_, f32[64,64000]{1,0:T(8,128)} %get-tuple-element.82.refs_3_), custom_call_target="tpu_custom_call", output_to_operand_aliasing={{0}: (3, {})} | custom-call | flops 402653184 | bytes 4194304 | tf_op jit(solution)/shard_map/cdf/pallas_call | solution.py:458
  205.0 3.6 %cdf.17 = (f32[64,64000]{1,0:T(8,128)}, f32[64,128]{1,0:T(8,128)S(1)}) custom-call(f32[64,2048]{1,0:T(8,128)} %copy-done.4, f32[64,2048]{1,0:T(8,128)} %collective-permute-done.5.refs_1_, f32[64,128]{1,0:T(8,128)S(1)} %get-tuple-element.83.refs_2_, f32[64,64000]{1,0:T(8,128)} %get-tuple-element.84.refs_3_), custom_call_target="tpu_custom_call", output_to_operand_aliasing={{0}: (3, {})} | custom-call | flops 201326592 | bytes 2097152 | tf_op jit(solution)/shard_map/cdf/pallas_call | solution.py:458
  208.6 0.7 copy-done.6
  209.3 2.9 %cdf.18 = (f32[64,64000]{1,0:T(8,128)}, f32[64,128]{1,0:T(8,128)S(1)}) custom-call(f32[64,1280]{1,0:T(8,128)} %copy-done.6, f32[64,1280]{1,0:T(8,128)} %collective-permute-done.3.refs_1_, f32[64,128]{1,0:T(8,128)S(1)} %get-tuple-element.85.refs_2_, f32[64,64000]{1,0:T(8,128)} %get-tuple-element.86.refs_3_), custom_call_target="tpu_custom_call", output_to_operand_aliasing={{0}: (3, {})} | custom-call | flops 125829120 | bytes 1310720 | tf_op jit(solution)/shard_map/cdf/pallas_call | solution.py:458
  212.2 1.0 cdf.19
  (26 shorter events, 0.1 us)
Async XLA Ops:
  100.8 60.7 %collective-permute-start.11 = (f32[64,4096]{1,0:T(8,128)}, f32[64,4096]{1,0:T(8,128)S(1)}, u32[]{:S(2)}, u32[]{:S(2)}) collective-permute-start(f32[64,4096]{1,0:T(8,128)} %get-tuple-element.63), channel_id=1, source_target_pairs={{0,1},{1,0},{2,3},{3,2},{4,5},{5,4},{6,7},{7,6}} | collective-permute-start | bytes 3145736 | tf_op jit(solution)/shard_map/ppermute | solution.py:484
  100.9 87.6 %collective-permute-start.6 = (f32[64,4096]{1,0:T(8,128)}, f32[64,4096]{1,0:T(8,128)S(1)}, u32[]{:S(2)}, u32[]{:S(2)}) collective-permute-start(f32[64,4096]{1,0:T(8,128)} %get-tuple-element.52), channel_id=1, source_target_pairs={{0,2},{1,3},{2,0},{3,1},{4,6},{5,7},{6,4},{7,5}} | collective-permute-start | bytes 3145736 | tf_op jit(solution)/shard_map/ppermute | solution.py:484
  100.9 88.7 %collective-permute-start.7 = (f32[64,4096]{1,0:T(8,128)}, f32[64,4096]{1,0:T(8,128)S(1)}, u32[]{:S(2)}, u32[]{:S(2)}) collective-permute-start(f32[64,4096]{1,0:T(8,128)} %get-tuple-element.53), channel_id=1, source_target_pairs={{0,3},{1,2},{2,1},{3,0},{4,7},{5,6},{6,5},{7,4}} | collective-permute-start | bytes 3145736 | tf_op jit(solution)/shard_map/ppermute | solution.py:484
  102.7 2.9 %collective-permute-start.9 = (f32[64,1280]{1,0:T(8,128)}, f32[64,1280]{1,0:T(8,128)S(1)}, u32[]{:S(2)}, u32[]{:S(2)}) collective-permute-start(f32[64,1280]{1,0:T(8,128)} %get-tuple-element.59), channel_id=1, source_target_pairs={{0,1},{1,0},{2,3},{3,2},{4,5},{5,4},{6,7},{7,6}} | collective-permute-start | bytes 983048 | tf_op jit(solution)/shard_map/ppermute | solution.py:484
  103.1 1.6 collective-permute-start.8
  104.7 0.6 copy-start.8
  105.3 55.0 %collective-permute-start.4 = (f32[64,2048]{1,0:T(8,128)}, f32[64,2048]{1,0:T(8,128)S(1)}, u32[]{:S(2)}, u32[]{:S(2)}) collective-permute-start(f32[64,2048]{1,0:T(8,128)} %get-tuple-element.50), channel_id=1, source_target_pairs={{0,2},{1,3},{2,0},{3,1},{4,6},{5,7},{6,4},{7,5}} | collective-permute-start | bytes 1572872 | tf_op jit(solution)/shard_map/ppermute | solution.py:484
  105.6 0.7 copy-start.7
  106.3 54.0 %collective-permute-start.10 = (f32[64,2048]{1,0:T(8,128)}, f32[64,2048]{1,0:T(8,128)S(1)}, u32[]{:S(2)}, u32[]{:S(2)}) collective-permute-start(f32[64,2048]{1,0:T(8,128)} %get-tuple-element.61), channel_id=1, source_target_pairs={{0,1},{1,0},{2,3},{3,2},{4,5},{5,4},{6,7},{7,6}} | collective-permute-start | bytes 1572872 | tf_op jit(solution)/shard_map/ppermute | solution.py:484
  160.3 1.2 copy-start.4
  160.3 44.6 %collective-permute-start.5 = (f32[64,2048]{1,0:T(8,128)}, f32[64,2048]{1,0:T(8,128)}, u32[]{:S(2)}, u32[]{:S(2)}) collective-permute-start(f32[64,2048]{1,0:T(8,128)} %get-tuple-element.51), channel_id=1, source_target_pairs={{0,3},{1,2},{2,1},{3,0},{4,7},{5,6},{6,5},{7,4}} | collective-permute-start | bytes 1572872 | tf_op jit(solution)/shard_map/ppermute | solution.py:484
  160.3 1.2 copy-start.5
  160.3 48.2 %collective-permute-start.2 = (f32[64,1280]{1,0:T(8,128)}, f32[64,1280]{1,0:T(8,128)S(1)}, u32[]{:S(2)}, u32[]{:S(2)}) collective-permute-start(f32[64,1280]{1,0:T(8,128)} %get-tuple-element.48), channel_id=1, source_target_pairs={{0,2},{1,3},{2,0},{3,1},{4,6},{5,7},{6,4},{7,5}} | collective-permute-start | bytes 983048 | tf_op jit(solution)/shard_map/ppermute | solution.py:484
  161.5 13.0 %copy-start.3 = (f32[64,4096]{1,0:T(8,128)}, f32[64,4096]{1,0:T(8,128)S(1)}, u32[]{:S(2)}) copy-start(f32[64,4096]{1,0:T(8,128)S(1)} %collective-permute-done.11.refs_1_) | copy-start | bytes 3145732
  161.5 47.1 %collective-permute-start.3 = (f32[64,1280]{1,0:T(8,128)}, f32[64,1280]{1,0:T(8,128)}, u32[]{:S(2)}, u32[]{:S(2)}) collective-permute-start(f32[64,1280]{1,0:T(8,128)} %get-tuple-element.49), channel_id=1, source_target_pairs={{0,3},{1,2},{2,1},{3,0},{4,7},{5,6},{6,5},{7,4}} | collective-permute-start | bytes 983048 | tf_op jit(solution)/shard_map/ppermute | solution.py:484
  164.3 0.8 copy-start
  183.6 5.0 %copy-start.10 = (f32[64,384]{1,0:T(8,128)S(1)}, f32[64,384]{1,0:T(8,128)}, u32[]{:S(2)}) copy-start(f32[64,384]{1,0:T(8,128)} %get-tuple-element.46) | copy-start | bytes 294916
  183.6 5.9 %copy-start.9 = (f32[64,384]{1,0:T(8,128)S(1)}, f32[64,384]{1,0:T(8,128)}, u32[]{:S(2)}) copy-start(f32[64,384]{1,0:T(8,128)} %get-tuple-element.47) | copy-start | bytes 294916
  188.6 10.8 %copy-start.1 = (f32[64,4096]{1,0:T(8,128)}, f32[64,4096]{1,0:T(8,128)S(1)}, u32[]{:S(2)}) copy-start(f32[64,4096]{1,0:T(8,128)S(1)} %collective-permute-done.6.refs_0_) | copy-start | bytes 3145732
  188.6 23.6 %collective-permute-start = (f32[64,384]{1,0:T(8,128)S(1)}, f32[64,384]{1,0:T(8,128)S(1)}, u32[]{:S(2)}, u32[]{:S(2)}) collective-permute-start(f32[64,384]{1,0:T(8,128)S(1)} %copy-done.10), channel_id=1, source_target_pairs={{0,2},{1,3},{2,0},{3,1},{4,6},{5,7},{6,4},{7,5}} | collective-permute-start | bytes 294920 | tf_op jit(solution)/shard_map/ppermute | solution.py:484
  189.6 9.8 %copy-start.2 = (f32[64,4096]{1,0:T(8,128)}, f32[64,4096]{1,0:T(8,128)S(1)}, u32[]{:S(2)}) copy-start(f32[64,4096]{1,0:T(8,128)S(1)} %collective-permute-done.7.refs_1_) | copy-start | bytes 3145732
  189.6 22.6 %collective-permute-start.1 = (f32[64,384]{1,0:T(8,128)S(1)}, f32[64,384]{1,0:T(8,128)S(1)}, u32[]{:S(2)}, u32[]{:S(2)}) collective-permute-start(f32[64,384]{1,0:T(8,128)S(1)} %copy-done.9), channel_id=1, source_target_pairs={{0,3},{1,2},{2,1},{3,0},{4,7},{5,6},{6,5},{7,4}} | collective-permute-start | bytes 294920 | tf_op jit(solution)/shard_map/ppermute | solution.py:484
  208.5 0.7 copy-start.6

commit v9 on v8

--- a/solution.py
+++ b/solution.py
@@ -105,10 +105,6 @@
         copy.start()
     for k in range(k_steps):
         fetch_first(k).start()
-    for copy in x_copies[:2]:
-        copy.start()
-    for i in range(SLOTS - 1):
-        fetch_w(0, jnp.int32(i)).start()
     barrier = pltpu.get_barrier_semaphore()
     for p in range(1, n_dev):
         pl.semaphore_signal(
@@ -186,6 +182,13 @@
 
     def far_step(k, _):
         fetch_first(k).wait()
+
+        @pl.when(k == 0)
+        def _():
+            for copy in x_copies[:2]:
+                copy.start()
+
+        fetch_w(0, k).start()
         multiply_first(k, far, batch)
         return 0
 

time: 214 us -> 213 us (level)
  no operation moved by 1% of the time
where the time goes in v9:
time: 213 us; the launch traced here: 212 us
  Pallas kernels  147 us (69%)
  waiting for transfers between devices  55.4 us (26%)
  starting transfers between devices  6.36 us (3%)
  local copies, waits for them, and re-layouts  2.85 us (1%)
    pallas_call x1, Pallas kernels, _logits(): pl.pallas_call(functools.partial(_logits_kernel, (n_dev, shard, segments,...  99.4 us
    ppermute x12, waiting for transfers between devices, swap(): return lax.ppermute(a, 'vp', [(i, i ^ p) for i in range(n_dev)])  55.4 us
    pallas_call x10, Pallas kernels, _cdf(): pl.pallas_call(functools.partial(_cdf_kernel, (peers, shard, base, width,...  46.1 us
    ppermute x12, starting transfers between devices, swap(): return lax.ppermute(a, 'vp', [(i, i ^ p) for i in range(n_dev)])  6.36 us
  transfers between devices with their start and end apart: 12, of which 2 were waited for; matrix products, arithmetic and copies ran while one was open for 0% of the time, Pallas kernels for 22%

profile of v9, /device:TPU:0, one launch (start us, length us, event | category | flops | bytes accessed | tf_op | source)
XLA Modules:
  0.0 212.4 jit_solution(8299939543760771097)
XLA Ops:
  0.6 99.4 %logits.1 = (f32[64,8192]{1,0:T(8,128)}, f32[64,8192]{1,0:T(8,128)}, f32[64,8192]{1,0:T(8,128)}, f32[64,8192]{1,0:T(8,128)}, f32[64,4096]{1,0:T(8,128)}, /*index...) custom-call(bf16[256,4096]{1,0:T(8,128)(2,1)} %x_ref.1, ...), custom_call_target="tpu_custom_call" | custom-call | flops 33554432000 | bytes 131072000 | tf_op jit(solution)/shard_map/logits/pallas_call | solution.py:305
  100.0 0.1 collective-permute-start.11
  100.2 1.7 collective-permute-start.7
  101.9 0.4 collective-permute-start.9
  102.3 0.1 collective-permute-start.8
  102.4 1.5 collective-permute-done.8.refs_1_
  103.9 0.6 copy-done.8
  104.6 0.3 collective-permute-start.4
  104.8 0.0 collective-permute-done.9.refs_1_
  104.8 0.7 copy-done.7
  105.5 0.1 collective-permute-start.10
  105.7 53.9 %collective-permute-done.4.refs_0_ = f32[64,2048]{1,0:T(8,128)S(1)} collective-permute-done((f32[64,2048]{1,0:T(8,128)}, f32[64,2048]{1,0:T(8,128)S(1)}, u32[]{:S(2)}, u32[]{:S(2)}) %collective-permute-start.4) | collective-permute-done | bytes 524320 | tf_op jit(solution)/shard_map/ppermute | solution.py:487
  159.5 0.0 collective-permute-done.10.refs_1_
  159.6 1.2 collective-permute-start.2
  160.7 0.0 collective-permute-done.11.refs_1_
  160.7 1.4 collective-permute-start.3
  162.1 1.5 merge.1
  163.6 0.8 copy-done
  164.3 9.4 %cdf.10 = (f32[64,64000]{1,0:T(8,128)}, f32[64,128]{1,0:T(8,128)S(1)}) custom-call(f32[64,8192]{1,0:T(8,128)} %get-tuple-element.64.refs_0_, f32[64,8192]{1,0:T(8,128)} %get-tuple-element.65.refs_1_, f32[64,128]{1,0:T(8,128)S(1)} %copy-done), custom_call_target="tpu_custom_call" | custom-call | flops 805306368 | bytes 8388608 | tf_op jit(solution)/shard_map/cdf/pallas_call | solution.py:461
  173.8 5.5 %cdf.11 = (f32[64,64000]{1,0:T(8,128)}, f32[64,128]{1,0:T(8,128)S(1)}) custom-call(f32[64,4096]{1,0:T(8,128)} %get-tuple-element.62.refs_0_, f32[64,4096]{1,0:T(8,128)} %copy-done.3, f32[64,128]{1,0:T(8,128)S(1)} %get-tuple-element.71.refs_2_, f32[64,64000]{1,0:T(8,128)} %get-tuple-element.72.refs_3_), custom_call_target="tpu_custom_call", output_to_operand_aliasing={{0}: (3, {})} | custom-call | flops 402653184 | bytes 4194304 | tf_op jit(solution)/shard_map/cdf/pallas_call | solution.py:461
  179.3 3.6 %cdf.12 = (f32[64,64000]{1,0:T(8,128)}, f32[64,128]{1,0:T(8,128)S(1)}) custom-call(f32[64,2048]{1,0:T(8,128)} %get-tuple-element.60.refs_0_, f32[64,2048]{1,0:T(8,128)} %copy-done.5, f32[64,128]{1,0:T(8,128)S(1)} %get-tuple-element.73.refs_2_, f32[64,64000]{1,0:T(8,128)} %get-tuple-element.74.refs_3_), custom_call_target="tpu_custom_call", output_to_operand_aliasing={{0}: (3, {})} | custom-call | flops 201326592 | bytes 2097152 | tf_op jit(solution)/shard_map/cdf/pallas_call | solution.py:461
  182.9 2.9 %cdf.13 = (f32[64,64000]{1,0:T(8,128)}, f32[64,128]{1,0:T(8,128)S(1)}) custom-call(f32[64,1280]{1,0:T(8,128)} %get-tuple-element.58.refs_0_, f32[64,1280]{1,0:T(8,128)} %copy-done.7, f32[64,128]{1,0:T(8,128)S(1)} %get-tuple-element.75.refs_2_, f32[64,64000]{1,0:T(8,128)} %get-tuple-element.76.refs_3_), custom_call_target="tpu_custom_call", output_to_operand_aliasing={{0}: (3, {})} | custom-call | flops 125829120 | bytes 1310720 | tf_op jit(solution)/shard_map/cdf/pallas_call | solution.py:461
  185.8 2.0 cdf.14
  187.8 1.0 collective-permute-start
  188.8 0.1 collective-permute-start.1
  188.9 9.7 %cdf.15 = (f32[64,64000]{1,0:T(8,128)}, f32[64,128]{1,0:T(8,128)S(1)}) custom-call(f32[64,8192]{1,0:T(8,128)} %get-tuple-element.54.refs_0_, f32[64,8192]{1,0:T(8,128)} %get-tuple-element.55.refs_1_, f32[64,128]{1,0:T(8,128)S(1)} %get-tuple-element.79.refs_2_, f32[64,64000]{1,0:T(8,128)} %get-tuple-element.80.refs_3_), custom_call_target="tpu_custom_call", output_to_operand_aliasing={{0}: (3, {})} | custom-call | flops 805306368 | bytes 8388608 | tf_op jit(solution)/shard_map/cdf/pallas_call | solution.py:461
  198.7 5.5 %cdf.16 = (f32[64,64000]{1,0:T(8,128)}, f32[64,128]{1,0:T(8,128)S(1)}) custom-call(f32[64,4096]{1,0:T(8,128)} %copy-done.1, f32[64,4096]{1,0:T(8,128)} %copy-done.2, f32[64,128]{1,0:T(8,128)S(1)} %get-tuple-element.81.refs_2_, f32[64,64000]{1,0:T(8,128)} %get-tuple-element.82.refs_3_), custom_call_target="tpu_custom_call", output_to_operand_aliasing={{0}: (3, {})} | custom-call | flops 402653184 | bytes 4194304 | tf_op jit(solution)/shard_map/cdf/pallas_call | solution.py:461
  204.2 3.6 %cdf.17 = (f32[64,64000]{1,0:T(8,128)}, f32[64,128]{1,0:T(8,128)S(1)}) custom-call(f32[64,2048]{1,0:T(8,128)} %copy-done.4, f32[64,2048]{1,0:T(8,128)} %collective-permute-done.5.refs_1_, f32[64,128]{1,0:T(8,128)S(1)} %get-tuple-element.83.refs_2_, f32[64,64000]{1,0:T(8,128)} %get-tuple-element.84.refs_3_), custom_call_target="tpu_custom_call", output_to_operand_aliasing={{0}: (3, {})} | custom-call | flops 201326592 | bytes 2097152 | tf_op jit(solution)/shard_map/cdf/pallas_call | solution.py:461
  207.8 0.0 collective-permute-done.2.refs_0_
  207.8 0.7 copy-done.6
  208.5 2.9 %cdf.18 = (f32[64,64000]{1,0:T(8,128)}, f32[64,128]{1,0:T(8,128)S(1)}) custom-call(f32[64,1280]{1,0:T(8,128)} %copy-done.6, f32[64,1280]{1,0:T(8,128)} %collective-permute-done.3.refs_1_, f32[64,128]{1,0:T(8,128)S(1)} %get-tuple-element.85.refs_2_, f32[64,64000]{1,0:T(8,128)} %get-tuple-element.86.refs_3_), custom_call_target="tpu_custom_call", output_to_operand_aliasing={{0}: (3, {})} | custom-call | flops 125829120 | bytes 1310720 | tf_op jit(solution)/shard_map/cdf/pallas_call | solution.py:461
  211.4 1.0 cdf.19
  (26 shorter events, 0.1 us)
Async XLA Ops:
  100.0 60.7 %collective-permute-start.11 = (f32[64,4096]{1,0:T(8,128)}, f32[64,4096]{1,0:T(8,128)S(1)}, u32[]{:S(2)}, u32[]{:S(2)}) collective-permute-start(f32[64,4096]{1,0:T(8,128)} %get-tuple-element.63), channel_id=1, source_target_pairs={{0,1},{1,0},{2,3},{3,2},{4,5},{5,4},{6,7},{7,6}} | collective-permute-start | bytes 3145736 | tf_op jit(solution)/shard_map/ppermute | solution.py:487
  100.2 87.6 %collective-permute-start.6 = (f32[64,4096]{1,0:T(8,128)}, f32[64,4096]{1,0:T(8,128)S(1)}, u32[]{:S(2)}, u32[]{:S(2)}) collective-permute-start(f32[64,4096]{1,0:T(8,128)} %get-tuple-element.52), channel_id=1, source_target_pairs={{0,2},{1,3},{2,0},{3,1},{4,6},{5,7},{6,4},{7,5}} | collective-permute-start | bytes 3145736 | tf_op jit(solution)/shard_map/ppermute | solution.py:487
  100.2 88.7 %collective-permute-start.7 = (f32[64,4096]{1,0:T(8,128)}, f32[64,4096]{1,0:T(8,128)S(1)}, u32[]{:S(2)}, u32[]{:S(2)}) collective-permute-start(f32[64,4096]{1,0:T(8,128)} %get-tuple-element.53), channel_id=1, source_target_pairs={{0,3},{1,2},{2,1},{3,0},{4,7},{5,6},{6,5},{7,4}} | collective-permute-start | bytes 3145736 | tf_op jit(solution)/shard_map/ppermute | solution.py:487
  101.9 2.9 %collective-permute-start.9 = (f32[64,1280]{1,0:T(8,128)}, f32[64,1280]{1,0:T(8,128)S(1)}, u32[]{:S(2)}, u32[]{:S(2)}) collective-permute-start(f32[64,1280]{1,0:T(8,128)} %get-tuple-element.59), channel_id=1, source_target_pairs={{0,1},{1,0},{2,3},{3,2},{4,5},{5,4},{6,7},{7,6}} | collective-permute-start | bytes 983048 | tf_op jit(solution)/shard_map/ppermute | solution.py:487
  102.3 1.6 collective-permute-start.8
  103.9 0.6 copy-start.8
  104.6 55.0 %collective-permute-start.4 = (f32[64,2048]{1,0:T(8,128)}, f32[64,2048]{1,0:T(8,128)S(1)}, u32[]{:S(2)}, u32[]{:S(2)}) collective-permute-start(f32[64,2048]{1,0:T(8,128)} %get-tuple-element.50), channel_id=1, source_target_pairs={{0,2},{1,3},{2,0},{3,1},{4,6},{5,7},{6,4},{7,5}} | collective-permute-start | bytes 1572872 | tf_op jit(solution)/shard_map/ppermute | solution.py:487
  104.8 0.7 copy-start.7
  105.5 54.0 %collective-permute-start.10 = (f32[64,2048]{1,0:T(8,128)}, f32[64,2048]{1,0:T(8,128)S(1)}, u32[]{:S(2)}, u32[]{:S(2)}) collective-permute-start(f32[64,2048]{1,0:T(8,128)} %get-tuple-element.61), channel_id=1, source_target_pairs={{0,1},{1,0},{2,3},{3,2},{4,5},{5,4},{6,7},{7,6}} | collective-permute-start | bytes 1572872 | tf_op jit(solution)/shard_map/ppermute | solution.py:487
  159.5 1.2 copy-start.4
  159.5 44.6 %collective-permute-start.5 = (f32[64,2048]{1,0:T(8,128)}, f32[64,2048]{1,0:T(8,128)}, u32[]{:S(2)}, u32[]{:S(2)}) collective-permute-start(f32[64,2048]{1,0:T(8,128)} %get-tuple-element.51), channel_id=1, source_target_pairs={{0,3},{1,2},{2,1},{3,0},{4,7},{5,6},{6,5},{7,4}} | collective-permute-start | bytes 1572872 | tf_op jit(solution)/shard_map/ppermute | solution.py:487
  159.6 1.2 copy-start.5
  159.6 48.2 %collective-permute-start.2 = (f32[64,1280]{1,0:T(8,128)}, f32[64,1280]{1,0:T(8,128)S(1)}, u32[]{:S(2)}, u32[]{:S(2)}) collective-permute-start(f32[64,1280]{1,0:T(8,128)} %get-tuple-element.48), channel_id=1, source_target_pairs={{0,2},{1,3},{2,0},{3,1},{4,6},{5,7},{6,4},{7,5}} | collective-permute-start | bytes 983048 | tf_op jit(solution)/shard_map/ppermute | solution.py:487
  160.7 13.0 %copy-start.3 = (f32[64,4096]{1,0:T(8,128)}, f32[64,4096]{1,0:T(8,128)S(1)}, u32[]{:S(2)}) copy-start(f32[64,4096]{1,0:T(8,128)S(1)} %collective-permute-done.11.refs_1_) | copy-start | bytes 3145732
  160.7 47.1 %collective-permute-start.3 = (f32[64,1280]{1,0:T(8,128)}, f32[64,1280]{1,0:T(8,128)}, u32[]{:S(2)}, u32[]{:S(2)}) collective-permute-start(f32[64,1280]{1,0:T(8,128)} %get-tuple-element.49), channel_id=1, source_target_pairs={{0,3},{1,2},{2,1},{3,0},{4,7},{5,6},{6,5},{7,4}} | collective-permute-start | bytes 983048 | tf_op jit(solution)/shard_map/ppermute | solution.py:487
  163.6 0.8 copy-start
  182.9 5.0 %copy-start.10 = (f32[64,384]{1,0:T(8,128)S(1)}, f32[64,384]{1,0:T(8,128)}, u32[]{:S(2)}) copy-start(f32[64,384]{1,0:T(8,128)} %get-tuple-element.46) | copy-start | bytes 294916
  182.9 5.9 %copy-start.9 = (f32[64,384]{1,0:T(8,128)S(1)}, f32[64,384]{1,0:T(8,128)}, u32[]{:S(2)}) copy-start(f32[64,384]{1,0:T(8,128)} %get-tuple-element.47) | copy-start | bytes 294916
  187.8 10.8 %copy-start.1 = (f32[64,4096]{1,0:T(8,128)}, f32[64,4096]{1,0:T(8,128)S(1)}, u32[]{:S(2)}) copy-start(f32[64,4096]{1,0:T(8,128)S(1)} %collective-permute-done.6.refs_0_) | copy-start | bytes 3145732
  187.8 23.6 %collective-permute-start = (f32[64,384]{1,0:T(8,128)S(1)}, f32[64,384]{1,0:T(8,128)S(1)}, u32[]{:S(2)}, u32[]{:S(2)}) collective-permute-start(f32[64,384]{1,0:T(8,128)S(1)} %copy-done.10), channel_id=1, source_target_pairs={{0,2},{1,3},{2,0},{3,1},{4,6},{5,7},{6,4},{7,5}} | collective-permute-start | bytes 294920 | tf_op jit(solution)/shard_map/ppermute | solution.py:487
  188.8 9.8 %copy-start.2 = (f32[64,4096]{1,0:T(8,128)}, f32[64,4096]{1,0:T(8,128)S(1)}, u32[]{:S(2)}) copy-start(f32[64,4096]{1,0:T(8,128)S(1)} %collective-permute-done.7.refs_1_) | copy-start | bytes 3145732
  188.8 22.6 %collective-permute-start.1 = (f32[64,384]{1,0:T(8,128)S(1)}, f32[64,384]{1,0:T(8,128)S(1)}, u32[]{:S(2)}, u32[]{:S(2)}) collective-permute-start(f32[64,384]{1,0:T(8,128)S(1)} %copy-done.9), channel_id=1, source_target_pairs={{0,3},{1,2},{2,1},{3,0},{4,7},{5,6},{6,5},{7,4}} | collective-permute-start | bytes 294920 | tf_op jit(solution)/shard_map/ppermute | solution.py:487
  207.8 0.7 copy-start.6

commit v10 on v9

--- a/solution.py
+++ b/solution.py
@@ -15,6 +15,7 @@
 SLOTS = 9
 FIRST = 256
 EARLY = ((256, 1), (512, 1), (1024, 1), (2048, 3))
+URGENT = 2
 LATE = (4096, 2048, 1280, 384)
 LATE_UNITS = ((2048, 2), (2048, 1), (1280, 1), (384, 1))
 STATS = 4
@@ -48,7 +49,7 @@
     batch, depth = xs.shape
     rows = batch // n_dev
     k_steps = depth // DEPTH
-    assert SLOTS == k_steps + 1
+    assert SLOTS == k_steps + 1 and all(n == 1 for _, n in EARLY[:URGENT])
 
     def rows_of(p):
         return pl.ds(pl.multiple_of(_peer(me, p) * rows, rows), rows)
@@ -214,6 +215,16 @@
             def body(k, _, seg=seg, i=i, n=n):
                 step = i * k_steps + k
                 ahead = step + SLOTS - 1
+                if seg < URGENT:
+                    fetch_w(seg, step).wait()
+
+                    @pl.when(k == k_steps - 1)
+                    def _():
+                        for later in range(k_steps):
+                            fetch_w(seg + 1, jnp.int32(later)).start()
+
+                    multiply(seg, step)
+                    return 0
 
                 @pl.when(ahead < n * k_steps)
                 def _():

time: 213 us -> 213 us (level)
  no operation moved by 1% of the time
where the time goes in v10:
time: 213 us
  Pallas kernels  148 us (69%)
  waiting for transfers between devices  55.4 us (26%)
  starting transfers between devices  6.37 us (3%)
  local copies, waits for them, and re-layouts  2.85 us (1%)
    pallas_call x1, Pallas kernels, _logits(): pl.pallas_call(functools.partial(_logits_kernel, (n_dev, shard, segments,...  100 us
    ppermute x12, waiting for transfers between devices, swap(): return lax.ppermute(a, 'vp', [(i, i ^ p) for i in range(n_dev)])  55.4 us
    pallas_call x10, Pallas kernels, _cdf(): pl.pallas_call(functools.partial(_cdf_kernel, (peers, shard, base, width,...  46.1 us
    ppermute x12, starting transfers between devices, swap(): return lax.ppermute(a, 'vp', [(i, i ^ p) for i in range(n_dev)])  6.37 us
  transfers between devices with their start and end apart: 12, of which 2 were waited for; matrix products, arithmetic and copies ran while one was open for 0% of the time, Pallas kernels for 22%

profile of v10, /device:TPU:0, one launch (start us, length us, event | category | flops | bytes accessed | tf_op | source)
XLA Modules:
  0.0 213.1 jit_solution(14601043601285844531)
XLA Ops:
  0.6 100.0 %logits.1 = (f32[64,8192]{1,0:T(8,128)}, f32[64,8192]{1,0:T(8,128)}, f32[64,8192]{1,0:T(8,128)}, f32[64,8192]{1,0:T(8,128)}, f32[64,4096]{1,0:T(8,128)}, /*index...) custom-call(bf16[256,4096]{1,0:T(8,128)(2,1)} %x_ref.1, ...), custom_call_target="tpu_custom_call" | custom-call | flops 33554432000 | bytes 131072000 | tf_op jit(solution)/shard_map/logits/pallas_call | solution.py:316
  100.6 0.1 collective-permute-start.11
  100.8 0.0 collective-permute-start.6
  100.8 1.7 collective-permute-start.7
  102.5 0.4 collective-permute-start.9
  102.9 0.1 collective-permute-start.8
  103.0 1.5 collective-permute-done.8.refs_1_
  104.5 0.6 copy-done.8
  105.2 0.3 collective-permute-start.4
  105.4 0.0 collective-permute-done.9.refs_1_
  105.4 0.7 copy-done.7
  106.2 0.1 collective-permute-start.10
  106.3 53.9 %collective-permute-done.4.refs_0_ = f32[64,2048]{1,0:T(8,128)S(1)} collective-permute-done((f32[64,2048]{1,0:T(8,128)}, f32[64,2048]{1,0:T(8,128)S(1)}, u32[]{:S(2)}, u32[]{:S(2)}) %collective-permute-start.4) | collective-permute-done | bytes 524320 | tf_op jit(solution)/shard_map/ppermute | solution.py:498
  160.2 0.0 collective-permute-start.5
  160.2 0.0 collective-permute-done.10.refs_1_
  160.2 1.2 collective-permute-start.2
  161.3 1.4 collective-permute-start.3
  162.7 1.5 merge.1
  164.2 0.8 copy-done
  165.0 9.4 %cdf.10 = (f32[64,64000]{1,0:T(8,128)}, f32[64,128]{1,0:T(8,128)S(1)}) custom-call(f32[64,8192]{1,0:T(8,128)} %get-tuple-element.64.refs_0_, f32[64,8192]{1,0:T(8,128)} %get-tuple-element.65.refs_1_, f32[64,128]{1,0:T(8,128)S(1)} %copy-done), custom_call_target="tpu_custom_call" | custom-call | flops 805306368 | bytes 8388608 | tf_op jit(solution)/shard_map/cdf/pallas_call | solution.py:472
  174.4 5.5 %cdf.11 = (f32[64,64000]{1,0:T(8,128)}, f32[64,128]{1,0:T(8,128)S(1)}) custom-call(f32[64,4096]{1,0:T(8,128)} %get-tuple-element.62.refs_0_, f32[64,4096]{1,0:T(8,128)} %copy-done.3, f32[64,128]{1,0:T(8,128)S(1)} %get-tuple-element.71.refs_2_, f32[64,64000]{1,0:T(8,128)} %get-tuple-element.72.refs_3_), custom_call_target="tpu_custom_call", output_to_operand_aliasing={{0}: (3, {})} | custom-call | flops 402653184 | bytes 4194304 | tf_op jit(solution)/shard_map/cdf/pallas_call | solution.py:472
  179.9 3.6 %cdf.12 = (f32[64,64000]{1,0:T(8,128)}, f32[64,128]{1,0:T(8,128)S(1)}) custom-call(f32[64,2048]{1,0:T(8,128)} %get-tuple-element.60.refs_0_, f32[64,2048]{1,0:T(8,128)} %copy-done.5, f32[64,128]{1,0:T(8,128)S(1)} %get-tuple-element.73.refs_2_, f32[64,64000]{1,0:T(8,128)} %get-tuple-element.74.refs_3_), custom_call_target="tpu_custom_call", output_to_operand_aliasing={{0}: (3, {})} | custom-call | flops 201326592 | bytes 2097152 | tf_op jit(solution)/shard_map/cdf/pallas_call | solution.py:472
  183.5 2.9 %cdf.13 = (f32[64,64000]{1,0:T(8,128)}, f32[64,128]{1,0:T(8,128)S(1)}) custom-call(f32[64,1280]{1,0:T(8,128)} %get-tuple-element.58.refs_0_, f32[64,1280]{1,0:T(8,128)} %copy-done.7, f32[64,128]{1,0:T(8,128)S(1)} %get-tuple-element.75.refs_2_, f32[64,64000]{1,0:T(8,128)} %get-tuple-element.76.refs_3_), custom_call_target="tpu_custom_call", output_to_operand_aliasing={{0}: (3, {})} | custom-call | flops 125829120 | bytes 1310720 | tf_op jit(solution)/shard_map/cdf/pallas_call | solution.py:472
  186.4 2.0 cdf.14
  188.4 1.0 collective-permute-start
  189.4 0.1 collective-permute-start.1
  189.5 9.7 %cdf.15 = (f32[64,64000]{1,0:T(8,128)}, f32[64,128]{1,0:T(8,128)S(1)}) custom-call(f32[64,8192]{1,0:T(8,128)} %get-tuple-element.54.refs_0_, f32[64,8192]{1,0:T(8,128)} %get-tuple-element.55.refs_1_, f32[64,128]{1,0:T(8,128)S(1)} %get-tuple-element.79.refs_2_, f32[64,64000]{1,0:T(8,128)} %get-tuple-element.80.refs_3_), custom_call_target="tpu_custom_call", output_to_operand_aliasing={{0}: (3, {})} | custom-call | flops 805306368 | bytes 8388608 | tf_op jit(solution)/shard_map/cdf/pallas_call | solution.py:472
  199.3 5.5 %cdf.16 = (f32[64,64000]{1,0:T(8,128)}, f32[64,128]{1,0:T(8,128)S(1)}) custom-call(f32[64,4096]{1,0:T(8,128)} %copy-done.1, f32[64,4096]{1,0:T(8,128)} %copy-done.2, f32[64,128]{1,0:T(8,128)S(1)} %get-tuple-element.81.refs_2_, f32[64,64000]{1,0:T(8,128)} %get-tuple-element.82.refs_3_), custom_call_target="tpu_custom_call", output_to_operand_aliasing={{0}: (3, {})} | custom-call | flops 402653184 | bytes 4194304 | tf_op jit(solution)/shard_map/cdf/pallas_call | solution.py:472
  204.8 3.6 %cdf.17 = (f32[64,64000]{1,0:T(8,128)}, f32[64,128]{1,0:T(8,128)S(1)}) custom-call(f32[64,2048]{1,0:T(8,128)} %copy-done.4, f32[64,2048]{1,0:T(8,128)} %collective-permute-done.5.refs_1_, f32[64,128]{1,0:T(8,128)S(1)} %get-tuple-element.83.refs_2_, f32[64,64000]{1,0:T(8,128)} %get-tuple-element.84.refs_3_), custom_call_target="tpu_custom_call", output_to_operand_aliasing={{0}: (3, {})} | custom-call | flops 201326592 | bytes 2097152 | tf_op jit(solution)/shard_map/cdf/pallas_call | solution.py:472
  208.4 0.7 copy-done.6
  209.1 2.9 %cdf.18 = (f32[64,64000]{1,0:T(8,128)}, f32[64,128]{1,0:T(8,128)S(1)}) custom-call(f32[64,1280]{1,0:T(8,128)} %copy-done.6, f32[64,1280]{1,0:T(8,128)} %collective-permute-done.3.refs_1_, f32[64,128]{1,0:T(8,128)S(1)} %get-tuple-element.85.refs_2_, f32[64,64000]{1,0:T(8,128)} %get-tuple-element.86.refs_3_), custom_call_target="tpu_custom_call", output_to_operand_aliasing={{0}: (3, {})} | custom-call | flops 125829120 | bytes 1310720 | tf_op jit(solution)/shard_map/cdf/pallas_call | solution.py:472
  212.0 1.0 cdf.19
  (26 shorter events, 0.1 us)
Async XLA Ops:
  100.6 60.7 %collective-permute-start.11 = (f32[64,4096]{1,0:T(8,128)}, f32[64,4096]{1,0:T(8,128)S(1)}, u32[]{:S(2)}, u32[]{:S(2)}) collective-permute-start(f32[64,4096]{1,0:T(8,128)} %get-tuple-element.63), channel_id=1, source_target_pairs={{0,1},{1,0},{2,3},{3,2},{4,5},{5,4},{6,7},{7,6}} | collective-permute-start | bytes 3145736 | tf_op jit(solution)/shard_map/ppermute | solution.py:498
  100.8 87.6 %collective-permute-start.6 = (f32[64,4096]{1,0:T(8,128)}, f32[64,4096]{1,0:T(8,128)S(1)}, u32[]{:S(2)}, u32[]{:S(2)}) collective-permute-start(f32[64,4096]{1,0:T(8,128)} %get-tuple-element.52), channel_id=1, source_target_pairs={{0,2},{1,3},{2,0},{3,1},{4,6},{5,7},{6,4},{7,5}} | collective-permute-start | bytes 3145736 | tf_op jit(solution)/shard_map/ppermute | solution.py:498
  100.8 88.7 %collective-permute-start.7 = (f32[64,4096]{1,0:T(8,128)}, f32[64,4096]{1,0:T(8,128)S(1)}, u32[]{:S(2)}, u32[]{:S(2)}) collective-permute-start(f32[64,4096]{1,0:T(8,128)} %get-tuple-element.53), channel_id=1, source_target_pairs={{0,3},{1,2},{2,1},{3,0},{4,7},{5,6},{6,5},{7,4}} | collective-permute-start | bytes 3145736 | tf_op jit(solution)/shard_map/ppermute | solution.py:498
  102.5 2.9 %collective-permute-start.9 = (f32[64,1280]{1,0:T(8,128)}, f32[64,1280]{1,0:T(8,128)S(1)}, u32[]{:S(2)}, u32[]{:S(2)}) collective-permute-start(f32[64,1280]{1,0:T(8,128)} %get-tuple-element.59), channel_id=1, source_target_pairs={{0,1},{1,0},{2,3},{3,2},{4,5},{5,4},{6,7},{7,6}} | collective-permute-start | bytes 983048 | tf_op jit(solution)/shard_map/ppermute | solution.py:498
  102.9 1.6 collective-permute-start.8
  104.5 0.6 copy-start.8
  105.2 55.0 %collective-permute-start.4 = (f32[64,2048]{1,0:T(8,128)}, f32[64,2048]{1,0:T(8,128)S(1)}, u32[]{:S(2)}, u32[]{:S(2)}) collective-permute-start(f32[64,2048]{1,0:T(8,128)} %get-tuple-element.50), channel_id=1, source_target_pairs={{0,2},{1,3},{2,0},{3,1},{4,6},{5,7},{6,4},{7,5}} | collective-permute-start | bytes 1572872 | tf_op jit(solution)/shard_map/ppermute | solution.py:498
  105.4 0.7 copy-start.7
  106.2 54.0 %collective-permute-start.10 = (f32[64,2048]{1,0:T(8,128)}, f32[64,2048]{1,0:T(8,128)S(1)}, u32[]{:S(2)}, u32[]{:S(2)}) collective-permute-start(f32[64,2048]{1,0:T(8,128)} %get-tuple-element.61), channel_id=1, source_target_pairs={{0,1},{1,0},{2,3},{3,2},{4,5},{5,4},{6,7},{7,6}} | collective-permute-start | bytes 1572872 | tf_op jit(solution)/shard_map/ppermute | solution.py:498
  160.2 1.2 copy-start.4
  160.2 44.6 %collective-permute-start.5 = (f32[64,2048]{1,0:T(8,128)}, f32[64,2048]{1,0:T(8,128)}, u32[]{:S(2)}, u32[]{:S(2)}) collective-permute-start(f32[64,2048]{1,0:T(8,128)} %get-tuple-element.51), channel_id=1, source_target_pairs={{0,3},{1,2},{2,1},{3,0},{4,7},{5,6},{6,5},{7,4}} | collective-permute-start | bytes 1572872 | tf_op jit(solution)/shard_map/ppermute | solution.py:498
  160.2 1.2 copy-start.5
  160.2 48.2 %collective-permute-start.2 = (f32[64,1280]{1,0:T(8,128)}, f32[64,1280]{1,0:T(8,128)S(1)}, u32[]{:S(2)}, u32[]{:S(2)}) collective-permute-start(f32[64,1280]{1,0:T(8,128)} %get-tuple-element.48), channel_id=1, source_target_pairs={{0,2},{1,3},{2,0},{3,1},{4,6},{5,7},{6,4},{7,5}} | collective-permute-start | bytes 983048 | tf_op jit(solution)/shard_map/ppermute | solution.py:498
  161.3 13.0 %copy-start.3 = (f32[64,4096]{1,0:T(8,128)}, f32[64,4096]{1,0:T(8,128)S(1)}, u32[]{:S(2)}) copy-start(f32[64,4096]{1,0:T(8,128)S(1)} %collective-permute-done.11.refs_1_) | copy-start | bytes 3145732
  161.3 47.1 %collective-permute-start.3 = (f32[64,1280]{1,0:T(8,128)}, f32[64,1280]{1,0:T(8,128)}, u32[]{:S(2)}, u32[]{:S(2)}) collective-permute-start(f32[64,1280]{1,0:T(8,128)} %get-tuple-element.49), channel_id=1, source_target_pairs={{0,3},{1,2},{2,1},{3,0},{4,7},{5,6},{6,5},{7,4}} | collective-permute-start | bytes 983048 | tf_op jit(solution)/shard_map/ppermute | solution.py:498
  164.2 0.8 copy-start
  183.5 5.0 %copy-start.10 = (f32[64,384]{1,0:T(8,128)S(1)}, f32[64,384]{1,0:T(8,128)}, u32[]{:S(2)}) copy-start(f32[64,384]{1,0:T(8,128)} %get-tuple-element.46) | copy-start | bytes 294916
  183.5 6.0 %copy-start.9 = (f32[64,384]{1,0:T(8,128)S(1)}, f32[64,384]{1,0:T(8,128)}, u32[]{:S(2)}) copy-start(f32[64,384]{1,0:T(8,128)} %get-tuple-element.47) | copy-start | bytes 294916
  188.4 10.8 %copy-start.1 = (f32[64,4096]{1,0:T(8,128)}, f32[64,4096]{1,0:T(8,128)S(1)}, u32[]{:S(2)}) copy-start(f32[64,4096]{1,0:T(8,128)S(1)} %collective-permute-done.6.refs_0_) | copy-start | bytes 3145732
  188.4 23.6 %collective-permute-start = (f32[64,384]{1,0:T(8,128)S(1)}, f32[64,384]{1,0:T(8,128)S(1)}, u32[]{:S(2)}, u32[]{:S(2)}) collective-permute-start(f32[64,384]{1,0:T(8,128)S(1)} %copy-done.10), channel_id=1, source_target_pairs={{0,2},{1,3},{2,0},{3,1},{4,6},{5,7},{6,4},{7,5}} | collective-permute-start | bytes 294920 | tf_op jit(solution)/shard_map/ppermute | solution.py:498
  189.4 9.8 %copy-start.2 = (f32[64,4096]{1,0:T(8,128)}, f32[64,4096]{1,0:T(8,128)S(1)}, u32[]{:S(2)}) copy-start(f32[64,4096]{1,0:T(8,128)S(1)} %collective-permute-done.7.refs_1_) | copy-start | bytes 3145732
  189.4 22.6 %collective-permute-start.1 = (f32[64,384]{1,0:T(8,128)S(1)}, f32[64,384]{1,0:T(8,128)S(1)}, u32[]{:S(2)}, u32[]{:S(2)}) collective-permute-start(f32[64,384]{1,0:T(8,128)S(1)} %copy-done.9), channel_id=1, source_target_pairs={{0,3},{1,2},{2,1},{3,0},{4,7},{5,6},{6,5},{7,4}} | collective-permute-start | bytes 294920 | tf_op jit(solution)/shard_map/ppermute | solution.py:498
  208.4 0.7 copy-start.6

commit v11 on v9

--- a/solution.py
+++ b/solution.py
@@ -14,9 +14,9 @@
 DEPTH = 512
 SLOTS = 9
 FIRST = 256
-EARLY = ((256, 1), (512, 1), (1024, 1), (2048, 3))
-LATE = (4096, 2048, 1280, 384)
-LATE_UNITS = ((2048, 2), (2048, 1), (1280, 1), (384, 1))
+EARLY = ((512, 15),)
+LATE = (4096, 2048, 1536, 384)
+LATE_UNITS = ((2048, 2), (2048, 1), (1536, 1), (384, 1))
 STATS = 4
 
 
@@ -208,46 +208,58 @@
     own.append(put_own(0, 0, FIRST))
     own[0].start()
 
+    def run_unit(seg, i):
+        n = segments[seg][1]
+
+        def body(k, _):
+            step = i * k_steps + k
+            ahead = step + SLOTS - 1
+
+            @pl.when(ahead < n * k_steps)
+            def _():
+                fetch_w(seg, ahead).start()
+
+            if seg + 1 < len(segments):
+                @pl.when(ahead >= n * k_steps)
+                def _():
+                    fetch_w(seg + 1, ahead - n * k_steps).start()
+
+            fetch_w(seg, step).wait()
+            multiply(seg, step)
+            return 0
+
+        lax.fori_loop(0, k_steps, body, 0)
+
     for seg, (width, n, chunk, col0, g0) in enumerate(segments):
+        if chunk is None:
+            u0 = len(own)
+
+            def early_unit(i, _, seg=seg, width=width, col0=col0, u0=u0):
+                run_unit(seg, i)
+                col = pl.multiple_of(col0 + i * width, LANES)
+                finish(col, width, zsend, col)
+                for p in (2, 3, 1):
+                    send(u0 + i, p, col, width).start()
+                put_own(u0 + i, col, width).start()
+                return 0
+
+            lax.fori_loop(0, n, early_unit, 0)
+            for i in range(n):
+                sent += [send(u0 + i, p, col0 + i * width, width) for p in (2, 3, 1)]
+                own.append(put_own(u0 + i, col0 + i * width, width))
+            continue
         for i in range(n):
-
-            def body(k, _, seg=seg, i=i, n=n):
-                step = i * k_steps + k
-                ahead = step + SLOTS - 1
-
-                @pl.when(ahead < n * k_steps)
-                def _():
-                    fetch_w(seg, ahead).start()
-
-                if seg + 1 < len(segments):
-                    @pl.when(ahead >= n * k_steps)
-                    def _():
-                        fetch_w(seg + 1, ahead - n * k_steps).start()
-
-                fetch_w(seg, step).wait()
-                multiply(seg, step)
-                return 0
-
-            lax.fori_loop(0, k_steps, body, 0)
-            col = col0 + i * width
-            if chunk is None:
-                finish(col, width, zsend, col)
-                u = len(own)
-                send_early(u, (2, 3, 1), col, width)
-                copy = put_own(u, col, width)
+            run_unit(seg, i)
+            slot = len(stored) % 2
+            if len(stored) >= 2:
+                for copy in stored[-2]:
+                    copy.wait()
+            finish(col0 + i * width, width, zbuf.at[slot], 0)
+            c, off = chunk
+            copies = put_late(slot, c, off + i * width, width)
+            for copy in copies:
                 copy.start()
-                own.append(copy)
-            else:
-                slot = len(stored) % 2
-                if len(stored) >= 2:
-                    for copy in stored[-2]:
-                        copy.wait()
-                finish(col, width, zbuf.at[slot], 0)
-                c, off = chunk
-                copies = put_late(slot, c, off + i * width, width)
-                for copy in copies:
-                    copy.start()
-                stored.append(copies)
+            stored.append(copies)
     m = m_ref[...]
     m_row = jnp.max(m, axis=1, keepdims=True)
     keep = jnp.exp(m - m_row)

time: 213 us -> 212 us (level)
  no operation moved by 1% of the time
where the time goes in v11:
time: 212 us; the launch traced here: 211 us
  Pallas kernels  146 us (69%)
  waiting for transfers between devices  55.2 us (26%)
  starting transfers between devices  6.54 us (3%)
  local copies, waits for them, and re-layouts  2.99 us (1%)
    pallas_call x1, Pallas kernels, _logits(): pl.pallas_call(functools.partial(_logits_kernel, (n_dev, shard, segments,...  98 us
    ppermute x12, waiting for transfers between devices, swap(): return lax.ppermute(a, 'vp', [(i, i ^ p) for i in range(n_dev)])  55.2 us
    pallas_call x10, Pallas kernels, _cdf(): pl.pallas_call(functools.partial(_cdf_kernel, (peers, shard, base, width,...  46.2 us
    ppermute x12, starting transfers between devices, swap(): return lax.ppermute(a, 'vp', [(i, i ^ p) for i in range(n_dev)])  6.54 us
  transfers between devices with their start and end apart: 12, of which 2 were waited for; matrix products, arithmetic and copies ran while one was open for 0% of the time, Pallas kernels for 22%

profile of v11, /device:TPU:0, one launch (start us, length us, event | category | flops | bytes accessed | tf_op | source)
XLA Modules:
  0.0 211.2 jit_solution(3187216614135659281)
XLA Ops:
  0.6 98.0 %logits.1 = (f32[64,7936]{1,0:T(8,128)}, f32[64,7936]{1,0:T(8,128)}, f32[64,7936]{1,0:T(8,128)}, f32[64,7936]{1,0:T(8,128)}, f32[64,4096]{1,0:T(8,128)}, /*index...) custom-call(bf16[256,4096]{1,0:T(8,128)(2,1)} %x_ref.1, ...), custom_call_target="tpu_custom_call" | custom-call | flops 33554432000 | bytes 131072000 | tf_op jit(solution)/shard_map/logits/pallas_call | solution.py:317
  98.6 0.1 collective-permute-start.11
  98.7 0.4 collective-permute-start.9
  99.1 0.0 collective-permute-start.6
  99.1 1.5 collective-permute-start.7
  100.6 0.7 collective-permute-start.8
  101.3 1.2 collective-permute-done.8.refs_1_
  102.4 0.6 copy-done.8
  103.1 0.2 collective-permute-start.4
  103.3 0.8 copy-done.7
  104.1 0.1 collective-permute-start.10
  104.2 54.0 %collective-permute-done.4.refs_0_ = f32[64,2048]{1,0:T(8,128)S(1)} collective-permute-done((f32[64,2048]{1,0:T(8,128)}, f32[64,2048]{1,0:T(8,128)S(1)}, u32[]{:S(2)}, u32[]{:S(2)}) %collective-permute-start.4) | collective-permute-done | bytes 524320 | tf_op jit(solution)/shard_map/ppermute | solution.py:499
  158.2 0.0 collective-permute-start.5
  158.2 0.0 collective-permute-done.10.refs_1_
  158.2 0.9 collective-permute-start.2
  159.1 0.1 copy-done.5
  159.2 1.6 collective-permute-start.3
  160.8 1.5 merge.1
  162.3 0.8 copy-done
  163.0 9.3 %cdf.10 = (f32[64,64000]{1,0:T(8,128)}, f32[64,128]{1,0:T(8,128)S(1)}) custom-call(f32[64,7936]{1,0:T(8,128)} %get-tuple-element.64.refs_0_, f32[64,7936]{1,0:T(8,128)} %get-tuple-element.65.refs_1_, f32[64,128]{1,0:T(8,128)S(1)} %copy-done), custom_call_target="tpu_custom_call" | custom-call | flops 780140544 | bytes 8126464 | tf_op jit(solution)/shard_map/cdf/pallas_call | solution.py:473
  172.3 5.5 %cdf.11 = (f32[64,64000]{1,0:T(8,128)}, f32[64,128]{1,0:T(8,128)S(1)}) custom-call(f32[64,4096]{1,0:T(8,128)} %get-tuple-element.62.refs_0_, f32[64,4096]{1,0:T(8,128)} %copy-done.3, f32[64,128]{1,0:T(8,128)S(1)} %get-tuple-element.71.refs_2_, f32[64,64000]{1,0:T(8,128)} %get-tuple-element.72.refs_3_), custom_call_target="tpu_custom_call", output_to_operand_aliasing={{0}: (3, {})} | custom-call | flops 402653184 | bytes 4194304 | tf_op jit(solution)/shard_map/cdf/pallas_call | solution.py:473
  177.8 3.6 %cdf.12 = (f32[64,64000]{1,0:T(8,128)}, f32[64,128]{1,0:T(8,128)S(1)}) custom-call(f32[64,2048]{1,0:T(8,128)} %get-tuple-element.60.refs_0_, f32[64,2048]{1,0:T(8,128)} %copy-done.5, f32[64,128]{1,0:T(8,128)S(1)} %get-tuple-element.73.refs_2_, f32[64,64000]{1,0:T(8,128)} %get-tuple-element.74.refs_3_), custom_call_target="tpu_custom_call", output_to_operand_aliasing={{0}: (3, {})} | custom-call | flops 201326592 | bytes 2097152 | tf_op jit(solution)/shard_map/cdf/pallas_call | solution.py:473
  181.4 3.1 %cdf.13 = (f32[64,64000]{1,0:T(8,128)}, f32[64,128]{1,0:T(8,128)S(1)}) custom-call(f32[64,1536]{1,0:T(8,128)} %get-tuple-element.58.refs_0_, f32[64,1536]{1,0:T(8,128)} %copy-done.7, f32[64,128]{1,0:T(8,128)S(1)} %get-tuple-element.75.refs_2_, f32[64,64000]{1,0:T(8,128)} %get-tuple-element.76.refs_3_), custom_call_target="tpu_custom_call", output_to_operand_aliasing={{0}: (3, {})} | custom-call | flops 150994944 | bytes 1572864 | tf_op jit(solution)/shard_map/cdf/pallas_call | solution.py:473
  184.5 2.0 cdf.14
  186.5 1.0 collective-permute-start
  187.5 0.1 collective-permute-start.1
  187.6 9.6 %cdf.15 = (f32[64,64000]{1,0:T(8,128)}, f32[64,128]{1,0:T(8,128)S(1)}) custom-call(f32[64,7936]{1,0:T(8,128)} %get-tuple-element.54.refs_0_, f32[64,7936]{1,0:T(8,128)} %get-tuple-element.55.refs_1_, f32[64,128]{1,0:T(8,128)S(1)} %get-tuple-element.79.refs_2_, f32[64,64000]{1,0:T(8,128)} %get-tuple-element.80.refs_3_), custom_call_target="tpu_custom_call", output_to_operand_aliasing={{0}: (3, {})} | custom-call | flops 780140544 | bytes 8126464 | tf_op jit(solution)/shard_map/cdf/pallas_call | solution.py:473
  197.2 5.5 %cdf.16 = (f32[64,64000]{1,0:T(8,128)}, f32[64,128]{1,0:T(8,128)S(1)}) custom-call(f32[64,4096]{1,0:T(8,128)} %copy-done.1, f32[64,4096]{1,0:T(8,128)} %copy-done.2, f32[64,128]{1,0:T(8,128)S(1)} %get-tuple-element.81.refs_2_, f32[64,64000]{1,0:T(8,128)} %get-tuple-element.82.refs_3_), custom_call_target="tpu_custom_call", output_to_operand_aliasing={{0}: (3, {})} | custom-call | flops 402653184 | bytes 4194304 | tf_op jit(solution)/shard_map/cdf/pallas_call | solution.py:473
  202.8 3.6 %cdf.17 = (f32[64,64000]{1,0:T(8,128)}, f32[64,128]{1,0:T(8,128)S(1)}) custom-call(f32[64,2048]{1,0:T(8,128)} %copy-done.4, f32[64,2048]{1,0:T(8,128)} %collective-permute-done.5.refs_1_, f32[64,128]{1,0:T(8,128)S(1)} %get-tuple-element.83.refs_2_, f32[64,64000]{1,0:T(8,128)} %get-tuple-element.84.refs_3_), custom_call_target="tpu_custom_call", output_to_operand_aliasing={{0}: (3, {})} | custom-call | flops 201326592 | bytes 2097152 | tf_op jit(solution)/shard_map/cdf/pallas_call | solution.py:473
  206.4 0.7 copy-done.6
  207.1 3.1 %cdf.18 = (f32[64,64000]{1,0:T(8,128)}, f32[64,128]{1,0:T(8,128)S(1)}) custom-call(f32[64,1536]{1,0:T(8,128)} %copy-done.6, f32[64,1536]{1,0:T(8,128)} %collective-permute-done.3.refs_1_, f32[64,128]{1,0:T(8,128)S(1)} %get-tuple-element.85.refs_2_, f32[64,64000]{1,0:T(8,128)} %get-tuple-element.86.refs_3_), custom_call_target="tpu_custom_call", output_to_operand_aliasing={{0}: (3, {})} | custom-call | flops 150994944 | bytes 1572864 | tf_op jit(solution)/shard_map/cdf/pallas_call | solution.py:473
  210.2 1.0 cdf.19
  (26 shorter events, 0.1 us)
Async XLA Ops:
  98.6 60.5 %collective-permute-start.11 = (f32[64,4096]{1,0:T(8,128)}, f32[64,4096]{1,0:T(8,128)S(1)}, u32[]{:S(2)}, u32[]{:S(2)}) collective-permute-start(f32[64,4096]{1,0:T(8,128)} %get-tuple-element.63), channel_id=1, source_target_pairs={{0,1},{1,0},{2,3},{3,2},{4,5},{5,4},{6,7},{7,6}} | collective-permute-start | bytes 3145736 | tf_op jit(solution)/shard_map/ppermute | solution.py:499
  98.7 4.6 %collective-permute-start.9 = (f32[64,1536]{1,0:T(8,128)}, f32[64,1536]{1,0:T(8,128)S(1)}, u32[]{:S(2)}, u32[]{:S(2)}) collective-permute-start(f32[64,1536]{1,0:T(8,128)} %get-tuple-element.59), channel_id=1, source_target_pairs={{0,1},{1,0},{2,3},{3,2},{4,5},{5,4},{6,7},{7,6}} | collective-permute-start | bytes 1179656 | tf_op jit(solution)/shard_map/ppermute | solution.py:499
  99.1 87.4 %collective-permute-start.6 = (f32[64,4096]{1,0:T(8,128)}, f32[64,4096]{1,0:T(8,128)S(1)}, u32[]{:S(2)}, u32[]{:S(2)}) collective-permute-start(f32[64,4096]{1,0:T(8,128)} %get-tuple-element.52), channel_id=1, source_target_pairs={{0,2},{1,3},{2,0},{3,1},{4,6},{5,7},{6,4},{7,5}} | collective-permute-start | bytes 3145736 | tf_op jit(solution)/shard_map/ppermute | solution.py:499
  99.1 88.4 %collective-permute-start.7 = (f32[64,4096]{1,0:T(8,128)}, f32[64,4096]{1,0:T(8,128)S(1)}, u32[]{:S(2)}, u32[]{:S(2)}) collective-permute-start(f32[64,4096]{1,0:T(8,128)} %get-tuple-element.53), channel_id=1, source_target_pairs={{0,3},{1,2},{2,1},{3,0},{4,7},{5,6},{6,5},{7,4}} | collective-permute-start | bytes 3145736 | tf_op jit(solution)/shard_map/ppermute | solution.py:499
  100.6 1.8 collective-permute-start.8
  102.4 0.6 copy-start.8
  103.1 55.2 %collective-permute-start.4 = (f32[64,2048]{1,0:T(8,128)}, f32[64,2048]{1,0:T(8,128)S(1)}, u32[]{:S(2)}, u32[]{:S(2)}) collective-permute-start(f32[64,2048]{1,0:T(8,128)} %get-tuple-element.50), channel_id=1, source_target_pairs={{0,2},{1,3},{2,0},{3,1},{4,6},{5,7},{6,4},{7,5}} | collective-permute-start | bytes 1572872 | tf_op jit(solution)/shard_map/ppermute | solution.py:499
  103.3 0.8 copy-start.7
  104.1 54.2 %collective-permute-start.10 = (f32[64,2048]{1,0:T(8,128)}, f32[64,2048]{1,0:T(8,128)S(1)}, u32[]{:S(2)}, u32[]{:S(2)}) collective-permute-start(f32[64,2048]{1,0:T(8,128)} %get-tuple-element.61), channel_id=1, source_target_pairs={{0,1},{1,0},{2,3},{3,2},{4,5},{5,4},{6,7},{7,6}} | collective-permute-start | bytes 1572872 | tf_op jit(solution)/shard_map/ppermute | solution.py:499
  158.2 0.9 copy-start.4
  158.2 44.6 %collective-permute-start.5 = (f32[64,2048]{1,0:T(8,128)}, f32[64,2048]{1,0:T(8,128)}, u32[]{:S(2)}, u32[]{:S(2)}) collective-permute-start(f32[64,2048]{1,0:T(8,128)} %get-tuple-element.51), channel_id=1, source_target_pairs={{0,3},{1,2},{2,1},{3,0},{4,7},{5,6},{6,5},{7,4}} | collective-permute-start | bytes 1572872 | tf_op jit(solution)/shard_map/ppermute | solution.py:499
  158.2 1.0 copy-start.5
  158.2 48.1 %collective-permute-start.2 = (f32[64,1536]{1,0:T(8,128)}, f32[64,1536]{1,0:T(8,128)S(1)}, u32[]{:S(2)}, u32[]{:S(2)}) collective-permute-start(f32[64,1536]{1,0:T(8,128)} %get-tuple-element.48), channel_id=1, source_target_pairs={{0,2},{1,3},{2,0},{3,1},{4,6},{5,7},{6,4},{7,5}} | collective-permute-start | bytes 1179656 | tf_op jit(solution)/shard_map/ppermute | solution.py:499
  159.1 13.2 %copy-start.3 = (f32[64,4096]{1,0:T(8,128)}, f32[64,4096]{1,0:T(8,128)S(1)}, u32[]{:S(2)}) copy-start(f32[64,4096]{1,0:T(8,128)S(1)} %collective-permute-done.11.refs_1_) | copy-start | bytes 3145732
  159.2 47.2 %collective-permute-start.3 = (f32[64,1536]{1,0:T(8,128)}, f32[64,1536]{1,0:T(8,128)}, u32[]{:S(2)}, u32[]{:S(2)}) collective-permute-start(f32[64,1536]{1,0:T(8,128)} %get-tuple-element.49), channel_id=1, source_target_pairs={{0,3},{1,2},{2,1},{3,0},{4,7},{5,6},{6,5},{7,4}} | collective-permute-start | bytes 1179656 | tf_op jit(solution)/shard_map/ppermute | solution.py:499
  162.2 0.8 copy-start
  181.4 5.1 %copy-start.10 = (f32[64,384]{1,0:T(8,128)S(1)}, f32[64,384]{1,0:T(8,128)}, u32[]{:S(2)}) copy-start(f32[64,384]{1,0:T(8,128)} %get-tuple-element.46) | copy-start | bytes 294916
  181.4 6.1 %copy-start.9 = (f32[64,384]{1,0:T(8,128)S(1)}, f32[64,384]{1,0:T(8,128)}, u32[]{:S(2)}) copy-start(f32[64,384]{1,0:T(8,128)} %get-tuple-element.47) | copy-start | bytes 294916
  186.5 10.7 %copy-start.1 = (f32[64,4096]{1,0:T(8,128)}, f32[64,4096]{1,0:T(8,128)S(1)}, u32[]{:S(2)}) copy-start(f32[64,4096]{1,0:T(8,128)S(1)} %collective-permute-done.6.refs_0_) | copy-start | bytes 3145732
  186.5 23.6 %collective-permute-start = (f32[64,384]{1,0:T(8,128)S(1)}, f32[64,384]{1,0:T(8,128)S(1)}, u32[]{:S(2)}, u32[]{:S(2)}) collective-permute-start(f32[64,384]{1,0:T(8,128)S(1)} %copy-done.10), channel_id=1, source_target_pairs={{0,2},{1,3},{2,0},{3,1},{4,6},{5,7},{6,4},{7,5}} | collective-permute-start | bytes 294920 | tf_op jit(solution)/shard_map/ppermute | solution.py:499
  187.5 9.7 %copy-start.2 = (f32[64,4096]{1,0:T(8,128)}, f32[64,4096]{1,0:T(8,128)S(1)}, u32[]{:S(2)}) copy-start(f32[64,4096]{1,0:T(8,128)S(1)} %collective-permute-done.7.refs_1_) | copy-start | bytes 3145732
  187.5 22.6 %collective-permute-start.1 = (f32[64,384]{1,0:T(8,128)S(1)}, f32[64,384]{1,0:T(8,128)S(1)}, u32[]{:S(2)}, u32[]{:S(2)}) collective-permute-start(f32[64,384]{1,0:T(8,128)S(1)} %copy-done.9), channel_id=1, source_target_pairs={{0,3},{1,2},{2,1},{3,0},{4,7},{5,6},{6,5},{7,4}} | collective-permute-start | bytes 294920 | tf_op jit(solution)/shard_map/ppermute | solution.py:499
  206.4 0.7 copy-start.6

commit v12 on v9

--- a/solution.py
+++ b/solution.py
@@ -14,9 +14,9 @@
 DEPTH = 512
 SLOTS = 9
 FIRST = 256
-EARLY = ((256, 1), (512, 1), (1024, 1), (2048, 3))
-LATE = (4096, 2048, 1280, 384)
-LATE_UNITS = ((2048, 2), (2048, 1), (1280, 1), (384, 1))
+EARLY = ((256, 1), (512, 1), (1024, 1), (2048, 2))
+LATE = (4096, 2048, 2048, 1280, 384)
+LATE_UNITS = ((2048, 2), (2048, 1), (2048, 1), (1280, 1), (384, 1))
 STATS = 4
 
 
@@ -30,7 +30,7 @@
 
 
 def _logits_kernel(cfg, x_ref, w_ref, invt_ref, tgt_ref, *refs):
-    n_dev, shard, segments, n_late = cfg
+    n_dev, shard, segments, n_early, n_late = cfg
     refs = list(refs)
 
     def take(n):
@@ -38,10 +38,11 @@
         del refs[:n]
         return out
 
-    early = take(n_dev)
+    early = [take(n_dev) for _ in range(n_early)]
     late = [take(n_dev) for _ in range(n_late)]
     packs = take(n_dev)
-    xs, wfirst, wbuf, acc, zsend, zbuf, invt_v, tgt_v, pack_v = take(9)
+    zsend = take(n_early)
+    xs, wfirst, wbuf, acc, zbuf, invt_v, tgt_v, pack_v = take(8)
     scale_rows, left_rows, tmp, m_ref, s_ref, t_ref = take(6)
     first_sem, w_sem, z_sem, x_sem, v_sem, own_sem, send_sem, recv_sem, pack_send, pack_recv = take(10)
     me = lax.axis_index("vp")
@@ -78,15 +79,13 @@
             for p in range(n_dev)
         ]
 
-    def put_own(u, off, width):
-        return pltpu.make_async_copy(
-            zsend.at[pl.ds(0, rows), pl.ds(off, width)], early[0].at[:, pl.ds(off, width)], own_sem.at[u]
-        )
-
-    def send(u, p, off, width):
+    def put_own(u):
+        return pltpu.make_async_copy(zsend[u].at[pl.ds(0, rows), :], early[u][0], own_sem.at[u])
+
+    def send(u, p):
         return pltpu.make_async_remote_copy(
-            src_ref=zsend.at[pl.ds(p * rows, rows), pl.ds(off, width)],
-            dst_ref=early[p].at[:, pl.ds(off, width)],
+            src_ref=zsend[u].at[pl.ds(p * rows, rows), :],
+            dst_ref=early[u][p],
             send_sem=send_sem.at[u, p],
             recv_sem=recv_sem.at[u, p],
             device_id={"vp": _peer(me, p)},
@@ -167,9 +166,9 @@
 
     sent, own, stored = [], [], []
 
-    def send_early(u, peers, col, width):
+    def send_early(u, peers):
         for p in peers:
-            copy = send(u, p, col, width)
+            copy = send(u, p)
             copy.start()
             sent.append(copy)
 
@@ -197,15 +196,15 @@
         return 0
 
     lax.fori_loop(0, k_steps, far_step, 0)
-    finish(0, FIRST, zsend, 0, far, batch)
+    finish(0, FIRST, zsend[0], 0, far, batch)
     pl.semaphore_wait(barrier, n_dev - 1)
-    send_early(0, (2, 3), 0, FIRST)
+    send_early(0, (2, 3))
     for copy in x_copies[:2]:
         copy.wait()
     lax.fori_loop(0, k_steps, near_step, 0)
-    finish(0, FIRST, zsend, 0, 0, far)
-    send_early(0, (1,), 0, FIRST)
-    own.append(put_own(0, 0, FIRST))
+    finish(0, FIRST, zsend[0], 0, 0, far)
+    send_early(0, (1,))
+    own.append(put_own(0))
     own[0].start()
 
     for seg, (width, n, chunk, col0, g0) in enumerate(segments):
@@ -231,10 +230,10 @@
             lax.fori_loop(0, k_steps, body, 0)
             col = col0 + i * width
             if chunk is None:
-                finish(col, width, zsend, col)
                 u = len(own)
-                send_early(u, (2, 3, 1), col, width)
-                copy = put_own(u, col, width)
+                finish(col, width, zsend[u], 0)
+                send_early(u, (2, 3, 1))
+                copy = put_own(u)
                 copy.start()
                 own.append(copy)
             else:
@@ -285,7 +284,8 @@
     rows = batch // n_dev
     segments, col, g0 = [], FIRST, 0
     chunk_of = {}
-    sent = begin = FIRST + sum(width * n for width, n in EARLY)
+    units = [FIRST] + [width for width, n in EARLY for _ in range(n)]
+    n_early, begin = len(units), sum(units)
     for c, width in enumerate(LATE):
         chunk_of.update({begin + i: (c, i) for i in range(0, width, LANES)})
         begin += width
@@ -294,25 +294,22 @@
         col += width * n
         g0 += n * (depth // DEPTH)
     assert col == shard == begin
-    n_early = 1 + sum(n for _, n in EARLY)
     hbm = pl.BlockSpec(memory_space=pltpu.HBM)
-    out_shape = [pltpu.HBM((rows, sent), jnp.float32)] * n_dev
-    out_shape += [pltpu.HBM((rows, width), jnp.float32) for width in LATE for _ in range(n_dev)]
+    out_shape = [pltpu.HBM((rows, width), jnp.float32) for width in [*units, *LATE] for _ in range(n_dev)]
     out_shape += [pltpu.HBM((STATS, batch), jnp.float32)] * n_dev
     table = pltpu.VMEM((batch, LANES), jnp.float32)
     widest = max(width for width, _ in EARLY + LATE_UNITS)
     dma = pltpu.SemaphoreType.DMA
     res = pl.pallas_call(
-        functools.partial(_logits_kernel, (n_dev, shard, segments, len(LATE))),
+        functools.partial(_logits_kernel, (n_dev, shard, segments, n_early, len(LATE))),
         in_specs=[hbm] * 4,
         out_specs=[hbm] * len(out_shape),
         out_shape=out_shape,
-        scratch_shapes=[
+        scratch_shapes=[pltpu.VMEM((batch, width), jnp.float32) for width in units] + [
             pltpu.VMEM((batch, depth), jnp.bfloat16),
             pltpu.VMEM((depth, FIRST), jnp.bfloat16),
             pltpu.VMEM((SLOTS, DEPTH, widest), jnp.bfloat16),
             pltpu.VMEM((batch, widest), jnp.float32),
-            pltpu.VMEM((batch, sent), jnp.float32),
             pltpu.VMEM((2, batch, widest), jnp.float32),
             pltpu.VMEM((1, batch), jnp.float32),
             pltpu.VMEM((1, batch), jnp.int32),
@@ -344,8 +341,8 @@
         ),
         name="logits",
     )(*(pltpu.with_memory_space_constraint(a, pltpu.HBM) for a in (x, w, invt, tgt)))
-    blocks = [res[c * n_dev:(c + 1) * n_dev] for c in range(len(LATE) + 2)]
-    return blocks[0], blocks[1:-1], blocks[-1]
+    blocks = [res[c * n_dev:(c + 1) * n_dev] for c in range(n_early + len(LATE) + 1)]
+    return blocks[:n_early], blocks[n_early:-1], blocks[-1]
 
 
 def _merge_kernel(n_dev, *refs):
@@ -395,13 +392,15 @@
 
 
 def _cdf_kernel(cfg, *refs):
-    peers, shard, base, width, first, last = cfg
+    peers, shard, base, widths, first, last = cfg
     n = len(peers)
-    params_ref = refs[n]
+    width = sum(widths)
+    parts, refs = [refs[a * n:(a + 1) * n] for a in range(len(widths))], refs[len(widths) * n:]
+    params_ref = refs[0]
     if last:
-        out_ref, y_ref, sems = refs[n + 2:]
+        out_ref, y_ref, sems = refs[2:]
     else:
-        out_ref, params_out, y_ref, sems = refs[n + (1 if first else 2):]
+        out_ref, params_out, y_ref, sems = refs[1 if first else 2:]
     me = lax.axis_index("vp")
     rows = params_ref.shape[0]
     params = params_ref[...]
@@ -412,32 +411,35 @@
     tri = jnp.where(k_id <= n_id, 1.0, 0.0).astype(jnp.bfloat16)
     lane = lax.broadcasted_iota(jnp.int32, (rows, LANES), 1)
 
-    def unit(col, wide, carries):
+    def unit(part, at, col, wide, carries):
         ends = []
         for j in range(n):
             cols = [pl.ds(col + t, LANES) for t in range(0, wide, LANES)]
-            e = jnp.concatenate([jnp.exp(refs[j][:, c] - top) for c in cols], axis=0)
+            e = jnp.concatenate([jnp.exp(part[j][:, c] - top) for c in cols], axis=0)
             hi = e.astype(jnp.bfloat16)
             r1 = e - hi.astype(jnp.float32)
             mid = r1.astype(jnp.bfloat16)
             lo = (r1 - mid.astype(jnp.float32)).astype(jnp.bfloat16)
             sums = jnp.dot(jnp.concatenate([hi, mid, lo], axis=1), tri, preferred_element_type=jnp.float32)
             carry = carries[j]
-            for t, c in enumerate(cols):
+            for t in range(len(cols)):
                 block = slice(t * rows, (t + 1) * rows)
-                y_ref[j, :, c] = (sums[block, :LANES] + carry) * inv
+                y_ref[j, :, pl.ds(at + col + t * LANES, LANES)] = (sums[block, :LANES] + carry) * inv
                 carry = carry + sums[block, LANES:]
             ends.append(carry)
         return tuple(ends)
 
     carries = tuple(jnp.broadcast_to(params[:, 2 + p:3 + p], (rows, LANES)) for p in peers)
-    n_full = width // UNIT
-    if n_full:
-        carries = lax.fori_loop(
-            0, n_full, lambda u, c: unit(pl.multiple_of(u * UNIT, UNIT), UNIT, c), carries
-        )
-    if width % UNIT:
-        carries = unit(n_full * UNIT, width % UNIT, carries)
+    at = 0
+    for part, wide in zip(parts, widths):
+        n_full = wide // UNIT
+        if n_full:
+            carries = lax.fori_loop(
+                0, n_full, lambda u, c, part=part, at=at: unit(part, at, pl.multiple_of(u * UNIT, UNIT), UNIT, c), carries
+            )
+        if wide % UNIT:
+            carries = unit(part, at, n_full * UNIT, wide % UNIT, carries)
+        at += wide
     copies = []
     updated = params
     for j, p in enumerate(peers):
@@ -453,14 +455,16 @@
 
 
 def _cdf(blocks, peers, params, out, n_dev, shard, base, last=False):
-    rows, width = blocks[0].shape
     n = len(peers)
+    rows = blocks[0].shape[0]
+    widths = tuple(b.shape[1] for b in blocks[::n])
+    width = sum(widths)
     first = out is None
     vmem = pl.BlockSpec(memory_space=pltpu.VMEM)
     hbm = pl.BlockSpec(memory_space=pl.ANY)
     return pl.pallas_call(
-        functools.partial(_cdf_kernel, (peers, shard, base, width, first, last)),
-        in_specs=[vmem] * (n + 1) + ([] if first else [hbm]),
+        functools.partial(_cdf_kernel, (peers, shard, base, widths, first, last)),
+        in_specs=[vmem] * (len(blocks) + 1) + ([] if first else [hbm]),
         out_specs=[hbm] + ([] if last else [vmem]),
         out_shape=[jax.ShapeDtypeStruct((rows, n_dev * shard), jnp.float32)]
         + ([] if last else [jax.ShapeDtypeStruct(params.shape, jnp.float32)]),
@@ -468,7 +472,7 @@
             pltpu.VMEM((n, rows, width), jnp.float32),
             pltpu.SemaphoreType.DMA((n,)),
         ],
-        input_output_aliases={} if first else {n + 1: 0},
+        input_output_aliases={} if first else {len(blocks) + 1: 0},
         compiler_params=pltpu.CompilerParams(vmem_limit_bytes=24 * 2**20),
         cost_estimate=pl.CostEstimate(
             flops=n * 2 * rows * width * 384,
@@ -492,12 +496,12 @@
             hidden, w_local, inv_temp.reshape(1, -1), target_ids.reshape(1, -1), n_dev
         )
         chunks = [(0, early)]
-        begin = early[0].shape[1]
+        begin = sum(made[0].shape[1] for made in early)
         for made in late:
             got = [made[0]]
             for p in range(1, n_dev):
                 got.append(swap(made[p], p))
-            chunks.append((begin, got))
+            chunks.append((begin, [got]))
             begin += made[0].shape[1]
         params, at_target = _merge(packs)
         out = None
@@ -505,7 +509,7 @@
         plan = [(k, peers) for peers in ((0, 1), (2, 3)) for k in range(final + 1)]
         for i, (k, peers) in enumerate(plan):
             begin, got = chunks[k]
-            blocks = [got[p] for p in peers]
+            blocks = [made[p] for made in got for p in peers]
             if k < final or peers[0] == 0:
                 blocks = [pltpu.with_memory_space_constraint(a, pltpu.HBM) for a in blocks]
             res = _cdf(blocks, peers, params, out, n_dev, shard, begin, i == len(plan) - 1)

time: 213 us -> 189 us (0.89)
  Pallas kernels: 147 us -> 127 us
  waiting for transfers between devices: 55.4 us -> 51 us
    pallas_call x1, Pallas kernels: 99.4 us -> 76.9 us  [_logits(): pl.pallas_call(functools.partial(_logits_kernel, (n_dev, shard, segments,...]
    ppermute x12 -> x15, waiting for transfers between devices: 55.4 us -> 51 us  [swap(): return lax.ppermute(a, 'vp', [(i, i ^ p) for i in range(n_dev)])]
    pallas_call x10 -> x12, Pallas kernels: 46.1 us -> 48.5 us  [_cdf(): pl.pallas_call(functools.partial(_cdf_kernel, (peers, shard, base, widths...]
    ppermute x12 -> x15, starting transfers between devices: 6.36 us -> 8.46 us  [swap(): return lax.ppermute(a, 'vp', [(i, i ^ p) for i in range(n_dev)])]
  transfers between devices with their start and end apart: 12 -> 15, of which waited for: 2 -> 9; matrix products, arithmetic and copies ran while one was open for 0% -> 0% of each run, Pallas kernels for 22% -> 26%
where the time goes in v12:
time: 189 us
  Pallas kernels  127 us (67%)
  waiting for transfers between devices  51 us (27%)
  starting transfers between devices  8.46 us (4%)
    pallas_call x1, Pallas kernels, _logits(): pl.pallas_call(functools.partial(_logits_kernel, (n_dev, shard, segments,...  76.9 us
    ppermute x15, waiting for transfers between devices, swap(): return lax.ppermute(a, 'vp', [(i, i ^ p) for i in range(n_dev)])  51 us
    pallas_call x12, Pallas kernels, _cdf(): pl.pallas_call(functools.partial(_cdf_kernel, (peers, shard, base, widths...  48.5 us
    ppermute x15, starting transfers between devices, swap(): return lax.ppermute(a, 'vp', [(i, i ^ p) for i in range(n_dev)])  8.46 us
  transfers between devices with their start and end apart: 15, of which 9 were waited for; matrix products, arithmetic and copies ran while one was open for 0% of the time, Pallas kernels for 26%

profile of v12, /device:TPU:0, one launch (start us, length us, event | category | flops | bytes accessed | tf_op | source)
XLA Modules:
  0.0 188.7 jit_solution(6533869152425516544)
XLA Ops:
  0.6 76.9 %logits.1 = (f32[64,256]{1,0:T(8,128)}, f32[64,256]{1,0:T(8,128)}, f32[64,256]{1,0:T(8,128)}, f32[64,256]{1,0:T(8,128)}, f32[64,256]{1,0:T(8,128)}, /*index=5*/f...) custom-call(bf16[256,4096]{1,0:T(8,128)(2,1)} %x_ref.1, ...), custom_call_target="tpu_custom_call" | custom-call | flops 33554432000 | bytes 131072000 | tf_op jit(solution)/shard_map/logits/pallas_call | solution.py:303
  77.5 2.0 %collective-permute-start.6 = (f32[64,2048]{1,0:T(8,128)}, f32[64,2048]{1,0:T(8,128)S(1)}, u32[]{:S(2)}, u32[]{:S(2)}) collective-permute-start(f32[64,2048]{1,0:T(8,128)} %get-tuple-element.80), channel_id=1, source_target_pairs={{0,2},{1,3},{2,0},{3,1},{4,6},{5,7},{6,4},{7,5}} | collective-permute-start | bytes 1572872 | tf_op jit(solution)/shard_map/ppermute | solution.py:491
  79.6 0.5 collective-permute-start.10
  80.1 1.5 collective-permute-done.10.refs_1_
  81.7 0.5 collective-permute-start.8
  82.2 10.3 %collective-permute-done.4.refs_0_ = f32[64,2048]{1,0:T(8,128)S(1)} collective-permute-done((f32[64,2048]{1,0:T(8,128)}, f32[64,2048]{1,0:T(8,128)S(1)}, u32[]{:S(2)}, u32[]{:S(2)}) %collective-permute-start.4) | collective-permute-done | bytes 524320 | tf_op jit(solution)/shard_map/ppermute | solution.py:491
  92.5 0.8 copy-done.4
  93.3 10.4 %collective-permute-done.6.refs_0_ = f32[64,2048]{1,0:T(8,128)S(1)} collective-permute-done((f32[64,2048]{1,0:T(8,128)}, f32[64,2048]{1,0:T(8,128)S(1)}, u32[]{:S(2)}, u32[]{:S(2)}) %collective-permute-start.6) | collective-permute-done | bytes 524320 | tf_op jit(solution)/shard_map/ppermute | solution.py:491
  103.8 9.5 %collective-permute-done.7.refs_1_ = f32[64,2048]{1,0:T(8,128)S(1)} collective-permute-done((f32[64,2048]{1,0:T(8,128)}, f32[64,2048]{1,0:T(8,128)S(1)}, u32[]{:S(2)}, u32[]{:S(2)}) %collective-permute-start.7) | collective-permute-done | bytes 524320 | tf_op jit(solution)/shard_map/ppermute | solution.py:491
  113.3 1.5 collective-permute-start.13
  114.8 1.7 collective-permute-done.13.refs_1_
  116.8 1.5 collective-permute-start.3
  118.3 1.5 merge.1
  119.8 0.8 copy-done
  120.6 7.2 %cdf.12 = (f32[64,64000]{1,0:T(8,128)}, f32[64,128]{1,0:T(8,128)S(1)}) custom-call(f32[64,256]{1,0:T(8,128)} %get-tuple-element.106.refs_0_, f32[64,256]{1,0:T(8,128)} %get-tuple-element.107.refs_1_, f32[64,256]{1,0:T(8,128)} %get-tuple-element.108.refs_2_, f32[64,256]{1,0:T(8,128)} %get-tuple-element.109.refs_3_, f32[64,512]{1,0:T(8,128)} %get-tuple-element.110.refs_4_, ...), custom_call_target="tpu_custom_call" | custom-call | flops 603979776 | bytes 6291456 | tf_op jit(solution)/shard_map/cdf/pallas_call | solution.py:465
  127.8 5.5 %cdf.13 = (f32[64,64000]{1,0:T(8,128)}, f32[64,128]{1,0:T(8,128)S(1)}) custom-call(f32[64,4096]{1,0:T(8,128)} %get-tuple-element.104.refs_0_, f32[64,4096]{1,0:T(8,128)} %copy-done.3, f32[64,128]{1,0:T(8,128)S(1)} %get-tuple-element.123.refs_2_, f32[64,64000]{1,0:T(8,128)} %get-tuple-element.124.refs_3_), custom_call_target="tpu_custom_call", output_to_operand_aliasing={{0}: (3, {})} | custom-call | flops 402653184 | bytes 4194304 | tf_op jit(solution)/shard_map/cdf/pallas_call | solution.py:465
  133.3 3.6 %cdf.14 = (f32[64,64000]{1,0:T(8,128)}, f32[64,128]{1,0:T(8,128)S(1)}) custom-call(f32[64,2048]{1,0:T(8,128)} %get-tuple-element.102.refs_0_, f32[64,2048]{1,0:T(8,128)} %copy-done.8, f32[64,128]{1,0:T(8,128)S(1)} %get-tuple-element.125.refs_2_, f32[64,64000]{1,0:T(8,128)} %get-tuple-element.126.refs_3_), custom_call_target="tpu_custom_call", output_to_operand_aliasing={{0}: (3, {})} | custom-call | flops 201326592 | bytes 2097152 | tf_op jit(solution)/shard_map/cdf/pallas_call | solution.py:465
  136.9 3.6 %cdf.15 = (f32[64,64000]{1,0:T(8,128)}, f32[64,128]{1,0:T(8,128)S(1)}) custom-call(f32[64,2048]{1,0:T(8,128)} %get-tuple-element.100.refs_0_, f32[64,2048]{1,0:T(8,128)} %copy-done.7, f32[64,128]{1,0:T(8,128)S(1)} %get-tuple-element.127.refs_2_, f32[64,64000]{1,0:T(8,128)} %get-tuple-element.128.refs_3_), custom_call_target="tpu_custom_call", output_to_operand_aliasing={{0}: (3, {})} | custom-call | flops 201326592 | bytes 2097152 | tf_op jit(solution)/shard_map/cdf/pallas_call | solution.py:465
  140.5 2.9 %cdf.16 = (f32[64,64000]{1,0:T(8,128)}, f32[64,128]{1,0:T(8,128)S(1)}) custom-call(f32[64,1280]{1,0:T(8,128)} %get-tuple-element.98.refs_0_, f32[64,1280]{1,0:T(8,128)} %copy-done.10, f32[64,128]{1,0:T(8,128)S(1)} %get-tuple-element.129.refs_2_, f32[64,64000]{1,0:T(8,128)} %get-tuple-element.130.refs_3_), custom_call_target="tpu_custom_call", output_to_operand_aliasing={{0}: (3, {})} | custom-call | flops 125829120 | bytes 1310720 | tf_op jit(solution)/shard_map/cdf/pallas_call | solution.py:465
  143.4 2.0 %cdf.17 = (f32[64,64000]{1,0:T(8,128)}, f32[64,128]{1,0:T(8,128)S(1)}) custom-call(f32[64,384]{1,0:T(8,128)} %get-tuple-element.96.refs_0_, f32[64,384]{1,0:T(8,128)} %copy-done.11, f32[64,128]{1,0:T(8,128)S(1)} %get-tuple-element.131.refs_2_, f32[64,64000]{1,0:T(8,128)} %get-tuple-element.132.refs_3_), custom_call_target="tpu_custom_call", output_to_operand_aliasing={{0}: (3, {})} | custom-call | flops 37748736 | bytes 393216 | tf_op jit(solution)/shard_map/cdf/pallas_call | solution.py:465
  145.4 0.4 collective-permute-start
  145.8 12.4 %collective-permute-done.9.refs_1_ = f32[64,4096]{1,0:T(8,128)S(1)} collective-permute-done((f32[64,4096]{1,0:T(8,128)}, f32[64,4096]{1,0:T(8,128)S(1)}, u32[]{:S(2)}, u32[]{:S(2)}) %collective-permute-start.9) | collective-permute-done | bytes 1048608 | tf_op jit(solution)/shard_map/ppermute | solution.py:491
  158.2 1.5 collective-permute-start.1
  159.8 7.2 %cdf.18 = (f32[64,64000]{1,0:T(8,128)}, f32[64,128]{1,0:T(8,128)S(1)}) custom-call(f32[64,256]{1,0:T(8,128)} %get-tuple-element.84.refs_0_, f32[64,256]{1,0:T(8,128)} %get-tuple-element.85.refs_1_, f32[64,256]{1,0:T(8,128)} %get-tuple-element.86.refs_2_, f32[64,256]{1,0:T(8,128)} %get-tuple-element.87.refs_3_, ...), custom_call_target="tpu_custom_call", output_to_operand_aliasing={{0}: (13, {})} | custom-call | flops 603979776 | bytes 6291456 | tf_op jit(solution)/shard_map/cdf/pallas_call | solution.py:465
  167.0 5.5 %cdf.19 = (f32[64,64000]{1,0:T(8,128)}, f32[64,128]{1,0:T(8,128)S(1)}) custom-call(f32[64,4096]{1,0:T(8,128)} %copy-done.1, f32[64,4096]{1,0:T(8,128)} %copy-done.2, f32[64,128]{1,0:T(8,128)S(1)} %get-tuple-element.135.refs_2_, f32[64,64000]{1,0:T(8,128)} %get-tuple-element.136.refs_3_), custom_call_target="tpu_custom_call", output_to_operand_aliasing={{0}: (3, {})} | custom-call | flops 402653184 | bytes 4194304 | tf_op jit(solution)/shard_map/cdf/pallas_call | solution.py:465
  172.6 3.6 %cdf.20 = (f32[64,64000]{1,0:T(8,128)}, f32[64,128]{1,0:T(8,128)S(1)}) custom-call(f32[64,2048]{1,0:T(8,128)} %copy-done.5, f32[64,2048]{1,0:T(8,128)} %copy-done.6, f32[64,128]{1,0:T(8,128)S(1)} %get-tuple-element.137.refs_2_, f32[64,64000]{1,0:T(8,128)} %get-tuple-element.138.refs_3_), custom_call_target="tpu_custom_call", output_to_operand_aliasing={{0}: (3, {})} | custom-call | flops 201326592 | bytes 2097152 | tf_op jit(solution)/shard_map/cdf/pallas_call | solution.py:465
  176.1 3.6 %cdf.21 = (f32[64,64000]{1,0:T(8,128)}, f32[64,128]{1,0:T(8,128)S(1)}) custom-call(f32[64,2048]{1,0:T(8,128)} %copy-done.4, f32[64,2048]{1,0:T(8,128)} %collective-permute-done.5.refs_1_, f32[64,128]{1,0:T(8,128)S(1)} %get-tuple-element.139.refs_2_, f32[64,64000]{1,0:T(8,128)} %get-tuple-element.140.refs_3_), custom_call_target="tpu_custom_call", output_to_operand_aliasing={{0}: (3, {})} | custom-call | flops 201326592 | bytes 2097152 | tf_op jit(solution)/shard_map/cdf/pallas_call | solution.py:465
  179.7 3.9 %collective-permute-done.3.refs_1_ = f32[64,1280]{1,0:T(8,128)} collective-permute-done((f32[64,1280]{1,0:T(8,128)}, f32[64,1280]{1,0:T(8,128)}, u32[]{:S(2)}, u32[]{:S(2)}) %collective-permute-start.3) | collective-permute-done | bytes 327712 | tf_op jit(solution)/shard_map/ppermute | solution.py:491
  183.6 2.9 %cdf.22 = (f32[64,64000]{1,0:T(8,128)}, f32[64,128]{1,0:T(8,128)S(1)}) custom-call(f32[64,1280]{1,0:T(8,128)} %copy-done.9, f32[64,1280]{1,0:T(8,128)} %collective-permute-done.3.refs_1_, f32[64,128]{1,0:T(8,128)S(1)} %get-tuple-element.141.refs_2_, f32[64,64000]{1,0:T(8,128)} %get-tuple-element.142.refs_3_), custom_call_target="tpu_custom_call", output_to_operand_aliasing={{0}: (3, {})} | custom-call | flops 125829120 | bytes 1310720 | tf_op jit(solution)/shard_map/cdf/pallas_call | solution.py:465
  186.5 0.8 collective-permute-done.refs_0_
  187.3 0.4 collective-permute-done.1.refs_1_
  187.7 1.0 cdf.23
  (40 shorter events, 0.4 us)
Async XLA Ops:
  77.5 15.0 %collective-permute-start.4 = (f32[64,2048]{1,0:T(8,128)}, f32[64,2048]{1,0:T(8,128)S(1)}, u32[]{:S(2)}, u32[]{:S(2)}) collective-permute-start(f32[64,2048]{1,0:T(8,128)} %get-tuple-element.78), channel_id=1, source_target_pairs={{0,2},{1,3},{2,0},{3,1},{4,6},{5,7},{6,4},{7,5}} | collective-permute-start | bytes 1572872 | tf_op jit(solution)/shard_map/ppermute | solution.py:491
  77.5 26.2 %collective-permute-start.6 = (f32[64,2048]{1,0:T(8,128)}, f32[64,2048]{1,0:T(8,128)S(1)}, u32[]{:S(2)}, u32[]{:S(2)}) collective-permute-start(f32[64,2048]{1,0:T(8,128)} %get-tuple-element.80), channel_id=1, source_target_pairs={{0,2},{1,3},{2,0},{3,1},{4,6},{5,7},{6,4},{7,5}} | collective-permute-start | bytes 1572872 | tf_op jit(solution)/shard_map/ppermute | solution.py:491
  79.6 2.1 %collective-permute-start.11 = (f32[64,1280]{1,0:T(8,128)}, f32[64,1280]{1,0:T(8,128)S(1)}, u32[]{:S(2)}, u32[]{:S(2)}) collective-permute-start(f32[64,1280]{1,0:T(8,128)} %get-tuple-element.99), channel_id=1, source_target_pairs={{0,1},{1,0},{2,3},{3,2},{4,5},{5,4},{6,7},{7,6}} | collective-permute-start | bytes 983048 | tf_op jit(solution)/shard_map/ppermute | solution.py:491
  79.6 2.0 %collective-permute-start.10 = (f32[64,384]{1,0:T(8,128)}, f32[64,384]{1,0:T(8,128)S(1)}, u32[]{:S(2)}, u32[]{:S(2)}) collective-permute-start(f32[64,384]{1,0:T(8,128)} %get-tuple-element.97), channel_id=1, source_target_pairs={{0,1},{1,0},{2,3},{3,2},{4,5},{5,4},{6,7},{7,6}} | collective-permute-start | bytes 294920 | tf_op jit(solution)/shard_map/ppermute | solution.py:491
  80.1 33.2 %collective-permute-start.7 = (f32[64,2048]{1,0:T(8,128)}, f32[64,2048]{1,0:T(8,128)S(1)}, u32[]{:S(2)}, u32[]{:S(2)}) collective-permute-start(f32[64,2048]{1,0:T(8,128)} %get-tuple-element.81), channel_id=1, source_target_pairs={{0,3},{1,2},{2,1},{3,0},{4,7},{5,6},{6,5},{7,4}} | collective-permute-start | bytes 1572872 | tf_op jit(solution)/shard_map/ppermute | solution.py:491
  81.5 22.2 %copy-start.11 = (f32[64,384]{1,0:T(8,128)}, f32[64,384]{1,0:T(8,128)S(1)}, u32[]{:S(2)}) copy-start(f32[64,384]{1,0:T(8,128)S(1)} %collective-permute-done.10.refs_1_) | copy-start | bytes 294916
  81.5 35.2 %collective-permute-start.14 = (f32[64,4096]{1,0:T(8,128)}, f32[64,4096]{1,0:T(8,128)S(1)}, u32[]{:S(2)}, u32[]{:S(2)}) collective-permute-start(f32[64,4096]{1,0:T(8,128)} %get-tuple-element.105), channel_id=1, source_target_pairs={{0,1},{1,0},{2,3},{3,2},{4,5},{5,4},{6,7},{7,6}} | collective-permute-start | bytes 3145736 | tf_op jit(solution)/shard_map/ppermute | solution.py:491
  81.7 10.9 %copy-start.10 = (f32[64,1280]{1,0:T(8,128)}, f32[64,1280]{1,0:T(8,128)S(1)}, u32[]{:S(2)}) copy-start(f32[64,1280]{1,0:T(8,128)S(1)} %collective-permute-done.11.refs_1_) | copy-start | bytes 983044
  81.7 63.7 %collective-permute-start.8 = (f32[64,4096]{1,0:T(8,128)}, f32[64,4096]{1,0:T(8,128)S(1)}, u32[]{:S(2)}, u32[]{:S(2)}) collective-permute-start(f32[64,4096]{1,0:T(8,128)} %get-tuple-element.82), channel_id=1, source_target_pairs={{0,2},{1,3},{2,0},{3,1},{4,6},{5,7},{6,4},{7,5}} | collective-permute-start | bytes 3145736 | tf_op jit(solution)/shard_map/ppermute | solution.py:491
  92.5 0.8 copy-start.4
  93.3 64.9 %collective-permute-start.9 = (f32[64,4096]{1,0:T(8,128)}, f32[64,4096]{1,0:T(8,128)S(1)}, u32[]{:S(2)}, u32[]{:S(2)}) collective-permute-start(f32[64,4096]{1,0:T(8,128)} %get-tuple-element.83), channel_id=1, source_target_pairs={{0,3},{1,2},{2,1},{3,0},{4,7},{5,6},{6,5},{7,4}} | collective-permute-start | bytes 3145736 | tf_op jit(solution)/shard_map/ppermute | solution.py:491
  103.8 13.0 %copy-start.5 = (f32[64,2048]{1,0:T(8,128)}, f32[64,2048]{1,0:T(8,128)S(1)}, u32[]{:S(2)}) copy-start(f32[64,2048]{1,0:T(8,128)S(1)} %collective-permute-done.6.refs_0_) | copy-start | bytes 1572868
  103.8 11.1 %collective-permute-start.12 = (f32[64,2048]{1,0:T(8,128)}, f32[64,2048]{1,0:T(8,128)S(1)}, u32[]{:S(2)}, u32[]{:S(2)}) collective-permute-start(f32[64,2048]{1,0:T(8,128)} %get-tuple-element.101), channel_id=1, source_target_pairs={{0,1},{1,0},{2,3},{3,2},{4,5},{5,4},{6,7},{7,6}} | collective-permute-start | bytes 1572872 | tf_op jit(solution)/shard_map/ppermute | solution.py:491
  113.3 3.5 %copy-start.6 = (f32[64,2048]{1,0:T(8,128)}, f32[64,2048]{1,0:T(8,128)S(1)}, u32[]{:S(2)}) copy-start(f32[64,2048]{1,0:T(8,128)S(1)} %collective-permute-done.7.refs_1_) | copy-start | bytes 1572868
  113.3 3.3 %collective-permute-start.13 = (f32[64,2048]{1,0:T(8,128)}, f32[64,2048]{1,0:T(8,128)S(1)}, u32[]{:S(2)}, u32[]{:S(2)}) collective-permute-start(f32[64,2048]{1,0:T(8,128)} %get-tuple-element.103), channel_id=1, source_target_pairs={{0,1},{1,0},{2,3},{3,2},{4,5},{5,4},{6,7},{7,6}} | collective-permute-start | bytes 1572872 | tf_op jit(solution)/shard_map/ppermute | solution.py:491
  114.8 3.5 %copy-start.7 = (f32[64,2048]{1,0:T(8,128)}, f32[64,2048]{1,0:T(8,128)S(1)}, u32[]{:S(2)}) copy-start(f32[64,2048]{1,0:T(8,128)S(1)} %collective-permute-done.12.refs_1_) | copy-start | bytes 1572868
  114.8 61.3 %collective-permute-start.5 = (f32[64,2048]{1,0:T(8,128)}, f32[64,2048]{1,0:T(8,128)}, u32[]{:S(2)}, u32[]{:S(2)}) collective-permute-start(f32[64,2048]{1,0:T(8,128)} %get-tuple-element.79), channel_id=1, source_target_pairs={{0,3},{1,2},{2,1},{3,0},{4,7},{5,6},{6,5},{7,4}} | collective-permute-start | bytes 1572872 | tf_op jit(solution)/shard_map/ppermute | solution.py:491
  116.6 1.8 copy-start.8
  116.6 63.1 %collective-permute-start.2 = (f32[64,1280]{1,0:T(8,128)}, f32[64,1280]{1,0:T(8,128)S(1)}, u32[]{:S(2)}, u32[]{:S(2)}) collective-permute-start(f32[64,1280]{1,0:T(8,128)} %get-tuple-element.76), channel_id=1, source_target_pairs={{0,2},{1,3},{2,0},{3,1},{4,6},{5,7},{6,4},{7,5}} | collective-permute-start | bytes 983048 | tf_op jit(solution)/shard_map/ppermute | solution.py:491
  116.8 11.0 %copy-start.3 = (f32[64,4096]{1,0:T(8,128)}, f32[64,4096]{1,0:T(8,128)S(1)}, u32[]{:S(2)}) copy-start(f32[64,4096]{1,0:T(8,128)S(1)} %collective-permute-done.14.refs_1_) | copy-start | bytes 3145732
  116.8 66.8 %collective-permute-start.3 = (f32[64,1280]{1,0:T(8,128)}, f32[64,1280]{1,0:T(8,128)}, u32[]{:S(2)}, u32[]{:S(2)}) collective-permute-start(f32[64,1280]{1,0:T(8,128)} %get-tuple-element.77), channel_id=1, source_target_pairs={{0,3},{1,2},{2,1},{3,0},{4,7},{5,6},{6,5},{7,4}} | collective-permute-start | bytes 983048 | tf_op jit(solution)/shard_map/ppermute | solution.py:491
  119.8 0.8 copy-start
  140.5 5.0 %copy-start.13 = (f32[64,384]{1,0:T(8,128)S(1)}, f32[64,384]{1,0:T(8,128)}, u32[]{:S(2)}) copy-start(f32[64,384]{1,0:T(8,128)} %get-tuple-element.74) | copy-start | bytes 294916
  140.5 17.8 %copy-start.12 = (f32[64,384]{1,0:T(8,128)S(1)}, f32[64,384]{1,0:T(8,128)}, u32[]{:S(2)}) copy-start(f32[64,384]{1,0:T(8,128)} %get-tuple-element.75) | copy-start | bytes 294916
  145.4 21.6 %copy-start.1 = (f32[64,4096]{1,0:T(8,128)}, f32[64,4096]{1,0:T(8,128)S(1)}, u32[]{:S(2)}) copy-start(f32[64,4096]{1,0:T(8,128)S(1)} %collective-permute-done.8.refs_0_) | copy-start | bytes 3145732
  145.4 41.9 %collective-permute-start = (f32[64,384]{1,0:T(8,128)S(1)}, f32[64,384]{1,0:T(8,128)S(1)}, u32[]{:S(2)}, u32[]{:S(2)}) collective-permute-start(f32[64,384]{1,0:T(8,128)S(1)} %copy-done.13), channel_id=1, source_target_pairs={{0,2},{1,3},{2,0},{3,1},{4,6},{5,7},{6,4},{7,5}} | collective-permute-start | bytes 294920 | tf_op jit(solution)/shard_map/ppermute | solution.py:491
  158.2 8.8 %copy-start.2 = (f32[64,4096]{1,0:T(8,128)}, f32[64,4096]{1,0:T(8,128)S(1)}, u32[]{:S(2)}) copy-start(f32[64,4096]{1,0:T(8,128)S(1)} %collective-permute-done.9.refs_1_) | copy-start | bytes 3145732
  158.2 29.5 %collective-permute-start.1 = (f32[64,384]{1,0:T(8,128)S(1)}, f32[64,384]{1,0:T(8,128)S(1)}, u32[]{:S(2)}, u32[]{:S(2)}) collective-permute-start(f32[64,384]{1,0:T(8,128)S(1)} %copy-done.12), channel_id=1, source_target_pairs={{0,3},{1,2},{2,1},{3,0},{4,7},{5,6},{6,5},{7,4}} | collective-permute-start | bytes 294920 | tf_op jit(solution)/shard_map/ppermute | solution.py:491
  179.7 3.9 %copy-start.9 = (f32[64,1280]{1,0:T(8,128)}, f32[64,1280]{1,0:T(8,128)S(1)}, u32[]{:S(2)}) copy-start(f32[64,1280]{1,0:T(8,128)S(1)} %collective-permute-done.2.refs_0_) | copy-start | bytes 983044

commit v13 on v12

--- a/solution.py
+++ b/solution.py
@@ -201,12 +201,16 @@
     send_early(0, (2, 3))
     for copy in x_copies[:2]:
         copy.wait()
-    lax.fori_loop(0, k_steps, near_step, 0)
-    finish(0, FIRST, zsend[0], 0, 0, far)
-    send_early(0, (1,))
-    own.append(put_own(0))
-    own[0].start()
-
+
+    def first_near():
+        lax.fori_loop(0, k_steps, near_step, 0)
+        finish(0, FIRST, zsend[0], 0, 0, far)
+        send_early(0, (1,))
+        copy = put_own(0)
+        copy.start()
+        own.append(copy)
+
+    early_units = 1
     for seg, (width, n, chunk, col0, g0) in enumerate(segments):
         for i in range(n):
 
@@ -230,12 +234,15 @@
             lax.fori_loop(0, k_steps, body, 0)
             col = col0 + i * width
             if chunk is None:
-                u = len(own)
+                u = early_units
+                early_units += 1
                 finish(col, width, zsend[u], 0)
                 send_early(u, (2, 3, 1))
                 copy = put_own(u)
                 copy.start()
                 own.append(copy)
+                if u == 2:
+                    first_near()
             else:
                 slot = len(stored) % 2
                 if len(stored) >= 2:
@@ -506,7 +513,8 @@
         params, at_target = _merge(packs)
         out = None
         final = len(chunks) - 1
-        plan = [(k, peers) for peers in ((0, 1), (2, 3)) for k in range(final + 1)]
+        plan = [(k, (0, 1)) for k in range(final + 1)] + [(k, (2, 3)) for k in range(final - 1)]
+        plan += [(k, (p,)) for p in (2, 3) for k in (final - 1, final)]
         for i, (k, peers) in enumerate(plan):
             begin, got = chunks[k]
             blocks = [made[p] for made in got for p in peers]

time: 189 us -> 193 us (1.021)
  Pallas kernels: 127 us -> 129 us
    pallas_call x12 -> x14, Pallas kernels: 48.5 us -> 51.3 us  [_cdf(): pl.pallas_call(functools.partial(_cdf_kernel, (peers, shard, base, widths...]
  transfers between devices with their start and end apart: 15 -> 15, of which waited for: 9 -> 7; matrix products, arithmetic and copies ran while one was open for 0% -> 0% of each run, Pallas kernels for 26% -> 27%
where the time goes in v13:
time: 193 us
  Pallas kernels  129 us (67%)
  waiting for transfers between devices  52.6 us (27%)
  starting transfers between devices  8.17 us (4%)
  local copies, waits for them, and re-layouts  2.32 us (1%)
    pallas_call x1, Pallas kernels, _logits(): pl.pallas_call(functools.partial(_logits_kernel, (n_dev, shard, segments,...  76 us
    ppermute x15, waiting for transfers between devices, swap(): return lax.ppermute(a, 'vp', [(i, i ^ p) for i in range(n_dev)])  52.6 us
    pallas_call x14, Pallas kernels, _cdf(): pl.pallas_call(functools.partial(_cdf_kernel, (peers, shard, base, widths...  51.3 us
    ppermute x15, starting transfers between devices, swap(): return lax.ppermute(a, 'vp', [(i, i ^ p) for i in range(n_dev)])  8.17 us
  transfers between devices with their start and end apart: 15, of which 7 were waited for; matrix products, arithmetic and copies ran while one was open for 0% of the time, Pallas kernels for 27%

profile of v13, /device:TPU:0, one launch (start us, length us, event | category | flops | bytes accessed | tf_op | source)
XLA Modules:
  0.0 192.7 jit_solution(4252710399054563508)
XLA Ops:
  0.6 76.0 %logits.1 = (f32[64,256]{1,0:T(8,128)}, f32[64,256]{1,0:T(8,128)}, f32[64,256]{1,0:T(8,128)}, f32[64,256]{1,0:T(8,128)}, f32[64,256]{1,0:T(8,128)}, /*index=5*/f...) custom-call(bf16[256,4096]{1,0:T(8,128)(2,1)} %x_ref.1, ...), custom_call_target="tpu_custom_call" | custom-call | flops 33554432000 | bytes 131072000 | tf_op jit(solution)/shard_map/logits/pallas_call | solution.py:310
  76.6 2.0 %collective-permute-start.6 = (f32[64,2048]{1,0:T(8,128)}, f32[64,2048]{1,0:T(8,128)S(1)}, u32[]{:S(2)}, u32[]{:S(2)}) collective-permute-start(f32[64,2048]{1,0:T(8,128)} %get-tuple-element.84), channel_id=1, source_target_pairs={{0,2},{1,3},{2,0},{3,1},{4,6},{5,7},{6,4},{7,5}} | collective-permute-start | bytes 1572872 | tf_op jit(solution)/shard_map/ppermute | solution.py:498
  78.6 0.5 collective-permute-start.10
  79.2 1.5 collective-permute-done.10.refs_1_
  80.8 0.5 collective-permute-start.8
  81.3 10.3 %collective-permute-done.4.refs_0_ = f32[64,2048]{1,0:T(8,128)S(1)} collective-permute-done((f32[64,2048]{1,0:T(8,128)}, f32[64,2048]{1,0:T(8,128)S(1)}, u32[]{:S(2)}, u32[]{:S(2)}) %collective-permute-start.4) | collective-permute-done | bytes 524320 | tf_op jit(solution)/shard_map/ppermute | solution.py:498
  91.6 0.8 copy-done.4
  92.4 10.4 %collective-permute-done.6.refs_0_ = f32[64,2048]{1,0:T(8,128)S(1)} collective-permute-done((f32[64,2048]{1,0:T(8,128)}, f32[64,2048]{1,0:T(8,128)S(1)}, u32[]{:S(2)}, u32[]{:S(2)}) %collective-permute-start.6) | collective-permute-done | bytes 524320 | tf_op jit(solution)/shard_map/ppermute | solution.py:498
  102.9 9.5 %collective-permute-done.7.refs_1_ = f32[64,2048]{1,0:T(8,128)S(1)} collective-permute-done((f32[64,2048]{1,0:T(8,128)}, f32[64,2048]{1,0:T(8,128)S(1)}, u32[]{:S(2)}, u32[]{:S(2)}) %collective-permute-start.7) | collective-permute-done | bytes 524320 | tf_op jit(solution)/shard_map/ppermute | solution.py:498
  112.4 1.5 collective-permute-start.13
  113.9 1.7 collective-permute-done.13.refs_1_
  115.9 1.5 collective-permute-start.1
  117.4 1.5 merge.1
  118.9 0.8 copy-done
  119.7 7.2 %cdf.14 = (f32[64,64000]{1,0:T(8,128)}, f32[64,128]{1,0:T(8,128)S(1)}) custom-call(f32[64,256]{1,0:T(8,128)} %get-tuple-element.110.refs_0_, f32[64,256]{1,0:T(8,128)} %get-tuple-element.111.refs_1_, f32[64,256]{1,0:T(8,128)} %get-tuple-element.112.refs_2_, f32[64,256]{1,0:T(8,128)} %get-tuple-element.113.refs_3_, f32[64,512]{1,0:T(8,128)} %get-tuple-element.114.refs_4_, ...), custom_call_target="tpu_custom_call" | custom-call | flops 603979776 | bytes 6291456 | tf_op jit(solution)/shard_map/cdf/pallas_call | solution.py:472
  126.9 5.5 %cdf.15 = (f32[64,64000]{1,0:T(8,128)}, f32[64,128]{1,0:T(8,128)S(1)}) custom-call(f32[64,4096]{1,0:T(8,128)} %get-tuple-element.108.refs_0_, f32[64,4096]{1,0:T(8,128)} %copy-done.3, f32[64,128]{1,0:T(8,128)S(1)} %get-tuple-element.127.refs_2_, f32[64,64000]{1,0:T(8,128)} %get-tuple-element.128.refs_3_), custom_call_target="tpu_custom_call", output_to_operand_aliasing={{0}: (3, {})} | custom-call | flops 402653184 | bytes 4194304 | tf_op jit(solution)/shard_map/cdf/pallas_call | solution.py:472
  132.4 3.6 %cdf.16 = (f32[64,64000]{1,0:T(8,128)}, f32[64,128]{1,0:T(8,128)S(1)}) custom-call(f32[64,2048]{1,0:T(8,128)} %get-tuple-element.106.refs_0_, f32[64,2048]{1,0:T(8,128)} %copy-done.8, f32[64,128]{1,0:T(8,128)S(1)} %get-tuple-element.129.refs_2_, f32[64,64000]{1,0:T(8,128)} %get-tuple-element.130.refs_3_), custom_call_target="tpu_custom_call", output_to_operand_aliasing={{0}: (3, {})} | custom-call | flops 201326592 | bytes 2097152 | tf_op jit(solution)/shard_map/cdf/pallas_call | solution.py:472
  136.0 3.6 %cdf.17 = (f32[64,64000]{1,0:T(8,128)}, f32[64,128]{1,0:T(8,128)S(1)}) custom-call(f32[64,2048]{1,0:T(8,128)} %get-tuple-element.104.refs_0_, f32[64,2048]{1,0:T(8,128)} %copy-done.7, f32[64,128]{1,0:T(8,128)S(1)} %get-tuple-element.131.refs_2_, f32[64,64000]{1,0:T(8,128)} %get-tuple-element.132.refs_3_), custom_call_target="tpu_custom_call", output_to_operand_aliasing={{0}: (3, {})} | custom-call | flops 201326592 | bytes 2097152 | tf_op jit(solution)/shard_map/cdf/pallas_call | solution.py:472
  139.6 2.9 %cdf.18 = (f32[64,64000]{1,0:T(8,128)}, f32[64,128]{1,0:T(8,128)S(1)}) custom-call(f32[64,1280]{1,0:T(8,128)} %get-tuple-element.102.refs_0_, f32[64,1280]{1,0:T(8,128)} %copy-done.10, f32[64,128]{1,0:T(8,128)S(1)} %get-tuple-element.133.refs_2_, f32[64,64000]{1,0:T(8,128)} %get-tuple-element.134.refs_3_), custom_call_target="tpu_custom_call", output_to_operand_aliasing={{0}: (3, {})} | custom-call | flops 125829120 | bytes 1310720 | tf_op jit(solution)/shard_map/cdf/pallas_call | solution.py:472
  142.5 2.0 %cdf.19 = (f32[64,64000]{1,0:T(8,128)}, f32[64,128]{1,0:T(8,128)S(1)}) custom-call(f32[64,384]{1,0:T(8,128)} %get-tuple-element.100.refs_0_, f32[64,384]{1,0:T(8,128)} %copy-done.11, f32[64,128]{1,0:T(8,128)S(1)} %get-tuple-element.135.refs_2_, f32[64,64000]{1,0:T(8,128)} %get-tuple-element.136.refs_3_), custom_call_target="tpu_custom_call", output_to_operand_aliasing={{0}: (3, {})} | custom-call | flops 37748736 | bytes 393216 | tf_op jit(solution)/shard_map/cdf/pallas_call | solution.py:472
  144.8 12.5 %collective-permute-done.9.refs_1_ = f32[64,4096]{1,0:T(8,128)S(1)} collective-permute-done((f32[64,4096]{1,0:T(8,128)}, f32[64,4096]{1,0:T(8,128)S(1)}, u32[]{:S(2)}, u32[]{:S(2)}) %collective-permute-start.9) | collective-permute-done | bytes 1048608 | tf_op jit(solution)/shard_map/ppermute | solution.py:498
  157.3 1.4 collective-permute-start.2
  158.7 7.2 %cdf.20 = (f32[64,64000]{1,0:T(8,128)}, f32[64,128]{1,0:T(8,128)S(1)}) custom-call(f32[64,256]{1,0:T(8,128)} %get-tuple-element.88.refs_0_, f32[64,256]{1,0:T(8,128)} %get-tuple-element.89.refs_1_, f32[64,256]{1,0:T(8,128)} %get-tuple-element.90.refs_2_, f32[64,256]{1,0:T(8,128)} %get-tuple-element.91.refs_3_, ...), custom_call_target="tpu_custom_call", output_to_operand_aliasing={{0}: (13, {})} | custom-call | flops 603979776 | bytes 6291456 | tf_op jit(solution)/shard_map/cdf/pallas_call | solution.py:472
  165.9 5.5 %cdf.21 = (f32[64,64000]{1,0:T(8,128)}, f32[64,128]{1,0:T(8,128)S(1)}) custom-call(f32[64,4096]{1,0:T(8,128)} %copy-done.1, f32[64,4096]{1,0:T(8,128)} %copy-done.2, f32[64,128]{1,0:T(8,128)S(1)} %get-tuple-element.139.refs_2_, f32[64,64000]{1,0:T(8,128)} %get-tuple-element.140.refs_3_), custom_call_target="tpu_custom_call", output_to_operand_aliasing={{0}: (3, {})} | custom-call | flops 402653184 | bytes 4194304 | tf_op jit(solution)/shard_map/cdf/pallas_call | solution.py:472
  171.5 3.6 %cdf.22 = (f32[64,64000]{1,0:T(8,128)}, f32[64,128]{1,0:T(8,128)S(1)}) custom-call(f32[64,2048]{1,0:T(8,128)} %copy-done.5, f32[64,2048]{1,0:T(8,128)} %copy-done.6, f32[64,128]{1,0:T(8,128)S(1)} %get-tuple-element.141.refs_2_, f32[64,64000]{1,0:T(8,128)} %get-tuple-element.142.refs_3_), custom_call_target="tpu_custom_call", output_to_operand_aliasing={{0}: (3, {})} | custom-call | flops 201326592 | bytes 2097152 | tf_op jit(solution)/shard_map/cdf/pallas_call | solution.py:472
  175.0 3.6 %cdf.23 = (f32[64,64000]{1,0:T(8,128)}, f32[64,128]{1,0:T(8,128)S(1)}) custom-call(f32[64,2048]{1,0:T(8,128)} %copy-done.4, f32[64,2048]{1,0:T(8,128)} %collective-permute-done.5.refs_1_, f32[64,128]{1,0:T(8,128)S(1)} %get-tuple-element.143.refs_2_, f32[64,64000]{1,0:T(8,128)} %get-tuple-element.144.refs_3_), custom_call_target="tpu_custom_call", output_to_operand_aliasing={{0}: (3, {})} | custom-call | flops 201326592 | bytes 2097152 | tf_op jit(solution)/shard_map/cdf/pallas_call | solution.py:472
  178.6 2.5 %cdf.24 = (f32[64,64000]{1,0:T(8,128)}, f32[64,128]{1,0:T(8,128)S(1)}) custom-call(f32[64,1280]{1,0:T(8,128)} %collective-permute-done.3.refs_0_, f32[64,128]{1,0:T(8,128)S(1)} %get-tuple-element.145.refs_1_, f32[64,64000]{1,0:T(8,128)} %get-tuple-element.146.refs_2_), custom_call_target="tpu_custom_call", output_to_operand_aliasing={{0}: (2, {})} | custom-call | flops 62914560 | bytes 655360 | tf_op jit(solution)/shard_map/cdf/pallas_call | solution.py:472
  181.1 6.6 %collective-permute-done.2.refs_0_ = f32[64,384]{1,0:T(8,128)S(1)} collective-permute-done((f32[64,384]{1,0:T(8,128)S(1)}, f32[64,384]{1,0:T(8,128)S(1)}, u32[]{:S(2)}, u32[]{:S(2)}) %collective-permute-start.2) | collective-permute-done | bytes 98336 | tf_op jit(solution)/shard_map/ppermute | solution.py:498
  187.7 0.9 cdf.25
  188.6 0.7 copy-done.9
  189.4 2.4 %cdf.26 = (f32[64,64000]{1,0:T(8,128)}, f32[64,128]{1,0:T(8,128)S(1)}) custom-call(f32[64,1280]{1,0:T(8,128)} %copy-done.9, f32[64,128]{1,0:T(8,128)S(1)} %get-tuple-element.149.refs_1_, f32[64,64000]{1,0:T(8,128)} %get-tuple-element.150.refs_2_), custom_call_target="tpu_custom_call", output_to_operand_aliasing={{0}: (2, {})} | custom-call | flops 62914560 | bytes 655360 | tf_op jit(solution)/shard_map/cdf/pallas_call | solution.py:472
  191.8 0.9 cdf.27
  (42 shorter events, 0.7 us)
Async XLA Ops:
  76.6 15.0 %collective-permute-start.4 = (f32[64,2048]{1,0:T(8,128)}, f32[64,2048]{1,0:T(8,128)S(1)}, u32[]{:S(2)}, u32[]{:S(2)}) collective-permute-start(f32[64,2048]{1,0:T(8,128)} %get-tuple-element.82), channel_id=1, source_target_pairs={{0,2},{1,3},{2,0},{3,1},{4,6},{5,7},{6,4},{7,5}} | collective-permute-start | bytes 1572872 | tf_op jit(solution)/shard_map/ppermute | solution.py:498
  76.6 26.2 %collective-permute-start.6 = (f32[64,2048]{1,0:T(8,128)}, f32[64,2048]{1,0:T(8,128)S(1)}, u32[]{:S(2)}, u32[]{:S(2)}) collective-permute-start(f32[64,2048]{1,0:T(8,128)} %get-tuple-element.84), channel_id=1, source_target_pairs={{0,2},{1,3},{2,0},{3,1},{4,6},{5,7},{6,4},{7,5}} | collective-permute-start | bytes 1572872 | tf_op jit(solution)/shard_map/ppermute | solution.py:498
  78.6 2.1 %collective-permute-start.11 = (f32[64,1280]{1,0:T(8,128)}, f32[64,1280]{1,0:T(8,128)S(1)}, u32[]{:S(2)}, u32[]{:S(2)}) collective-permute-start(f32[64,1280]{1,0:T(8,128)} %get-tuple-element.103), channel_id=1, source_target_pairs={{0,1},{1,0},{2,3},{3,2},{4,5},{5,4},{6,7},{7,6}} | collective-permute-start | bytes 983048 | tf_op jit(solution)/shard_map/ppermute | solution.py:498
  78.6 2.0 %collective-permute-start.10 = (f32[64,384]{1,0:T(8,128)}, f32[64,384]{1,0:T(8,128)S(1)}, u32[]{:S(2)}, u32[]{:S(2)}) collective-permute-start(f32[64,384]{1,0:T(8,128)} %get-tuple-element.101), channel_id=1, source_target_pairs={{0,1},{1,0},{2,3},{3,2},{4,5},{5,4},{6,7},{7,6}} | collective-permute-start | bytes 294920 | tf_op jit(solution)/shard_map/ppermute | solution.py:498
  79.2 33.2 %collective-permute-start.7 = (f32[64,2048]{1,0:T(8,128)}, f32[64,2048]{1,0:T(8,128)S(1)}, u32[]{:S(2)}, u32[]{:S(2)}) collective-permute-start(f32[64,2048]{1,0:T(8,128)} %get-tuple-element.85), channel_id=1, source_target_pairs={{0,3},{1,2},{2,1},{3,0},{4,7},{5,6},{6,5},{7,4}} | collective-permute-start | bytes 1572872 | tf_op jit(solution)/shard_map/ppermute | solution.py:498
  80.6 22.2 %copy-start.11 = (f32[64,384]{1,0:T(8,128)}, f32[64,384]{1,0:T(8,128)S(1)}, u32[]{:S(2)}) copy-start(f32[64,384]{1,0:T(8,128)S(1)} %collective-permute-done.10.refs_1_) | copy-start | bytes 294916
  80.6 35.2 %collective-permute-start.14 = (f32[64,4096]{1,0:T(8,128)}, f32[64,4096]{1,0:T(8,128)S(1)}, u32[]{:S(2)}, u32[]{:S(2)}) collective-permute-start(f32[64,4096]{1,0:T(8,128)} %get-tuple-element.109), channel_id=1, source_target_pairs={{0,1},{1,0},{2,3},{3,2},{4,5},{5,4},{6,7},{7,6}} | collective-permute-start | bytes 3145736 | tf_op jit(solution)/shard_map/ppermute | solution.py:498
  80.8 10.9 %copy-start.10 = (f32[64,1280]{1,0:T(8,128)}, f32[64,1280]{1,0:T(8,128)S(1)}, u32[]{:S(2)}) copy-start(f32[64,1280]{1,0:T(8,128)S(1)} %collective-permute-done.11.refs_1_) | copy-start | bytes 983044
  80.8 63.7 %collective-permute-start.8 = (f32[64,4096]{1,0:T(8,128)}, f32[64,4096]{1,0:T(8,128)S(1)}, u32[]{:S(2)}, u32[]{:S(2)}) collective-permute-start(f32[64,4096]{1,0:T(8,128)} %get-tuple-element.86), channel_id=1, source_target_pairs={{0,2},{1,3},{2,0},{3,1},{4,6},{5,7},{6,4},{7,5}} | collective-permute-start | bytes 3145736 | tf_op jit(solution)/shard_map/ppermute | solution.py:498
  91.6 0.8 copy-start.4
  92.4 64.9 %collective-permute-start.9 = (f32[64,4096]{1,0:T(8,128)}, f32[64,4096]{1,0:T(8,128)S(1)}, u32[]{:S(2)}, u32[]{:S(2)}) collective-permute-start(f32[64,4096]{1,0:T(8,128)} %get-tuple-element.87), channel_id=1, source_target_pairs={{0,3},{1,2},{2,1},{3,0},{4,7},{5,6},{6,5},{7,4}} | collective-permute-start | bytes 3145736 | tf_op jit(solution)/shard_map/ppermute | solution.py:498
  102.9 13.0 %copy-start.5 = (f32[64,2048]{1,0:T(8,128)}, f32[64,2048]{1,0:T(8,128)S(1)}, u32[]{:S(2)}) copy-start(f32[64,2048]{1,0:T(8,128)S(1)} %collective-permute-done.6.refs_0_) | copy-start | bytes 1572868
  102.9 11.1 %collective-permute-start.12 = (f32[64,2048]{1,0:T(8,128)}, f32[64,2048]{1,0:T(8,128)S(1)}, u32[]{:S(2)}, u32[]{:S(2)}) collective-permute-start(f32[64,2048]{1,0:T(8,128)} %get-tuple-element.105), channel_id=1, source_target_pairs={{0,1},{1,0},{2,3},{3,2},{4,5},{5,4},{6,7},{7,6}} | collective-permute-start | bytes 1572872 | tf_op jit(solution)/shard_map/ppermute | solution.py:498
  112.4 3.5 %copy-start.6 = (f32[64,2048]{1,0:T(8,128)}, f32[64,2048]{1,0:T(8,128)S(1)}, u32[]{:S(2)}) copy-start(f32[64,2048]{1,0:T(8,128)S(1)} %collective-permute-done.7.refs_1_) | copy-start | bytes 1572868
  112.4 3.3 %collective-permute-start.13 = (f32[64,2048]{1,0:T(8,128)}, f32[64,2048]{1,0:T(8,128)S(1)}, u32[]{:S(2)}, u32[]{:S(2)}) collective-permute-start(f32[64,2048]{1,0:T(8,128)} %get-tuple-element.107), channel_id=1, source_target_pairs={{0,1},{1,0},{2,3},{3,2},{4,5},{5,4},{6,7},{7,6}} | collective-permute-start | bytes 1572872 | tf_op jit(solution)/shard_map/ppermute | solution.py:498
  113.9 3.5 %copy-start.7 = (f32[64,2048]{1,0:T(8,128)}, f32[64,2048]{1,0:T(8,128)S(1)}, u32[]{:S(2)}) copy-start(f32[64,2048]{1,0:T(8,128)S(1)} %collective-permute-done.12.refs_1_) | copy-start | bytes 1572868
  113.9 61.1 %collective-permute-start.5 = (f32[64,2048]{1,0:T(8,128)}, f32[64,2048]{1,0:T(8,128)}, u32[]{:S(2)}, u32[]{:S(2)}) collective-permute-start(f32[64,2048]{1,0:T(8,128)} %get-tuple-element.83), channel_id=1, source_target_pairs={{0,3},{1,2},{2,1},{3,0},{4,7},{5,6},{6,5},{7,4}} | collective-permute-start | bytes 1572872 | tf_op jit(solution)/shard_map/ppermute | solution.py:498
  115.7 1.8 copy-start.8
  115.7 62.9 %collective-permute-start.3 = (f32[64,1280]{1,0:T(8,128)}, f32[64,1280]{1,0:T(8,128)}, u32[]{:S(2)}, u32[]{:S(2)}) collective-permute-start(f32[64,1280]{1,0:T(8,128)} %get-tuple-element.81), channel_id=1, source_target_pairs={{0,2},{1,3},{2,0},{3,1},{4,6},{5,7},{6,4},{7,5}} | collective-permute-start | bytes 983048 | tf_op jit(solution)/shard_map/ppermute | solution.py:498
  115.9 11.0 %copy-start.3 = (f32[64,4096]{1,0:T(8,128)}, f32[64,4096]{1,0:T(8,128)S(1)}, u32[]{:S(2)}) copy-start(f32[64,4096]{1,0:T(8,128)S(1)} %collective-permute-done.14.refs_1_) | copy-start | bytes 3145732
  115.9 72.7 %collective-permute-start.1 = (f32[64,1280]{1,0:T(8,128)}, f32[64,1280]{1,0:T(8,128)S(1)}, u32[]{:S(2)}, u32[]{:S(2)}) collective-permute-start(f32[64,1280]{1,0:T(8,128)} %get-tuple-element.79), channel_id=1, source_target_pairs={{0,3},{1,2},{2,1},{3,0},{4,7},{5,6},{6,5},{7,4}} | collective-permute-start | bytes 983048 | tf_op jit(solution)/shard_map/ppermute | solution.py:498
  118.9 0.8 copy-start
  139.6 5.0 %copy-start.12 = (f32[64,384]{1,0:T(8,128)S(1)}, f32[64,384]{1,0:T(8,128)}, u32[]{:S(2)}) copy-start(f32[64,384]{1,0:T(8,128)} %get-tuple-element.78) | copy-start | bytes 294916
  139.6 17.8 %copy-start.13 = (f32[64,384]{1,0:T(8,128)S(1)}, f32[64,384]{1,0:T(8,128)}, u32[]{:S(2)}) copy-start(f32[64,384]{1,0:T(8,128)} %get-tuple-element.80) | copy-start | bytes 294916
  144.5 21.4 %copy-start.1 = (f32[64,4096]{1,0:T(8,128)}, f32[64,4096]{1,0:T(8,128)S(1)}, u32[]{:S(2)}) copy-start(f32[64,4096]{1,0:T(8,128)S(1)} %collective-permute-done.8.refs_0_) | copy-start | bytes 3145732
  144.5 47.3 %collective-permute-start = (f32[64,384]{1,0:T(8,128)S(1)}, f32[64,384]{1,0:T(8,128)S(1)}, u32[]{:S(2)}, u32[]{:S(2)}) collective-permute-start(f32[64,384]{1,0:T(8,128)S(1)} %copy-done.12), channel_id=1, source_target_pairs={{0,3},{1,2},{2,1},{3,0},{4,7},{5,6},{6,5},{7,4}} | collective-permute-start | bytes 294920 | tf_op jit(solution)/shard_map/ppermute | solution.py:498
  157.3 8.6 %copy-start.2 = (f32[64,4096]{1,0:T(8,128)}, f32[64,4096]{1,0:T(8,128)S(1)}, u32[]{:S(2)}) copy-start(f32[64,4096]{1,0:T(8,128)S(1)} %collective-permute-done.9.refs_1_) | copy-start | bytes 3145732
  157.3 30.3 %collective-permute-start.2 = (f32[64,384]{1,0:T(8,128)S(1)}, f32[64,384]{1,0:T(8,128)S(1)}, u32[]{:S(2)}, u32[]{:S(2)}) collective-permute-start(f32[64,384]{1,0:T(8,128)S(1)} %copy-done.13), channel_id=1, source_target_pairs={{0,2},{1,3},{2,0},{3,1},{4,6},{5,7},{6,4},{7,5}} | collective-permute-start | bytes 294920 | tf_op jit(solution)/shard_map/ppermute | solution.py:498
  188.6 0.7 copy-start.9

commit v14 on v13

--- a/solution.py
+++ b/solution.py
@@ -15,8 +15,8 @@
 SLOTS = 9
 FIRST = 256
 EARLY = ((256, 1), (512, 1), (1024, 1), (2048, 2))
-LATE = (4096, 2048, 2048, 1280, 384)
-LATE_UNITS = ((2048, 2), (2048, 1), (2048, 1), (1280, 1), (384, 1))
+LATE = (4096, 2048, 2432, 1024, 256)
+LATE_UNITS = ((2048, 2), (2048, 1), (2432, 1), (1024, 1), (256, 1))
 STATS = 4
 
 
@@ -513,8 +513,7 @@
         params, at_target = _merge(packs)
         out = None
         final = len(chunks) - 1
-        plan = [(k, (0, 1)) for k in range(final + 1)] + [(k, (2, 3)) for k in range(final - 1)]
-        plan += [(k, (p,)) for p in (2, 3) for k in (final - 1, final)]
+        plan = [(k, peers) for peers in ((0, 1), (2, 3)) for k in range(final + 1)]
         for i, (k, peers) in enumerate(plan):
             begin, got = chunks[k]
             blocks = [made[p] for made in got for p in peers]

time: 193 us -> 190 us (0.984)
  waiting for transfers between devices: 52.6 us -> 49.5 us
  Pallas kernels: 129 us -> 126 us
    ppermute x15, waiting for transfers between devices: 52.6 us -> 49.5 us  [swap(): return lax.ppermute(a, 'vp', [(i, i ^ p) for i in range(n_dev)])]
    pallas_call x14 -> x12, Pallas kernels: 51.3 us -> 48.5 us  [_cdf(): pl.pallas_call(functools.partial(_cdf_kernel, (peers, shard, base, widths...]
  transfers between devices with their start and end apart: 15 -> 15, of which waited for: 7 -> 8; matrix products, arithmetic and copies ran while one was open for 0% -> 0% of each run, Pallas kernels for 27% -> 26%
where the time goes in v14:
time: 190 us; the launch traced here: 188 us
  Pallas kernels  126 us (66%)
  waiting for transfers between devices  49.5 us (26%)
  starting transfers between devices  9.69 us (5%)
  local copies, waits for them, and re-layouts  2.29 us (1%)
    pallas_call x1, Pallas kernels, _logits(): pl.pallas_call(functools.partial(_logits_kernel, (n_dev, shard, segments,...  76 us
    ppermute x15, waiting for transfers between devices, swap(): return lax.ppermute(a, 'vp', [(i, i ^ p) for i in range(n_dev)])  49.5 us
    pallas_call x12, Pallas kernels, _cdf(): pl.pallas_call(functools.partial(_cdf_kernel, (peers, shard, base, widths...  48.5 us
    ppermute x15, starting transfers between devices, swap(): return lax.ppermute(a, 'vp', [(i, i ^ p) for i in range(n_dev)])  9.69 us
  transfers between devices with their start and end apart: 15, of which 8 were waited for; matrix products, arithmetic and copies ran while one was open for 0% of the time, Pallas kernels for 26%

profile of v14, /device:TPU:0, one launch (start us, length us, event | category | flops | bytes accessed | tf_op | source)
XLA Modules:
  0.0 188.3 jit_solution(4420379065773787201)
XLA Ops:
  0.6 76.0 %logits.1 = (f32[64,256]{1,0:T(8,128)}, f32[64,256]{1,0:T(8,128)}, f32[64,256]{1,0:T(8,128)}, f32[64,256]{1,0:T(8,128)}, f32[64,256]{1,0:T(8,128)}, /*index=5*/f...) custom-call(bf16[256,4096]{1,0:T(8,128)(2,1)} %x_ref.1, ...), custom_call_target="tpu_custom_call" | custom-call | flops 33554432000 | bytes 131072000 | tf_op jit(solution)/shard_map/logits/pallas_call | solution.py:310
  76.6 1.4 collective-permute-start.7
  78.1 0.7 collective-permute-start.11
  78.8 0.5 collective-permute-start.10
  79.3 1.7 collective-permute-done.10.refs_1_
  81.4 10.2 %collective-permute-done.6.refs_0_ = f32[64,2048]{1,0:T(8,128)S(1)} collective-permute-done((f32[64,2048]{1,0:T(8,128)}, f32[64,2048]{1,0:T(8,128)S(1)}, u32[]{:S(2)}, u32[]{:S(2)}) %collective-permute-start.6) | collective-permute-done | bytes 524320 | tf_op jit(solution)/shard_map/ppermute | solution.py:498
  91.6 9.5 %collective-permute-done.7.refs_1_ = f32[64,2048]{1,0:T(8,128)S(1)} collective-permute-done((f32[64,2048]{1,0:T(8,128)}, f32[64,2048]{1,0:T(8,128)S(1)}, u32[]{:S(2)}, u32[]{:S(2)}) %collective-permute-start.7) | collective-permute-done | bytes 524320 | tf_op jit(solution)/shard_map/ppermute | solution.py:498
  101.2 0.8 copy-done.5
  102.0 1.1 collective-permute-start.9
  103.5 12.8 %collective-permute-done.4.refs_0_ = f32[64,2432]{1,0:T(8,128)} collective-permute-done((f32[64,2432]{1,0:T(8,128)}, f32[64,2432]{1,0:T(8,128)}, u32[]{:S(2)}, u32[]{:S(2)}) %collective-permute-start.4) | collective-permute-done | bytes 622624 | tf_op jit(solution)/shard_map/ppermute | solution.py:498
  116.3 1.5 merge.1
  117.8 1.8 collective-permute-start.3
  119.6 0.8 copy-done
  120.3 7.2 %cdf.12 = (f32[64,64000]{1,0:T(8,128)}, f32[64,128]{1,0:T(8,128)S(1)}) custom-call(f32[64,256]{1,0:T(8,128)} %get-tuple-element.106.refs_0_, f32[64,256]{1,0:T(8,128)} %get-tuple-element.107.refs_1_, f32[64,256]{1,0:T(8,128)} %get-tuple-element.108.refs_2_, f32[64,256]{1,0:T(8,128)} %get-tuple-element.109.refs_3_, f32[64,512]{1,0:T(8,128)} %get-tuple-element.110.refs_4_, ...), custom_call_target="tpu_custom_call" | custom-call | flops 603979776 | bytes 6291456 | tf_op jit(solution)/shard_map/cdf/pallas_call | solution.py:472
  127.6 5.5 %cdf.13 = (f32[64,64000]{1,0:T(8,128)}, f32[64,128]{1,0:T(8,128)S(1)}) custom-call(f32[64,4096]{1,0:T(8,128)} %get-tuple-element.104.refs_0_, f32[64,4096]{1,0:T(8,128)} %copy-done.3, f32[64,128]{1,0:T(8,128)S(1)} %get-tuple-element.123.refs_2_, f32[64,64000]{1,0:T(8,128)} %get-tuple-element.124.refs_3_), custom_call_target="tpu_custom_call", output_to_operand_aliasing={{0}: (3, {})} | custom-call | flops 402653184 | bytes 4194304 | tf_op jit(solution)/shard_map/cdf/pallas_call | solution.py:472
  133.1 3.6 %cdf.14 = (f32[64,64000]{1,0:T(8,128)}, f32[64,128]{1,0:T(8,128)S(1)}) custom-call(f32[64,2048]{1,0:T(8,128)} %get-tuple-element.102.refs_0_, f32[64,2048]{1,0:T(8,128)} %collective-permute-done.13.refs_1_, f32[64,128]{1,0:T(8,128)S(1)} %get-tuple-element.125.refs_2_, f32[64,64000]{1,0:T(8,128)} %get-tuple-element.126.refs_3_), custom_call_target="tpu_custom_call", output_to_operand_aliasing={{0}: (3, {})} | custom-call | flops 201326592 | bytes 2097152 | tf_op jit(solution)/shard_map/cdf/pallas_call | solution.py:472
  136.7 4.0 %cdf.15 = (f32[64,64000]{1,0:T(8,128)}, f32[64,128]{1,0:T(8,128)S(1)}) custom-call(f32[64,2432]{1,0:T(8,128)} %get-tuple-element.100.refs_0_, f32[64,2432]{1,0:T(8,128)} %collective-permute-done.12.refs_1_, f32[64,128]{1,0:T(8,128)S(1)} %get-tuple-element.127.refs_2_, f32[64,64000]{1,0:T(8,128)} %get-tuple-element.128.refs_3_), custom_call_target="tpu_custom_call", output_to_operand_aliasing={{0}: (3, {})} | custom-call | flops 239075328 | bytes 2490368 | tf_op jit(solution)/shard_map/cdf/pallas_call | solution.py:472
  140.6 2.6 %cdf.16 = (f32[64,64000]{1,0:T(8,128)}, f32[64,128]{1,0:T(8,128)S(1)}) custom-call(f32[64,1024]{1,0:T(8,128)} %get-tuple-element.98.refs_0_, f32[64,1024]{1,0:T(8,128)} %copy-done.8, f32[64,128]{1,0:T(8,128)S(1)} %get-tuple-element.129.refs_2_, f32[64,64000]{1,0:T(8,128)} %get-tuple-element.130.refs_3_), custom_call_target="tpu_custom_call", output_to_operand_aliasing={{0}: (3, {})} | custom-call | flops 100663296 | bytes 1048576 | tf_op jit(solution)/shard_map/cdf/pallas_call | solution.py:472
  143.3 1.9 cdf.17
  145.1 7.2 %cdf.18 = (f32[64,64000]{1,0:T(8,128)}, f32[64,128]{1,0:T(8,128)S(1)}) custom-call(f32[64,256]{1,0:T(8,128)} %get-tuple-element.84.refs_0_, f32[64,256]{1,0:T(8,128)} %get-tuple-element.85.refs_1_, f32[64,256]{1,0:T(8,128)} %get-tuple-element.86.refs_2_, f32[64,256]{1,0:T(8,128)} %get-tuple-element.87.refs_3_, ...), custom_call_target="tpu_custom_call", output_to_operand_aliasing={{0}: (13, {})} | custom-call | flops 603979776 | bytes 6291456 | tf_op jit(solution)/shard_map/cdf/pallas_call | solution.py:472
  152.4 1.7 collective-permute-start
  154.1 5.3 %collective-permute-done.9.refs_1_ = f32[64,4096]{1,0:T(8,128)S(1)} collective-permute-done((f32[64,4096]{1,0:T(8,128)}, f32[64,4096]{1,0:T(8,128)S(1)}, u32[]{:S(2)}, u32[]{:S(2)}) %collective-permute-start.9) | collective-permute-done | bytes 1048608 | tf_op jit(solution)/shard_map/ppermute | solution.py:498
  159.4 1.5 collective-permute-start.1
  161.0 5.5 %cdf.19 = (f32[64,64000]{1,0:T(8,128)}, f32[64,128]{1,0:T(8,128)S(1)}) custom-call(f32[64,4096]{1,0:T(8,128)} %copy-done.1, f32[64,4096]{1,0:T(8,128)} %copy-done.2, f32[64,128]{1,0:T(8,128)S(1)} %get-tuple-element.135.refs_2_, f32[64,64000]{1,0:T(8,128)} %get-tuple-element.136.refs_3_), custom_call_target="tpu_custom_call", output_to_operand_aliasing={{0}: (3, {})} | custom-call | flops 402653184 | bytes 4194304 | tf_op jit(solution)/shard_map/cdf/pallas_call | solution.py:472
  166.5 3.6 %cdf.20 = (f32[64,64000]{1,0:T(8,128)}, f32[64,128]{1,0:T(8,128)S(1)}) custom-call(f32[64,2048]{1,0:T(8,128)} %copy-done.4, f32[64,2048]{1,0:T(8,128)} %copy-done.5, f32[64,128]{1,0:T(8,128)S(1)} %get-tuple-element.137.refs_2_, f32[64,64000]{1,0:T(8,128)} %get-tuple-element.138.refs_3_), custom_call_target="tpu_custom_call", output_to_operand_aliasing={{0}: (3, {})} | custom-call | flops 201326592 | bytes 2097152 | tf_op jit(solution)/shard_map/cdf/pallas_call | solution.py:472
  170.1 2.8 %collective-permute-done.5.refs_1_ = f32[64,2432]{1,0:T(8,128)} collective-permute-done((f32[64,2432]{1,0:T(8,128)}, f32[64,2432]{1,0:T(8,128)}, u32[]{:S(2)}, u32[]{:S(2)}) %collective-permute-start.5) | collective-permute-done | bytes 622624 | tf_op jit(solution)/shard_map/ppermute | solution.py:498
  172.9 4.0 %cdf.21 = (f32[64,64000]{1,0:T(8,128)}, f32[64,128]{1,0:T(8,128)S(1)}) custom-call(f32[64,2432]{1,0:T(8,128)} %collective-permute-done.4.refs_0_, f32[64,2432]{1,0:T(8,128)} %collective-permute-done.5.refs_1_, f32[64,128]{1,0:T(8,128)S(1)} %get-tuple-element.139.refs_2_, f32[64,64000]{1,0:T(8,128)} %get-tuple-element.140.refs_3_), custom_call_target="tpu_custom_call", output_to_operand_aliasing={{0}: (3, {})} | custom-call | flops 239075328 | bytes 2490368 | tf_op jit(solution)/shard_map/cdf/pallas_call | solution.py:472
  176.8 3.3 %collective-permute-done.2.refs_0_ = f32[64,1024]{1,0:T(8,128)S(1)} collective-permute-done((f32[64,1024]{1,0:T(8,128)}, f32[64,1024]{1,0:T(8,128)S(1)}, u32[]{:S(2)}, u32[]{:S(2)}) %collective-permute-start.2) | collective-permute-done | bytes 262176 | tf_op jit(solution)/shard_map/ppermute | solution.py:498
  180.1 3.9 %collective-permute-done.3.refs_1_ = f32[64,1024]{1,0:T(8,128)S(1)} collective-permute-done((f32[64,1024]{1,0:T(8,128)}, f32[64,1024]{1,0:T(8,128)S(1)}, u32[]{:S(2)}, u32[]{:S(2)}) %collective-permute-start.3) | collective-permute-done | bytes 262176 | tf_op jit(solution)/shard_map/ppermute | solution.py:498
  184.0 0.7 copy-done.7
  184.7 2.6 %cdf.22 = (f32[64,64000]{1,0:T(8,128)}, f32[64,128]{1,0:T(8,128)S(1)}) custom-call(f32[64,1024]{1,0:T(8,128)} %copy-done.6, f32[64,1024]{1,0:T(8,128)} %copy-done.7, f32[64,128]{1,0:T(8,128)S(1)} %get-tuple-element.141.refs_2_, f32[64,64000]{1,0:T(8,128)} %get-tuple-element.142.refs_3_), custom_call_target="tpu_custom_call", output_to_operand_aliasing={{0}: (3, {})} | custom-call | flops 100663296 | bytes 1048576 | tf_op jit(solution)/shard_map/cdf/pallas_call | solution.py:472
  187.3 1.0 cdf.23
  (36 shorter events, 0.9 us)
Async XLA Ops:
  76.6 15.0 %collective-permute-start.6 = (f32[64,2048]{1,0:T(8,128)}, f32[64,2048]{1,0:T(8,128)S(1)}, u32[]{:S(2)}, u32[]{:S(2)}) collective-permute-start(f32[64,2048]{1,0:T(8,128)} %get-tuple-element.80), channel_id=1, source_target_pairs={{0,2},{1,3},{2,0},{3,1},{4,6},{5,7},{6,4},{7,5}} | collective-permute-start | bytes 1572872 | tf_op jit(solution)/shard_map/ppermute | solution.py:498
  76.6 24.5 %collective-permute-start.7 = (f32[64,2048]{1,0:T(8,128)}, f32[64,2048]{1,0:T(8,128)S(1)}, u32[]{:S(2)}, u32[]{:S(2)}) collective-permute-start(f32[64,2048]{1,0:T(8,128)} %get-tuple-element.81), channel_id=1, source_target_pairs={{0,3},{1,2},{2,1},{3,0},{4,7},{5,6},{6,5},{7,4}} | collective-permute-start | bytes 1572872 | tf_op jit(solution)/shard_map/ppermute | solution.py:498
  78.1 3.3 %collective-permute-start.11 = (f32[64,1024]{1,0:T(8,128)}, f32[64,1024]{1,0:T(8,128)S(1)}, u32[]{:S(2)}, u32[]{:S(2)}) collective-permute-start(f32[64,1024]{1,0:T(8,128)} %get-tuple-element.99), channel_id=1, source_target_pairs={{0,1},{1,0},{2,3},{3,2},{4,5},{5,4},{6,7},{7,6}} | collective-permute-start | bytes 786440 | tf_op jit(solution)/shard_map/ppermute | solution.py:498
  78.8 24.3 %collective-permute-start.13 = (f32[64,2048]{1,0:T(8,128)}, f32[64,2048]{1,0:T(8,128)}, u32[]{:S(2)}, u32[]{:S(2)}) collective-permute-start(f32[64,2048]{1,0:T(8,128)} %get-tuple-element.103), channel_id=1, source_target_pairs={{0,1},{1,0},{2,3},{3,2},{4,5},{5,4},{6,7},{7,6}} | collective-permute-start | bytes 1572872 | tf_op jit(solution)/shard_map/ppermute | solution.py:498
  78.8 2.3 %collective-permute-start.10 = (f32[64,256]{1,0:T(8,128)}, f32[64,256]{1,0:T(8,128)S(1)}, u32[]{:S(2)}, u32[]{:S(2)}) collective-permute-start(f32[64,256]{1,0:T(8,128)} %get-tuple-element.97), channel_id=1, source_target_pairs={{0,1},{1,0},{2,3},{3,2},{4,5},{5,4},{6,7},{7,6}} | collective-permute-start | bytes 196616 | tf_op jit(solution)/shard_map/ppermute | solution.py:498
  81.0 62.2 %copy-start.9 = (f32[64,256]{1,0:T(8,128)}, f32[64,256]{1,0:T(8,128)S(1)}, u32[]{:S(2)}) copy-start(f32[64,256]{1,0:T(8,128)S(1)} %collective-permute-done.10.refs_1_) | copy-start | bytes 196612
  81.0 36.8 %collective-permute-start.14 = (f32[64,4096]{1,0:T(8,128)}, f32[64,4096]{1,0:T(8,128)S(1)}, u32[]{:S(2)}, u32[]{:S(2)}) collective-permute-start(f32[64,4096]{1,0:T(8,128)} %get-tuple-element.105), channel_id=1, source_target_pairs={{0,1},{1,0},{2,3},{3,2},{4,5},{5,4},{6,7},{7,6}} | collective-permute-start | bytes 3145736 | tf_op jit(solution)/shard_map/ppermute | solution.py:498
  81.4 59.2 %copy-start.8 = (f32[64,1024]{1,0:T(8,128)}, f32[64,1024]{1,0:T(8,128)S(1)}, u32[]{:S(2)}) copy-start(f32[64,1024]{1,0:T(8,128)S(1)} %collective-permute-done.11.refs_1_) | copy-start | bytes 786436
  81.4 34.9 %collective-permute-start.4 = (f32[64,2432]{1,0:T(8,128)}, f32[64,2432]{1,0:T(8,128)}, u32[]{:S(2)}, u32[]{:S(2)}) collective-permute-start(f32[64,2432]{1,0:T(8,128)} %get-tuple-element.78), channel_id=1, source_target_pairs={{0,2},{1,3},{2,0},{3,1},{4,6},{5,7},{6,4},{7,5}} | collective-permute-start | bytes 1867784 | tf_op jit(solution)/shard_map/ppermute | solution.py:498
  91.6 9.5 %copy-start.4 = (f32[64,2048]{1,0:T(8,128)}, f32[64,2048]{1,0:T(8,128)S(1)}, u32[]{:S(2)}) copy-start(f32[64,2048]{1,0:T(8,128)S(1)} %collective-permute-done.6.refs_0_) | copy-start | bytes 1572868
  91.6 60.7 %collective-permute-start.8 = (f32[64,4096]{1,0:T(8,128)}, f32[64,4096]{1,0:T(8,128)S(1)}, u32[]{:S(2)}, u32[]{:S(2)}) collective-permute-start(f32[64,4096]{1,0:T(8,128)} %get-tuple-element.82), channel_id=1, source_target_pairs={{0,2},{1,3},{2,0},{3,1},{4,6},{5,7},{6,4},{7,5}} | collective-permute-start | bytes 3145736 | tf_op jit(solution)/shard_map/ppermute | solution.py:498
  101.1 0.8 copy-start.5
  102.0 57.5 %collective-permute-start.9 = (f32[64,4096]{1,0:T(8,128)}, f32[64,4096]{1,0:T(8,128)S(1)}, u32[]{:S(2)}, u32[]{:S(2)}) collective-permute-start(f32[64,4096]{1,0:T(8,128)} %get-tuple-element.83), channel_id=1, source_target_pairs={{0,3},{1,2},{2,1},{3,0},{4,7},{5,6},{6,5},{7,4}} | collective-permute-start | bytes 3145736 | tf_op jit(solution)/shard_map/ppermute | solution.py:498
  103.1 14.7 %collective-permute-start.12 = (f32[64,2432]{1,0:T(8,128)}, f32[64,2432]{1,0:T(8,128)}, u32[]{:S(2)}, u32[]{:S(2)}) collective-permute-start(f32[64,2432]{1,0:T(8,128)} %get-tuple-element.101), channel_id=1, source_target_pairs={{0,1},{1,0},{2,3},{3,2},{4,5},{5,4},{6,7},{7,6}} | collective-permute-start | bytes 1867784 | tf_op jit(solution)/shard_map/ppermute | solution.py:498
  116.3 56.6 %collective-permute-start.5 = (f32[64,2432]{1,0:T(8,128)}, f32[64,2432]{1,0:T(8,128)}, u32[]{:S(2)}, u32[]{:S(2)}) collective-permute-start(f32[64,2432]{1,0:T(8,128)} %get-tuple-element.79), channel_id=1, source_target_pairs={{0,3},{1,2},{2,1},{3,0},{4,7},{5,6},{6,5},{7,4}} | collective-permute-start | bytes 1867784 | tf_op jit(solution)/shard_map/ppermute | solution.py:498
  117.8 62.3 %collective-permute-start.2 = (f32[64,1024]{1,0:T(8,128)}, f32[64,1024]{1,0:T(8,128)S(1)}, u32[]{:S(2)}, u32[]{:S(2)}) collective-permute-start(f32[64,1024]{1,0:T(8,128)} %get-tuple-element.76), channel_id=1, source_target_pairs={{0,2},{1,3},{2,0},{3,1},{4,6},{5,7},{6,4},{7,5}} | collective-permute-start | bytes 786440 | tf_op jit(solution)/shard_map/ppermute | solution.py:498
  117.8 9.8 %copy-start.3 = (f32[64,4096]{1,0:T(8,128)}, f32[64,4096]{1,0:T(8,128)S(1)}, u32[]{:S(2)}) copy-start(f32[64,4096]{1,0:T(8,128)S(1)} %collective-permute-done.14.refs_1_) | copy-start | bytes 3145732
  117.8 66.2 %collective-permute-start.3 = (f32[64,1024]{1,0:T(8,128)}, f32[64,1024]{1,0:T(8,128)S(1)}, u32[]{:S(2)}, u32[]{:S(2)}) collective-permute-start(f32[64,1024]{1,0:T(8,128)} %get-tuple-element.77), channel_id=1, source_target_pairs={{0,3},{1,2},{2,1},{3,0},{4,7},{5,6},{6,5},{7,4}} | collective-permute-start | bytes 786440 | tf_op jit(solution)/shard_map/ppermute | solution.py:498
  119.6 0.8 copy-start
  143.2 9.2 %copy-start.11 = (f32[64,256]{1,0:T(8,128)S(1)}, f32[64,256]{1,0:T(8,128)}, u32[]{:S(2)}) copy-start(f32[64,256]{1,0:T(8,128)} %get-tuple-element.74) | copy-start | bytes 196612
  143.2 16.2 %copy-start.10 = (f32[64,256]{1,0:T(8,128)S(1)}, f32[64,256]{1,0:T(8,128)}, u32[]{:S(2)}) copy-start(f32[64,256]{1,0:T(8,128)} %get-tuple-element.75) | copy-start | bytes 196612
  152.4 8.6 %copy-start.1 = (f32[64,4096]{1,0:T(8,128)}, f32[64,4096]{1,0:T(8,128)S(1)}, u32[]{:S(2)}) copy-start(f32[64,4096]{1,0:T(8,128)S(1)} %collective-permute-done.8.refs_0_) | copy-start | bytes 3145732
  152.4 34.9 %collective-permute-start = (f32[64,256]{1,0:T(8,128)S(1)}, f32[64,256]{1,0:T(8,128)S(1)}, u32[]{:S(2)}, u32[]{:S(2)}) collective-permute-start(f32[64,256]{1,0:T(8,128)S(1)} %copy-done.11), channel_id=1, source_target_pairs={{0,2},{1,3},{2,0},{3,1},{4,6},{5,7},{6,4},{7,5}} | collective-permute-start | bytes 196616 | tf_op jit(solution)/shard_map/ppermute | solution.py:498
  159.4 1.6 copy-start.2
  159.4 27.9 %collective-permute-start.1 = (f32[64,256]{1,0:T(8,128)S(1)}, f32[64,256]{1,0:T(8,128)S(1)}, u32[]{:S(2)}, u32[]{:S(2)}) collective-permute-start(f32[64,256]{1,0:T(8,128)S(1)} %copy-done.10), channel_id=1, source_target_pairs={{0,3},{1,2},{2,1},{3,0},{4,7},{5,6},{6,5},{7,4}} | collective-permute-start | bytes 196616 | tf_op jit(solution)/shard_map/ppermute | solution.py:498
  180.1 3.9 %copy-start.6 = (f32[64,1024]{1,0:T(8,128)}, f32[64,1024]{1,0:T(8,128)S(1)}, u32[]{:S(2)}) copy-start(f32[64,1024]{1,0:T(8,128)S(1)} %collective-permute-done.2.refs_0_) | copy-start | bytes 786436
  184.0 0.7 copy-start.7
